TPU v7x, 256 devices: a whole 4x4x8 slice. The times are simulated.
256 devices in a mesh: gx: 16 (over z, core), gy: 4 (over x), gz: 4 (over y).
Axes of the slice: x: 4, y: 4, z: 8, core: 2. Of those that a mesh axis runs over, the one named last changes fastest.
Arguments:
- velocity: float32 [3, 1024, 128, 512], P(None, 'gx', 'gz', 'gy'), may hold values from -6 to 6
- tile_turbine: int32 [16, 4, 4, 2], P('gx', 'gz', 'gy'), may hold values from 0 to 63
- tile_plane: int32 [16, 4, 4, 2], P('gx', 'gz', 'gy'), may hold values from 0 to 63
- tile_weight: bfloat16 [16, 4, 4, 2, 384, 4096], P('gx', 'gz', 'gy'), may hold values from -0.09375 to 0.09375
- chord: float32 [64, 384], replicated, may hold values from 0.25 to 1
Outputs:
- predicted: float32 [3, 1024, 128, 512], P(None, 'gx', 'gz', 'gy')
- forces: float32 [64, 1152], replicated
All inputs are finite; a program needn't handle non-finite values.
Results may differ from a plain program's by a relative error of at most 0.0032.
Values sent between devices are 32-bit elements; how exact they have to be, the bound alone decides.
No kernel may reach another device: no remote copies, remote signals or barrier semaphores. Data moves between devices by JAX's collectives and lax.ppermute only.
A program may use at most 128 MiB of HBM per device.

v0:
```python
import jax
import jax.numpy as jnp
from jax import lax
from jax.sharding import PartitionSpec as P

DIRS = (-3, -1, -2)


def padded_2(block, sides, width):
    for axis, dim in sides:
        count = lax.axis_size(axis)
        forward = [(i, i + 1) for i in range(count - 1)]
        backward = [(target, source) for source, target in forward]
        low = lax.ppermute(
            lax.slice_in_dim(block, block.shape[dim] - width, None, axis=dim), axis, forward
        )
        high = lax.ppermute(lax.slice_in_dim(block, 0, width, axis=dim), axis, backward)
        block = jnp.concatenate([low, block, high], axis=dim)
    return block


def shifted(p, axis, step):
    idx = [slice(1, -1), slice(1, -1), slice(1, -1)]
    idx[axis + 3] = slice(1 + step, p.shape[axis] - 1 + step)
    lead = [slice(None)] * (p.ndim - 3)
    return p[tuple(lead + idx)]


def strain_viscosity(p):
    grads = [
        [0.5 * (shifted(p[c], DIRS[d], 1) - shifted(p[c], DIRS[d], -1)) for d in range(3)]
        for c in range(3)
    ]
    total = jnp.zeros_like(grads[0][0])
    for c in range(3):
        for d in range(3):
            strain = 0.5 * (grads[c][d] + grads[d][c])
            total = total + strain * strain
    return 0.05 + 1.0 * jnp.sqrt(2.0 * total + 1e-06)


def advance(padded, nu_padded):
    nu_here = shifted(nu_padded, -1, 0)
    result = []
    for c in range(3):
        center = shifted(padded[c], -1, 0)
        advect = jnp.zeros_like(center)
        spread = jnp.zeros_like(center)
        for d in range(3):
            upper = shifted(padded[c], DIRS[d], 1)
            lower = shifted(padded[c], DIRS[d], -1)
            advect = advect + shifted(padded[d], -1, 0) * 0.5 * (upper - lower)
            nu_up = 0.5 * (nu_here + shifted(nu_padded, DIRS[d], 1))
            nu_low = 0.5 * (nu_here + shifted(nu_padded, DIRS[d], -1))
            spread = spread + nu_up * (upper - center) - nu_low * (center - lower)
        result.append(center + 0.25 * (spread - advect))
    return jnp.stack(result)


def actuate(velocity_probe, coef):
    rows = velocity_probe.shape[0]
    parts = velocity_probe.reshape(rows, 3, -1)
    magnitude = jnp.sqrt(jnp.sum(parts * parts, axis=1) + 1e-06)
    return (-2.0 * coef[:, None, :] * magnitude[:, None, :] * parts).reshape(rows, -1)


def body(velocity, tile_turbine, tile_plane, tile_weight, chord):
    cx = velocity.shape[1]
    vertical_coord = velocity.shape[2]
    spanwise_coord = velocity.shape[3]
    tile_count = tile_turbine.shape[3]
    actuator_count = tile_weight.shape[4]
    nturb = chord.shape[0]
    turbine_list = tile_turbine.reshape(tile_count)
    rotor_planes = tile_plane.reshape(tile_count)
    spread_weights = tile_weight.reshape(
        tile_count, actuator_count, vertical_coord * spanwise_coord
    )
    flat = velocity.reshape(3, cx, vertical_coord * spanwise_coord)
    picks = (rotor_planes[:, None] == jnp.arange(cx, dtype=jnp.int32)[None, :]).astype(jnp.float32)
    tiles = jnp.einsum("sx,cxq->scq", picks, flat, precision=lax.Precision.HIGHEST).astype(
        jnp.bfloat16
    )
    block_local = jnp.einsum(
        "spq,scq->scp", spread_weights, tiles, preferred_element_type=jnp.float32
    )
    owning_block = (turbine_list[:, None] == jnp.arange(nturb, dtype=jnp.int32)[None, :]).astype(
        jnp.float32
    )
    partial_sample = jnp.einsum(
        "yr,yw->rw",
        owning_block,
        block_local.reshape(tile_count, -1),
        precision=lax.Precision.HIGHEST,
    )
    rows = lax.axis_size("gx")
    per_row = nturb // rows
    received = lax.all_to_all(
        partial_sample.reshape(rows, per_row, -1), "gx", split_axis=0, concat_axis=0, tiled=True
    )
    owned = lax.psum(jnp.sum(received, axis=0), ("gy", "gz"))
    owned_coef = lax.dynamic_slice_in_dim(chord, lax.axis_index("gx") * per_row, per_row, 0)
    forces = lax.all_gather(actuate(owned, owned_coef), "gx", axis=0, tiled=True)
    tile_force = jnp.dot(owning_block, forces, precision=lax.Precision.HIGHEST).astype(jnp.bfloat16)
    forces_sent = jnp.einsum(
        "axz,ahx->ahz",
        spread_weights,
        tile_force.reshape(tile_count, 3, actuator_count),
        preferred_element_type=jnp.float32,
    )
    impulse = jnp.einsum(
        "sx,scq->cxq", picks, forces_sent, precision=lax.Precision.HIGHEST
    ).reshape(3, cx, vertical_coord, spanwise_coord)
    padded = padded_2(velocity, (("gx", 1), ("gy", 3), ("gz", 2)), 1)
    viscosity = strain_viscosity(padded)
    nu_padded = padded_2(viscosity, (("gx", 0), ("gy", 2), ("gz", 1)), 1)
    predicted = advance(padded, nu_padded) + impulse
    return (predicted, forces)


def solution(mesh):
    placed = (
        P(None, "gx", "gz", "gy"),
        P("gx", "gz", "gy", None),
        P("gx", "gz", "gy", None),
        P("gx", "gz", "gy", None, None, None),
        P(),
    )
    return jax.shard_map(
        body,
        mesh=mesh,
        in_specs=placed,
        out_specs=(P(None, "gx", "gz", "gy"), P()),
        check_vma=False,
    )
```

profile of v0, /device:TPU:1, one launch (start us, length us, event | category | flops | bytes accessed | tf_op | source)
XLA Modules:
  0.0 237.4 jit_solution(2430142811792057786)
XLA Ops:
  1.5 4.9 %collective-permute-start = (f32[3,1,32,128]{3,2,1,0:T(8,128)S(1)}, f32[3,1,32,128]{3,2,1,0:T(8,128)S(1)}, u32[]{:S(2)}, u32[]{:S(2)}) collective-permute-start(f32[3,1,32,128]{3,2,1,0:T(8,128)S(1)} %get-tuple-element.16), channel_id=1, source_target_pairs={{0,16},{16,32},{32,48},{48,64},{64,80},{80,96},{96,112},{112,128},... | collective-permute-start | bytes 147464 | tf_op jit(solution)/shard_map/ppermute | solution.py:14
  11.8 3.9 %fusion.30 = (f32[3,66,32,1]{3,2,1,0:T(8,128)}, f32[3,66,32,1]{3,2,1,0:T(8,128)}) fusion(f32[3,66,32,128]{3,2,1,0:T(8,128)S(1)} %constant_dynamic-update-slice_fusion), kind=kLoop, calls=%fused_computation.87 | loop fusion | bytes 101376 | tf_op jit(solution)/shard_map/slice | solution.py:15
  15.7 2.8 %copy.29 = f32[3,66,32,1]{1,2,3,0:T(8,128)S(1)} copy(f32[3,66,32,1]{3,2,1,0:T(8,128)} %get-tuple-element.13) | data formatting | bytes 50688 | tf_op jit(solution)/shard_map/slice | solution.py:15
  18.5 3.1 %collective-permute-start.2 = (f32[3,66,32,1]{1,2,3,0:T(8,128)S(1)}, f32[3,66,32,1]{1,2,3,0:T(8,128)S(1)}, u32[]{:S(2)}, u32[]{:S(2)}) collective-permute-start(f32[3,66,32,1]{1,2,3,0:T(8,128)S(1)} %copy.29), channel_id=1, source_target_pairs={{0,4},{4,8},{8,12},{1,5},{5,9},{9,13},{2,6},{6,10},{10,14},{3,7},{... | collective-permute-start | bytes 76040 | tf_op jit(solution)/shard_map/ppermute | solution.py:14
  21.6 2.8 %copy.30 = f32[3,66,32,1]{1,2,3,0:T(8,128)S(1)} copy(f32[3,66,32,1]{3,2,1,0:T(8,128)} %get-tuple-element.14) | data formatting | bytes 50688 | tf_op jit(solution)/shard_map/slice | solution.py:17
  25.7 4.6 %reshape.47 = f32[3,64,4096]{2,1,0:T(8,128)} reshape(f32[3,64,32,128]{3,2,1,0:T(8,128)} %param.5) | data formatting | bytes 6291456 | tf_op jit(solution)/shard_map/reshape | solution.py:79
  30.3 2.7 %copy.31 = f32[3,66,32,1]{3,2,1,0:T(8,128)} copy(f32[3,66,32,1]{1,2,3,0:T(8,128)S(1)} %collective-permute-done.2) | data formatting | bytes 50688 | tf_op jit(solution)/shard_map/ppermute | solution.py:14
  33.0 2.7 %copy.32 = f32[3,66,32,1]{3,2,1,0:T(8,128)} copy(f32[3,66,32,1]{1,2,3,0:T(8,128)S(1)} %collective-permute-done.3) | data formatting | bytes 50688 | tf_op jit(solution)/shard_map/ppermute | solution.py:17
  35.7 3.4 %pad_maximum_fusion.22 = (f32[3,66,1,130]{3,2,1,0:T(1,128)S(1)}, f32[3,66,1,130]{3,2,1,0:T(1,128)S(1)}) fusion(f32[3,66,32,1]{3,2,1,0:T(8,128)} %copy.32, f32[3,66,32,128]{3,2,1,0:T(8,128)S(1)} %constant_dynamic-update-slice_fusion, f32[3,66,32,1]{3,2,1,0:T(8,128)} %copy.31), kind=kLoop, calls=%fused_computation.60 | loop fusion | flops 102960 | bytes 3500640 | tf_op jit(solution)/shard_map/slice | solution.py:15
  39.1 3.3 %collective-permute-start.4 = (f32[3,66,1,130]{3,2,1,0:T(1,128)S(1)}, f32[3,66,1,130]{3,2,1,0:T(1,128)S(1)}, u32[]{:S(2)}, u32[]{:S(2)}) collective-permute-start(f32[3,66,1,130]{3,2,1,0:T(1,128)S(1)} %get-tuple-element.6), channel_id=1, source_target_pairs={{0,1},{1,2},{2,3},{4,5},{5,6},{6,7},{8,9},{9,10},{10,11},{12,13},{... | collective-permute-start | bytes 308888 | tf_op jit(solution)/shard_map/ppermute | solution.py:14
  45.8 4.1 %collective-permute-done.5 = f32[3,66,1,130]{3,2,1,0:T(1,128)S(1)} collective-permute-done((f32[3,66,1,130]{3,2,1,0:T(1,128)S(1)}, f32[3,66,1,130]{3,2,1,0:T(1,128)S(1)}, u32[]{:S(2)}, u32[]{:S(2)}) %collective-permute-start.5) | collective-permute-done | bytes 102992 | tf_op jit(solution)/shard_map/ppermute | solution.py:17
  49.9 4.0 %pad_maximum_fusion = f32[3,66,34,130]{3,2,1,0:T(8,128)S(1)} fusion(f32[3,66,1,130]{3,2,1,0:T(1,128)S(1)} %collective-permute-done.5, f32[3,66,32,1]{3,2,1,0:T(8,128)S(1)} %copy-done.7, f32[3,66,32,128]{3,2,1,0:T(8,128)S(1)} %constant_dynamic-update-slice_fusion, f32[3,66,32,1]{3,2,1,0:T(8,128)S(1)} %copy-done.6, f32[3,66,1,130]{3,2,1,0:T(1,128)S(1)} %collective-permute-done.4), kind=kLoop, calls=%fused_computation | loop fusion | flops 3500640 | bytes 7001280 | tf_op jit(solution)/shard_map/concatenate | solution.py:18
  54.5 4.8 %sqrt_add_fusion = f32[64,32,128]{2,1,0:T(8,128)S(1)} fusion(f32[66,34,130]{2,1,0:T(8,128)S(1)} %get-tuple-element.10, f32[66,34,130]{2,1,0:T(8,128)S(1)} %get-tuple-element.8, f32[66,34,130]{2,1,0:T(8,128)S(1)} %get-tuple-element.9), kind=kLoop, calls=%fused_computation.45 | loop fusion | flops 9961472 | bytes 19922944 | tf_op jit(solution)/shard_map/add | solution.py:39
  61.2 5.5 %collective-permute-start.7 = (f32[1,32,128]{2,1,0:T(8,128)S(1)}, f32[1,32,128]{2,1,0:T(8,128)S(1)}, u32[]{:S(2)}, u32[]{:S(2)}) collective-permute-start(f32[1,32,128]{2,1,0:T(8,128)S(1)} %get-tuple-element.19), channel_id=1, source_target_pairs={{0,16},{16,32},{32,48},{48,64},{64,80},{80,96},{96,112},{112,128},... | collective-permute-start | bytes 49160 | tf_op jit(solution)/shard_map/ppermute | solution.py:14
  66.8 4.5 %fusion.2 = f32[2,3,384]{2,1,0:T(4,128)S(1)} fusion(bf16[1,1,1,2,384,4096]{5,4,3,2,1,0:T(8,128)(2,1)} %param.8, bf16[2,3,4096]{2,0,1:T(2,128)(2,1)S(1)} %convolution_convert_fusion), kind=kOutput, calls=%fused_computation.3 | convolution fusion | flops 18874368 | bytes 6349824 | tf_op jit(solution)/shard_map/spq,scq->scp/dot_general | solution.py:84
  78.2 4.6 %collective-permute-start.9 = (f32[66,32,1]{0,1,2:T(8,128)S(1)}, f32[66,32,1]{0,1,2:T(8,128)S(1)}, u32[]{:S(2)}, u32[]{:S(2)}) collective-permute-start(f32[66,32,1]{0,1,2:T(8,128)S(1)} %copy.35), channel_id=1, source_target_pairs={{0,4},{4,8},{8,12},{1,5},{5,9},{9,13},{2,6},{6,10},{10,14},{3,7},{... | collective-permute-start | bytes 25352 | tf_op jit(solution)/shard_map/ppermute | solution.py:14
  89.8 4.0 %collective-permute-start.11 = (f32[66,1,130]{2,1,0:T(1,128)S(1)}, f32[66,1,130]{2,1,0:T(1,128)S(1)}, u32[]{:S(2)}, u32[]{:S(2)}) collective-permute-start(f32[66,1,130]{2,1,0:T(1,128)S(1)} %get-tuple-element.11), channel_id=1, source_target_pairs={{0,1},{1,2},{2,3},{4,5},{5,6},{6,7},{8,9},{9,10},{10,11},{12,13},{... | collective-permute-start | bytes 102968 | tf_op jit(solution)/shard_map/ppermute | solution.py:14
  95.1 7.6 %all-to-all-start = ((f32[16,4,1152]{2,1,0:T(4,128)}), f32[16,4,1152]{2,1,0:T(4,128)S(1)}, u32[]{:S(2)}, u32[]{:S(2)}) async-start(f32[16,4,1152]{2,1,0:T(4,128)} %copy.40), calls=%async_computation | async-start | bytes 589824 | tf_op jit(solution)/shard_map/all_to_all | solution.py:98
  102.7 17.9 %add_bitcast_fusion.2 = f32[1,64,32,128]{3,2,1,0:T(8,128)} fusion(f32[66,34,130]{2,1,0:T(8,128)} %copy-done.2, f32[66,34,130]{2,1,0:T(8,128)S(1)} %get-tuple-element.8, f32[66,34,130]{2,1,0:T(8,128)} %copy-done, f32[64,32,128]{2,1,0:T(8,128)} %copy-done.4, f32[1,32,128]{2,1,0:T(8,128)S(1)} %collective-permute-done.6, ...), kind=kLoop, calls=%fused_computation.44 | loop fusion | flops 15990784 | bytes 11652640 | tf_op jit(solution)/shard_map/stack | solution.py:57
  120.7 7.1 %add_bitcast_fusion.1 = f32[1,64,32,128]{3,2,1,0:T(8,128)} fusion(f32[66,34,130]{2,1,0:T(8,128)S(1)} %get-tuple-element.8, f32[66,34,130]{2,1,0:T(8,128)S(1)} %copy-done.3, f32[66,34,130]{2,1,0:T(8,128)S(1)} %copy-done.1, f32[64,32,128]{2,1,0:T(8,128)S(1)} %copy-done.5, f32[1,32,128]{2,1,0:T(8,128)S(1)} %collective-permute-done.6, ...), kind=kLoop, calls=%fused_computation.43 | loop fusion | flops 15990784 | bytes 11652640 | tf_op jit(solution)/shard_map/stack | solution.py:57
  127.9 7.1 %add_bitcast_fusion = f32[1,64,32,128]{3,2,1,0:T(8,128)} fusion(f32[66,34,130]{2,1,0:T(8,128)S(1)} %copy-done.1, f32[66,34,130]{2,1,0:T(8,128)S(1)} %copy-done.3, f32[66,34,130]{2,1,0:T(8,128)S(1)} %get-tuple-element.8, f32[64,32,128]{2,1,0:T(8,128)S(1)} %copy-done.5, f32[1,32,128]{2,1,0:T(8,128)S(1)} %collective-permute-done.6, ...), kind=kLoop, calls=%fused_computation.42 | loop fusion | flops 15990784 | bytes 11652640 | tf_op jit(solution)/shard_map/stack | solution.py:57
  135.0 59.5 %psum.7 = f32[4,1152]{1,0:T(4,128)S(1)} all-reduce(f32[4,1152]{1,0:T(4,128)S(1)} %reduce_sum.18), channel_id=1, replica_groups=mesh['gx'=16,'gy'=4,'gz'=4] {'gy','gz'}, use_global_device_ids=true, to_apply=%region_1.0 | all-reduce | flops 4608 | bytes 36864 | tf_op jit(solution)/shard_map/psum | solution.py:101
  195.3 32.2 %all-gather = f32[16,4,1152]{2,1,0:T(4,128)S(1)} all-gather(f32[1,4,1152]{2,1,0:T(4,128)S(1)} %multiply_bitcast_fusion), channel_id=1, replica_groups=mesh['gx'=16,'gy'=4,'gz'=4] {'gx'}, dimensions={0}, use_global_device_ids=true | all-gather | bytes 313344 | tf_op jit(solution)/shard_map/all_gather | solution.py:103
  227.9 3.7 %fusion = f32[2,3,4096]{2,1,0:T(4,128)S(1)} fusion(bf16[2,3,384]{2,1,0:T(4,128)(2,1)S(1)} %reshape.50, bf16[1,1,1,2,384,4096]{5,4,3,2,1,0:T(8,128)(2,1)} %param.8), kind=kOutput, calls=%fused_computation.1 | convolution fusion | flops 18874368 | bytes 6394368 | tf_op jit(solution)/shard_map/axz,ahx->ahz/dot_general | solution.py:105
  (82 shorter events, 35.3 us)
Async XLA Ops:
  1.5 6.9 %collective-permute-start = (f32[3,1,32,128]{3,2,1,0:T(8,128)S(1)}, f32[3,1,32,128]{3,2,1,0:T(8,128)S(1)}, u32[]{:S(2)}, u32[]{:S(2)}) collective-permute-start(f32[3,1,32,128]{3,2,1,0:T(8,128)S(1)} %get-tuple-element.16), channel_id=1, source_target_pairs={{0,16},{16,32},{32,48},{48,64},{64,80},{80,96},{96,112},{112,128},... | collective-permute-start | bytes 147464 | tf_op jit(solution)/shard_map/ppermute | solution.py:14
  6.4 5.4 %collective-permute-start.1 = (f32[3,1,32,128]{3,2,1,0:T(8,128)S(1)}, f32[3,1,32,128]{3,2,1,0:T(8,128)S(1)}, u32[]{:S(2)}, u32[]{:S(2)}) collective-permute-start(f32[3,1,32,128]{3,2,1,0:T(8,128)S(1)} %get-tuple-element.15), channel_id=1, source_target_pairs={{16,0},{32,16},{48,32},{64,48},{80,64},{96,80},{112,96},{128,112},... | collective-permute-start | bytes 147464 | tf_op jit(solution)/shard_map/ppermute | solution.py:17
  18.5 11.8 %collective-permute-start.2 = (f32[3,66,32,1]{1,2,3,0:T(8,128)S(1)}, f32[3,66,32,1]{1,2,3,0:T(8,128)S(1)}, u32[]{:S(2)}, u32[]{:S(2)}) collective-permute-start(f32[3,66,32,1]{1,2,3,0:T(8,128)S(1)} %copy.29), channel_id=1, source_target_pairs={{0,4},{4,8},{8,12},{1,5},{5,9},{9,13},{2,6},{6,10},{10,14},{3,7},{... | collective-permute-start | bytes 76040 | tf_op jit(solution)/shard_map/ppermute | solution.py:14
  24.4 8.6 %collective-permute-start.3 = (f32[3,66,32,1]{1,2,3,0:T(8,128)S(1)}, f32[3,66,32,1]{1,2,3,0:T(8,128)S(1)}, u32[]{:S(2)}, u32[]{:S(2)}) collective-permute-start(f32[3,66,32,1]{1,2,3,0:T(8,128)S(1)} %copy.30), channel_id=1, source_target_pairs={{4,0},{8,4},{12,8},{5,1},{9,5},{13,9},{6,2},{10,6},{14,10},{7,3},{... | collective-permute-start | bytes 76040 | tf_op jit(solution)/shard_map/ppermute | solution.py:17
  35.7 8.1 %copy-start.10 = (f32[3,64,4096]{2,1,0:T(8,128)S(1)}, f32[3,64,4096]{2,1,0:T(8,128)}, u32[]{:S(2)}) copy-start(f32[3,64,4096]{2,1,0:T(8,128)} %reshape.47) | copy-start | bytes 9437188
  35.7 8.1 %copy-start.16 = (s32[1,1,1,2]{3,2,1,0:T(1,128)S(1)}, s32[1,1,1,2]{3,2,1,0:T(1,128)}, u32[]{:S(2)}) copy-start(s32[1,1,1,2]{3,2,1,0:T(1,128)} %param.7) | copy-start | bytes 28
  35.7 14.2 %copy-start.6 = (f32[3,66,32,1]{3,2,1,0:T(8,128)S(1)}, f32[3,66,32,1]{3,2,1,0:T(8,128)}, u32[]{:S(2)}) copy-start(f32[3,66,32,1]{3,2,1,0:T(8,128)} %copy.31) | copy-start | bytes 76036
  35.7 14.2 %copy-start.7 = (f32[3,66,32,1]{3,2,1,0:T(8,128)S(1)}, f32[3,66,32,1]{3,2,1,0:T(8,128)}, u32[]{:S(2)}) copy-start(f32[3,66,32,1]{3,2,1,0:T(8,128)} %copy.32) | copy-start | bytes 76036
  39.1 6.6 %collective-permute-start.4 = (f32[3,66,1,130]{3,2,1,0:T(1,128)S(1)}, f32[3,66,1,130]{3,2,1,0:T(1,128)S(1)}, u32[]{:S(2)}, u32[]{:S(2)}) collective-permute-start(f32[3,66,1,130]{3,2,1,0:T(1,128)S(1)} %get-tuple-element.6), channel_id=1, source_target_pairs={{0,1},{1,2},{2,3},{4,5},{5,6},{6,7},{8,9},{9,10},{10,11},{12,13},{... | collective-permute-start | bytes 308888 | tf_op jit(solution)/shard_map/ppermute | solution.py:14
  42.5 7.4 %collective-permute-start.5 = (f32[3,66,1,130]{3,2,1,0:T(1,128)S(1)}, f32[3,66,1,130]{3,2,1,0:T(1,128)S(1)}, u32[]{:S(2)}, u32[]{:S(2)}) collective-permute-start(f32[3,66,1,130]{3,2,1,0:T(1,128)S(1)} %get-tuple-element.7), channel_id=1, source_target_pairs={{1,0},{2,1},{3,2},{5,4},{6,5},{7,6},{9,8},{10,9},{11,10},{13,12},{... | collective-permute-start | bytes 308888 | tf_op jit(solution)/shard_map/ppermute | solution.py:17
  59.3 12.0 %copy-start.4 = (f32[64,32,128]{2,1,0:T(8,128)}, f32[64,32,128]{2,1,0:T(8,128)S(1)}, u32[]{:S(2)}) copy-start(f32[64,32,128]{2,1,0:T(8,128)S(1)} %sqrt_add_fusion) | copy-start | bytes 3145732
  59.3 12.0 %collective-permute-start.6 = (f32[1,32,128]{2,1,0:T(8,128)S(1)}, f32[1,32,128]{2,1,0:T(8,128)S(1)}, u32[]{:S(2)}, u32[]{:S(2)}) collective-permute-start(f32[1,32,128]{2,1,0:T(8,128)S(1)} %get-tuple-element.20), channel_id=1, source_target_pairs={{16,0},{32,16},{48,32},{64,48},{80,64},{96,80},{112,96},{128,112},... | collective-permute-start | bytes 49160 | tf_op jit(solution)/shard_map/ppermute | solution.py:17
  61.2 10.1 %collective-permute-start.7 = (f32[1,32,128]{2,1,0:T(8,128)S(1)}, f32[1,32,128]{2,1,0:T(8,128)S(1)}, u32[]{:S(2)}, u32[]{:S(2)}) collective-permute-start(f32[1,32,128]{2,1,0:T(8,128)S(1)} %get-tuple-element.19), channel_id=1, source_target_pairs={{0,16},{16,32},{32,48},{48,64},{64,80},{80,96},{96,112},{112,128},... | collective-permute-start | bytes 49160 | tf_op jit(solution)/shard_map/ppermute | solution.py:14
  75.0 7.8 %collective-permute-start.8 = (f32[66,32,1]{0,1,2:T(8,128)S(1)}, f32[66,32,1]{0,1,2:T(8,128)S(1)}, u32[]{:S(2)}, u32[]{:S(2)}) collective-permute-start(f32[66,32,1]{0,1,2:T(8,128)S(1)} %copy.33), channel_id=1, source_target_pairs={{4,0},{8,4},{12,8},{5,1},{9,5},{13,9},{6,2},{10,6},{14,10},{7,3},{... | collective-permute-start | bytes 25352 | tf_op jit(solution)/shard_map/ppermute | solution.py:17
  76.3 17.5 %copy-start.15 = (s32[1,1,1,2]{3,2,1,0:T(1,128)S(1)}, s32[1,1,1,2]{3,2,1,0:T(1,128)}, u32[]{:S(2)}) copy-start(s32[1,1,1,2]{3,2,1,0:T(1,128)} %param.6) | copy-start | bytes 28
  78.2 6.6 %collective-permute-start.9 = (f32[66,32,1]{0,1,2:T(8,128)S(1)}, f32[66,32,1]{0,1,2:T(8,128)S(1)}, u32[]{:S(2)}, u32[]{:S(2)}) collective-permute-start(f32[66,32,1]{0,1,2:T(8,128)S(1)} %copy.35), channel_id=1, source_target_pairs={{0,4},{4,8},{8,12},{1,5},{5,9},{9,13},{2,6},{6,10},{10,14},{3,7},{... | collective-permute-start | bytes 25352 | tf_op jit(solution)/shard_map/ppermute | solution.py:14
  88.5 14.2 %collective-permute-start.10 = (f32[66,1,130]{2,1,0:T(1,128)S(1)}, f32[66,1,130]{2,1,0:T(1,128)S(1)}, u32[]{:S(2)}, u32[]{:S(2)}) collective-permute-start(f32[66,1,130]{2,1,0:T(1,128)S(1)} %get-tuple-element.12), channel_id=1, source_target_pairs={{1,0},{2,1},{3,2},{5,4},{6,5},{7,6},{9,8},{10,9},{11,10},{13,12},{... | collective-permute-start | bytes 102968 | tf_op jit(solution)/shard_map/ppermute | solution.py:17
  89.8 12.9 %collective-permute-start.11 = (f32[66,1,130]{2,1,0:T(1,128)S(1)}, f32[66,1,130]{2,1,0:T(1,128)S(1)}, u32[]{:S(2)}, u32[]{:S(2)}) collective-permute-start(f32[66,1,130]{2,1,0:T(1,128)S(1)} %get-tuple-element.11), channel_id=1, source_target_pairs={{0,1},{1,2},{2,3},{4,5},{5,6},{6,7},{8,9},{9,10},{10,11},{12,13},{... | collective-permute-start | bytes 102968 | tf_op jit(solution)/shard_map/ppermute | solution.py:14
  95.1 39.9 %all-to-all-start = ((f32[16,4,1152]{2,1,0:T(4,128)}), f32[16,4,1152]{2,1,0:T(4,128)S(1)}, u32[]{:S(2)}, u32[]{:S(2)}) async-start(f32[16,4,1152]{2,1,0:T(4,128)} %copy.40), calls=%async_computation | async-start | bytes 589824 | tf_op jit(solution)/shard_map/all_to_all | solution.py:98
  102.7 18.0 %copy-start.1 = (f32[66,34,130]{2,1,0:T(8,128)S(1)}, f32[66,34,130]{2,1,0:T(8,128)}, u32[]{:S(2)}) copy-start(f32[66,34,130]{2,1,0:T(8,128)} %copy-done) | copy-start | bytes 3500644
  102.7 18.0 %copy-start.3 = (f32[66,34,130]{2,1,0:T(8,128)S(1)}, f32[66,34,130]{2,1,0:T(8,128)}, u32[]{:S(2)}) copy-start(f32[66,34,130]{2,1,0:T(8,128)} %copy-done.2) | copy-start | bytes 3500644
  102.7 18.0 %copy-start.5 = (f32[64,32,128]{2,1,0:T(8,128)S(1)}, f32[64,32,128]{2,1,0:T(8,128)}, u32[]{:S(2)}) copy-start(f32[64,32,128]{2,1,0:T(8,128)} %copy-done.4) | copy-start | bytes 3145732
  102.7 18.0 %copy-start.8 = (f32[66,32,1]{2,1,0:T(8,128)S(1)}, f32[66,32,1]{2,1,0:T(8,128)}, u32[]{:S(2)}) copy-start(f32[66,32,1]{2,1,0:T(8,128)} %copy.34) | copy-start | bytes 25348
  102.7 18.0 %copy-start.9 = (f32[66,32,1]{2,1,0:T(8,128)S(1)}, f32[66,32,1]{2,1,0:T(8,128)}, u32[]{:S(2)}) copy-start(f32[66,32,1]{2,1,0:T(8,128)} %copy.36) | copy-start | bytes 25348
  (6 other events, 18.2 us)
where the time goes:
time: 238 us; the launch traced here: 237 us
  blocking collectives  91.7 us (39%)
  other arithmetic  49.5 us (21%)
  starting transfers between devices  42.1 us (18%)
  local copies, waits for them, and re-layouts  35.2 us (15%)
  matrix products  11.5 us (5%)
  waiting for transfers between devices  6.24 us (3%)
    psum x1, blocking collectives, body(): owned = lax.psum(jnp.sum(received, axis=0), ('gy', 'gz'))  59.5 us
    all_gather x1, blocking collectives, body(): lax.all_gather(actuate(owned, owned_coef), 'gx', axis=0, tiled=True)  32.2 us
    another operation x3, other arithmetic, advance(): return jnp.stack(result)  32.2 us
    ppermute x6, starting transfers between devices, padded_2(): lax.ppermute(lax.slice_in_dim(block, block.shape[dim] - width, None, axis...  25.5 us
    slice x5, local copies, waits for them, and re-layouts, padded_2(): lax.slice_in_dim(block, block.shape[dim] - width, None, axis=dim)  10.3 us
    ppermute x6, starting transfers between devices, padded_2(): lax.ppermute(lax.slice_in_dim(block, 0, width, axis=dim), axis, backward)  8.99 us
    all_to_all x1, starting transfers between devices, body(): lax.all_to_all(partial_sample.reshape(rows, per_row, -1), 'gx', split_axi...  7.6 us
    concatenate x3, other arithmetic, padded_2(): block = jnp.concatenate([low, block, high], axis=dim)  5.95 us
  transfers between devices with their start and end apart: 13, of which 3 were waited for; matrix products, arithmetic and copies ran while one was open for 23% of the time, Pallas kernels for 0%

commit v1 on v0

--- a/solution.py
+++ b/solution.py
@@ -93,14 +93,8 @@
         block_local.reshape(tile_count, -1),
         precision=lax.Precision.HIGHEST,
     )
-    rows = lax.axis_size("gx")
-    per_row = nturb // rows
-    received = lax.all_to_all(
-        partial_sample.reshape(rows, per_row, -1), "gx", split_axis=0, concat_axis=0, tiled=True
-    )
-    owned = lax.psum(jnp.sum(received, axis=0), ("gy", "gz"))
-    owned_coef = lax.dynamic_slice_in_dim(chord, lax.axis_index("gx") * per_row, per_row, 0)
-    forces = lax.all_gather(actuate(owned, owned_coef), "gx", axis=0, tiled=True)
+    sample = lax.psum(partial_sample, ("gx", "gy", "gz"))
+    forces = actuate(sample, chord)
     tile_force = jnp.dot(owning_block, forces, precision=lax.Precision.HIGHEST).astype(jnp.bfloat16)
     forces_sent = jnp.einsum(
         "axz,ahx->ahz",

time: 238 us -> 376 us (1.58)
  waiting for transfers between devices: 6.24 us -> 239 us
  blocking collectives: 91.7 us -> 0 us
  between operations: 1.1 us -> 14.5 us
  starting transfers between devices: 42.1 us -> 32.9 us
  other arithmetic: 49.5 us -> 42.5 us
    psum x0 -> x1, waiting for transfers between devices: none -> 238 us  [body(): sample = lax.psum(partial_sample, ('gx', 'gy', 'gz'))]
    psum x1 -> x0, blocking collectives: 59.5 us -> none  [body(): owned = lax.psum(jnp.sum(received, axis=0), ('gy', 'gz'))]
    all_gather x1 -> x0, blocking collectives: 32.2 us -> none  [body(): lax.all_gather(actuate(owned, owned_coef), 'gx', axis=0, tiled=True)]
    another operation x3, other arithmetic: 32.2 us -> 17.4 us  [advance(): return jnp.stack(result)]
    all_to_all x1 -> x0, starting transfers between devices: 7.6 us -> none  [body(): lax.all_to_all(partial_sample.reshape(rows, per_row, -1), 'gx', split_axi...]
    ppermute x6, waiting for transfers between devices: 5.38 us -> 0.02 us  [padded_2(): lax.ppermute(lax.slice_in_dim(block, 0, width, axis=dim), axis, backward)]
  transfers between devices with their start and end apart: 13 -> 13, of which waited for: 3 -> 2; matrix products, arithmetic and copies ran while one was open for 23% -> 10% of each run, Pallas kernels for 0% -> 0%
where the time goes in v1:
time: 376 us; the launch traced here: 375 us
  waiting for transfers between devices  239 us (64%)
  other arithmetic  42.5 us (11%)
  local copies, waits for them, and re-layouts  34.3 us (9%)
  starting transfers between devices  32.9 us (9%)
  between operations  14.5 us (4%)
  matrix products  12.4 us (3%)
    psum x1, waiting for transfers between devices, body(): sample = lax.psum(partial_sample, ('gx', 'gy', 'gz'))  238 us
    ppermute x6, starting transfers between devices, padded_2(): lax.ppermute(lax.slice_in_dim(block, block.shape[dim] - width, None, axis...  23.4 us
    another operation x3, other arithmetic, advance(): return jnp.stack(result)  17.4 us
    slice x5, local copies, waits for them, and re-layouts, padded_2(): lax.slice_in_dim(block, block.shape[dim] - width, None, axis=dim)  10.3 us
    ppermute x6, starting transfers between devices, padded_2(): lax.ppermute(lax.slice_in_dim(block, 0, width, axis=dim), axis, backward)  9.49 us
    concatenate x3, other arithmetic, padded_2(): block = jnp.concatenate([low, block, high], axis=dim)  9.16 us
  transfers between devices with their start and end apart: 13, of which 2 were waited for; matrix products, arithmetic and copies ran while one was open for 10% of the time, Pallas kernels for 0%

profile of v1, /device:TPU:1, one launch (start us, length us, event | category | flops | bytes accessed | tf_op | source)
XLA Modules:
  0.0 375.2 jit_solution(18153228875391277242)
XLA Ops:
  8.0 4.9 %collective-permute-start = (f32[3,1,32,128]{3,2,1,0:T(8,128)S(1)}, f32[3,1,32,128]{3,2,1,0:T(8,128)S(1)}, u32[]{:S(2)}, u32[]{:S(2)}) collective-permute-start(f32[3,1,32,128]{3,2,1,0:T(8,128)S(1)} %get-tuple-element.16), channel_id=1, source_target_pairs={{0,16},{16,32},{32,48},{48,64},{64,80},{80,96},{96,112},{112,128},... | collective-permute-start | bytes 147464 | tf_op jit(solution)/shard_map/ppermute | solution.py:14
  13.0 1.9 collective-permute-start.1
  14.9 2.9 reshape.28
  18.9 4.7 %fusion.4 = f32[1,2,3,384]{3,2,1,0:T(4,128)S(1)} fusion(bf16[1,1,1,2,384,4096]{5,4,3,2,1,0:T(8,128)(2,1)} %param.8, bf16[2,3,4096]{2,0,1:T(2,128)(2,1)S(1)} %convolution_convert_fusion), kind=kOutput, calls=%fused_computation.11 | convolution fusion | flops 18874368 | bytes 6349824 | tf_op jit(solution)/shard_map/spq,scq->scp/dot_general | solution.py:84
  24.0 3.9 %fusion.29 = (f32[3,66,32,1]{3,2,1,0:T(8,128)}, f32[3,66,32,1]{3,2,1,0:T(8,128)}) fusion(f32[3,66,32,128]{3,2,1,0:T(8,128)S(1)} %constant_dynamic-update-slice_fusion), kind=kLoop, calls=%fused_computation.83 | loop fusion | bytes 101376 | tf_op jit(solution)/shard_map/slice | solution.py:15
  27.9 2.8 copy.27
  30.7 3.1 collective-permute-start.2
  33.8 2.8 copy.28
  39.1 2.7 copy.29
  41.8 2.7 copy.30
  44.5 4.0 %pad_maximum_fusion.22 = (f32[3,66,1,130]{3,2,1,0:T(1,128)}, f32[3,66,1,130]{3,2,1,0:T(1,128)}) fusion(f32[3,66,32,1]{3,2,1,0:T(8,128)} %copy.30, f32[3,66,32,128]{3,2,1,0:T(8,128)S(1)} %constant_dynamic-update-slice_fusion, f32[3,66,32,1]{3,2,1,0:T(8,128)} %copy.29), kind=kLoop, calls=%fused_computation.61 | loop fusion | flops 102960 | bytes 3500640 | tf_op jit(solution)/shard_map/slice | solution.py:15
  48.5 3.9 %collective-permute-start.4 = (f32[3,66,1,130]{3,2,1,0:T(1,128)}, f32[3,66,1,130]{3,2,1,0:T(1,128)}, u32[]{:S(2)}, u32[]{:S(2)}) collective-permute-start(f32[3,66,1,130]{3,2,1,0:T(1,128)} %get-tuple-element.6), channel_id=1, source_target_pairs={{0,1},{1,2},{2,3},{4,5},{5,6},{6,7},{8,9},{9,10},{10,11},{12,13},{... | collective-permute-start | bytes 308888 | tf_op jit(solution)/shard_map/ppermute | solution.py:14
  53.8 238.0 %all-reduce.2.cloned.1.call-done = f32[64,1152]{1,0:T(8,128)} async-done(((f32[64,1152]{1,0:T(8,128)}), f32[64,1152]{1,0:T(8,128)}) %all-reduce.2.cloned.1.call-update) | async-done | bytes 294928 | tf_op jit(solution)/shard_map/psum | solution.py:96
  298.6 6.0 %pad_maximum_fusion = f32[3,66,34,130]{3,2,1,0:T(8,128)S(1)} fusion(f32[3,66,1,130]{3,2,1,0:T(1,128)} %collective-permute-done.5, f32[3,66,32,1]{3,2,1,0:T(8,128)} %copy.30, f32[3,66,32,128]{3,2,1,0:T(8,128)S(1)} %constant_dynamic-update-slice_fusion, f32[3,66,32,1]{3,2,1,0:T(8,128)} %copy.29, f32[3,66,1,130]{3,2,1,0:T(1,128)} %collective-permute-done.4), kind=kLoop, calls=%fused_computation | loop fusion | flops 3500640 | bytes 7001280 | tf_op jit(solution)/shard_map/concatenate | solution.py:18
  305.1 4.8 %sqrt_add_fusion = f32[64,32,128]{2,1,0:T(8,128)S(1)} fusion(f32[66,34,130]{2,1,0:T(8,128)S(1)} %get-tuple-element.10, f32[66,34,130]{2,1,0:T(8,128)S(1)} %get-tuple-element.8, f32[66,34,130]{2,1,0:T(8,128)S(1)} %get-tuple-element.9), kind=kLoop, calls=%fused_computation.46 | loop fusion | flops 9961472 | bytes 19922944 | tf_op jit(solution)/shard_map/add | solution.py:39
  311.0 2.3 collective-permute-start.6
  313.2 3.3 collective-permute-start.7
  325.4 4.0 %collective-permute-start.9 = (f32[66,32,1]{0,1,2:T(8,128)S(1)}, f32[66,32,1]{0,1,2:T(8,128)S(1)}, u32[]{:S(2)}, u32[]{:S(2)}) collective-permute-start(f32[66,32,1]{0,1,2:T(8,128)S(1)} %copy.33), channel_id=1, source_target_pairs={{0,4},{4,8},{8,12},{1,5},{5,9},{9,13},{2,6},{6,10},{10,14},{3,7},{... | collective-permute-start | bytes 25352 | tf_op jit(solution)/shard_map/ppermute | solution.py:14
  329.4 3.7 fusion
  340.1 4.2 %collective-permute-start.11 = (f32[66,1,130]{2,1,0:T(1,128)S(1)}, f32[66,1,130]{2,1,0:T(1,128)S(1)}, u32[]{:S(2)}, u32[]{:S(2)}) collective-permute-start(f32[66,1,130]{2,1,0:T(1,128)S(1)} %get-tuple-element.11), channel_id=1, source_target_pairs={{0,1},{1,2},{2,3},{4,5},{5,6},{6,7},{8,9},{9,10},{10,11},{12,13},{... | collective-permute-start | bytes 102968 | tf_op jit(solution)/shard_map/ppermute | solution.py:14
  348.5 5.8 %add_bitcast_fusion.2 = f32[1,64,32,128]{3,2,1,0:T(8,128)S(1)} fusion(f32[66,34,130]{2,1,0:T(8,128)S(1)} %copy-done.3, f32[66,34,130]{2,1,0:T(8,128)S(1)} %get-tuple-element.8, f32[66,34,130]{2,1,0:T(8,128)S(1)} %copy-done.1, f32[64,32,128]{2,1,0:T(8,128)S(1)} %copy-done.5, f32[1,32,128]{2,1,0:T(8,128)S(1)} %collective-permute-done.6, ...), kind=kLoop, calls=%fused_computation.45 | loop fusion | flops 15990784 | bytes 11652640 | tf_op jit(solution)/shard_map/stack | solution.py:57
  354.3 5.8 %add_bitcast_fusion.1 = f32[1,64,32,128]{3,2,1,0:T(8,128)S(1)} fusion(f32[66,34,130]{2,1,0:T(8,128)S(1)} %get-tuple-element.8, f32[66,34,130]{2,1,0:T(8,128)S(1)} %copy-done.3, f32[66,34,130]{2,1,0:T(8,128)S(1)} %copy-done.1, f32[64,32,128]{2,1,0:T(8,128)S(1)} %copy-done.5, f32[1,32,128]{2,1,0:T(8,128)S(1)} %collective-permute-done.6, ...), kind=kLoop, calls=%fused_computation.44 | loop fusion | flops 15990784 | bytes 11652640 | tf_op jit(solution)/shard_map/stack | solution.py:57
  360.1 5.8 %add_bitcast_fusion = f32[1,64,32,128]{3,2,1,0:T(8,128)S(1)} fusion(f32[66,34,130]{2,1,0:T(8,128)S(1)} %copy-done.1, f32[66,34,130]{2,1,0:T(8,128)S(1)} %copy-done.3, f32[66,34,130]{2,1,0:T(8,128)S(1)} %get-tuple-element.8, f32[64,32,128]{2,1,0:T(8,128)S(1)} %copy-done.5, f32[1,32,128]{2,1,0:T(8,128)S(1)} %collective-permute-done.6, ...), kind=kLoop, calls=%fused_computation.43 | loop fusion | flops 15990784 | bytes 11652640 | tf_op jit(solution)/shard_map/stack | solution.py:57
  366.0 2.4 bitcast_add_fusion
  (71 shorter events, 34.3 us)
Async XLA Ops:
  7.2 284.7 %all-reduce.2.cloned.1.call-start = ((), (), s32[]{:S(2)}) async-start(), calls=%async_computation | async-start | bytes 589824 | tf_op jit(solution)/shard_map/psum | solution.py:96
  8.0 15.6 %collective-permute-start = (f32[3,1,32,128]{3,2,1,0:T(8,128)S(1)}, f32[3,1,32,128]{3,2,1,0:T(8,128)S(1)}, u32[]{:S(2)}, u32[]{:S(2)}) collective-permute-start(f32[3,1,32,128]{3,2,1,0:T(8,128)S(1)} %get-tuple-element.16), channel_id=1, source_target_pairs={{0,16},{16,32},{32,48},{48,64},{64,80},{80,96},{96,112},{112,128},... | collective-permute-start | bytes 147464 | tf_op jit(solution)/shard_map/ppermute | solution.py:14
  13.0 4.8 %copy-start.12 = (s32[1,1,1,2]{3,2,1,0:T(1,128)S(1)}, s32[1,1,1,2]{3,2,1,0:T(1,128)}, u32[]{:S(2)}) copy-start(s32[1,1,1,2]{3,2,1,0:T(1,128)} %param.7) | copy-start | bytes 28
  13.0 11.0 %collective-permute-start.1 = (f32[3,1,32,128]{3,2,1,0:T(8,128)S(1)}, f32[3,1,32,128]{3,2,1,0:T(8,128)S(1)}, u32[]{:S(2)}, u32[]{:S(2)}) collective-permute-start(f32[3,1,32,128]{3,2,1,0:T(8,128)S(1)} %get-tuple-element.15), channel_id=1, source_target_pairs={{16,0},{32,16},{48,32},{64,48},{80,64},{96,80},{112,96},{128,112},... | collective-permute-start | bytes 147464 | tf_op jit(solution)/shard_map/ppermute | solution.py:17
  18.9 4.7 %copy-start.8 = (f32[3,64,32,128]{3,2,1,0:T(8,128)S(1)}, f32[3,64,32,128]{3,2,1,0:T(8,128)}, u32[]{:S(2)}) copy-start(f32[3,64,32,128]{3,2,1,0:T(8,128)} %param.5) | copy-start | bytes 9437188
  27.9 10.1 %copy-start.11 = (s32[1,1,1,2]{3,2,1,0:T(1,128)S(1)}, s32[1,1,1,2]{3,2,1,0:T(1,128)}, u32[]{:S(2)}) copy-start(s32[1,1,1,2]{3,2,1,0:T(1,128)} %param.6) | copy-start | bytes 28
  30.7 8.4 %collective-permute-start.2 = (f32[3,66,32,1]{1,2,3,0:T(8,128)S(1)}, f32[3,66,32,1]{1,2,3,0:T(8,128)S(1)}, u32[]{:S(2)}, u32[]{:S(2)}) collective-permute-start(f32[3,66,32,1]{1,2,3,0:T(8,128)S(1)} %copy.27), channel_id=1, source_target_pairs={{0,4},{4,8},{8,12},{1,5},{5,9},{9,13},{2,6},{6,10},{10,14},{3,7},{... | collective-permute-start | bytes 76040 | tf_op jit(solution)/shard_map/ppermute | solution.py:14
  36.6 5.2 %collective-permute-start.3 = (f32[3,66,32,1]{1,2,3,0:T(8,128)S(1)}, f32[3,66,32,1]{1,2,3,0:T(8,128)S(1)}, u32[]{:S(2)}, u32[]{:S(2)}) collective-permute-start(f32[3,66,32,1]{1,2,3,0:T(8,128)S(1)} %copy.28), channel_id=1, source_target_pairs={{4,0},{8,4},{12,8},{5,1},{9,5},{13,9},{6,2},{10,6},{14,10},{7,3},{... | collective-permute-start | bytes 76040 | tf_op jit(solution)/shard_map/ppermute | solution.py:17
  48.5 250.1 %collective-permute-start.4 = (f32[3,66,1,130]{3,2,1,0:T(1,128)}, f32[3,66,1,130]{3,2,1,0:T(1,128)}, u32[]{:S(2)}, u32[]{:S(2)}) collective-permute-start(f32[3,66,1,130]{3,2,1,0:T(1,128)} %get-tuple-element.6), channel_id=1, source_target_pairs={{0,1},{1,2},{2,3},{4,5},{5,6},{6,7},{8,9},{9,10},{10,11},{12,13},{... | collective-permute-start | bytes 308888 | tf_op jit(solution)/shard_map/ppermute | solution.py:14
  52.4 246.2 %collective-permute-start.5 = (f32[3,66,1,130]{3,2,1,0:T(1,128)}, f32[3,66,1,130]{3,2,1,0:T(1,128)}, u32[]{:S(2)}, u32[]{:S(2)}) collective-permute-start(f32[3,66,1,130]{3,2,1,0:T(1,128)} %get-tuple-element.7), channel_id=1, source_target_pairs={{1,0},{2,1},{3,2},{5,4},{6,5},{7,6},{9,8},{10,9},{11,10},{13,12},{... | collective-permute-start | bytes 308888 | tf_op jit(solution)/shard_map/ppermute | solution.py:17
  291.9 6.6 %copy-start.9 = (f32[64,1152]{1,0:T(8,128)S(1)}, f32[64,1152]{1,0:T(8,128)}, u32[]{:S(2)}) copy-start(f32[64,1152]{1,0:T(8,128)} %all-reduce.2.cloned.1.call-done) | copy-start | bytes 884740
  298.5 18.0 %copy-start.10 = (f32[64,1152]{1,0:T(8,128)}, f32[64,1152]{1,0:T(8,128)S(1)}, u32[]{:S(2)}) copy-start(f32[64,1152]{1,0:T(8,128)S(1)} %mul.301) | copy-start | bytes 884740
  305.1 4.8 %copy-start = (f32[66,34,130]{2,1,0:T(8,128)}, f32[66,34,130]{2,1,0:T(8,128)S(1)}, u32[]{:S(2)}) copy-start(f32[66,34,130]{2,1,0:T(8,128)S(1)} %get-tuple-element.9) | copy-start | bytes 3500644
  305.1 4.8 %copy-start.2 = (f32[66,34,130]{2,1,0:T(8,128)}, f32[66,34,130]{2,1,0:T(8,128)S(1)}, u32[]{:S(2)}) copy-start(f32[66,34,130]{2,1,0:T(8,128)S(1)} %get-tuple-element.10) | copy-start | bytes 3500644
  311.0 5.8 %collective-permute-start.6 = (f32[1,32,128]{2,1,0:T(8,128)S(1)}, f32[1,32,128]{2,1,0:T(8,128)S(1)}, u32[]{:S(2)}, u32[]{:S(2)}) collective-permute-start(f32[1,32,128]{2,1,0:T(8,128)S(1)} %get-tuple-element.20), channel_id=1, source_target_pairs={{16,0},{32,16},{48,32},{64,48},{80,64},{96,80},{112,96},{128,112},... | collective-permute-start | bytes 49160 | tf_op jit(solution)/shard_map/ppermute | solution.py:17
  313.2 4.2 %collective-permute-start.7 = (f32[1,32,128]{2,1,0:T(8,128)S(1)}, f32[1,32,128]{2,1,0:T(8,128)S(1)}, u32[]{:S(2)}, u32[]{:S(2)}) collective-permute-start(f32[1,32,128]{2,1,0:T(8,128)S(1)} %get-tuple-element.19), channel_id=1, source_target_pairs={{0,16},{16,32},{32,48},{48,64},{64,80},{80,96},{96,112},{112,128},... | collective-permute-start | bytes 49160 | tf_op jit(solution)/shard_map/ppermute | solution.py:14
  322.3 10.8 %collective-permute-start.8 = (f32[66,32,1]{0,1,2:T(8,128)S(1)}, f32[66,32,1]{0,1,2:T(8,128)S(1)}, u32[]{:S(2)}, u32[]{:S(2)}) collective-permute-start(f32[66,32,1]{0,1,2:T(8,128)S(1)} %copy.31), channel_id=1, source_target_pairs={{4,0},{8,4},{12,8},{5,1},{9,5},{13,9},{6,2},{10,6},{14,10},{7,3},{... | collective-permute-start | bytes 25352 | tf_op jit(solution)/shard_map/ppermute | solution.py:17
  325.4 9.6 %collective-permute-start.9 = (f32[66,32,1]{0,1,2:T(8,128)S(1)}, f32[66,32,1]{0,1,2:T(8,128)S(1)}, u32[]{:S(2)}, u32[]{:S(2)}) collective-permute-start(f32[66,32,1]{0,1,2:T(8,128)S(1)} %copy.33), channel_id=1, source_target_pairs={{0,4},{4,8},{8,12},{1,5},{5,9},{9,13},{2,6},{6,10},{10,14},{3,7},{... | collective-permute-start | bytes 25352 | tf_op jit(solution)/shard_map/ppermute | solution.py:14
  338.8 7.7 %collective-permute-start.10 = (f32[66,1,130]{2,1,0:T(1,128)S(1)}, f32[66,1,130]{2,1,0:T(1,128)S(1)}, u32[]{:S(2)}, u32[]{:S(2)}) collective-permute-start(f32[66,1,130]{2,1,0:T(1,128)S(1)} %get-tuple-element.12), channel_id=1, source_target_pairs={{1,0},{2,1},{3,2},{5,4},{6,5},{7,6},{9,8},{10,9},{11,10},{13,12},{... | collective-permute-start | bytes 102968 | tf_op jit(solution)/shard_map/ppermute | solution.py:17
  340.1 6.4 %collective-permute-start.11 = (f32[66,1,130]{2,1,0:T(1,128)S(1)}, f32[66,1,130]{2,1,0:T(1,128)S(1)}, u32[]{:S(2)}, u32[]{:S(2)}) collective-permute-start(f32[66,1,130]{2,1,0:T(1,128)S(1)} %get-tuple-element.11), channel_id=1, source_target_pairs={{0,1},{1,2},{2,3},{4,5},{5,6},{6,7},{8,9},{9,10},{10,11},{12,13},{... | collective-permute-start | bytes 102968 | tf_op jit(solution)/shard_map/ppermute | solution.py:14
  344.3 2.2 copy-start.5
  344.3 2.2 copy-start.6
  344.3 2.2 copy-start.7
  345.9 2.6 copy-start.3
  (2 other events, 2.8 us)
Sparse Core Ops, SparseCore 0:
  39.2 252.6 all-reduce.1

commit v2 on v0

--- a/solution.py
+++ b/solution.py
@@ -98,9 +98,20 @@
     received = lax.all_to_all(
         partial_sample.reshape(rows, per_row, -1), "gx", split_axis=0, concat_axis=0, tiled=True
     )
-    owned = lax.psum(jnp.sum(received, axis=0), ("gy", "gz"))
+    owned = jnp.sum(received, axis=0)
+    for axis in ("gy", "gz"):
+        count = lax.axis_size(axis)
+        step = 1
+        while step < count:
+            pairs = [(i, i ^ step) for i in range(count)]
+            owned = owned + lax.ppermute(owned, axis, pairs)
+            step *= 2
     owned_coef = lax.dynamic_slice_in_dim(chord, lax.axis_index("gx") * per_row, per_row, 0)
-    forces = lax.all_gather(actuate(owned, owned_coef), "gx", axis=0, tiled=True)
+    owned_force = actuate(owned, owned_coef)
+    forces = lax.all_to_all(
+        jnp.broadcast_to(owned_force[None], (rows,) + owned_force.shape),
+        "gx", split_axis=0, concat_axis=0, tiled=True,
+    ).reshape(nturb, -1)
     tile_force = jnp.dot(owning_block, forces, precision=lax.Precision.HIGHEST).astype(jnp.bfloat16)
     forces_sent = jnp.einsum(
         "axz,ahx->ahz",

time: 238 us -> 181 us (0.76)
  blocking collectives: 91.7 us -> 0 us
  starting transfers between devices: 42.1 us -> 63.8 us
  other arithmetic: 49.5 us -> 64.9 us
  waiting for transfers between devices: 6.24 us -> 2.84 us
    psum x1 -> x0, blocking collectives: 59.5 us -> none  [body(): owned = lax.psum(jnp.sum(received, axis=0), ('gy', 'gz'))]
    all_gather x1 -> x0, blocking collectives: 32.2 us -> none  [body(): lax.all_gather(actuate(owned, owned_coef), 'gx', axis=0, tiled=True)]
    another operation x3, other arithmetic: 32.2 us -> 44.8 us  [advance(): return jnp.stack(result)]
    all_to_all x0 -> x1, starting transfers between devices: none -> 12.4 us  [body(): lax.all_to_all(jnp.broadcast_to(owned_force[None], (rows,) + owned_force....]
    ppermute x0 -> x4, starting transfers between devices: none -> 6.9 us  [body(): owned = owned + lax.ppermute(owned, axis, pairs)]
    ppermute x6, waiting for transfers between devices: 5.38 us -> 0.02 us  [padded_2(): lax.ppermute(lax.slice_in_dim(block, 0, width, axis=dim), axis, backward)]
    all_to_all x1, starting transfers between devices: 7.6 us -> 11 us  [body(): lax.all_to_all(partial_sample.reshape(rows, per_row, -1), 'gx', split_axi...]
  transfers between devices with their start and end apart: 13 -> 18, of which waited for: 3 -> 2; matrix products, arithmetic and copies ran while one was open for 23% -> 48% of each run, Pallas kernels for 0% -> 0%
where the time goes in v2:
time: 181 us; the launch traced here: 180 us
  other arithmetic  64.9 us (36%)
  starting transfers between devices  63.8 us (35%)
  local copies, waits for them, and re-layouts  34 us (19%)
  matrix products  13.6 us (8%)
  waiting for transfers between devices  2.84 us (2%)
    another operation x3, other arithmetic, advance(): return jnp.stack(result)  44.8 us
    ppermute x6, starting transfers between devices, padded_2(): lax.ppermute(lax.slice_in_dim(block, block.shape[dim] - width, None, axis...  24.4 us
    all_to_all x1, starting transfers between devices, body(): lax.all_to_all(jnp.broadcast_to(owned_force[None], (rows,) + owned_force....  12.4 us
    all_to_all x1, starting transfers between devices, body(): lax.all_to_all(partial_sample.reshape(rows, per_row, -1), 'gx', split_axi...  11 us
    slice x5, local copies, waits for them, and re-layouts, padded_2(): lax.slice_in_dim(block, block.shape[dim] - width, None, axis=dim)  10.3 us
    ppermute x6, starting transfers between devices, padded_2(): lax.ppermute(lax.slice_in_dim(block, 0, width, axis=dim), axis, backward)  9.09 us
    concatenate x3, other arithmetic, padded_2(): block = jnp.concatenate([low, block, high], axis=dim)  8.22 us
    ppermute x4, starting transfers between devices, body(): owned = owned + lax.ppermute(owned, axis, pairs)  6.9 us
  transfers between devices with their start and end apart: 18, of which 2 were waited for; matrix products, arithmetic and copies ran while one was open for 48% of the time, Pallas kernels for 0%

profile of v2, /device:TPU:1, one launch (start us, length us, event | category | flops | bytes accessed | tf_op | source)
XLA Modules:
  0.0 180.2 jit_solution(7197476737017129049)
XLA Ops:
  1.5 4.9 %collective-permute-start = (f32[3,1,32,128]{3,2,1,0:T(8,128)S(1)}, f32[3,1,32,128]{3,2,1,0:T(8,128)S(1)}, u32[]{:S(2)}, u32[]{:S(2)}) collective-permute-start(f32[3,1,32,128]{3,2,1,0:T(8,128)S(1)} %get-tuple-element.18), channel_id=1, source_target_pairs={{0,16},{16,32},{32,48},{48,64},{64,80},{80,96},{96,112},{112,128},... | collective-permute-start | bytes 147464 | tf_op jit(solution)/shard_map/ppermute | solution.py:14
  8.3 4.6 %reshape.55 = f32[3,64,4096]{2,1,0:T(8,128)} reshape(f32[3,64,32,128]{3,2,1,0:T(8,128)} %param.5) | data formatting | bytes 6291456 | tf_op jit(solution)/shard_map/reshape | solution.py:79
  12.9 3.0 %convolution_convert_fusion = bf16[2,3,4096]{2,0,1:T(2,128)(2,1)S(1)} fusion(f32[3,64,4096]{2,1,0:T(8,128)} %reshape.55, s32[2]{0:T(128)S(1)} %bitcast.45), kind=kOutput, calls=%fused_computation.5 | convolution fusion | flops 18899072 | bytes 3194888 | tf_op jit(solution)/shard_map/sx,cxq->scq/dot_general | solution.py:81
  15.9 4.7 %fusion.2 = f32[2,3,384]{2,1,0:T(4,128)S(1)} fusion(bf16[1,1,1,2,384,4096]{5,4,3,2,1,0:T(8,128)(2,1)} %param.8, bf16[2,3,4096]{2,0,1:T(2,128)(2,1)S(1)} %convolution_convert_fusion), kind=kOutput, calls=%fused_computation.3 | convolution fusion | flops 18874368 | bytes 6349824 | tf_op jit(solution)/shard_map/spq,scq->scp/dot_general | solution.py:84
  21.0 3.8 %fusion.31 = (f32[3,66,32,1]{3,2,1,0:T(8,128)}, f32[3,66,32,1]{3,2,1,0:T(8,128)}) fusion(f32[3,66,32,128]{3,2,1,0:T(8,128)S(1)} %constant_dynamic-update-slice_fusion), kind=kLoop, calls=%fused_computation.87 | loop fusion | bytes 101376 | tf_op jit(solution)/shard_map/slice | solution.py:15
  24.8 2.8 %copy.30 = f32[3,66,32,1]{1,2,3,0:T(8,128)S(1)} copy(f32[3,66,32,1]{3,2,1,0:T(8,128)} %get-tuple-element.16) | data formatting | bytes 50688 | tf_op jit(solution)/shard_map/slice | solution.py:17
  28.9 2.8 %copy.29 = f32[3,66,32,1]{1,2,3,0:T(8,128)S(1)} copy(f32[3,66,32,1]{3,2,1,0:T(8,128)} %get-tuple-element.15) | data formatting | bytes 50688 | tf_op jit(solution)/shard_map/slice | solution.py:15
  31.8 4.0 %collective-permute-start.2 = (f32[3,66,32,1]{1,2,3,0:T(8,128)S(1)}, f32[3,66,32,1]{1,2,3,0:T(8,128)S(1)}, u32[]{:S(2)}, u32[]{:S(2)}) collective-permute-start(f32[3,66,32,1]{1,2,3,0:T(8,128)S(1)} %copy.29), channel_id=1, source_target_pairs={{0,4},{4,8},{8,12},{1,5},{5,9},{9,13},{2,6},{6,10},{10,14},{3,7},{... | collective-permute-start | bytes 76040 | tf_op jit(solution)/shard_map/ppermute | solution.py:14
  35.8 2.7 %copy.32 = f32[3,66,32,1]{3,2,1,0:T(8,128)} copy(f32[3,66,32,1]{1,2,3,0:T(8,128)S(1)} %collective-permute-done.3) | data formatting | bytes 50688 | tf_op jit(solution)/shard_map/ppermute | solution.py:17
  38.5 2.7 %copy.31 = f32[3,66,32,1]{3,2,1,0:T(8,128)} copy(f32[3,66,32,1]{1,2,3,0:T(8,128)S(1)} %collective-permute-done.2) | data formatting | bytes 50688 | tf_op jit(solution)/shard_map/ppermute | solution.py:14
  41.2 3.8 %pad_maximum_fusion.22 = (f32[3,66,1,130]{3,2,1,0:T(1,128)S(1)}, f32[3,66,1,130]{3,2,1,0:T(1,128)S(1)}) fusion(f32[3,66,32,1]{3,2,1,0:T(8,128)} %copy.32, f32[3,66,32,128]{3,2,1,0:T(8,128)} %copy-done.2, f32[3,66,32,1]{3,2,1,0:T(8,128)} %copy.31), kind=kLoop, calls=%fused_computation.60 | loop fusion | flops 102960 | bytes 3500640 | tf_op jit(solution)/shard_map/slice | solution.py:15
  46.2 4.0 %collective-permute-start.4 = (f32[3,66,1,130]{3,2,1,0:T(1,128)S(1)}, f32[3,66,1,130]{3,2,1,0:T(1,128)S(1)}, u32[]{:S(2)}, u32[]{:S(2)}) collective-permute-start(f32[3,66,1,130]{3,2,1,0:T(1,128)S(1)} %get-tuple-element.8), channel_id=1, source_target_pairs={{0,1},{1,2},{2,3},{4,5},{5,6},{6,7},{8,9},{9,10},{10,11},{12,13},{... | collective-permute-start | bytes 308888 | tf_op jit(solution)/shard_map/ppermute | solution.py:14
  51.5 11.0 %all-to-all-start = ((f32[16,4,1152]{2,1,0:T(4,128)}), f32[16,4,1152]{2,1,0:T(4,128)S(1)}, u32[]{:S(2)}, u32[]{:S(2)}) async-start(f32[16,4,1152]{2,1,0:T(4,128)} %copy.40), calls=%async_computation | async-start | bytes 589824 | tf_op jit(solution)/shard_map/all_to_all | solution.py:98
  62.6 6.3 %pad_maximum_fusion = f32[3,66,34,130]{3,2,1,0:T(8,128)S(1)} fusion(f32[3,66,1,130]{3,2,1,0:T(1,128)S(1)} %collective-permute-done.5, f32[3,66,32,1]{3,2,1,0:T(8,128)} %copy.32, f32[3,66,32,128]{3,2,1,0:T(8,128)} %copy-done.2, f32[3,66,32,1]{3,2,1,0:T(8,128)} %copy.31, f32[3,66,1,130]{3,2,1,0:T(1,128)S(1)} %collective-permute-done.4), kind=kLoop, calls=%fused_computation | loop fusion | flops 3500640 | bytes 7001280 | tf_op jit(solution)/shard_map/concatenate | solution.py:18
  69.4 4.8 %sqrt_add_fusion = f32[64,32,128]{2,1,0:T(8,128)S(1)} fusion(f32[66,34,130]{2,1,0:T(8,128)S(1)} %get-tuple-element.12, f32[66,34,130]{2,1,0:T(8,128)S(1)} %get-tuple-element.10, f32[66,34,130]{2,1,0:T(8,128)S(1)} %get-tuple-element.11), kind=kLoop, calls=%fused_computation.45 | loop fusion | flops 9961472 | bytes 19922944 | tf_op jit(solution)/shard_map/add | solution.py:39
  76.3 3.5 %collective-permute-start.7 = (f32[1,32,128]{2,1,0:T(8,128)S(1)}, f32[1,32,128]{2,1,0:T(8,128)S(1)}, u32[]{:S(2)}, u32[]{:S(2)}) collective-permute-start(f32[1,32,128]{2,1,0:T(8,128)S(1)} %get-tuple-element.21), channel_id=1, source_target_pairs={{0,16},{16,32},{32,48},{48,64},{64,80},{80,96},{96,112},{112,128},... | collective-permute-start | bytes 49160 | tf_op jit(solution)/shard_map/ppermute | solution.py:14
  87.5 4.0 %collective-permute-start.9 = (f32[66,32,1]{0,1,2:T(8,128)S(1)}, f32[66,32,1]{0,1,2:T(8,128)S(1)}, u32[]{:S(2)}, u32[]{:S(2)}) collective-permute-start(f32[66,32,1]{0,1,2:T(8,128)S(1)} %copy.35), channel_id=1, source_target_pairs={{0,4},{4,8},{8,12},{1,5},{5,9},{9,13},{2,6},{6,10},{10,14},{3,7},{... | collective-permute-start | bytes 25352 | tf_op jit(solution)/shard_map/ppermute | solution.py:14
  99.9 4.0 %collective-permute-start.11 = (f32[66,1,130]{2,1,0:T(1,128)S(1)}, f32[66,1,130]{2,1,0:T(1,128)S(1)}, u32[]{:S(2)}, u32[]{:S(2)}) collective-permute-start(f32[66,1,130]{2,1,0:T(1,128)S(1)} %get-tuple-element.13), channel_id=1, source_target_pairs={{0,1},{1,2},{2,3},{4,5},{5,6},{6,7},{8,9},{9,10},{10,11},{12,13},{... | collective-permute-start | bytes 102968 | tf_op jit(solution)/shard_map/ppermute | solution.py:14
  109.7 18.0 %add_bitcast_fusion = f32[1,64,32,128]{3,2,1,0:T(8,128)} fusion(f32[66,34,130]{2,1,0:T(8,128)} %copy-done, f32[66,34,130]{2,1,0:T(8,128)} %copy-done.1, f32[66,34,130]{2,1,0:T(8,128)S(1)} %get-tuple-element.10, f32[64,32,128]{2,1,0:T(8,128)} %copy-done.3, f32[1,32,128]{2,1,0:T(8,128)S(1)} %collective-permute-done.6, ...), kind=kLoop, calls=%fused_computation.42 | loop fusion | flops 15990784 | bytes 11652640 | tf_op jit(solution)/shard_map/stack | solution.py:57
  129.5 8.9 %add_bitcast_fusion.1 = f32[1,64,32,128]{3,2,1,0:T(8,128)} fusion(f32[66,34,130]{2,1,0:T(8,128)S(1)} %get-tuple-element.10, f32[66,34,130]{2,1,0:T(8,128)} %copy-done.1, f32[66,34,130]{2,1,0:T(8,128)} %copy-done, f32[64,32,128]{2,1,0:T(8,128)S(1)} %copy-done.4, f32[1,32,128]{2,1,0:T(8,128)S(1)} %collective-permute-done.6, ...), kind=kLoop, calls=%fused_computation.43 | loop fusion | flops 15990784 | bytes 11652640 | tf_op jit(solution)/shard_map/stack | solution.py:57
  140.0 12.4 %all-to-all-start.1 = ((f32[16,4,1152]{2,1,0:T(4,128)}), f32[16,4,1152]{2,1,0:T(4,128)S(1)}, u32[]{:S(2)}, u32[]{:S(2)}) async-start(f32[16,4,1152]{2,1,0:T(4,128)} %broadcast_in_dim.2), calls=%async_computation.1 | async-start | bytes 589824 | tf_op jit(solution)/shard_map/all_to_all | solution.py:111
  152.3 18.0 %add_bitcast_fusion.2 = f32[1,64,32,128]{3,2,1,0:T(8,128)} fusion(f32[66,34,130]{2,1,0:T(8,128)} %copy-done.1, f32[66,34,130]{2,1,0:T(8,128)S(1)} %get-tuple-element.10, f32[66,34,130]{2,1,0:T(8,128)} %copy-done, f32[64,32,128]{2,1,0:T(8,128)} %copy-done.3, f32[1,32,128]{2,1,0:T(8,128)S(1)} %collective-permute-done.6, ...), kind=kLoop, calls=%fused_computation.44 | loop fusion | flops 15990784 | bytes 11652640 | tf_op jit(solution)/shard_map/stack | solution.py:57
  170.7 3.7 %fusion = f32[2,3,4096]{2,1,0:T(4,128)S(1)} fusion(bf16[2,3,384]{2,1,0:T(4,128)(2,1)S(1)} %reshape.59, bf16[1,1,1,2,384,4096]{5,4,3,2,1,0:T(8,128)(2,1)} %param.8), kind=kOutput, calls=%fused_computation.1 | convolution fusion | flops 18874368 | bytes 6394368 | tf_op jit(solution)/shard_map/axz,ahx->ahz/dot_general | solution.py:116
  177.8 2.4 %bitcast_add_fusion = f32[3,64,32,128]{3,2,1,0:T(8,128)} fusion(f32[1,64,32,128]{3,2,1,0:T(8,128)S(1)} %copy-done.8, f32[1,64,32,128]{3,2,1,0:T(8,128)S(1)} %copy-done.9, f32[1,64,32,128]{3,2,1,0:T(8,128)S(1)} %copy-done.10, f32[3,64,32,128]{3,2,1,0:T(8,128)S(1)} %bitcast.40), kind=kLoop, calls=%fused_computation.6 | loop fusion | flops 2359296 | bytes 9437184 | tf_op jit(solution)/shard_map/add | solution.py:128
  (88 shorter events, 38.4 us)
Async XLA Ops:
  1.5 19.1 %collective-permute-start = (f32[3,1,32,128]{3,2,1,0:T(8,128)S(1)}, f32[3,1,32,128]{3,2,1,0:T(8,128)S(1)}, u32[]{:S(2)}, u32[]{:S(2)}) collective-permute-start(f32[3,1,32,128]{3,2,1,0:T(8,128)S(1)} %get-tuple-element.18), channel_id=1, source_target_pairs={{0,16},{16,32},{32,48},{48,64},{64,80},{80,96},{96,112},{112,128},... | collective-permute-start | bytes 147464 | tf_op jit(solution)/shard_map/ppermute | solution.py:14
  6.4 6.5 %copy-start.13 = (s32[1,1,1,2]{3,2,1,0:T(1,128)S(1)}, s32[1,1,1,2]{3,2,1,0:T(1,128)}, u32[]{:S(2)}) copy-start(s32[1,1,1,2]{3,2,1,0:T(1,128)} %param.7) | copy-start | bytes 28
  6.4 14.6 %collective-permute-start.1 = (f32[3,1,32,128]{3,2,1,0:T(8,128)S(1)}, f32[3,1,32,128]{3,2,1,0:T(8,128)S(1)}, u32[]{:S(2)}, u32[]{:S(2)}) collective-permute-start(f32[3,1,32,128]{3,2,1,0:T(8,128)S(1)} %get-tuple-element.17), channel_id=1, source_target_pairs={{16,0},{32,16},{48,32},{64,48},{80,64},{96,80},{112,96},{128,112},... | collective-permute-start | bytes 147464 | tf_op jit(solution)/shard_map/ppermute | solution.py:17
  27.6 8.1 %collective-permute-start.3 = (f32[3,66,32,1]{1,2,3,0:T(8,128)S(1)}, f32[3,66,32,1]{1,2,3,0:T(8,128)S(1)}, u32[]{:S(2)}, u32[]{:S(2)}) collective-permute-start(f32[3,66,32,1]{1,2,3,0:T(8,128)S(1)} %copy.30), channel_id=1, source_target_pairs={{4,0},{8,4},{12,8},{5,1},{9,5},{13,9},{6,2},{10,6},{14,10},{7,3},{... | collective-permute-start | bytes 76040 | tf_op jit(solution)/shard_map/ppermute | solution.py:17
  31.8 6.7 %collective-permute-start.2 = (f32[3,66,32,1]{1,2,3,0:T(8,128)S(1)}, f32[3,66,32,1]{1,2,3,0:T(8,128)S(1)}, u32[]{:S(2)}, u32[]{:S(2)}) collective-permute-start(f32[3,66,32,1]{1,2,3,0:T(8,128)S(1)} %copy.29), channel_id=1, source_target_pairs={{0,4},{4,8},{8,12},{1,5},{5,9},{9,13},{2,6},{6,10},{10,14},{3,7},{... | collective-permute-start | bytes 76040 | tf_op jit(solution)/shard_map/ppermute | solution.py:14
  41.2 9.1 %copy-start.12 = (s32[1,1,1,2]{3,2,1,0:T(1,128)S(1)}, s32[1,1,1,2]{3,2,1,0:T(1,128)}, u32[]{:S(2)}) copy-start(s32[1,1,1,2]{3,2,1,0:T(1,128)} %param.6) | copy-start | bytes 28
  44.9 17.6 %collective-permute-start.5 = (f32[3,66,1,130]{3,2,1,0:T(1,128)S(1)}, f32[3,66,1,130]{3,2,1,0:T(1,128)S(1)}, u32[]{:S(2)}, u32[]{:S(2)}) collective-permute-start(f32[3,66,1,130]{3,2,1,0:T(1,128)S(1)} %get-tuple-element.9), channel_id=1, source_target_pairs={{1,0},{2,1},{3,2},{5,4},{6,5},{7,6},{9,8},{10,9},{11,10},{13,12},{... | collective-permute-start | bytes 308888 | tf_op jit(solution)/shard_map/ppermute | solution.py:17
  46.2 16.3 %collective-permute-start.4 = (f32[3,66,1,130]{3,2,1,0:T(1,128)S(1)}, f32[3,66,1,130]{3,2,1,0:T(1,128)S(1)}, u32[]{:S(2)}, u32[]{:S(2)}) collective-permute-start(f32[3,66,1,130]{3,2,1,0:T(1,128)S(1)} %get-tuple-element.8), channel_id=1, source_target_pairs={{0,1},{1,2},{2,3},{4,5},{5,6},{6,7},{8,9},{9,10},{10,11},{12,13},{... | collective-permute-start | bytes 308888 | tf_op jit(solution)/shard_map/ppermute | solution.py:14
  51.5 43.8 %all-to-all-start = ((f32[16,4,1152]{2,1,0:T(4,128)}), f32[16,4,1152]{2,1,0:T(4,128)S(1)}, u32[]{:S(2)}, u32[]{:S(2)}) async-start(f32[16,4,1152]{2,1,0:T(4,128)} %copy.40), calls=%async_computation | async-start | bytes 589824 | tf_op jit(solution)/shard_map/all_to_all | solution.py:98
  74.2 8.3 %copy-start.3 = (f32[64,32,128]{2,1,0:T(8,128)}, f32[64,32,128]{2,1,0:T(8,128)S(1)}, u32[]{:S(2)}) copy-start(f32[64,32,128]{2,1,0:T(8,128)S(1)} %sqrt_add_fusion) | copy-start | bytes 3145732
  74.3 5.6 %collective-permute-start.6 = (f32[1,32,128]{2,1,0:T(8,128)S(1)}, f32[1,32,128]{2,1,0:T(8,128)S(1)}, u32[]{:S(2)}, u32[]{:S(2)}) collective-permute-start(f32[1,32,128]{2,1,0:T(8,128)S(1)} %get-tuple-element.22), channel_id=1, source_target_pairs={{16,0},{32,16},{48,32},{64,48},{80,64},{96,80},{112,96},{128,112},... | collective-permute-start | bytes 49160 | tf_op jit(solution)/shard_map/ppermute | solution.py:17
  76.3 4.4 %collective-permute-start.7 = (f32[1,32,128]{2,1,0:T(8,128)S(1)}, f32[1,32,128]{2,1,0:T(8,128)S(1)}, u32[]{:S(2)}, u32[]{:S(2)}) collective-permute-start(f32[1,32,128]{2,1,0:T(8,128)S(1)} %get-tuple-element.21), channel_id=1, source_target_pairs={{0,16},{16,32},{32,48},{48,64},{64,80},{80,96},{96,112},{112,128},... | collective-permute-start | bytes 49160 | tf_op jit(solution)/shard_map/ppermute | solution.py:14
  84.4 7.1 %collective-permute-start.8 = (f32[66,32,1]{0,1,2:T(8,128)S(1)}, f32[66,32,1]{0,1,2:T(8,128)S(1)}, u32[]{:S(2)}, u32[]{:S(2)}) collective-permute-start(f32[66,32,1]{0,1,2:T(8,128)S(1)} %copy.33), channel_id=1, source_target_pairs={{4,0},{8,4},{12,8},{5,1},{9,5},{13,9},{6,2},{10,6},{14,10},{7,3},{... | collective-permute-start | bytes 25352 | tf_op jit(solution)/shard_map/ppermute | solution.py:17
  87.5 5.9 %collective-permute-start.9 = (f32[66,32,1]{0,1,2:T(8,128)S(1)}, f32[66,32,1]{0,1,2:T(8,128)S(1)}, u32[]{:S(2)}, u32[]{:S(2)}) collective-permute-start(f32[66,32,1]{0,1,2:T(8,128)S(1)} %copy.35), channel_id=1, source_target_pairs={{0,4},{4,8},{8,12},{1,5},{5,9},{9,13},{2,6},{6,10},{10,14},{3,7},{... | collective-permute-start | bytes 25352 | tf_op jit(solution)/shard_map/ppermute | solution.py:14
  95.4 8.5 %collective-permute-start.12 = (f32[4,1152]{1,0:T(4,128)S(1)}, f32[4,1152]{1,0:T(4,128)S(1)}, u32[]{:S(2)}, u32[]{:S(2)}) collective-permute-start(f32[4,1152]{1,0:T(4,128)S(1)} %reduce_sum.18), channel_id=1, source_target_pairs={{0,4},{4,0},{8,12},{12,8},{1,5},{5,1},{9,13},{13,9},{2,6},{6,2},{1... | collective-permute-start | bytes 55304 | tf_op jit(solution)/shard_map/ppermute | solution.py:107
  98.6 11.2 %collective-permute-start.10 = (f32[66,1,130]{2,1,0:T(1,128)S(1)}, f32[66,1,130]{2,1,0:T(1,128)S(1)}, u32[]{:S(2)}, u32[]{:S(2)}) collective-permute-start(f32[66,1,130]{2,1,0:T(1,128)S(1)} %get-tuple-element.14), channel_id=1, source_target_pairs={{1,0},{2,1},{3,2},{5,4},{6,5},{7,6},{9,8},{10,9},{11,10},{13,12},{... | collective-permute-start | bytes 102968 | tf_op jit(solution)/shard_map/ppermute | solution.py:17
  99.9 9.9 %collective-permute-start.11 = (f32[66,1,130]{2,1,0:T(1,128)S(1)}, f32[66,1,130]{2,1,0:T(1,128)S(1)}, u32[]{:S(2)}, u32[]{:S(2)}) collective-permute-start(f32[66,1,130]{2,1,0:T(1,128)S(1)} %get-tuple-element.13), channel_id=1, source_target_pairs={{0,1},{1,2},{2,3},{4,5},{5,6},{6,7},{8,9},{9,10},{10,11},{12,13},{... | collective-permute-start | bytes 102968 | tf_op jit(solution)/shard_map/ppermute | solution.py:14
  103.9 4.2 %collective-permute-start.13 = (f32[4,1152]{1,0:T(4,128)S(1)}, f32[4,1152]{1,0:T(4,128)S(1)}, u32[]{:S(2)}, u32[]{:S(2)}) collective-permute-start(f32[4,1152]{1,0:T(4,128)S(1)} %add.188), channel_id=1, source_target_pairs={{0,8},{4,12},{8,0},{12,4},{1,9},{5,13},{9,1},{13,5},{2,10},{6,14},... | collective-permute-start | bytes 55304 | tf_op jit(solution)/shard_map/ppermute | solution.py:107
  108.1 21.4 %copy-start.4 = (f32[64,32,128]{2,1,0:T(8,128)S(1)}, f32[64,32,128]{2,1,0:T(8,128)}, u32[]{:S(2)}) copy-start(f32[64,32,128]{2,1,0:T(8,128)} %copy-done.3) | copy-start | bytes 3145732
  108.1 21.4 %copy-start.5 = (f32[66,32,1]{2,1,0:T(8,128)S(1)}, f32[66,32,1]{2,1,0:T(8,128)}, u32[]{:S(2)}) copy-start(f32[66,32,1]{2,1,0:T(8,128)} %copy.34) | copy-start | bytes 25348
  108.1 21.4 %copy-start.6 = (f32[66,32,1]{2,1,0:T(8,128)S(1)}, f32[66,32,1]{2,1,0:T(8,128)}, u32[]{:S(2)}) copy-start(f32[66,32,1]{2,1,0:T(8,128)} %copy.36) | copy-start | bytes 25348
  108.1 19.6 %collective-permute-start.14 = (f32[4,1152]{1,0:T(4,128)S(1)}, f32[4,1152]{1,0:T(4,128)S(1)}, u32[]{:S(2)}, u32[]{:S(2)}) collective-permute-start(f32[4,1152]{1,0:T(4,128)S(1)} %add.189), channel_id=1, source_target_pairs={{0,1},{1,0},{2,3},{3,2},{4,5},{5,4},{6,7},{7,6},{8,9},{9,8},{10,11... | collective-permute-start | bytes 55304 | tf_op jit(solution)/shard_map/ppermute | solution.py:107
  127.8 10.6 %collective-permute-start.15 = (f32[4,1152]{1,0:T(4,128)S(1)}, f32[4,1152]{1,0:T(4,128)S(1)}, u32[]{:S(2)}, u32[]{:S(2)}) collective-permute-start(f32[4,1152]{1,0:T(4,128)S(1)} %add.190), channel_id=1, source_target_pairs={{0,2},{1,3},{2,0},{3,1},{4,6},{5,7},{6,4},{7,5},{8,10},{9,11},{10,... | collective-permute-start | bytes 55304 | tf_op jit(solution)/shard_map/ppermute | solution.py:107
  140.0 30.4 %all-to-all-start.1 = ((f32[16,4,1152]{2,1,0:T(4,128)}), f32[16,4,1152]{2,1,0:T(4,128)S(1)}, u32[]{:S(2)}, u32[]{:S(2)}) async-start(f32[16,4,1152]{2,1,0:T(4,128)} %broadcast_in_dim.2), calls=%async_computation.1 | async-start | bytes 589824 | tf_op jit(solution)/shard_map/all_to_all | solution.py:111
  (8 other events, 26.8 us)

commit v3 on v2

v3 whole, which is shorter than its diff:
```python
import jax
import jax.numpy as jnp
from jax import lax
from jax.experimental import pallas as pl
from jax.experimental.pallas import tpu as pltpu
from jax.sharding import PartitionSpec as P

INTERPRET = False


def actuate(velocity_probe, coef):
    rows = velocity_probe.shape[0]
    parts = velocity_probe.reshape(rows, 3, -1)
    magnitude = jnp.sqrt(jnp.sum(parts * parts, axis=1) + 1e-06)
    return (-2.0 * coef[:, None, :] * magnitude[:, None, :] * parts).reshape(rows, -1)


def faces(block, lead):
    out = []
    for axis, dim in (("gx", lead), ("gz", lead + 1), ("gy", lead + 2)):
        count = lax.axis_size(axis)
        forward = [(i, i + 1) for i in range(count - 1)]
        backward = [(target, source) for source, target in forward]
        size = block.shape[dim]
        low = lax.ppermute(lax.index_in_dim(block, size - 1, dim, keepdims=False), axis, forward)
        high = lax.ppermute(lax.index_in_dim(block, 0, dim, keepdims=False), axis, backward)
        if axis == "gy":
            low = jnp.swapaxes(low, -1, -2)
            high = jnp.swapaxes(high, -1, -2)
        out += [low, high]
    return out


def neighbours(ref, xlo, xhi, zlo, zhi, ylo, yhi, lead, x, centre):
    nx = ref.shape[-3]
    nz, ny = centre.shape
    sub = lax.broadcasted_iota(jnp.int32, (nz, ny), 0)
    lane = lax.broadcasted_iota(jnp.int32, (nz, ny), 1)
    column = lax.broadcasted_iota(jnp.int32, (nz, nx), 1)
    prev = ref[lead + (jnp.maximum(x - 1, 0),)]
    nxt = ref[lead + (jnp.minimum(x + 1, nx - 1),)]
    xm = jnp.where(x == 0, xlo[lead], prev)
    xp = jnp.where(x == nx - 1, xhi[lead], nxt)
    zl = zlo[lead + (pl.ds(x, 1), slice(None))]
    zh = zhi[lead + (pl.ds(x, 1), slice(None))]
    zm = jnp.where(sub == 0, zl, pltpu.roll(centre, 1, 0))
    zp = jnp.where(sub == nz - 1, zh, pltpu.roll(centre, nz - 1, 0))
    yl = jnp.sum(jnp.where(column == x, ylo[lead], 0.0), axis=1, keepdims=True)
    yh = jnp.sum(jnp.where(column == x, yhi[lead], 0.0), axis=1, keepdims=True)
    ym = jnp.where(lane == 0, yl, pltpu.roll(centre, 1, 1))
    yp = jnp.where(lane == ny - 1, yh, pltpu.roll(centre, ny - 1, 1))
    return xm, xp, ym, yp, zm, zp


def viscosity_kernel(u, xlo, xhi, zlo, zhi, ylo, yhi, nu):
    def plane(x, carry):
        grads = []
        for c in range(3):
            xm, xp, ym, yp, zm, zp = neighbours(u, xlo, xhi, zlo, zhi, ylo, yhi, (c,), x, u[c, x])
            grads.append([0.5 * (xp - xm), 0.5 * (yp - ym), 0.5 * (zp - zm)])
        total = jnp.zeros_like(grads[0][0])
        for c in range(3):
            for d in range(3):
                strain = 0.5 * (grads[c][d] + grads[d][c])
                total = total + strain * strain
        nu[x] = 0.05 + 1.0 * jnp.sqrt(2.0 * total + 1e-06)
        return carry

    lax.fori_loop(0, u.shape[1], plane, 0)


def advance_kernel(planes, u, xlo, xhi, zlo, zhi, ylo, yhi, nu, nxlo, nxhi, nzlo, nzhi, nylo, nyhi, sent, out):
    slots = sent.shape[0]

    def plane(x, carry):
        here = nu[x]
        nxm, nxp, nym, nyp, nzm, nzp = neighbours(nu, nxlo, nxhi, nzlo, nzhi, nylo, nyhi, (), x, here)
        nu_up = [0.5 * (here + nxp), 0.5 * (here + nyp), 0.5 * (here + nzp)]
        nu_low = [0.5 * (here + nxm), 0.5 * (here + nym), 0.5 * (here + nzm)]
        centres = [u[c, x] for c in range(3)]
        for c in range(3):
            center = centres[c]
            xm, xp, ym, yp, zm, zp = neighbours(u, xlo, xhi, zlo, zhi, ylo, yhi, (c,), x, center)
            upper = (xp, yp, zp)
            lower = (xm, ym, zm)
            advect = jnp.zeros_like(center)
            spread = jnp.zeros_like(center)
            for d in range(3):
                advect = advect + centres[d] * 0.5 * (upper[d] - lower[d])
                spread = spread + nu_up[d] * (upper[d] - center) - nu_low[d] * (center - lower[d])
            impulse = jnp.zeros_like(center)
            for s in range(slots):
                impulse = impulse + jnp.where(planes[s] == x, sent[s, c], 0.0)
            out[c, x] = center + 0.25 * (spread - advect) + impulse
        return carry

    lax.fori_loop(0, u.shape[1], plane, 0)


def vmem_call(kernel, out_shape, count, smem=0):
    specs = [pl.BlockSpec(memory_space=pltpu.SMEM)] * smem
    specs += [pl.BlockSpec(memory_space=pltpu.VMEM)] * (count - smem)
    return pl.pallas_call(
        kernel,
        out_shape=out_shape,
        in_specs=specs,
        out_specs=pl.BlockSpec(memory_space=pltpu.VMEM),
        interpret=INTERPRET,
    )


def stencil(velocity, planes, sent):
    u_faces = faces(velocity, 1)
    nu = vmem_call(
        viscosity_kernel, jax.ShapeDtypeStruct(velocity.shape[1:], jnp.float32), 7
    )(velocity, *u_faces)
    nu_faces = faces(nu, 0)
    return vmem_call(
        advance_kernel, jax.ShapeDtypeStruct(velocity.shape, jnp.float32), 16, smem=1
    )(planes, velocity, *u_faces, nu, *nu_faces, sent)


def body(velocity, tile_turbine, tile_plane, tile_weight, chord):
    cx = velocity.shape[1]
    vertical_coord = velocity.shape[2]
    spanwise_coord = velocity.shape[3]
    tile_count = tile_turbine.shape[3]
    actuator_count = tile_weight.shape[4]
    nturb = chord.shape[0]
    turbine_list = tile_turbine.reshape(tile_count)
    rotor_planes = tile_plane.reshape(tile_count)
    spread_weights = tile_weight.reshape(
        tile_count, actuator_count, vertical_coord * spanwise_coord
    )
    flat = velocity.reshape(3, cx, vertical_coord * spanwise_coord)
    picks = (rotor_planes[:, None] == jnp.arange(cx, dtype=jnp.int32)[None, :]).astype(jnp.float32)
    tiles = jnp.einsum("sx,cxq->scq", picks, flat, precision=lax.Precision.HIGHEST).astype(
        jnp.bfloat16
    )
    block_local = jnp.einsum(
        "spq,scq->scp", spread_weights, tiles, preferred_element_type=jnp.float32
    )
    owning_block = (turbine_list[:, None] == jnp.arange(nturb, dtype=jnp.int32)[None, :]).astype(
        jnp.float32
    )
    partial_sample = jnp.einsum(
        "yr,yw->rw",
        owning_block,
        block_local.reshape(tile_count, -1),
        precision=lax.Precision.HIGHEST,
    )
    rows = lax.axis_size("gx")
    per_row = nturb // rows
    received = lax.all_to_all(
        partial_sample.reshape(rows, per_row, -1), "gx", split_axis=0, concat_axis=0, tiled=True
    )
    owned = jnp.sum(received, axis=0)
    for axis in ("gy", "gz"):
        count = lax.axis_size(axis)
        step = 1
        while step < count:
            pairs = [(i, i ^ step) for i in range(count)]
            owned = owned + lax.ppermute(owned, axis, pairs)
            step *= 2
    owned_coef = lax.dynamic_slice_in_dim(chord, lax.axis_index("gx") * per_row, per_row, 0)
    owned_force = actuate(owned, owned_coef)
    forces = lax.all_to_all(
        jnp.broadcast_to(owned_force[None], (rows,) + owned_force.shape),
        "gx", split_axis=0, concat_axis=0, tiled=True,
    ).reshape(nturb, -1)
    tile_force = jnp.dot(owning_block, forces, precision=lax.Precision.HIGHEST).astype(jnp.bfloat16)
    forces_sent = jnp.einsum(
        "axz,ahx->ahz",
        spread_weights,
        tile_force.reshape(tile_count, 3, actuator_count),
        preferred_element_type=jnp.float32,
    ).reshape(tile_count, 3, vertical_coord, spanwise_coord)
    predicted = stencil(velocity[:, :, :, :], rotor_planes, forces_sent)
    return (predicted, forces)


def solution(mesh):
    placed = (
        P(None, "gx", "gz", "gy"),
        P("gx", "gz", "gy", None),
        P("gx", "gz", "gy", None),
        P("gx", "gz", "gy", None, None, None),
        P(),
    )
    return jax.shard_map(
        body,
        mesh=mesh,
        in_specs=placed,
        out_specs=(P(None, "gx", "gz", "gy"), P()),
        check_vma=False,
    )
```

time: 181 us -> 138 us (0.76)
  the two profiles are of different devices: /device:TPU:1 before, /device:TPU:44 now
where the time goes in v3:
time: 138 us; the launch traced here: 137 us
  starting transfers between devices  44.4 us (32%)
  Pallas kernels  33.7 us (24%)
  local copies, waits for them, and re-layouts  22.2 us (16%)
  blocking collectives  18.6 us (13%)
  matrix products  10.2 us (7%)
  waiting for transfers between devices  6.35 us (5%)
    all_to_all x1, blocking collectives, body(): lax.all_to_all(partial_sample.reshape(rows, per_row, -1), 'gx', split_axi...  18.6 us
    ppermute x6, starting transfers between devices, faces(): lax.ppermute(lax.index_in_dim(block, 0, dim, keepdims=False), axis, backw...  18.2 us
    pallas_call x1, Pallas kernels, stencil(): vmem_call(advance_kernel, jax.ShapeDtypeStruct(velocity.shape, jnp.float3...  18 us
    pallas_call x1, Pallas kernels, stencil(): vmem_call(viscosity_kernel, jax.ShapeDtypeStruct(velocity.shape[1:], jnp....  15.7 us
    ppermute x6, starting transfers between devices, faces(): lax.ppermute(lax.index_in_dim(block, size - 1, dim, keepdims=False), axis...  14.7 us
    unnamed x36, local copies, waits for them, and re-layouts  8.44 us
    slice x4, local copies, waits for them, and re-layouts, faces(): lax.index_in_dim(block, 0, dim, keepdims=False)  7.73 us
    all_to_all x1, starting transfers between devices, body(): lax.all_to_all(jnp.broadcast_to(owned_force[None], (rows,) + owned_force....  6.29 us
  transfers between devices with their start and end apart: 17, of which 3 were waited for; matrix products, arithmetic and copies ran while one was open for 15% of the time, Pallas kernels for 11%

profile of v3, /device:TPU:44, one launch (start us, length us, event | category | flops | bytes accessed | tf_op | source)
XLA Modules:
  0.0 137.2 jit_solution(16861810130482055334)
XLA Ops:
  0.7 2.9 %reshape.59 = f32[3,64,4096]{2,1,0:T(8,128)S(1)} reshape(f32[3,64,32,128]{3,2,1,0:T(8,128)} %u.3) | data formatting | bytes 6291456 | tf_op jit(solution)/shard_map/reshape | solution.py:135
  4.7 4.7 %fusion.2 = f32[2,3,384]{2,1,0:T(4,128)S(1)} fusion(bf16[1,1,1,2,384,4096]{5,4,3,2,1,0:T(8,128)(2,1)} %param.8, bf16[2,3,4096]{2,0,1:T(2,128)(2,1)S(1)} %convolution_convert_fusion), kind=kOutput, calls=%fused_computation.2 | convolution fusion | flops 18874368 | bytes 6349824 | tf_op jit(solution)/shard_map/spq,scq->scp/dot_general | solution.py:140
  10.0 18.6 %all_to_all.10 = f32[16,4,1152]{2,1,0:T(4,128)S(1)} all-to-all(f32[16,4,1152]{2,1,0:T(4,128)S(1)} %copy.40), channel_id=1, replica_groups=mesh['gx'=16,'gy'=4,'gz'=4] {'gx'}, dimensions={0} | all-to-all | bytes 589824 | tf_op jit(solution)/shard_map/all_to_all | solution.py:154
  30.7 3.5 %collective-permute-start.2 = (f32[3,64,128]{2,1,0:T(8,128)}, f32[3,64,128]{2,1,0:T(8,128)S(1)}, u32[]{:S(2)}, u32[]{:S(2)}) collective-permute-start(f32[3,64,128]{2,1,0:T(8,128)} %bitcast.3), channel_id=1, source_target_pairs={{0,1},{1,2},{2,3},{4,5},{5,6},{6,7},{8,9},{9,10},{10,11},{12,13},{... | collective-permute-start | bytes 294920 | tf_op jit(solution)/shard_map/ppermute | solution.py:25
  34.1 2.4 %collective-permute-start.3 = (f32[3,64,128]{2,1,0:T(8,128)S(1)}, f32[3,64,128]{2,1,0:T(8,128)S(1)}, u32[]{:S(2)}, u32[]{:S(2)}) collective-permute-start(f32[3,64,128]{2,1,0:T(8,128)S(1)} %bitcast.54), channel_id=1, source_target_pairs={{1,0},{2,1},{3,2},{5,4},{6,5},{7,6},{9,8},{10,9},{11,10},{13,12},{... | collective-permute-start | bytes 294920 | tf_op jit(solution)/shard_map/ppermute | solution.py:26
  37.4 3.9 %fusion.17 = (f32[3,64,32,1]{3,2,1,0:T(8,128)}, f32[3,64,32,1]{3,2,1,0:T(8,128)}) fusion(f32[3,64,32,128]{3,2,1,0:T(8,128)S(1)} %copy-done), kind=kLoop, calls=%fused_computation.25 | loop fusion | bytes 98304 | tf_op jit(solution)/shard_map/slice | solution.py:26
  41.3 3.2 %copy.48 = f32[3,64,32,1]{1,2,0,3:T(8,128)} copy(f32[3,64,32,1]{3,2,1,0:T(8,128)} %get-tuple-element.5) | data formatting | bytes 49152
  44.5 3.0 %collective-permute-start.4 = (f32[3,64,32]{1,2,0:T(8,128)}, f32[3,64,32]{1,2,0:T(8,128)S(1)}, u32[]{:S(2)}, u32[]{:S(2)}) collective-permute-start(f32[3,64,32]{1,2,0:T(8,128)} %bitcast.57), channel_id=1, source_target_pairs={{0,4},{4,8},{8,12},{1,5},{5,9},{9,13},{2,6},{6,10},{10,14},{3,7},{... | collective-permute-start | bytes 73736 | tf_op jit(solution)/shard_map/ppermute | solution.py:25
  50.7 3.2 %collective-permute-start.1 = (f32[3,32,128]{2,1,0:T(8,128)}, f32[3,32,128]{2,1,0:T(8,128)S(1)}, u32[]{:S(2)}, u32[]{:S(2)}) collective-permute-start(f32[3,32,128]{2,1,0:T(8,128)} %get-tuple-element.8), channel_id=1, source_target_pairs={{16,0},{32,16},{48,32},{64,48},{80,64},{96,80},{112,96},{128,112},... | collective-permute-start | bytes 147464 | tf_op jit(solution)/shard_map/ppermute | solution.py:26
  53.9 2.7 %copy.49 = f32[3,64,32,1]{1,2,0,3:T(8,128)S(1)} copy(f32[3,64,32,1]{3,2,1,0:T(8,128)} %get-tuple-element.4) | data formatting | bytes 49152
  56.6 2.8 %collective-permute-start.5 = (f32[3,64,32]{1,2,0:T(8,128)S(1)}, f32[3,64,32]{1,2,0:T(8,128)S(1)}, u32[]{:S(2)}, u32[]{:S(2)}) collective-permute-start(f32[3,64,32]{1,2,0:T(8,128)S(1)} %bitcast.58), channel_id=1, source_target_pairs={{4,0},{8,4},{12,8},{5,1},{9,5},{13,9},{6,2},{10,6},{14,10},{7,3},{... | collective-permute-start | bytes 73736 | tf_op jit(solution)/shard_map/ppermute | solution.py:26
  59.4 3.2 %collective-permute-done.5 = f32[3,64,32]{1,2,0:T(8,128)S(1)} collective-permute-done((f32[3,64,32]{1,2,0:T(8,128)S(1)}, f32[3,64,32]{1,2,0:T(8,128)S(1)}, u32[]{:S(2)}, u32[]{:S(2)}) %collective-permute-start.5) | collective-permute-done | bytes 24608 | tf_op jit(solution)/shard_map/ppermute | solution.py:26
  62.6 3.0 %collective-permute-start.15 = (f32[4,1152]{1,0:T(4,128)S(1)}, f32[4,1152]{1,0:T(4,128)S(1)}, u32[]{:S(2)}, u32[]{:S(2)}) collective-permute-start(f32[4,1152]{1,0:T(4,128)S(1)} %add.28), channel_id=1, source_target_pairs={{0,2},{1,3},{2,0},{3,1},{4,6},{5,7},{6,4},{7,5},{8,10},{9,11},{10,... | collective-permute-start | bytes 55304 | tf_op jit(solution)/shard_map/ppermute | solution.py:163
  66.3 15.7 %shard_map.68.nu = f32[64,32,128]{2,1,0:T(8,128)} custom-call(f32[3,64,32,128]{3,2,1,0:T(8,128)} %u.3, f32[3,32,128]{2,1,0:T(8,128)} %copy-done.5, f32[3,32,128]{2,1,0:T(8,128)} %copy-done.6, f32[3,64,128]{2,1,0:T(8,128)} %copy-done.2, f32[3,64,128]{2,1,0:T(8,128)} %copy-done.3, f32[3,32,64]{2,1,0:T(8,128)} %bitcast.50, f32[3,32,64]{2,1,0:T(8,128)} %bitcast.52), custom_call_target="tpu_custom_call" | custom-call | tf_op jit(solution)/shard_map/pallas_call | solution.py:114
  83.5 6.3 %all-to-all-start.1 = ((f32[16,4,1152]{2,1,0:T(4,128)}), f32[16,4,1152]{2,1,0:T(4,128)S(1)}, u32[]{:S(2)}, u32[]{:S(2)}) async-start(f32[16,4,1152]{2,1,0:T(4,128)} %broadcast_in_dim.2), calls=%async_computation.1 | async-start | bytes 589824 | tf_op jit(solution)/shard_map/all_to_all | solution.py:167
  90.5 2.0 %collective-permute-start.6 = (f32[32,128]{1,0:T(8,128)S(1)}, f32[32,128]{1,0:T(8,128)S(1)}, u32[]{:S(2)}, u32[]{:S(2)}) collective-permute-start(f32[32,128]{1,0:T(8,128)S(1)} %get-tuple-element.15), channel_id=1, source_target_pairs={{0,16},{16,32},{32,48},{48,64},{64,80},{80,96},{96,112},{112,128},... | collective-permute-start | bytes 49160 | tf_op jit(solution)/shard_map/ppermute | solution.py:25
  92.6 3.5 %collective-permute-start.7 = (f32[32,128]{1,0:T(8,128)S(1)}, f32[32,128]{1,0:T(8,128)S(1)}, u32[]{:S(2)}, u32[]{:S(2)}) collective-permute-start(f32[32,128]{1,0:T(8,128)S(1)} %get-tuple-element.14), channel_id=1, source_target_pairs={{16,0},{32,16},{48,32},{64,48},{80,64},{96,80},{112,96},{128,112},... | collective-permute-start | bytes 49160 | tf_op jit(solution)/shard_map/ppermute | solution.py:26
  97.2 2.4 %collective-permute-start.8 = (f32[64,128]{1,0:T(8,128)S(1)}, f32[64,128]{1,0:T(8,128)S(1)}, u32[]{:S(2)}, u32[]{:S(2)}) collective-permute-start(f32[64,128]{1,0:T(8,128)S(1)} %bitcast.60), channel_id=1, source_target_pairs={{0,1},{1,2},{2,3},{4,5},{5,6},{6,7},{8,9},{9,10},{10,11},{12,13},{... | collective-permute-start | bytes 98312 | tf_op jit(solution)/shard_map/ppermute | solution.py:25
  99.6 3.5 %collective-permute-start.9 = (f32[64,128]{1,0:T(8,128)S(1)}, f32[64,128]{1,0:T(8,128)S(1)}, u32[]{:S(2)}, u32[]{:S(2)}) collective-permute-start(f32[64,128]{1,0:T(8,128)S(1)} %bitcast.59), channel_id=1, source_target_pairs={{1,0},{2,1},{3,2},{5,4},{6,5},{7,6},{9,8},{10,9},{11,10},{13,12},{... | collective-permute-start | bytes 98312 | tf_op jit(solution)/shard_map/ppermute | solution.py:26
  103.0 2.0 %fusion.19 = (f32[64,32,1]{2,1,0:T(8,128)S(1)}, f32[64,32,1]{2,1,0:T(8,128)S(1)}) fusion(f32[64,32,128]{2,1,0:T(8,128)} %shard_map.68.nu), kind=kLoop, calls=%fused_computation.27 | loop fusion | bytes 32768 | tf_op jit(solution)/shard_map/slice | solution.py:26
  108.6 2.7 %collective-permute-done.10 = f32[64,32]{0,1:T(8,128)S(1)} collective-permute-done((f32[64,32]{0,1:T(8,128)S(1)}, f32[64,32]{0,1:T(8,128)S(1)}, u32[]{:S(2)}, u32[]{:S(2)}) %collective-permute-start.10) | collective-permute-done | bytes 8224 | tf_op jit(solution)/shard_map/ppermute | solution.py:25
  111.3 2.8 %collective-permute-start.11 = (f32[64,32]{0,1:T(8,128)S(1)}, f32[64,32]{0,1:T(8,128)S(1)}, u32[]{:S(2)}, u32[]{:S(2)}) collective-permute-start(f32[64,32]{0,1:T(8,128)S(1)} %bitcast.63), channel_id=1, source_target_pairs={{4,0},{8,4},{12,8},{5,1},{9,5},{13,9},{6,2},{10,6},{14,10},{7,3},{... | collective-permute-start | bytes 24584 | tf_op jit(solution)/shard_map/ppermute | solution.py:26
  114.1 3.7 %fusion = f32[2,3,4096]{2,1,0:T(4,128)S(1)} fusion(bf16[2,3,384]{2,1,0:T(4,128)(2,1)S(1)} %reshape.63, bf16[1,1,1,2,384,4096]{5,4,3,2,1,0:T(8,128)(2,1)} %param.8), kind=kOutput, calls=%fused_computation | convolution fusion | flops 18874368 | bytes 6394368 | tf_op jit(solution)/shard_map/axz,ahx->ahz/dot_general | solution.py:172
  119.2 18.0 %shard_map.69 = f32[3,64,32,128]{3,2,1,0:T(8,128)} custom-call(s32[2]{0:T(128)} %bitcast.67, f32[3,64,32,128]{3,2,1,0:T(8,128)} %u.3, f32[3,32,128]{2,1,0:T(8,128)} %copy-done.5, f32[3,32,128]{2,1,0:T(8,128)} %copy-done.6, f32[3,64,128]{2,1,0:T(8,128)} %copy-done.2, f32[3,64,128]{2,1,0:T(8,128)} %copy-done.3, f32[3,32,64]{2,1,0:T(8,128)} %bitcast.51, ...), custom_call_target="tpu_custom_call" | custom-call | tf_op jit(solution)/shard_map/pallas_call | solution.py:118
  (77 shorter events, 16.7 us)
Async XLA Ops:
  0.6 2.9 %copy-start.15 = (s32[1,1,1,2]{3,2,1,0:T(1,128)S(1)}, s32[1,1,1,2]{3,2,1,0:T(1,128)}, u32[]{:S(2)}) copy-start(s32[1,1,1,2]{3,2,1,0:T(1,128)} %param.7) | copy-start | bytes 28
  4.7 4.7 %copy-start.14 = (s32[1,1,1,2]{3,2,1,0:T(1,128)S(1)}, s32[1,1,1,2]{3,2,1,0:T(1,128)}, u32[]{:S(2)}) copy-start(s32[1,1,1,2]{3,2,1,0:T(1,128)} %param.6) | copy-start | bytes 28
  4.7 25.2 %copy-start = (f32[3,64,32,128]{3,2,1,0:T(8,128)S(1)}, f32[3,64,32,128]{3,2,1,0:T(8,128)}, u32[]{:S(2)}) copy-start(f32[3,64,32,128]{3,2,1,0:T(8,128)} %u.3) | copy-start | bytes 9437188
  28.6 7.9 %collective-permute-start.12 = (f32[4,1152]{1,0:T(4,128)S(1)}, f32[4,1152]{1,0:T(4,128)S(1)}, u32[]{:S(2)}, u32[]{:S(2)}) collective-permute-start(f32[4,1152]{1,0:T(4,128)S(1)} %reduce_sum.18), channel_id=1, source_target_pairs={{0,4},{4,0},{8,12},{12,8},{1,5},{5,1},{9,13},{13,9},{2,6},{6,2},{1... | collective-permute-start | bytes 55304 | tf_op jit(solution)/shard_map/ppermute | solution.py:163
  30.7 35.0 %collective-permute-start.2 = (f32[3,64,128]{2,1,0:T(8,128)}, f32[3,64,128]{2,1,0:T(8,128)S(1)}, u32[]{:S(2)}, u32[]{:S(2)}) collective-permute-start(f32[3,64,128]{2,1,0:T(8,128)} %bitcast.3), channel_id=1, source_target_pairs={{0,1},{1,2},{2,3},{4,5},{5,6},{6,7},{8,9},{9,10},{10,11},{12,13},{... | collective-permute-start | bytes 294920 | tf_op jit(solution)/shard_map/ppermute | solution.py:25
  34.1 31.5 %collective-permute-start.3 = (f32[3,64,128]{2,1,0:T(8,128)S(1)}, f32[3,64,128]{2,1,0:T(8,128)S(1)}, u32[]{:S(2)}, u32[]{:S(2)}) collective-permute-start(f32[3,64,128]{2,1,0:T(8,128)S(1)} %bitcast.54), channel_id=1, source_target_pairs={{1,0},{2,1},{3,2},{5,4},{6,5},{7,6},{9,8},{10,9},{11,10},{13,12},{... | collective-permute-start | bytes 294920 | tf_op jit(solution)/shard_map/ppermute | solution.py:26
  36.5 11.0 %collective-permute-start.13 = (f32[4,1152]{1,0:T(4,128)S(1)}, f32[4,1152]{1,0:T(4,128)S(1)}, u32[]{:S(2)}, u32[]{:S(2)}) collective-permute-start(f32[4,1152]{1,0:T(4,128)S(1)} %add.26), channel_id=1, source_target_pairs={{0,8},{4,12},{8,0},{12,4},{1,9},{5,13},{9,1},{13,5},{2,10},{6,14},... | collective-permute-start | bytes 55304 | tf_op jit(solution)/shard_map/ppermute | solution.py:163
  44.5 6.2 %collective-permute-start.4 = (f32[3,64,32]{1,2,0:T(8,128)}, f32[3,64,32]{1,2,0:T(8,128)S(1)}, u32[]{:S(2)}, u32[]{:S(2)}) collective-permute-start(f32[3,64,32]{1,2,0:T(8,128)} %bitcast.57), channel_id=1, source_target_pairs={{0,4},{4,8},{8,12},{1,5},{5,9},{9,13},{2,6},{6,10},{10,14},{3,7},{... | collective-permute-start | bytes 73736 | tf_op jit(solution)/shard_map/ppermute | solution.py:25
  47.6 9.0 %collective-permute-start.14 = (f32[4,1152]{1,0:T(4,128)S(1)}, f32[4,1152]{1,0:T(4,128)S(1)}, u32[]{:S(2)}, u32[]{:S(2)}) collective-permute-start(f32[4,1152]{1,0:T(4,128)S(1)} %add.27), channel_id=1, source_target_pairs={{0,1},{1,0},{2,3},{3,2},{4,5},{5,4},{6,7},{7,6},{8,9},{9,8},{10,11... | collective-permute-start | bytes 55304 | tf_op jit(solution)/shard_map/ppermute | solution.py:163
  48.3 17.3 %collective-permute-start = (f32[3,32,128]{2,1,0:T(8,128)}, f32[3,32,128]{2,1,0:T(8,128)S(1)}, u32[]{:S(2)}, u32[]{:S(2)}) collective-permute-start(f32[3,32,128]{2,1,0:T(8,128)} %get-tuple-element.9), channel_id=1, source_target_pairs={{0,16},{16,32},{32,48},{48,64},{64,80},{80,96},{96,112},{112,128},... | collective-permute-start | bytes 147464 | tf_op jit(solution)/shard_map/ppermute | solution.py:25
  50.7 15.0 %copy-start.4 = (f32[3,64,32]{1,2,0:T(8,128)}, f32[3,64,32]{1,2,0:T(8,128)S(1)}, u32[]{:S(2)}) copy-start(f32[3,64,32]{1,2,0:T(8,128)S(1)} %collective-permute-done.4) | copy-start | bytes 73732
  50.7 14.9 %collective-permute-start.1 = (f32[3,32,128]{2,1,0:T(8,128)}, f32[3,32,128]{2,1,0:T(8,128)S(1)}, u32[]{:S(2)}, u32[]{:S(2)}) collective-permute-start(f32[3,32,128]{2,1,0:T(8,128)} %get-tuple-element.8), channel_id=1, source_target_pairs={{16,0},{32,16},{48,32},{64,48},{80,64},{96,80},{112,96},{128,112},... | collective-permute-start | bytes 147464 | tf_op jit(solution)/shard_map/ppermute | solution.py:26
  56.6 6.0 %collective-permute-start.5 = (f32[3,64,32]{1,2,0:T(8,128)S(1)}, f32[3,64,32]{1,2,0:T(8,128)S(1)}, u32[]{:S(2)}, u32[]{:S(2)}) collective-permute-start(f32[3,64,32]{1,2,0:T(8,128)S(1)} %bitcast.58), channel_id=1, source_target_pairs={{4,0},{8,4},{12,8},{5,1},{9,5},{13,9},{6,2},{10,6},{14,10},{7,3},{... | collective-permute-start | bytes 73736 | tf_op jit(solution)/shard_map/ppermute | solution.py:26
  62.6 3.1 %copy-start.7 = (f32[3,64,32]{1,2,0:T(8,128)}, f32[3,64,32]{1,2,0:T(8,128)S(1)}, u32[]{:S(2)}) copy-start(f32[3,64,32]{1,2,0:T(8,128)S(1)} %collective-permute-done.5) | copy-start | bytes 73732
  62.6 19.4 %collective-permute-start.15 = (f32[4,1152]{1,0:T(4,128)S(1)}, f32[4,1152]{1,0:T(4,128)S(1)}, u32[]{:S(2)}, u32[]{:S(2)}) collective-permute-start(f32[4,1152]{1,0:T(4,128)S(1)} %add.28), channel_id=1, source_target_pairs={{0,2},{1,3},{2,0},{3,1},{4,6},{5,7},{6,4},{7,5},{8,10},{9,11},{10,... | collective-permute-start | bytes 55304 | tf_op jit(solution)/shard_map/ppermute | solution.py:163
  83.5 24.7 %all-to-all-start.1 = ((f32[16,4,1152]{2,1,0:T(4,128)}), f32[16,4,1152]{2,1,0:T(4,128)S(1)}, u32[]{:S(2)}, u32[]{:S(2)}) async-start(f32[16,4,1152]{2,1,0:T(4,128)} %broadcast_in_dim.2), calls=%async_computation.1 | async-start | bytes 589824 | tf_op jit(solution)/shard_map/all_to_all | solution.py:167
  90.5 28.0 %collective-permute-start.6 = (f32[32,128]{1,0:T(8,128)S(1)}, f32[32,128]{1,0:T(8,128)S(1)}, u32[]{:S(2)}, u32[]{:S(2)}) collective-permute-start(f32[32,128]{1,0:T(8,128)S(1)} %get-tuple-element.15), channel_id=1, source_target_pairs={{0,16},{16,32},{32,48},{48,64},{64,80},{80,96},{96,112},{112,128},... | collective-permute-start | bytes 49160 | tf_op jit(solution)/shard_map/ppermute | solution.py:25
  92.6 26.0 %collective-permute-start.7 = (f32[32,128]{1,0:T(8,128)S(1)}, f32[32,128]{1,0:T(8,128)S(1)}, u32[]{:S(2)}, u32[]{:S(2)}) collective-permute-start(f32[32,128]{1,0:T(8,128)S(1)} %get-tuple-element.14), channel_id=1, source_target_pairs={{16,0},{32,16},{48,32},{64,48},{80,64},{96,80},{112,96},{128,112},... | collective-permute-start | bytes 49160 | tf_op jit(solution)/shard_map/ppermute | solution.py:26
  97.2 21.4 %collective-permute-start.8 = (f32[64,128]{1,0:T(8,128)S(1)}, f32[64,128]{1,0:T(8,128)S(1)}, u32[]{:S(2)}, u32[]{:S(2)}) collective-permute-start(f32[64,128]{1,0:T(8,128)S(1)} %bitcast.60), channel_id=1, source_target_pairs={{0,1},{1,2},{2,3},{4,5},{5,6},{6,7},{8,9},{9,10},{10,11},{12,13},{... | collective-permute-start | bytes 98312 | tf_op jit(solution)/shard_map/ppermute | solution.py:25
  99.6 19.0 %collective-permute-start.9 = (f32[64,128]{1,0:T(8,128)S(1)}, f32[64,128]{1,0:T(8,128)S(1)}, u32[]{:S(2)}, u32[]{:S(2)}) collective-permute-start(f32[64,128]{1,0:T(8,128)S(1)} %bitcast.59), channel_id=1, source_target_pairs={{1,0},{2,1},{3,2},{5,4},{6,5},{7,6},{9,8},{10,9},{11,10},{13,12},{... | collective-permute-start | bytes 98312 | tf_op jit(solution)/shard_map/ppermute | solution.py:26
  105.7 5.6 %collective-permute-start.10 = (f32[64,32]{0,1:T(8,128)S(1)}, f32[64,32]{0,1:T(8,128)S(1)}, u32[]{:S(2)}, u32[]{:S(2)}) collective-permute-start(f32[64,32]{0,1:T(8,128)S(1)} %bitcast.64), channel_id=1, source_target_pairs={{0,4},{4,8},{8,12},{1,5},{5,9},{9,13},{2,6},{6,10},{10,14},{3,7},{... | collective-permute-start | bytes 24584 | tf_op jit(solution)/shard_map/ppermute | solution.py:25
  108.3 9.5 %copy-start.1 = (f32[64,1152]{1,0:T(8,128)}, f32[64,1152]{1,0:T(8,128)S(1)}, u32[]{:S(2)}) copy-start(f32[64,1152]{1,0:T(8,128)S(1)} %reshape.62) | copy-start | bytes 884740
  111.3 6.5 %copy-start.12 = (f32[64,32]{0,1:T(8,128)}, f32[64,32]{0,1:T(8,128)S(1)}, u32[]{:S(2)}) copy-start(f32[64,32]{0,1:T(8,128)S(1)} %collective-permute-done.10) | copy-start | bytes 24580
  111.3 7.2 %collective-permute-start.11 = (f32[64,32]{0,1:T(8,128)S(1)}, f32[64,32]{0,1:T(8,128)S(1)}, u32[]{:S(2)}, u32[]{:S(2)}) collective-permute-start(f32[64,32]{0,1:T(8,128)S(1)} %bitcast.63), channel_id=1, source_target_pairs={{4,0},{8,4},{12,8},{5,1},{9,5},{13,9},{6,2},{10,6},{14,10},{7,3},{... | collective-permute-start | bytes 24584 | tf_op jit(solution)/shard_map/ppermute | solution.py:26
  (9 other events, 5.6 us)

commit v4 on v3

--- a/solution.py
+++ b/solution.py
@@ -149,25 +149,28 @@
         block_local.reshape(tile_count, -1),
         precision=lax.Precision.HIGHEST,
     )
-    rows = lax.axis_size("gx")
-    per_row = nturb // rows
-    received = lax.all_to_all(
-        partial_sample.reshape(rows, per_row, -1), "gx", split_axis=0, concat_axis=0, tiled=True
+    everyone = ("gx", "gy", "gz")
+    devices = lax.axis_size(everyone)
+    pieces = devices // nturb
+    width = actuator_count // pieces
+    scattered = (
+        partial_sample.reshape(nturb, 3, pieces, width).transpose(0, 2, 1, 3).reshape(devices, -1)
     )
-    owned = jnp.sum(received, axis=0)
-    for axis in ("gy", "gz"):
-        count = lax.axis_size(axis)
-        step = 1
-        while step < count:
-            pairs = [(i, i ^ step) for i in range(count)]
-            owned = owned + lax.ppermute(owned, axis, pairs)
-            step *= 2
-    owned_coef = lax.dynamic_slice_in_dim(chord, lax.axis_index("gx") * per_row, per_row, 0)
+    received = lax.all_to_all(scattered, everyone, split_axis=0, concat_axis=0, tiled=True)
+    owned = jnp.sum(received, axis=0).reshape(1, -1)
+    owned_coef = lax.dynamic_slice_in_dim(
+        chord.reshape(devices, width), lax.axis_index(everyone), 1, 0
+    )
     owned_force = actuate(owned, owned_coef)
-    forces = lax.all_to_all(
-        jnp.broadcast_to(owned_force[None], (rows,) + owned_force.shape),
-        "gx", split_axis=0, concat_axis=0, tiled=True,
-    ).reshape(nturb, -1)
+    forces = (
+        lax.all_to_all(
+            jnp.broadcast_to(owned_force, (devices, owned_force.shape[1])),
+            everyone, split_axis=0, concat_axis=0, tiled=True,
+        )
+        .reshape(nturb, pieces, 3, width)
+        .transpose(0, 2, 1, 3)
+        .reshape(nturb, -1)
+    )
     tile_force = jnp.dot(owning_block, forces, precision=lax.Precision.HIGHEST).astype(jnp.bfloat16)
     forces_sent = jnp.einsum(
         "axz,ahx->ahz",

time: 138 us -> 143 us (1.036)
  the two profiles are of different devices: /device:TPU:44 before, /device:TPU:138 now
where the time goes in v4:
time: 143 us
  starting transfers between devices  66 us (46%)
  Pallas kernels  33.7 us (24%)
  local copies, waits for them, and re-layouts  27.6 us (19%)
  matrix products  10.2 us (7%)
  waiting for transfers between devices  2.84 us (2%)
    ppermute x6, starting transfers between devices, faces(): lax.ppermute(lax.index_in_dim(block, 0, dim, keepdims=False), axis, backw...  21.2 us
    pallas_call x1, Pallas kernels, stencil(): vmem_call(advance_kernel, jax.ShapeDtypeStruct(velocity.shape, jnp.float3...  18 us
    ppermute x6, starting transfers between devices, faces(): lax.ppermute(lax.index_in_dim(block, size - 1, dim, keepdims=False), axis...  17.9 us
    pallas_call x1, Pallas kernels, stencil(): vmem_call(viscosity_kernel, jax.ShapeDtypeStruct(velocity.shape[1:], jnp....  15.7 us
    all_to_all x1, starting transfers between devices, body(): lax.all_to_all(scattered, everyone, split_axis=0, concat_axis=0, tiled=True)  13.5 us
    all_to_all x1, starting transfers between devices, body(): lax.all_to_all(jnp.broadcast_to(owned_force, (devices, owned_force.shape[...  13.4 us
    unnamed x31, local copies, waits for them, and re-layouts  8.4 us
    slice x4, local copies, waits for them, and re-layouts, faces(): lax.index_in_dim(block, 0, dim, keepdims=False)  8.1 us
  transfers between devices with their start and end apart: 14, of which 1 were waited for; matrix products, arithmetic and copies ran while one was open for 22% of the time, Pallas kernels for 11%

profile of v4, /device:TPU:138, one launch (start us, length us, event | category | flops | bytes accessed | tf_op | source)
XLA Modules:
  0.0 142.6 jit_solution(13342677754097494484)
XLA Ops:
  0.6 2.2 %fusion.17 = (f32[3,64,1,128]{3,2,1,0:T(1,128)}, f32[3,64,1,128]{3,2,1,0:T(1,128)}) fusion(f32[3,64,32,128]{3,2,1,0:T(8,128)} %u.3), kind=kLoop, calls=%fused_computation.24 | loop fusion | bytes 393216 | tf_op jit(solution)/shard_map/slice | solution.py:26
  2.8 3.5 %collective-permute-start.2 = (f32[3,64,128]{2,1,0:T(8,128)}, f32[3,64,128]{2,1,0:T(8,128)}, u32[]{:S(2)}, u32[]{:S(2)}) collective-permute-start(f32[3,64,128]{2,1,0:T(8,128)} %bitcast.3), channel_id=1, source_target_pairs={{0,1},{1,2},{2,3},{4,5},{5,6},{6,7},{8,9},{9,10},{10,11},{12,13},{... | collective-permute-start | bytes 294920 | tf_op jit(solution)/shard_map/ppermute | solution.py:25
  6.3 3.1 %collective-permute-start.3 = (f32[3,64,128]{2,1,0:T(8,128)}, f32[3,64,128]{2,1,0:T(8,128)}, u32[]{:S(2)}, u32[]{:S(2)}) collective-permute-start(f32[3,64,128]{2,1,0:T(8,128)} %bitcast.4), channel_id=1, source_target_pairs={{1,0},{2,1},{3,2},{5,4},{6,5},{7,6},{9,8},{10,9},{11,10},{13,12},{... | collective-permute-start | bytes 294920 | tf_op jit(solution)/shard_map/ppermute | solution.py:26
  9.4 2.9 %reshape.102 = f32[3,64,4096]{2,1,0:T(8,128)S(1)} reshape(f32[3,64,32,128]{3,2,1,0:T(8,128)} %u.3) | data formatting | bytes 6291456 | tf_op jit(solution)/shard_map/reshape | solution.py:135
  13.5 4.7 %fusion.4 = f32[1,2,3,384]{3,2,1,0:T(4,128)S(1)} fusion(bf16[1,1,1,2,384,4096]{5,4,3,2,1,0:T(8,128)(2,1)} %param.8, bf16[2,3,4096]{2,0,1:T(2,128)(2,1)S(1)} %convolution_convert_fusion), kind=kOutput, calls=%fused_computation.7 | convolution fusion | flops 18874368 | bytes 6349824 | tf_op jit(solution)/shard_map/spq,scq->scp/dot_general | solution.py:140
  19.7 2.5 %all_to_all.13 = f32[256,1,288]{2,1,0:T(1,128)} reshape(f32[64,4,3,96]{3,2,1,0:T(4,128)} %copy.76) | data formatting | bytes 589824 | tf_op jit(solution)/shard_map/all_to_all | solution.py:159
  22.2 13.5 %all-to-all-start = ((f32[256,1,288]{2,1,0:T(1,128)}), f32[256,1,288]{2,1,0:T(1,128)S(1)}, u32[]{:S(2)}, u32[]{:S(2)}) async-start(f32[256,1,288]{2,1,0:T(1,128)} %all_to_all.13), calls=%async_computation | async-start | bytes 786432 | tf_op jit(solution)/shard_map/all_to_all | solution.py:159
  35.7 3.8 %fusion.16 = (f32[3,64,32,1]{3,2,1,0:T(8,128)}, f32[3,64,32,1]{3,2,1,0:T(8,128)}) fusion(f32[3,64,32,128]{3,2,1,0:T(8,128)S(1)} %copy-done), kind=kLoop, calls=%fused_computation.23 | loop fusion | bytes 98304 | tf_op jit(solution)/shard_map/slice | solution.py:26
  39.6 3.2 %copy.87 = f32[3,64,32,1]{1,2,0,3:T(8,128)} copy(f32[3,64,32,1]{3,2,1,0:T(8,128)} %get-tuple-element.3) | data formatting | bytes 49152
  42.8 3.4 %collective-permute-start.4 = (f32[3,64,32]{1,2,0:T(8,128)}, f32[3,64,32]{1,2,0:T(8,128)}, u32[]{:S(2)}, u32[]{:S(2)}) collective-permute-start(f32[3,64,32]{1,2,0:T(8,128)} %bitcast.70), channel_id=1, source_target_pairs={{0,4},{4,8},{8,12},{1,5},{5,9},{9,13},{2,6},{6,10},{10,14},{3,7},{... | collective-permute-start | bytes 73736 | tf_op jit(solution)/shard_map/ppermute | solution.py:25
  46.9 2.0 %collective-permute-start = (f32[3,32,128]{2,1,0:T(8,128)}, f32[3,32,128]{2,1,0:T(8,128)S(1)}, u32[]{:S(2)}, u32[]{:S(2)}) collective-permute-start(f32[3,32,128]{2,1,0:T(8,128)} %get-tuple-element.7), channel_id=1, source_target_pairs={{0,16},{16,32},{32,48},{48,64},{64,80},{80,96},{96,112},{112,128},... | collective-permute-start | bytes 147464 | tf_op jit(solution)/shard_map/ppermute | solution.py:25
  48.9 4.9 %collective-permute-start.1 = (f32[3,32,128]{2,1,0:T(8,128)}, f32[3,32,128]{2,1,0:T(8,128)S(1)}, u32[]{:S(2)}, u32[]{:S(2)}) collective-permute-start(f32[3,32,128]{2,1,0:T(8,128)} %get-tuple-element.6), channel_id=1, source_target_pairs={{16,0},{32,16},{48,32},{64,48},{80,64},{96,80},{112,96},{128,112},... | collective-permute-start | bytes 147464 | tf_op jit(solution)/shard_map/ppermute | solution.py:26
  53.8 2.7 %copy.88 = f32[3,64,32,1]{1,2,0,3:T(8,128)S(1)} copy(f32[3,64,32,1]{3,2,1,0:T(8,128)} %get-tuple-element.2) | data formatting | bytes 49152
  56.4 3.0 %collective-permute-start.5 = (f32[3,64,32]{1,2,0:T(8,128)S(1)}, f32[3,64,32]{1,2,0:T(8,128)S(1)}, u32[]{:S(2)}, u32[]{:S(2)}) collective-permute-start(f32[3,64,32]{1,2,0:T(8,128)S(1)} %bitcast.69), channel_id=1, source_target_pairs={{4,0},{8,4},{12,8},{5,1},{9,5},{13,9},{6,2},{10,6},{14,10},{7,3},{... | collective-permute-start | bytes 73736 | tf_op jit(solution)/shard_map/ppermute | solution.py:26
  59.6 2.8 %collective-permute-done.5 = f32[3,64,32]{1,2,0:T(8,128)S(1)} collective-permute-done((f32[3,64,32]{1,2,0:T(8,128)S(1)}, f32[3,64,32]{1,2,0:T(8,128)S(1)}, u32[]{:S(2)}, u32[]{:S(2)}) %collective-permute-start.5) | collective-permute-done | bytes 24608 | tf_op jit(solution)/shard_map/ppermute | solution.py:26
  63.1 15.7 %shard_map.68.nu = f32[64,32,128]{2,1,0:T(8,128)} custom-call(f32[3,64,32,128]{3,2,1,0:T(8,128)} %u.3, f32[3,32,128]{2,1,0:T(8,128)} %copy-done.3, f32[3,32,128]{2,1,0:T(8,128)} %copy-done.4, f32[3,64,128]{2,1,0:T(8,128)} %collective-permute-done.2.zlo, f32[3,64,128]{2,1,0:T(8,128)} %collective-permute-done.3.zhi, f32[3,32,64]{2,1,0:T(8,128)} %bitcast.6.ylo, ...), custom_call_target="tpu_custom_call" | custom-call | tf_op jit(solution)/shard_map/pallas_call | solution.py:114
  80.3 13.4 %all-to-all-start.1 = ((f32[256,1,288]{2,1,0:T(1,128)}), f32[256,1,288]{2,1,0:T(1,128)S(1)}, u32[]{:S(2)}, u32[]{:S(2)}) async-start(f32[256,1,288]{2,1,0:T(1,128)} %broadcast_in_dim.2), calls=%async_computation.1 | async-start | bytes 786432 | tf_op jit(solution)/shard_map/all_to_all | solution.py:166
  97.1 4.7 %collective-permute-start.7 = (f32[32,128]{1,0:T(8,128)}, f32[32,128]{1,0:T(8,128)}, u32[]{:S(2)}, u32[]{:S(2)}) collective-permute-start(f32[32,128]{1,0:T(8,128)} %get-tuple-element.12), channel_id=1, source_target_pairs={{16,0},{32,16},{48,32},{64,48},{80,64},{96,80},{112,96},{128,112},... | collective-permute-start | bytes 49160 | tf_op jit(solution)/shard_map/ppermute | solution.py:26
  103.5 3.4 %collective-permute-start.8 = (f32[64,128]{1,0:T(8,128)}, f32[64,128]{1,0:T(8,128)}, u32[]{:S(2)}, u32[]{:S(2)}) collective-permute-start(f32[64,128]{1,0:T(8,128)} %bitcast.11), channel_id=1, source_target_pairs={{0,1},{1,2},{2,3},{4,5},{5,6},{6,7},{8,9},{9,10},{10,11},{12,13},{... | collective-permute-start | bytes 98312 | tf_op jit(solution)/shard_map/ppermute | solution.py:25
  107.0 3.0 %collective-permute-start.9 = (f32[64,128]{1,0:T(8,128)}, f32[64,128]{1,0:T(8,128)}, u32[]{:S(2)}, u32[]{:S(2)}) collective-permute-start(f32[64,128]{1,0:T(8,128)} %bitcast.12), channel_id=1, source_target_pairs={{1,0},{2,1},{3,2},{5,4},{6,5},{7,6},{9,8},{10,9},{11,10},{13,12},{... | collective-permute-start | bytes 98312 | tf_op jit(solution)/shard_map/ppermute | solution.py:26
  111.0 3.6 %collective-permute-start.10 = (f32[64,32]{0,1:T(8,128)S(1)}, f32[64,32]{0,1:T(8,128)S(1)}, u32[]{:S(2)}, u32[]{:S(2)}) collective-permute-start(f32[64,32]{0,1:T(8,128)S(1)} %bitcast.75), channel_id=1, source_target_pairs={{0,4},{4,8},{8,12},{1,5},{5,9},{9,13},{2,6},{6,10},{10,14},{3,7},{... | collective-permute-start | bytes 24584 | tf_op jit(solution)/shard_map/ppermute | solution.py:25
  117.1 2.5 %collective-permute-start.11 = (f32[64,32]{0,1:T(8,128)S(1)}, f32[64,32]{0,1:T(8,128)S(1)}, u32[]{:S(2)}, u32[]{:S(2)}) collective-permute-start(f32[64,32]{0,1:T(8,128)S(1)} %bitcast.74), channel_id=1, source_target_pairs={{4,0},{8,4},{12,8},{5,1},{9,5},{13,9},{6,2},{10,6},{14,10},{7,3},{... | collective-permute-start | bytes 24584 | tf_op jit(solution)/shard_map/ppermute | solution.py:26
  119.5 3.7 %fusion = f32[2,3,4096]{2,1,0:T(4,128)S(1)} fusion(bf16[2,3,384]{2,1,0:T(4,128)(2,1)S(1)} %reshape.107, bf16[1,1,1,2,384,4096]{5,4,3,2,1,0:T(8,128)(2,1)} %param.8), kind=kOutput, calls=%fused_computation | convolution fusion | flops 18874368 | bytes 6394368 | tf_op jit(solution)/shard_map/axz,ahx->ahz/dot_general | solution.py:175
  124.6 18.0 %shard_map.69 = f32[3,64,32,128]{3,2,1,0:T(8,128)} custom-call(s32[2]{0:T(128)} %bitcast.78, f32[3,64,32,128]{3,2,1,0:T(8,128)} %u.3, f32[3,32,128]{2,1,0:T(8,128)} %copy-done.3, f32[3,32,128]{2,1,0:T(8,128)} %copy-done.4, f32[3,64,128]{2,1,0:T(8,128)} %collective-permute-done.2.zlo, f32[3,64,128]{2,1,0:T(8,128)} %collective-permute-done.3.zhi, ...), custom_call_target="tpu_custom_call" | custom-call | tf_op jit(solution)/shard_map/pallas_call | solution.py:118
  (68 shorter events, 15.4 us)
Async XLA Ops:
  2.8 59.6 %collective-permute-start.2 = (f32[3,64,128]{2,1,0:T(8,128)}, f32[3,64,128]{2,1,0:T(8,128)}, u32[]{:S(2)}, u32[]{:S(2)}) collective-permute-start(f32[3,64,128]{2,1,0:T(8,128)} %bitcast.3), channel_id=1, source_target_pairs={{0,1},{1,2},{2,3},{4,5},{5,6},{6,7},{8,9},{9,10},{10,11},{12,13},{... | collective-permute-start | bytes 294920 | tf_op jit(solution)/shard_map/ppermute | solution.py:25
  6.3 6.0 %copy-start.12 = (s32[1,1,1,2]{3,2,1,0:T(1,128)S(1)}, s32[1,1,1,2]{3,2,1,0:T(1,128)}, u32[]{:S(2)}) copy-start(s32[1,1,1,2]{3,2,1,0:T(1,128)} %param.7) | copy-start | bytes 28
  6.3 56.1 %collective-permute-start.3 = (f32[3,64,128]{2,1,0:T(8,128)}, f32[3,64,128]{2,1,0:T(8,128)}, u32[]{:S(2)}, u32[]{:S(2)}) collective-permute-start(f32[3,64,128]{2,1,0:T(8,128)} %bitcast.4), channel_id=1, source_target_pairs={{1,0},{2,1},{3,2},{5,4},{6,5},{7,6},{9,8},{10,9},{11,10},{13,12},{... | collective-permute-start | bytes 294920 | tf_op jit(solution)/shard_map/ppermute | solution.py:26
  13.4 4.8 %copy-start.10 = (s32[1,1,1,2]{3,2,1,0:T(1,128)S(1)}, s32[1,1,1,2]{3,2,1,0:T(1,128)}, u32[]{:S(2)}) copy-start(s32[1,1,1,2]{3,2,1,0:T(1,128)} %param.6) | copy-start | bytes 28
  13.4 22.3 %copy-start = (f32[3,64,32,128]{3,2,1,0:T(8,128)S(1)}, f32[3,64,32,128]{3,2,1,0:T(8,128)}, u32[]{:S(2)}) copy-start(f32[3,64,32,128]{3,2,1,0:T(8,128)} %u.3) | copy-start | bytes 9437188
  22.2 56.5 %all-to-all-start = ((f32[256,1,288]{2,1,0:T(1,128)}), f32[256,1,288]{2,1,0:T(1,128)S(1)}, u32[]{:S(2)}, u32[]{:S(2)}) async-start(f32[256,1,288]{2,1,0:T(1,128)} %all_to_all.13), calls=%async_computation | async-start | bytes 786432 | tf_op jit(solution)/shard_map/all_to_all | solution.py:159
  42.8 13.6 %collective-permute-start.4 = (f32[3,64,32]{1,2,0:T(8,128)}, f32[3,64,32]{1,2,0:T(8,128)}, u32[]{:S(2)}, u32[]{:S(2)}) collective-permute-start(f32[3,64,32]{1,2,0:T(8,128)} %bitcast.70), channel_id=1, source_target_pairs={{0,4},{4,8},{8,12},{1,5},{5,9},{9,13},{2,6},{6,10},{10,14},{3,7},{... | collective-permute-start | bytes 73736 | tf_op jit(solution)/shard_map/ppermute | solution.py:25
  46.9 12.6 %copy-start.6 = (f32[64,384]{1,0:T(8,128)S(1)}, f32[64,384]{1,0:T(8,128)}, u32[]{:S(2)}) copy-start(f32[64,384]{1,0:T(8,128)} %param.9) | copy-start | bytes 294916
  46.9 15.6 %collective-permute-start = (f32[3,32,128]{2,1,0:T(8,128)}, f32[3,32,128]{2,1,0:T(8,128)S(1)}, u32[]{:S(2)}, u32[]{:S(2)}) collective-permute-start(f32[3,32,128]{2,1,0:T(8,128)} %get-tuple-element.7), channel_id=1, source_target_pairs={{0,16},{16,32},{32,48},{48,64},{64,80},{80,96},{96,112},{112,128},... | collective-permute-start | bytes 147464 | tf_op jit(solution)/shard_map/ppermute | solution.py:25
  48.9 13.5 %collective-permute-start.1 = (f32[3,32,128]{2,1,0:T(8,128)}, f32[3,32,128]{2,1,0:T(8,128)S(1)}, u32[]{:S(2)}, u32[]{:S(2)}) collective-permute-start(f32[3,32,128]{2,1,0:T(8,128)} %get-tuple-element.6), channel_id=1, source_target_pairs={{16,0},{32,16},{48,32},{64,48},{80,64},{96,80},{112,96},{128,112},... | collective-permute-start | bytes 147464 | tf_op jit(solution)/shard_map/ppermute | solution.py:26
  56.4 6.0 %collective-permute-start.5 = (f32[3,64,32]{1,2,0:T(8,128)S(1)}, f32[3,64,32]{1,2,0:T(8,128)S(1)}, u32[]{:S(2)}, u32[]{:S(2)}) collective-permute-start(f32[3,64,32]{1,2,0:T(8,128)S(1)} %bitcast.69), channel_id=1, source_target_pairs={{4,0},{8,4},{12,8},{5,1},{9,5},{13,9},{6,2},{10,6},{14,10},{7,3},{... | collective-permute-start | bytes 73736 | tf_op jit(solution)/shard_map/ppermute | solution.py:26
  62.4 0.6 copy-start.3
  62.4 0.7 copy-start.4
  78.8 31.2 %copy-start.1 = (f32[64,32,128]{2,1,0:T(8,128)S(1)}, f32[64,32,128]{2,1,0:T(8,128)}, u32[]{:S(2)}) copy-start(f32[64,32,128]{2,1,0:T(8,128)} %shard_map.68.nu) | copy-start | bytes 3145732
  80.3 34.9 %all-to-all-start.1 = ((f32[256,1,288]{2,1,0:T(1,128)}), f32[256,1,288]{2,1,0:T(1,128)S(1)}, u32[]{:S(2)}, u32[]{:S(2)}) async-start(f32[256,1,288]{2,1,0:T(1,128)} %broadcast_in_dim.2), calls=%async_computation.1 | async-start | bytes 786432 | tf_op jit(solution)/shard_map/all_to_all | solution.py:166
  95.0 28.9 %collective-permute-start.6 = (f32[32,128]{1,0:T(8,128)}, f32[32,128]{1,0:T(8,128)S(1)}, u32[]{:S(2)}, u32[]{:S(2)}) collective-permute-start(f32[32,128]{1,0:T(8,128)} %get-tuple-element.13), channel_id=1, source_target_pairs={{0,16},{16,32},{32,48},{48,64},{64,80},{80,96},{96,112},{112,128},... | collective-permute-start | bytes 49160 | tf_op jit(solution)/shard_map/ppermute | solution.py:25
  97.1 26.9 %collective-permute-start.7 = (f32[32,128]{1,0:T(8,128)}, f32[32,128]{1,0:T(8,128)}, u32[]{:S(2)}, u32[]{:S(2)}) collective-permute-start(f32[32,128]{1,0:T(8,128)} %get-tuple-element.12), channel_id=1, source_target_pairs={{16,0},{32,16},{48,32},{64,48},{80,64},{96,80},{112,96},{128,112},... | collective-permute-start | bytes 49160 | tf_op jit(solution)/shard_map/ppermute | solution.py:26
  103.5 20.5 %collective-permute-start.8 = (f32[64,128]{1,0:T(8,128)}, f32[64,128]{1,0:T(8,128)}, u32[]{:S(2)}, u32[]{:S(2)}) collective-permute-start(f32[64,128]{1,0:T(8,128)} %bitcast.11), channel_id=1, source_target_pairs={{0,1},{1,2},{2,3},{4,5},{5,6},{6,7},{8,9},{9,10},{10,11},{12,13},{... | collective-permute-start | bytes 98312 | tf_op jit(solution)/shard_map/ppermute | solution.py:25
  107.0 17.0 %collective-permute-start.9 = (f32[64,128]{1,0:T(8,128)}, f32[64,128]{1,0:T(8,128)}, u32[]{:S(2)}, u32[]{:S(2)}) collective-permute-start(f32[64,128]{1,0:T(8,128)} %bitcast.12), channel_id=1, source_target_pairs={{1,0},{2,1},{3,2},{5,4},{6,5},{7,6},{9,8},{10,9},{11,10},{13,12},{... | collective-permute-start | bytes 98312 | tf_op jit(solution)/shard_map/ppermute | solution.py:26
  110.3 6.4 %copy-start.11 = (s32[1,1,1,2]{3,2,1,0:T(1,128)S(1)}, s32[1,1,1,2]{3,2,1,0:T(1,128)}, u32[]{:S(2)}) copy-start(s32[1,1,1,2]{3,2,1,0:T(1,128)} %param.6) | copy-start | bytes 28
  111.0 6.1 %collective-permute-start.10 = (f32[64,32]{0,1:T(8,128)S(1)}, f32[64,32]{0,1:T(8,128)S(1)}, u32[]{:S(2)}, u32[]{:S(2)}) collective-permute-start(f32[64,32]{0,1:T(8,128)S(1)} %bitcast.75), channel_id=1, source_target_pairs={{0,4},{4,8},{8,12},{1,5},{5,9},{9,13},{2,6},{6,10},{10,14},{3,7},{... | collective-permute-start | bytes 24584 | tf_op jit(solution)/shard_map/ppermute | solution.py:25
  116.8 6.5 %copy-start.2 = (f32[64,1152]{1,0:T(8,128)}, f32[64,1152]{1,0:T(8,128)S(1)}, u32[]{:S(2)}) copy-start(f32[64,1152]{1,0:T(8,128)S(1)} %reshape.106) | copy-start | bytes 884740
  117.1 6.2 %copy-start.8 = (f32[64,32]{0,1:T(8,128)}, f32[64,32]{0,1:T(8,128)S(1)}, u32[]{:S(2)}) copy-start(f32[64,32]{0,1:T(8,128)S(1)} %collective-permute-done.10) | copy-start | bytes 24580
  117.1 6.9 %collective-permute-start.11 = (f32[64,32]{0,1:T(8,128)S(1)}, f32[64,32]{0,1:T(8,128)S(1)}, u32[]{:S(2)}, u32[]{:S(2)}) collective-permute-start(f32[64,32]{0,1:T(8,128)S(1)} %bitcast.74), channel_id=1, source_target_pairs={{4,0},{8,4},{12,8},{5,1},{9,5},{13,9},{6,2},{10,6},{14,10},{7,3},{... | collective-permute-start | bytes 24584 | tf_op jit(solution)/shard_map/ppermute | solution.py:26
  (3 other events, 1.8 us)

commit v5 on v3

--- a/solution.py
+++ b/solution.py
@@ -15,20 +15,40 @@
     return (-2.0 * coef[:, None, :] * magnitude[:, None, :] * parts).reshape(rows, -1)
 
 
-def faces(block, lead):
+def exchange(first, last):
     out = []
-    for axis, dim in (("gx", lead), ("gz", lead + 1), ("gy", lead + 2)):
+    for axis, lo, hi in zip(("gx", "gz", "gy"), last, first):
         count = lax.axis_size(axis)
         forward = [(i, i + 1) for i in range(count - 1)]
         backward = [(target, source) for source, target in forward]
-        size = block.shape[dim]
-        low = lax.ppermute(lax.index_in_dim(block, size - 1, dim, keepdims=False), axis, forward)
-        high = lax.ppermute(lax.index_in_dim(block, 0, dim, keepdims=False), axis, backward)
-        if axis == "gy":
-            low = jnp.swapaxes(low, -1, -2)
-            high = jnp.swapaxes(high, -1, -2)
-        out += [low, high]
+        out += [lax.ppermute(lo, axis, forward), lax.ppermute(hi, axis, backward)]
     return out
+
+
+def keep_edges(plane, x, nz, ny, cols, rows_first, rows_last, lead):
+    column = lax.broadcasted_iota(jnp.int32, cols[0].shape, 1)
+    rows_first[lead + (pl.ds(x, 1), slice(None))] = plane[0:1, :]
+    rows_last[lead + (pl.ds(x, 1), slice(None))] = plane[nz - 1 : nz, :]
+    return (
+        jnp.where(column == x, plane[:, 0:1], cols[0]),
+        jnp.where(column == x, plane[:, ny - 1 : ny], cols[1]),
+    )
+
+
+def edges_kernel(u, zfirst, zlast, yfirst, ylast):
+    nx, nz, ny = u.shape[1:]
+
+    def plane(x, carry):
+        out = []
+        for c in range(3):
+            out += keep_edges(u[c, x], x, nz, ny, carry[2 * c : 2 * c + 2], zfirst, zlast, (c,))
+        return tuple(out)
+
+    zero = jnp.zeros(yfirst.shape[1:], jnp.float32)
+    cols = lax.fori_loop(0, nx, plane, (zero,) * 6)
+    for c in range(3):
+        yfirst[c] = cols[2 * c]
+        ylast[c] = cols[2 * c + 1]
 
 
 def neighbours(ref, xlo, xhi, zlo, zhi, ylo, yhi, lead, x, centre):
@@ -52,7 +72,9 @@
     return xm, xp, ym, yp, zm, zp
 
 
-def viscosity_kernel(u, xlo, xhi, zlo, zhi, ylo, yhi, nu):
+def viscosity_kernel(u, xlo, xhi, zlo, zhi, ylo, yhi, nu, zfirst, zlast, yfirst, ylast):
+    nz, ny = u.shape[2:]
+
     def plane(x, carry):
         grads = []
         for c in range(3):
@@ -63,10 +85,12 @@
             for d in range(3):
                 strain = 0.5 * (grads[c][d] + grads[d][c])
                 total = total + strain * strain
-        nu[x] = 0.05 + 1.0 * jnp.sqrt(2.0 * total + 1e-06)
-        return carry
-
-    lax.fori_loop(0, u.shape[1], plane, 0)
+        here = 0.05 + 1.0 * jnp.sqrt(2.0 * total + 1e-06)
+        nu[x] = here
+        return keep_edges(here, x, nz, ny, carry, zfirst, zlast, ())
+
+    zero = jnp.zeros(yfirst.shape, jnp.float32)
+    yfirst[...], ylast[...] = lax.fori_loop(0, u.shape[1], plane, (zero, zero))
 
 
 def advance_kernel(planes, u, xlo, xhi, zlo, zhi, ylo, yhi, nu, nxlo, nxhi, nzlo, nzhi, nylo, nyhi, sent, out):
@@ -104,19 +128,30 @@
         kernel,
         out_shape=out_shape,
         in_specs=specs,
-        out_specs=pl.BlockSpec(memory_space=pltpu.VMEM),
+        out_specs=jax.tree.map(lambda _: pl.BlockSpec(memory_space=pltpu.VMEM), out_shape),
         interpret=INTERPRET,
     )
 
 
 def stencil(velocity, planes, sent):
-    u_faces = faces(velocity, 1)
-    nu = vmem_call(
-        viscosity_kernel, jax.ShapeDtypeStruct(velocity.shape[1:], jnp.float32), 7
+    nx, nz, ny = velocity.shape[1:]
+    f32 = jnp.float32
+    zfirst, zlast, yfirst, ylast = vmem_call(
+        edges_kernel,
+        (jax.ShapeDtypeStruct((3, nx, ny), f32),) * 2 + (jax.ShapeDtypeStruct((3, nz, nx), f32),) * 2,
+        1,
+    )(velocity)
+    u_faces = exchange((velocity[:, 0], zfirst, yfirst), (velocity[:, nx - 1], zlast, ylast))
+    nu, nzfirst, nzlast, nyfirst, nylast = vmem_call(
+        viscosity_kernel,
+        (jax.ShapeDtypeStruct((nx, nz, ny), f32),)
+        + (jax.ShapeDtypeStruct((nx, ny), f32),) * 2
+        + (jax.ShapeDtypeStruct((nz, nx), f32),) * 2,
+        7,
     )(velocity, *u_faces)
-    nu_faces = faces(nu, 0)
+    nu_faces = exchange((nu[0], nzfirst, nyfirst), (nu[nx - 1], nzlast, nylast))
     return vmem_call(
-        advance_kernel, jax.ShapeDtypeStruct(velocity.shape, jnp.float32), 16, smem=1
+        advance_kernel, jax.ShapeDtypeStruct(velocity.shape, f32), 16, smem=1
     )(planes, velocity, *u_faces, nu, *nu_faces, sent)
 
 
@@ -132,11 +167,9 @@
     spread_weights = tile_weight.reshape(
         tile_count, actuator_count, vertical_coord * spanwise_coord
     )
-    flat = velocity.reshape(3, cx, vertical_coord * spanwise_coord)
-    picks = (rotor_planes[:, None] == jnp.arange(cx, dtype=jnp.int32)[None, :]).astype(jnp.float32)
-    tiles = jnp.einsum("sx,cxq->scq", picks, flat, precision=lax.Precision.HIGHEST).astype(
-        jnp.bfloat16
-    )
+    tiles = jnp.stack(
+        [lax.dynamic_index_in_dim(velocity, rotor_planes[s], 1, keepdims=False) for s in range(tile_count)]
+    ).reshape(tile_count, 3, vertical_coord * spanwise_coord).astype(jnp.bfloat16)
     block_local = jnp.einsum(
         "spq,scq->scp", spread_weights, tiles, preferred_element_type=jnp.float32
     )

time: 138 us -> 148 us (1.072)
  the two profiles are of different devices: /device:TPU:44 before, /device:TPU:1 now
where the time goes in v5:
time: 148 us; the launch traced here: 146 us
  starting transfers between devices  46.4 us (31%)
  Pallas kernels  46.1 us (31%)
  blocking collectives  22 us (15%)
  waiting for transfers between devices  9.57 us (6%)
  matrix products  8.89 us (6%)
  local copies, waits for them, and re-layouts  7.42 us (5%)
  between operations  4.88 us (3%)
    ppermute x12, starting transfers between devices, exchange(): out += [lax.ppermute(lo, axis, forward), lax.ppermute(hi, axis, backward)]  30.9 us
    all_to_all x1, blocking collectives, body(): lax.all_to_all(partial_sample.reshape(rows, per_row, -1), 'gx', split_axi...  22 us
    pallas_call x1, Pallas kernels, stencil(): vmem_call(viscosity_kernel, (jax.ShapeDtypeStruct((nx, nz, ny), f32),) +...  19.2 us
    pallas_call x1, Pallas kernels, stencil(): vmem_call(advance_kernel, jax.ShapeDtypeStruct(velocity.shape, f32), 16,...  18 us
    pallas_call x1, Pallas kernels, stencil(): vmem_call(edges_kernel, (jax.ShapeDtypeStruct((3, nx, ny), f32),) * 2 + (...  8.93 us
    ppermute x4, starting transfers between devices, body(): owned = owned + lax.ppermute(owned, axis, pairs)  8.25 us
    all_to_all x1, starting transfers between devices, body(): lax.all_to_all(jnp.broadcast_to(owned_force[None], (rows,) + owned_force....  7.21 us
    ppermute x4, waiting for transfers between devices, body(): owned = owned + lax.ppermute(owned, axis, pairs)  5.73 us
  transfers between devices with their start and end apart: 17, of which 5 were waited for; matrix products, arithmetic and copies ran while one was open for 4% of the time, Pallas kernels for 19%

profile of v5, /device:TPU:1, one launch (start us, length us, event | category | flops | bytes accessed | tf_op | source)
XLA Modules:
  0.0 146.2 jit_solution(4334161532131473876)
XLA Ops:
  0.6 1.3 fusion.16
  6.7 4.5 %fusion.2 = f32[2,3,384]{2,1,0:T(4,128)S(1)} fusion(bf16[1,1,1,2,384,4096]{5,4,3,2,1,0:T(8,128)(2,1)} %param.8, bf16[1,3,4096]{2,1,0:T(4,128)(2,1)S(1)} %stack.10, bf16[1,3,4096]{2,1,0:T(4,128)(2,1)S(1)} %stack.9), kind=kOutput, calls=%fused_computation.2 | convolution fusion | flops 18972672 | bytes 6349824 | tf_op jit(solution)/shard_map/spq,scq->scp/dot_general | solution.py:173
  11.9 22.0 %all_to_all.10 = f32[16,4,1152]{2,1,0:T(4,128)S(1)} all-to-all(f32[16,4,1152]{2,1,0:T(4,128)S(1)} %copy.15), channel_id=1, replica_groups=mesh['gx'=16,'gy'=4,'gz'=4] {'gx'}, dimensions={0} | all-to-all | bytes 589824 | tf_op jit(solution)/shard_map/all_to_all | solution.py:187
  35.3 1.8 %collective-permute-done.12 = f32[4,1152]{1,0:T(4,128)S(1)} collective-permute-done((f32[4,1152]{1,0:T(4,128)S(1)}, f32[4,1152]{1,0:T(4,128)S(1)}, u32[]{:S(2)}, u32[]{:S(2)}) %collective-permute-start.12) | collective-permute-done | bytes 18464 | tf_op jit(solution)/shard_map/ppermute | solution.py:196
  37.1 2.7 %collective-permute-start.13 = (f32[4,1152]{1,0:T(4,128)S(1)}, f32[4,1152]{1,0:T(4,128)S(1)}, u32[]{:S(2)}, u32[]{:S(2)}) collective-permute-start(f32[4,1152]{1,0:T(4,128)S(1)} %add.35), channel_id=1, source_target_pairs={{0,8},{4,12},{8,0},{12,4},{1,9},{5,13},{9,1},{13,5},{2,10},{6,14},... | collective-permute-start | bytes 55304 | tf_op jit(solution)/shard_map/ppermute | solution.py:196
  39.9 1.4 collective-permute-done.13
  41.2 1.3 collective-permute-start.14
  42.5 1.3 collective-permute-done.14
  43.9 2.9 %collective-permute-start.15 = (f32[4,1152]{1,0:T(4,128)S(1)}, f32[4,1152]{1,0:T(4,128)S(1)}, u32[]{:S(2)}, u32[]{:S(2)}) collective-permute-start(f32[4,1152]{1,0:T(4,128)S(1)} %add.37), channel_id=1, source_target_pairs={{0,2},{1,3},{2,0},{3,1},{4,6},{5,7},{6,4},{7,5},{8,10},{9,11},{10,... | collective-permute-start | bytes 55304 | tf_op jit(solution)/shard_map/ppermute | solution.py:196
  49.5 7.2 %all-to-all-start.1 = ((f32[16,4,1152]{2,1,0:T(4,128)}), f32[16,4,1152]{2,1,0:T(4,128)S(1)}, u32[]{:S(2)}, u32[]{:S(2)}) async-start(f32[16,4,1152]{2,1,0:T(4,128)} %broadcast_in_dim.2), calls=%async_computation.1 | async-start | bytes 589824 | tf_op jit(solution)/shard_map/all_to_all | solution.py:200
  56.7 8.9 %shard_map.68 = (f32[3,64,128]{2,1,0:T(8,128)}, f32[3,64,128]{2,1,0:T(8,128)}, f32[3,32,64]{2,1,0:T(8,128)}, f32[3,32,64]{2,1,0:T(8,128)}) custom-call(f32[3,64,32,128]{3,2,1,0:T(8,128)} %u.5), custom_call_target="tpu_custom_call" | custom-call | tf_op jit(solution)/shard_map/pallas_call | solution.py:139
  65.7 3.1 %collective-permute-start.4 = (f32[3,32,64]{2,1,0:T(8,128)}, f32[3,32,64]{2,1,0:T(8,128)S(1)}, u32[]{:S(2)}, u32[]{:S(2)}) collective-permute-start(f32[3,32,64]{2,1,0:T(8,128)} %get-tuple-element.13), channel_id=1, source_target_pairs={{0,4},{4,8},{8,12},{1,5},{5,9},{9,13},{2,6},{6,10},{10,14},{3,7},{... | collective-permute-start | bytes 73736 | tf_op jit(solution)/shard_map/ppermute | solution.py:24
  68.8 3.2 %collective-permute-start.2 = (f32[3,64,128]{2,1,0:T(8,128)}, f32[3,64,128]{2,1,0:T(8,128)S(1)}, u32[]{:S(2)}, u32[]{:S(2)}) collective-permute-start(f32[3,64,128]{2,1,0:T(8,128)} %get-tuple-element.11), channel_id=1, source_target_pairs={{0,1},{1,2},{2,3},{4,5},{5,6},{6,7},{8,9},{9,10},{10,11},{12,13},{... | collective-permute-start | bytes 294920 | tf_op jit(solution)/shard_map/ppermute | solution.py:24
  72.0 1.3 collective-permute-start.3
  74.1 2.7 %collective-permute-start.1 = (f32[3,32,128]{2,1,0:T(8,128)S(1)}, f32[3,32,128]{2,1,0:T(8,128)S(1)}, u32[]{:S(2)}, u32[]{:S(2)}) collective-permute-start(f32[3,32,128]{2,1,0:T(8,128)S(1)} %get-tuple-element.24), channel_id=1, source_target_pairs={{16,0},{32,16},{48,32},{64,48},{80,64},{96,80},{112,96},{128,112},... | collective-permute-start | bytes 147464 | tf_op jit(solution)/shard_map/ppermute | solution.py:24
  76.8 3.3 %collective-permute-start = (f32[3,32,128]{2,1,0:T(8,128)S(1)}, f32[3,32,128]{2,1,0:T(8,128)S(1)}, u32[]{:S(2)}, u32[]{:S(2)}) collective-permute-start(f32[3,32,128]{2,1,0:T(8,128)S(1)} %get-tuple-element.25), channel_id=1, source_target_pairs={{0,16},{16,32},{32,48},{48,64},{64,80},{80,96},{96,112},{112,128},... | collective-permute-start | bytes 147464 | tf_op jit(solution)/shard_map/ppermute | solution.py:24
  81.5 3.8 %collective-permute-done.5.yhi = f32[3,32,64]{2,1,0:T(8,128)S(1)} collective-permute-done((f32[3,32,64]{2,1,0:T(8,128)}, f32[3,32,64]{2,1,0:T(8,128)S(1)}, u32[]{:S(2)}, u32[]{:S(2)}) %collective-permute-start.5) | collective-permute-done | bytes 24608 | tf_op jit(solution)/shard_map/ppermute | solution.py:24
  86.6 19.2 %shard_map.69 = (f32[64,32,128]{2,1,0:T(8,128)}, f32[64,128]{1,0:T(8,128)}, f32[64,128]{1,0:T(8,128)}, f32[32,64]{1,0:T(8,128)}, f32[32,64]{1,0:T(8,128)}) custom-call(f32[3,64,32,128]{3,2,1,0:T(8,128)} %u.5, f32[3,32,128]{2,1,0:T(8,128)} %copy-done.5, f32[3,32,128]{2,1,0:T(8,128)} %copy-done.4, f32[3,64,128]{2,1,0:T(8,128)} %copy-done.1, ...), custom_call_target="tpu_custom_call" | custom-call | tf_op jit(solution)/shard_map/pallas_call | solution.py:145
  105.8 3.1 %collective-permute-start.10 = (f32[32,64]{1,0:T(8,128)}, f32[32,64]{1,0:T(8,128)S(1)}, u32[]{:S(2)}, u32[]{:S(2)}) collective-permute-start(f32[32,64]{1,0:T(8,128)} %get-tuple-element.18), channel_id=1, source_target_pairs={{0,4},{4,8},{8,12},{1,5},{5,9},{9,13},{2,6},{6,10},{10,14},{3,7},{... | collective-permute-start | bytes 24584 | tf_op jit(solution)/shard_map/ppermute | solution.py:24
  110.9 2.4 %collective-permute-start.7 = (f32[32,128]{1,0:T(8,128)S(1)}, f32[32,128]{1,0:T(8,128)S(1)}, u32[]{:S(2)}, u32[]{:S(2)}) collective-permute-start(f32[32,128]{1,0:T(8,128)S(1)} %get-tuple-element.26), channel_id=1, source_target_pairs={{16,0},{32,16},{48,32},{64,48},{80,64},{96,80},{112,96},{128,112},... | collective-permute-start | bytes 49160 | tf_op jit(solution)/shard_map/ppermute | solution.py:24
  113.4 3.7 %collective-permute-start.6 = (f32[32,128]{1,0:T(8,128)S(1)}, f32[32,128]{1,0:T(8,128)S(1)}, u32[]{:S(2)}, u32[]{:S(2)}) collective-permute-start(f32[32,128]{1,0:T(8,128)S(1)} %get-tuple-element.27), channel_id=1, source_target_pairs={{0,16},{16,32},{32,48},{48,64},{64,80},{80,96},{96,112},{112,128},... | collective-permute-start | bytes 49160 | tf_op jit(solution)/shard_map/ppermute | solution.py:24
  117.0 4.3 %collective-permute-start.8 = (f32[64,128]{1,0:T(8,128)}, f32[64,128]{1,0:T(8,128)S(1)}, u32[]{:S(2)}, u32[]{:S(2)}) collective-permute-start(f32[64,128]{1,0:T(8,128)} %get-tuple-element.16), channel_id=1, source_target_pairs={{0,1},{1,2},{2,3},{4,5},{5,6},{6,7},{8,9},{9,10},{10,11},{12,13},{... | collective-permute-start | bytes 98312 | tf_op jit(solution)/shard_map/ppermute | solution.py:24
  123.0 3.7 %fusion = f32[2,3,4096]{2,1,0:T(4,128)S(1)} fusion(bf16[2,3,384]{2,1,0:T(4,128)(2,1)S(1)} %reshape.71, bf16[1,1,1,2,384,4096]{5,4,3,2,1,0:T(8,128)(2,1)} %param.8), kind=kOutput, calls=%fused_computation | convolution fusion | flops 18874368 | bytes 6394368 | tf_op jit(solution)/shard_map/axz,ahx->ahz/dot_general | solution.py:205
  128.1 18.0 %shard_map.70 = f32[3,64,32,128]{3,2,1,0:T(8,128)} custom-call(s32[2]{0:T(128)} %bitcast.32, f32[3,64,32,128]{3,2,1,0:T(8,128)} %u.5, f32[3,32,128]{2,1,0:T(8,128)} %copy-done.5, f32[3,32,128]{2,1,0:T(8,128)} %copy-done.4, f32[3,64,128]{2,1,0:T(8,128)} %copy-done.1, f32[3,64,128]{2,1,0:T(8,128)} %copy-done.2, f32[3,32,64]{2,1,0:T(8,128)} %copy-done.3, ...), custom_call_target="tpu_custom_call" | custom-call | tf_op jit(solution)/shard_map/pallas_call | solution.py:153
  (68 shorter events, 14.0 us)
Async XLA Ops:
  0.6 10.6 %copy-start.13 = (s32[1,1,1,2]{3,2,1,0:T(1,128)S(1)}, s32[1,1,1,2]{3,2,1,0:T(1,128)}, u32[]{:S(2)}) copy-start(s32[1,1,1,2]{3,2,1,0:T(1,128)} %param.6) | copy-start | bytes 28
  34.0 3.1 %collective-permute-start.12 = (f32[4,1152]{1,0:T(4,128)S(1)}, f32[4,1152]{1,0:T(4,128)S(1)}, u32[]{:S(2)}, u32[]{:S(2)}) collective-permute-start(f32[4,1152]{1,0:T(4,128)S(1)} %reduce_sum.18), channel_id=1, source_target_pairs={{0,4},{4,0},{8,12},{12,8},{1,5},{5,1},{9,13},{13,9},{2,6},{6,2},{1... | collective-permute-start | bytes 55304 | tf_op jit(solution)/shard_map/ppermute | solution.py:196
  37.1 4.1 %collective-permute-start.13 = (f32[4,1152]{1,0:T(4,128)S(1)}, f32[4,1152]{1,0:T(4,128)S(1)}, u32[]{:S(2)}, u32[]{:S(2)}) collective-permute-start(f32[4,1152]{1,0:T(4,128)S(1)} %add.35), channel_id=1, source_target_pairs={{0,8},{4,12},{8,0},{12,4},{1,9},{5,13},{9,1},{13,5},{2,10},{6,14},... | collective-permute-start | bytes 55304 | tf_op jit(solution)/shard_map/ppermute | solution.py:196
  41.2 2.6 %collective-permute-start.14 = (f32[4,1152]{1,0:T(4,128)S(1)}, f32[4,1152]{1,0:T(4,128)S(1)}, u32[]{:S(2)}, u32[]{:S(2)}) collective-permute-start(f32[4,1152]{1,0:T(4,128)S(1)} %add.36), channel_id=1, source_target_pairs={{0,1},{1,0},{2,3},{3,2},{4,5},{5,4},{6,7},{7,6},{8,9},{9,8},{10,11... | collective-permute-start | bytes 55304 | tf_op jit(solution)/shard_map/ppermute | solution.py:196
  43.9 4.1 %collective-permute-start.15 = (f32[4,1152]{1,0:T(4,128)S(1)}, f32[4,1152]{1,0:T(4,128)S(1)}, u32[]{:S(2)}, u32[]{:S(2)}) collective-permute-start(f32[4,1152]{1,0:T(4,128)S(1)} %add.37), channel_id=1, source_target_pairs={{0,2},{1,3},{2,0},{3,1},{4,6},{5,7},{6,4},{7,5},{8,10},{9,11},{10,... | collective-permute-start | bytes 55304 | tf_op jit(solution)/shard_map/ppermute | solution.py:196
  49.5 71.8 %all-to-all-start.1 = ((f32[16,4,1152]{2,1,0:T(4,128)}), f32[16,4,1152]{2,1,0:T(4,128)S(1)}, u32[]{:S(2)}, u32[]{:S(2)}) async-start(f32[16,4,1152]{2,1,0:T(4,128)} %broadcast_in_dim.2), calls=%async_computation.1 | async-start | bytes 589824 | tf_op jit(solution)/shard_map/all_to_all | solution.py:200
  65.7 14.5 %collective-permute-start.4 = (f32[3,32,64]{2,1,0:T(8,128)}, f32[3,32,64]{2,1,0:T(8,128)S(1)}, u32[]{:S(2)}, u32[]{:S(2)}) collective-permute-start(f32[3,32,64]{2,1,0:T(8,128)} %get-tuple-element.13), channel_id=1, source_target_pairs={{0,4},{4,8},{8,12},{1,5},{5,9},{9,13},{2,6},{6,10},{10,14},{3,7},{... | collective-permute-start | bytes 73736 | tf_op jit(solution)/shard_map/ppermute | solution.py:24
  68.8 16.5 %collective-permute-start.2 = (f32[3,64,128]{2,1,0:T(8,128)}, f32[3,64,128]{2,1,0:T(8,128)S(1)}, u32[]{:S(2)}, u32[]{:S(2)}) collective-permute-start(f32[3,64,128]{2,1,0:T(8,128)} %get-tuple-element.11), channel_id=1, source_target_pairs={{0,1},{1,2},{2,3},{4,5},{5,6},{6,7},{8,9},{9,10},{10,11},{12,13},{... | collective-permute-start | bytes 294920 | tf_op jit(solution)/shard_map/ppermute | solution.py:24
  72.0 13.3 %collective-permute-start.3 = (f32[3,64,128]{2,1,0:T(8,128)}, f32[3,64,128]{2,1,0:T(8,128)S(1)}, u32[]{:S(2)}, u32[]{:S(2)}) collective-permute-start(f32[3,64,128]{2,1,0:T(8,128)} %get-tuple-element.12), channel_id=1, source_target_pairs={{1,0},{2,1},{3,2},{5,4},{6,5},{7,6},{9,8},{10,9},{11,10},{13,12},{... | collective-permute-start | bytes 294920 | tf_op jit(solution)/shard_map/ppermute | solution.py:24
  74.1 11.2 %collective-permute-start.1 = (f32[3,32,128]{2,1,0:T(8,128)S(1)}, f32[3,32,128]{2,1,0:T(8,128)S(1)}, u32[]{:S(2)}, u32[]{:S(2)}) collective-permute-start(f32[3,32,128]{2,1,0:T(8,128)S(1)} %get-tuple-element.24), channel_id=1, source_target_pairs={{16,0},{32,16},{48,32},{64,48},{80,64},{96,80},{112,96},{128,112},... | collective-permute-start | bytes 147464 | tf_op jit(solution)/shard_map/ppermute | solution.py:24
  76.8 8.5 %collective-permute-start = (f32[3,32,128]{2,1,0:T(8,128)S(1)}, f32[3,32,128]{2,1,0:T(8,128)S(1)}, u32[]{:S(2)}, u32[]{:S(2)}) collective-permute-start(f32[3,32,128]{2,1,0:T(8,128)S(1)} %get-tuple-element.25), channel_id=1, source_target_pairs={{0,16},{16,32},{32,48},{48,64},{64,80},{80,96},{96,112},{112,128},... | collective-permute-start | bytes 147464 | tf_op jit(solution)/shard_map/ppermute | solution.py:24
  80.2 5.2 %copy-start.3 = (f32[3,32,64]{2,1,0:T(8,128)}, f32[3,32,64]{2,1,0:T(8,128)S(1)}, u32[]{:S(2)}) copy-start(f32[3,32,64]{2,1,0:T(8,128)S(1)} %collective-permute-done.4.ylo) | copy-start | bytes 73732
  80.2 5.1 %collective-permute-start.5 = (f32[3,32,64]{2,1,0:T(8,128)}, f32[3,32,64]{2,1,0:T(8,128)S(1)}, u32[]{:S(2)}, u32[]{:S(2)}) collective-permute-start(f32[3,32,64]{2,1,0:T(8,128)} %get-tuple-element.14), channel_id=1, source_target_pairs={{4,0},{8,4},{12,8},{5,1},{9,5},{13,9},{6,2},{10,6},{14,10},{7,3},{... | collective-permute-start | bytes 73736 | tf_op jit(solution)/shard_map/ppermute | solution.py:24
  85.3 0.6 copy-start.4
  85.3 0.7 copy-start.5
  85.3 0.7 copy-start.1
  105.8 15.9 %collective-permute-start.10 = (f32[32,64]{1,0:T(8,128)}, f32[32,64]{1,0:T(8,128)S(1)}, u32[]{:S(2)}, u32[]{:S(2)}) collective-permute-start(f32[32,64]{1,0:T(8,128)} %get-tuple-element.18), channel_id=1, source_target_pairs={{0,4},{4,8},{8,12},{1,5},{5,9},{9,13},{2,6},{6,10},{10,14},{3,7},{... | collective-permute-start | bytes 24584 | tf_op jit(solution)/shard_map/ppermute | solution.py:24
  108.9 18.6 %collective-permute-start.11 = (f32[32,64]{1,0:T(8,128)}, f32[32,64]{1,0:T(8,128)S(1)}, u32[]{:S(2)}, u32[]{:S(2)}) collective-permute-start(f32[32,64]{1,0:T(8,128)} %get-tuple-element.19), channel_id=1, source_target_pairs={{4,0},{8,4},{12,8},{5,1},{9,5},{13,9},{6,2},{10,6},{14,10},{7,3},{... | collective-permute-start | bytes 24584 | tf_op jit(solution)/shard_map/ppermute | solution.py:24
  110.9 16.5 %collective-permute-start.7 = (f32[32,128]{1,0:T(8,128)S(1)}, f32[32,128]{1,0:T(8,128)S(1)}, u32[]{:S(2)}, u32[]{:S(2)}) collective-permute-start(f32[32,128]{1,0:T(8,128)S(1)} %get-tuple-element.26), channel_id=1, source_target_pairs={{16,0},{32,16},{48,32},{64,48},{80,64},{96,80},{112,96},{128,112},... | collective-permute-start | bytes 49160 | tf_op jit(solution)/shard_map/ppermute | solution.py:24
  113.4 14.1 %collective-permute-start.6 = (f32[32,128]{1,0:T(8,128)S(1)}, f32[32,128]{1,0:T(8,128)S(1)}, u32[]{:S(2)}, u32[]{:S(2)}) collective-permute-start(f32[32,128]{1,0:T(8,128)S(1)} %get-tuple-element.27), channel_id=1, source_target_pairs={{0,16},{16,32},{32,48},{48,64},{64,80},{80,96},{96,112},{112,128},... | collective-permute-start | bytes 49160 | tf_op jit(solution)/shard_map/ppermute | solution.py:24
  117.0 10.5 %collective-permute-start.8 = (f32[64,128]{1,0:T(8,128)}, f32[64,128]{1,0:T(8,128)S(1)}, u32[]{:S(2)}, u32[]{:S(2)}) collective-permute-start(f32[64,128]{1,0:T(8,128)} %get-tuple-element.16), channel_id=1, source_target_pairs={{0,1},{1,2},{2,3},{4,5},{5,6},{6,7},{8,9},{9,10},{10,11},{12,13},{... | collective-permute-start | bytes 98312 | tf_op jit(solution)/shard_map/ppermute | solution.py:24
  121.4 24.7 %copy-start = (f32[64,1152]{1,0:T(8,128)}, f32[64,1152]{1,0:T(8,128)S(1)}, u32[]{:S(2)}) copy-start(f32[64,1152]{1,0:T(8,128)S(1)} %reshape.70) | copy-start | bytes 884740
  121.7 5.8 %copy-start.9 = (f32[32,64]{1,0:T(8,128)}, f32[32,64]{1,0:T(8,128)S(1)}, u32[]{:S(2)}) copy-start(f32[32,64]{1,0:T(8,128)S(1)} %collective-permute-done.10.nylo) | copy-start | bytes 24580
  121.7 5.8 %collective-permute-start.9 = (f32[64,128]{1,0:T(8,128)}, f32[64,128]{1,0:T(8,128)S(1)}, u32[]{:S(2)}, u32[]{:S(2)}) collective-permute-start(f32[64,128]{1,0:T(8,128)} %get-tuple-element.17), channel_id=1, source_target_pairs={{1,0},{2,1},{3,2},{5,4},{6,5},{7,6},{9,8},{10,9},{11,10},{13,12},{... | collective-permute-start | bytes 98312 | tf_op jit(solution)/shard_map/ppermute | solution.py:24
  (7 other events, 4.3 us)

commit v6 on v3

--- a/solution.py
+++ b/solution.py
@@ -31,12 +31,17 @@
     return out
 
 
-def neighbours(ref, xlo, xhi, zlo, zhi, ylo, yhi, lead, x, centre):
+def halo_columns(ycols, x):
+    nx = ycols.shape[1]
+    pick = (lax.broadcasted_iota(jnp.int32, (nx, 128), 0) == x).astype(jnp.float32)
+    return jnp.dot(ycols[...], pick, precision=lax.Precision.HIGHEST, preferred_element_type=jnp.float32)
+
+
+def neighbours(ref, xlo, xhi, zlo, zhi, yl, yh, lead, x, centre):
     nx = ref.shape[-3]
     nz, ny = centre.shape
     sub = lax.broadcasted_iota(jnp.int32, (nz, ny), 0)
     lane = lax.broadcasted_iota(jnp.int32, (nz, ny), 1)
-    column = lax.broadcasted_iota(jnp.int32, (nz, nx), 1)
     prev = ref[lead + (jnp.maximum(x - 1, 0),)]
     nxt = ref[lead + (jnp.minimum(x + 1, nx - 1),)]
     xm = jnp.where(x == 0, xlo[lead], prev)
@@ -45,18 +50,21 @@
     zh = zhi[lead + (pl.ds(x, 1), slice(None))]
     zm = jnp.where(sub == 0, zl, pltpu.roll(centre, 1, 0))
     zp = jnp.where(sub == nz - 1, zh, pltpu.roll(centre, nz - 1, 0))
-    yl = jnp.sum(jnp.where(column == x, ylo[lead], 0.0), axis=1, keepdims=True)
-    yh = jnp.sum(jnp.where(column == x, yhi[lead], 0.0), axis=1, keepdims=True)
     ym = jnp.where(lane == 0, yl, pltpu.roll(centre, 1, 1))
     yp = jnp.where(lane == ny - 1, yh, pltpu.roll(centre, ny - 1, 1))
     return xm, xp, ym, yp, zm, zp
 
 
-def viscosity_kernel(u, xlo, xhi, zlo, zhi, ylo, yhi, nu):
+def viscosity_kernel(u, xlo, xhi, zlo, zhi, ycols, nu):
+    nz = u.shape[2]
+
     def plane(x, carry):
+        cols = halo_columns(ycols, x)
         grads = []
         for c in range(3):
-            xm, xp, ym, yp, zm, zp = neighbours(u, xlo, xhi, zlo, zhi, ylo, yhi, (c,), x, u[c, x])
+            yl = cols[nz * c : nz * (c + 1)]
+            yh = cols[nz * (c + 3) : nz * (c + 4)]
+            xm, xp, ym, yp, zm, zp = neighbours(u, xlo, xhi, zlo, zhi, yl, yh, (c,), x, u[c, x])
             grads.append([0.5 * (xp - xm), 0.5 * (yp - ym), 0.5 * (zp - zm)])
         total = jnp.zeros_like(grads[0][0])
         for c in range(3):
@@ -69,18 +77,24 @@
     lax.fori_loop(0, u.shape[1], plane, 0)
 
 
-def advance_kernel(planes, u, xlo, xhi, zlo, zhi, ylo, yhi, nu, nxlo, nxhi, nzlo, nzhi, nylo, nyhi, sent, out):
+def advance_kernel(planes, u, xlo, xhi, zlo, zhi, nu, nxlo, nxhi, nzlo, nzhi, ycols, sent, out):
     slots = sent.shape[0]
+    nz = u.shape[2]
 
     def plane(x, carry):
+        cols = halo_columns(ycols, x)
         here = nu[x]
-        nxm, nxp, nym, nyp, nzm, nzp = neighbours(nu, nxlo, nxhi, nzlo, nzhi, nylo, nyhi, (), x, here)
+        nyl = cols[nz * 6 : nz * 7]
+        nyh = cols[nz * 7 : nz * 8]
+        nxm, nxp, nym, nyp, nzm, nzp = neighbours(nu, nxlo, nxhi, nzlo, nzhi, nyl, nyh, (), x, here)
         nu_up = [0.5 * (here + nxp), 0.5 * (here + nyp), 0.5 * (here + nzp)]
         nu_low = [0.5 * (here + nxm), 0.5 * (here + nym), 0.5 * (here + nzm)]
         centres = [u[c, x] for c in range(3)]
         for c in range(3):
             center = centres[c]
-            xm, xp, ym, yp, zm, zp = neighbours(u, xlo, xhi, zlo, zhi, ylo, yhi, (c,), x, center)
+            yl = cols[nz * c : nz * (c + 1)]
+            yh = cols[nz * (c + 3) : nz * (c + 4)]
+            xm, xp, ym, yp, zm, zp = neighbours(u, xlo, xhi, zlo, zhi, yl, yh, (c,), x, center)
             upper = (xp, yp, zp)
             lower = (xm, ym, zm)
             advect = jnp.zeros_like(center)
@@ -110,14 +124,17 @@
 
 
 def stencil(velocity, planes, sent):
+    nx = velocity.shape[1]
     u_faces = faces(velocity, 1)
+    u_cols = jnp.concatenate(u_faces[4:], axis=0)
     nu = vmem_call(
-        viscosity_kernel, jax.ShapeDtypeStruct(velocity.shape[1:], jnp.float32), 7
-    )(velocity, *u_faces)
+        viscosity_kernel, jax.ShapeDtypeStruct(velocity.shape[1:], jnp.float32), 6
+    )(velocity, *u_faces[:4], u_cols.reshape(-1, nx))
     nu_faces = faces(nu, 0)
+    cols = jnp.concatenate([u_cols] + [f[None] for f in nu_faces[4:]], axis=0)
     return vmem_call(
-        advance_kernel, jax.ShapeDtypeStruct(velocity.shape, jnp.float32), 16, smem=1
-    )(planes, velocity, *u_faces, nu, *nu_faces, sent)
+        advance_kernel, jax.ShapeDtypeStruct(velocity.shape, jnp.float32), 13, smem=1
+    )(planes, velocity, *u_faces[:4], nu, *nu_faces[:4], cols.reshape(-1, nx), sent)
 
 
 def body(velocity, tile_turbine, tile_plane, tile_weight, chord):

time: 138 us -> 146 us (1.058)
  the two profiles are of different devices: /device:TPU:44 before, /device:TPU:1 now
where the time goes in v6:
time: 146 us; the launch traced here: 145 us
  starting transfers between devices  54.4 us (37%)
  Pallas kernels  41.6 us (28%)
  local copies, waits for them, and re-layouts  22.8 us (16%)
  waiting for transfers between devices  11.4 us (8%)
  matrix products  10.2 us (7%)
  other arithmetic  4.1 us (3%)
    pallas_call x1, Pallas kernels, stencil(): vmem_call(advance_kernel, jax.ShapeDtypeStruct(velocity.shape, jnp.float3...  22.4 us
    ppermute x6, starting transfers between devices, faces(): lax.ppermute(lax.index_in_dim(block, size - 1, dim, keepdims=False), axis...  19.5 us
    pallas_call x1, Pallas kernels, stencil(): vmem_call(viscosity_kernel, jax.ShapeDtypeStruct(velocity.shape[1:], jnp....  19.3 us
    all_to_all x1, starting transfers between devices, body(): lax.all_to_all(partial_sample.reshape(rows, per_row, -1), 'gx', split_axi...  9.97 us
    ppermute x6, starting transfers between devices, faces(): lax.ppermute(lax.index_in_dim(block, 0, dim, keepdims=False), axis, backw...  8.99 us
    ppermute x4, starting transfers between devices, body(): owned = owned + lax.ppermute(owned, axis, pairs)  8.54 us
    unnamed x28, local copies, waits for them, and re-layouts  7.78 us
    all_to_all x1, starting transfers between devices, body(): lax.all_to_all(jnp.broadcast_to(owned_force[None], (rows,) + owned_force....  7.39 us
  transfers between devices with their start and end apart: 18, of which 4 were waited for; matrix products, arithmetic and copies ran while one was open for 18% of the time, Pallas kernels for 13%

profile of v6, /device:TPU:1, one launch (start us, length us, event | category | flops | bytes accessed | tf_op | source)
XLA Modules:
  0.0 145.4 jit_solution(16315087313784216309)
XLA Ops:
  0.7 2.9 %reshape.67 = f32[3,64,4096]{2,1,0:T(8,128)S(1)} reshape(f32[3,64,32,128]{3,2,1,0:T(8,128)} %u.3) | data formatting | bytes 6291456 | tf_op jit(solution)/shard_map/reshape | solution.py:152
  4.7 4.7 %fusion.2 = f32[2,3,384]{2,1,0:T(4,128)S(1)} fusion(bf16[1,1,1,2,384,4096]{5,4,3,2,1,0:T(8,128)(2,1)} %param.8, bf16[2,3,4096]{2,0,1:T(2,128)(2,1)S(1)} %convolution_convert_fusion), kind=kOutput, calls=%fused_computation.2 | convolution fusion | flops 18874368 | bytes 6349824 | tf_op jit(solution)/shard_map/spq,scq->scp/dot_general | solution.py:157
  10.7 10.0 %all-to-all-start = ((f32[16,4,1152]{2,1,0:T(4,128)}), f32[16,4,1152]{2,1,0:T(4,128)S(1)}, u32[]{:S(2)}, u32[]{:S(2)}) async-start(f32[16,4,1152]{2,1,0:T(4,128)} %copy.39), calls=%async_computation | async-start | bytes 589824 | tf_op jit(solution)/shard_map/all_to_all | solution.py:171
  21.3 3.5 %collective-permute-start = (f32[3,32,128]{2,1,0:T(8,128)}, f32[3,32,128]{2,1,0:T(8,128)S(1)}, u32[]{:S(2)}, u32[]{:S(2)}) collective-permute-start(f32[3,32,128]{2,1,0:T(8,128)} %get-tuple-element.9), channel_id=1, source_target_pairs={{0,16},{16,32},{32,48},{48,64},{64,80},{80,96},{96,112},{112,128},... | collective-permute-start | bytes 147464 | tf_op jit(solution)/shard_map/ppermute | solution.py:25
  24.8 1.9 %collective-permute-start.1 = (f32[3,32,128]{2,1,0:T(8,128)}, f32[3,32,128]{2,1,0:T(8,128)S(1)}, u32[]{:S(2)}, u32[]{:S(2)}) collective-permute-start(f32[3,32,128]{2,1,0:T(8,128)} %get-tuple-element.8), channel_id=1, source_target_pairs={{16,0},{32,16},{48,32},{64,48},{80,64},{96,80},{112,96},{128,112},... | collective-permute-start | bytes 147464 | tf_op jit(solution)/shard_map/ppermute | solution.py:26
  26.8 6.3 %all-to-all-done = f32[16,4,1152]{2,1,0:T(4,128)S(1)} async-done(((f32[16,4,1152]{2,1,0:T(4,128)}), f32[16,4,1152]{2,1,0:T(4,128)S(1)}, u32[]{:S(2)}, u32[]{:S(2)}) %all-to-all-start) | async-done | bytes 294944 | tf_op jit(solution)/shard_map/all_to_all | solution.py:171
  35.0 3.8 %fusion.17 = (f32[3,64,32,1]{3,2,1,0:T(8,128)}, f32[3,64,32,1]{3,2,1,0:T(8,128)}) fusion(f32[3,64,32,128]{3,2,1,0:T(8,128)S(1)} %copy-done), kind=kLoop, calls=%fused_computation.27 | loop fusion | bytes 98304 | tf_op jit(solution)/shard_map/slice | solution.py:25
  38.8 3.3 %copy.48 = f32[3,64,32,1]{1,2,3,0:T(8,128)} copy(f32[3,64,32,1]{3,2,1,0:T(8,128)} %get-tuple-element.5) | data formatting | bytes 49152
  43.3 3.3 %copy.47 = f32[3,64,32,1]{1,2,0,3:T(8,128)} copy(f32[3,64,32,1]{3,2,1,0:T(8,128)} %get-tuple-element.4) | data formatting | bytes 49152
  46.6 4.0 %collective-permute-start.4 = (f32[3,64,32]{1,2,0:T(8,128)}, f32[3,64,32]{1,2,0:T(8,128)S(1)}, u32[]{:S(2)}, u32[]{:S(2)}) collective-permute-start(f32[3,64,32]{1,2,0:T(8,128)} %bitcast.5), channel_id=1, source_target_pairs={{0,4},{4,8},{8,12},{1,5},{5,9},{9,13},{2,6},{6,10},{10,14},{3,7},{... | collective-permute-start | bytes 73736 | tf_op jit(solution)/shard_map/ppermute | solution.py:25
  51.2 2.5 %collective-permute-start.13 = (f32[4,1152]{1,0:T(4,128)}, f32[4,1152]{1,0:T(4,128)}, u32[]{:S(2)}, u32[]{:S(2)}) collective-permute-start(f32[4,1152]{1,0:T(4,128)} %add.26), channel_id=1, source_target_pairs={{0,8},{4,12},{8,0},{12,4},{1,9},{5,13},{9,1},{13,5},{2,10},{6,14},... | collective-permute-start | bytes 55304 | tf_op jit(solution)/shard_map/ppermute | solution.py:180
  53.8 1.8 %collective-permute-done.13 = f32[4,1152]{1,0:T(4,128)} collective-permute-done((f32[4,1152]{1,0:T(4,128)}, f32[4,1152]{1,0:T(4,128)}, u32[]{:S(2)}, u32[]{:S(2)}) %collective-permute-start.13) | collective-permute-done | bytes 18464 | tf_op jit(solution)/shard_map/ppermute | solution.py:180
  55.6 3.2 %collective-permute-start.2 = (f32[3,64,128]{2,1,0:T(8,128)S(1)}, f32[3,64,128]{2,1,0:T(8,128)S(1)}, u32[]{:S(2)}, u32[]{:S(2)}) collective-permute-start(f32[3,64,128]{2,1,0:T(8,128)S(1)} %bitcast.63), channel_id=1, source_target_pairs={{0,1},{1,2},{2,3},{4,5},{5,6},{6,7},{8,9},{9,10},{10,11},{12,13},{... | collective-permute-start | bytes 294920 | tf_op jit(solution)/shard_map/ppermute | solution.py:25
  60.9 2.2 %collective-permute-start.14 = (f32[4,1152]{1,0:T(4,128)S(1)}, f32[4,1152]{1,0:T(4,128)S(1)}, u32[]{:S(2)}, u32[]{:S(2)}) collective-permute-start(f32[4,1152]{1,0:T(4,128)S(1)} %add.27), channel_id=1, source_target_pairs={{0,1},{1,0},{2,3},{3,2},{4,5},{5,4},{6,7},{7,6},{8,9},{9,8},{10,11... | collective-permute-start | bytes 55304 | tf_op jit(solution)/shard_map/ppermute | solution.py:180
  65.6 19.3 %shard_map.68.nu = f32[64,32,128]{2,1,0:T(8,128)} custom-call(f32[3,64,32,128]{3,2,1,0:T(8,128)} %u.3, f32[3,32,128]{2,1,0:T(8,128)} %copy-done.4, f32[3,32,128]{2,1,0:T(8,128)} %copy-done.5, f32[3,64,128]{2,1,0:T(8,128)} %copy-done.2, f32[3,64,128]{2,1,0:T(8,128)} %copy-done.3, f32[192,64]{1,0:T(8,128)} %bitcast.57), custom_call_target="tpu_custom_call" | custom-call | tf_op jit(solution)/shard_map/pallas_call | solution.py:130
  84.9 2.7 %collective-permute-start.15 = (f32[4,1152]{1,0:T(4,128)S(1)}, f32[4,1152]{1,0:T(4,128)S(1)}, u32[]{:S(2)}, u32[]{:S(2)}) collective-permute-start(f32[4,1152]{1,0:T(4,128)S(1)} %add.28), channel_id=1, source_target_pairs={{0,2},{1,3},{2,0},{3,1},{4,6},{5,7},{6,4},{7,5},{8,10},{9,11},{10,... | collective-permute-start | bytes 55304 | tf_op jit(solution)/shard_map/ppermute | solution.py:180
  87.6 2.0 %fusion.19 = (f32[64,32,1]{2,1,0:T(8,128)S(1)}, f32[64,32,1]{2,1,0:T(8,128)S(1)}) fusion(f32[64,32,128]{2,1,0:T(8,128)} %shard_map.68.nu), kind=kLoop, calls=%fused_computation.29 | loop fusion | bytes 32768 | tf_op jit(solution)/shard_map/slice | solution.py:25
  92.1 4.0 %collective-permute-start.10 = (f32[64,32]{0,1:T(8,128)S(1)}, f32[64,32]{0,1:T(8,128)S(1)}, u32[]{:S(2)}, u32[]{:S(2)}) collective-permute-start(f32[64,32]{0,1:T(8,128)S(1)} %bitcast.68), channel_id=1, source_target_pairs={{0,4},{4,8},{8,12},{1,5},{5,9},{9,13},{2,6},{6,10},{10,14},{3,7},{... | collective-permute-start | bytes 24584 | tf_op jit(solution)/shard_map/ppermute | solution.py:25
  97.6 7.4 %all-to-all-start.1 = ((f32[16,4,1152]{2,1,0:T(4,128)}), f32[16,4,1152]{2,1,0:T(4,128)S(1)}, u32[]{:S(2)}, u32[]{:S(2)}) async-start(f32[16,4,1152]{2,1,0:T(4,128)} %broadcast_in_dim.8), calls=%async_computation.1 | async-start | bytes 589824 | tf_op jit(solution)/shard_map/all_to_all | solution.py:184
  106.8 3.5 %collective-permute-start.6 = (f32[32,128]{1,0:T(8,128)S(1)}, f32[32,128]{1,0:T(8,128)S(1)}, u32[]{:S(2)}, u32[]{:S(2)}) collective-permute-start(f32[32,128]{1,0:T(8,128)S(1)} %get-tuple-element.15), channel_id=1, source_target_pairs={{0,16},{16,32},{32,48},{48,64},{64,80},{80,96},{96,112},{112,128},... | collective-permute-start | bytes 49160 | tf_op jit(solution)/shard_map/ppermute | solution.py:25
  110.4 1.9 %collective-permute-start.7 = (f32[32,128]{1,0:T(8,128)S(1)}, f32[32,128]{1,0:T(8,128)S(1)}, u32[]{:S(2)}, u32[]{:S(2)}) collective-permute-start(f32[32,128]{1,0:T(8,128)S(1)} %get-tuple-element.14), channel_id=1, source_target_pairs={{16,0},{32,16},{48,32},{64,48},{80,64},{96,80},{112,96},{128,112},... | collective-permute-start | bytes 49160 | tf_op jit(solution)/shard_map/ppermute | solution.py:26
  115.6 2.0 %all-to-all-done.1 = f32[16,4,1152]{2,1,0:T(4,128)S(1)} async-done(((f32[16,4,1152]{2,1,0:T(4,128)}), f32[16,4,1152]{2,1,0:T(4,128)S(1)}, u32[]{:S(2)}, u32[]{:S(2)}) %all-to-all-start.1) | async-done | bytes 294944 | tf_op jit(solution)/shard_map/all_to_all | solution.py:184
  118.0 3.7 %fusion = f32[2,3,4096]{2,1,0:T(4,128)S(1)} fusion(bf16[2,3,384]{2,1,0:T(4,128)(2,1)S(1)} %reshape.71, bf16[1,1,1,2,384,4096]{5,4,3,2,1,0:T(8,128)(2,1)} %param.8), kind=kOutput, calls=%fused_computation | convolution fusion | flops 18874368 | bytes 6394368 | tf_op jit(solution)/shard_map/axz,ahx->ahz/dot_general | solution.py:189
  123.1 22.4 %shard_map.69 = f32[3,64,32,128]{3,2,1,0:T(8,128)} custom-call(s32[2]{0:T(128)} %bitcast.74, f32[3,64,32,128]{3,2,1,0:T(8,128)} %u.3, f32[3,32,128]{2,1,0:T(8,128)} %copy-done.4, f32[3,32,128]{2,1,0:T(8,128)} %copy-done.5, f32[3,64,128]{2,1,0:T(8,128)} %copy-done.2, f32[3,64,128]{2,1,0:T(8,128)} %copy-done.3, f32[64,32,128]{2,1,0:T(8,128)} %shard_map.68.nu, ...), custom_call_target="tpu_custom_call" | custom-call | tf_op jit(solution)/shard_map/pallas_call | solution.py:135
  (74 shorter events, 22.4 us)
Async XLA Ops:
  0.6 2.9 %copy-start.12 = (s32[1,1,1,2]{3,2,1,0:T(1,128)S(1)}, s32[1,1,1,2]{3,2,1,0:T(1,128)}, u32[]{:S(2)}) copy-start(s32[1,1,1,2]{3,2,1,0:T(1,128)} %param.7) | copy-start | bytes 28
  4.7 4.7 %copy-start.11 = (s32[1,1,1,2]{3,2,1,0:T(1,128)S(1)}, s32[1,1,1,2]{3,2,1,0:T(1,128)}, u32[]{:S(2)}) copy-start(s32[1,1,1,2]{3,2,1,0:T(1,128)} %param.6) | copy-start | bytes 28
  4.7 16.0 %copy-start = (f32[3,64,32,128]{3,2,1,0:T(8,128)S(1)}, f32[3,64,32,128]{3,2,1,0:T(8,128)}, u32[]{:S(2)}) copy-start(f32[3,64,32,128]{3,2,1,0:T(8,128)} %u.3) | copy-start | bytes 9437188
  10.7 22.4 %all-to-all-start = ((f32[16,4,1152]{2,1,0:T(4,128)}), f32[16,4,1152]{2,1,0:T(4,128)S(1)}, u32[]{:S(2)}, u32[]{:S(2)}) async-start(f32[16,4,1152]{2,1,0:T(4,128)} %copy.39), calls=%async_computation | async-start | bytes 589824 | tf_op jit(solution)/shard_map/all_to_all | solution.py:171
  21.3 42.4 %collective-permute-start = (f32[3,32,128]{2,1,0:T(8,128)}, f32[3,32,128]{2,1,0:T(8,128)S(1)}, u32[]{:S(2)}, u32[]{:S(2)}) collective-permute-start(f32[3,32,128]{2,1,0:T(8,128)} %get-tuple-element.9), channel_id=1, source_target_pairs={{0,16},{16,32},{32,48},{48,64},{64,80},{80,96},{96,112},{112,128},... | collective-permute-start | bytes 147464 | tf_op jit(solution)/shard_map/ppermute | solution.py:25
  24.8 38.9 %collective-permute-start.1 = (f32[3,32,128]{2,1,0:T(8,128)}, f32[3,32,128]{2,1,0:T(8,128)S(1)}, u32[]{:S(2)}, u32[]{:S(2)}) collective-permute-start(f32[3,32,128]{2,1,0:T(8,128)} %get-tuple-element.8), channel_id=1, source_target_pairs={{16,0},{32,16},{48,32},{64,48},{80,64},{96,80},{112,96},{128,112},... | collective-permute-start | bytes 147464 | tf_op jit(solution)/shard_map/ppermute | solution.py:26
  33.7 16.8 %collective-permute-start.12 = (f32[4,1152]{1,0:T(4,128)}, f32[4,1152]{1,0:T(4,128)S(1)}, u32[]{:S(2)}, u32[]{:S(2)}) collective-permute-start(f32[4,1152]{1,0:T(4,128)} %reduce_sum.18), channel_id=1, source_target_pairs={{0,4},{4,0},{8,12},{12,8},{1,5},{5,1},{9,13},{13,9},{2,6},{6,2},{1... | collective-permute-start | bytes 55304 | tf_op jit(solution)/shard_map/ppermute | solution.py:180
  38.8 11.8 %copy-start.6 = (f32[4,1152]{1,0:T(4,128)S(1)}, f32[4,1152]{1,0:T(4,128)}, u32[]{:S(2)}) copy-start(f32[4,1152]{1,0:T(4,128)} %reduce_sum.18) | copy-start | bytes 55300
  42.0 17.5 %collective-permute-start.5 = (f32[3,64,32]{1,2,0:T(8,128)}, f32[3,64,32]{1,2,0:T(8,128)S(1)}, u32[]{:S(2)}, u32[]{:S(2)}) collective-permute-start(f32[3,64,32]{1,2,0:T(8,128)} %bitcast.7), channel_id=1, source_target_pairs={{4,0},{8,4},{12,8},{5,1},{9,5},{13,9},{6,2},{10,6},{14,10},{7,3},{... | collective-permute-start | bytes 73736 | tf_op jit(solution)/shard_map/ppermute | solution.py:26
  46.6 14.3 %collective-permute-start.4 = (f32[3,64,32]{1,2,0:T(8,128)}, f32[3,64,32]{1,2,0:T(8,128)S(1)}, u32[]{:S(2)}, u32[]{:S(2)}) collective-permute-start(f32[3,64,32]{1,2,0:T(8,128)} %bitcast.5), channel_id=1, source_target_pairs={{0,4},{4,8},{8,12},{1,5},{5,9},{9,13},{2,6},{6,10},{10,14},{3,7},{... | collective-permute-start | bytes 73736 | tf_op jit(solution)/shard_map/ppermute | solution.py:25
  51.2 4.4 %collective-permute-start.13 = (f32[4,1152]{1,0:T(4,128)}, f32[4,1152]{1,0:T(4,128)}, u32[]{:S(2)}, u32[]{:S(2)}) collective-permute-start(f32[4,1152]{1,0:T(4,128)} %add.26), channel_id=1, source_target_pairs={{0,8},{4,12},{8,0},{12,4},{1,9},{5,13},{9,1},{13,5},{2,10},{6,14},... | collective-permute-start | bytes 55304 | tf_op jit(solution)/shard_map/ppermute | solution.py:180
  55.6 8.1 %collective-permute-start.2 = (f32[3,64,128]{2,1,0:T(8,128)S(1)}, f32[3,64,128]{2,1,0:T(8,128)S(1)}, u32[]{:S(2)}, u32[]{:S(2)}) collective-permute-start(f32[3,64,128]{2,1,0:T(8,128)S(1)} %bitcast.63), channel_id=1, source_target_pairs={{0,1},{1,2},{2,3},{4,5},{5,6},{6,7},{8,9},{9,10},{10,11},{12,13},{... | collective-permute-start | bytes 294920 | tf_op jit(solution)/shard_map/ppermute | solution.py:25
  59.6 5.4 %collective-permute-start.3 = (f32[3,64,128]{2,1,0:T(8,128)S(1)}, f32[3,64,128]{2,1,0:T(8,128)S(1)}, u32[]{:S(2)}, u32[]{:S(2)}) collective-permute-start(f32[3,64,128]{2,1,0:T(8,128)S(1)} %bitcast.62), channel_id=1, source_target_pairs={{1,0},{2,1},{3,2},{5,4},{6,5},{7,6},{9,8},{10,9},{11,10},{13,12},{... | collective-permute-start | bytes 294920 | tf_op jit(solution)/shard_map/ppermute | solution.py:26
  60.9 24.0 %collective-permute-start.14 = (f32[4,1152]{1,0:T(4,128)S(1)}, f32[4,1152]{1,0:T(4,128)S(1)}, u32[]{:S(2)}, u32[]{:S(2)}) collective-permute-start(f32[4,1152]{1,0:T(4,128)S(1)} %add.27), channel_id=1, source_target_pairs={{0,1},{1,0},{2,3},{3,2},{4,5},{5,4},{6,7},{7,6},{8,9},{9,8},{10,11... | collective-permute-start | bytes 55304 | tf_op jit(solution)/shard_map/ppermute | solution.py:180
  63.7 1.2 copy-start.4
  84.9 11.2 %collective-permute-start.15 = (f32[4,1152]{1,0:T(4,128)S(1)}, f32[4,1152]{1,0:T(4,128)S(1)}, u32[]{:S(2)}, u32[]{:S(2)}) collective-permute-start(f32[4,1152]{1,0:T(4,128)S(1)} %add.28), channel_id=1, source_target_pairs={{0,2},{1,3},{2,0},{3,1},{4,6},{5,7},{6,4},{7,5},{8,10},{9,11},{10,... | collective-permute-start | bytes 55304 | tf_op jit(solution)/shard_map/ppermute | solution.py:180
  90.2 23.4 %collective-permute-start.11 = (f32[64,32]{0,1:T(8,128)S(1)}, f32[64,32]{0,1:T(8,128)S(1)}, u32[]{:S(2)}, u32[]{:S(2)}) collective-permute-start(f32[64,32]{0,1:T(8,128)S(1)} %bitcast.69), channel_id=1, source_target_pairs={{4,0},{8,4},{12,8},{5,1},{9,5},{13,9},{6,2},{10,6},{14,10},{7,3},{... | collective-permute-start | bytes 24584 | tf_op jit(solution)/shard_map/ppermute | solution.py:26
  92.1 22.8 %collective-permute-start.10 = (f32[64,32]{0,1:T(8,128)S(1)}, f32[64,32]{0,1:T(8,128)S(1)}, u32[]{:S(2)}, u32[]{:S(2)}) collective-permute-start(f32[64,32]{0,1:T(8,128)S(1)} %bitcast.68), channel_id=1, source_target_pairs={{0,4},{4,8},{8,12},{1,5},{5,9},{9,13},{2,6},{6,10},{10,14},{3,7},{... | collective-permute-start | bytes 24584 | tf_op jit(solution)/shard_map/ppermute | solution.py:25
  97.6 20.0 %all-to-all-start.1 = ((f32[16,4,1152]{2,1,0:T(4,128)}), f32[16,4,1152]{2,1,0:T(4,128)S(1)}, u32[]{:S(2)}, u32[]{:S(2)}) async-start(f32[16,4,1152]{2,1,0:T(4,128)} %broadcast_in_dim.8), calls=%async_computation.1 | async-start | bytes 589824 | tf_op jit(solution)/shard_map/all_to_all | solution.py:184
  106.8 15.6 %collective-permute-start.6 = (f32[32,128]{1,0:T(8,128)S(1)}, f32[32,128]{1,0:T(8,128)S(1)}, u32[]{:S(2)}, u32[]{:S(2)}) collective-permute-start(f32[32,128]{1,0:T(8,128)S(1)} %get-tuple-element.15), channel_id=1, source_target_pairs={{0,16},{16,32},{32,48},{48,64},{64,80},{80,96},{96,112},{112,128},... | collective-permute-start | bytes 49160 | tf_op jit(solution)/shard_map/ppermute | solution.py:25
  110.4 12.1 %collective-permute-start.7 = (f32[32,128]{1,0:T(8,128)S(1)}, f32[32,128]{1,0:T(8,128)S(1)}, u32[]{:S(2)}, u32[]{:S(2)}) collective-permute-start(f32[32,128]{1,0:T(8,128)S(1)} %get-tuple-element.14), channel_id=1, source_target_pairs={{16,0},{32,16},{48,32},{64,48},{80,64},{96,80},{112,96},{128,112},... | collective-permute-start | bytes 49160 | tf_op jit(solution)/shard_map/ppermute | solution.py:26
  112.3 10.1 %collective-permute-start.8 = (f32[64,128]{1,0:T(8,128)S(1)}, f32[64,128]{1,0:T(8,128)S(1)}, u32[]{:S(2)}, u32[]{:S(2)}) collective-permute-start(f32[64,128]{1,0:T(8,128)S(1)} %bitcast.67), channel_id=1, source_target_pairs={{0,1},{1,2},{2,3},{4,5},{5,6},{6,7},{8,9},{9,10},{10,11},{12,13},{... | collective-permute-start | bytes 98312 | tf_op jit(solution)/shard_map/ppermute | solution.py:25
  113.6 8.8 %collective-permute-start.9 = (f32[64,128]{1,0:T(8,128)S(1)}, f32[64,128]{1,0:T(8,128)S(1)}, u32[]{:S(2)}, u32[]{:S(2)}) collective-permute-start(f32[64,128]{1,0:T(8,128)S(1)} %bitcast.66), channel_id=1, source_target_pairs={{1,0},{2,1},{3,2},{5,4},{6,5},{7,6},{9,8},{10,9},{11,10},{13,12},{... | collective-permute-start | bytes 98312 | tf_op jit(solution)/shard_map/ppermute | solution.py:26
  117.7 4.0 %copy-start.1 = (f32[64,1152]{1,0:T(8,128)}, f32[64,1152]{1,0:T(8,128)S(1)}, u32[]{:S(2)}) copy-start(f32[64,1152]{1,0:T(8,128)S(1)} %reshape.70) | copy-start | bytes 884740
  (7 other events, 5.5 us)

commit v7 on v3

--- a/solution.py
+++ b/solution.py
@@ -16,18 +16,24 @@
 
 
 def faces(block, lead):
+    ny = block.shape[-1]
+    ends = (lax.broadcasted_iota(jnp.int32, (2, ny), 1) == jnp.array([[0], [ny - 1]])).astype(jnp.float32)
+    letters = "cxzy"[1 - lead :]
+    columns = jnp.einsum(
+        letters + ",ky->k" + letters[:-3] + "zx", block, ends, precision=lax.Precision.HIGHEST
+    )
     out = []
-    for axis, dim in (("gx", lead), ("gz", lead + 1), ("gy", lead + 2)):
+    for axis, dim in (("gx", lead), ("gz", lead + 1), ("gy", None)):
         count = lax.axis_size(axis)
         forward = [(i, i + 1) for i in range(count - 1)]
         backward = [(target, source) for source, target in forward]
-        size = block.shape[dim]
-        low = lax.ppermute(lax.index_in_dim(block, size - 1, dim, keepdims=False), axis, forward)
-        high = lax.ppermute(lax.index_in_dim(block, 0, dim, keepdims=False), axis, backward)
-        if axis == "gy":
-            low = jnp.swapaxes(low, -1, -2)
-            high = jnp.swapaxes(high, -1, -2)
-        out += [low, high]
+        if dim is None:
+            first, last = columns[0], columns[1]
+        else:
+            size = block.shape[dim]
+            first = lax.index_in_dim(block, 0, dim, keepdims=False)
+            last = lax.index_in_dim(block, size - 1, dim, keepdims=False)
+        out += [lax.ppermute(last, axis, forward), lax.ppermute(first, axis, backward)]
     return out
 
 
@@ -132,11 +138,9 @@
     spread_weights = tile_weight.reshape(
         tile_count, actuator_count, vertical_coord * spanwise_coord
     )
-    flat = velocity.reshape(3, cx, vertical_coord * spanwise_coord)
-    picks = (rotor_planes[:, None] == jnp.arange(cx, dtype=jnp.int32)[None, :]).astype(jnp.float32)
-    tiles = jnp.einsum("sx,cxq->scq", picks, flat, precision=lax.Precision.HIGHEST).astype(
-        jnp.bfloat16
-    )
+    tiles = jnp.stack(
+        [lax.dynamic_index_in_dim(velocity, rotor_planes[s], 1, keepdims=False) for s in range(tile_count)]
+    ).reshape(tile_count, 3, vertical_coord * spanwise_coord).astype(jnp.bfloat16)
     block_local = jnp.einsum(
         "spq,scq->scp", spread_weights, tiles, preferred_element_type=jnp.float32
     )

time: 138 us -> 129 us (0.935)
  the two profiles are of different devices: /device:TPU:44 before, /device:TPU:1 now
where the time goes in v7:
time: 129 us; the launch traced here: 128 us
  starting transfers between devices  53.5 us (41%)
  Pallas kernels  33.6 us (26%)
  matrix products  16.8 us (13%)
  local copies, waits for them, and re-layouts  11.2 us (9%)
  waiting for transfers between devices  6.98 us (5%)
  between operations  4.97 us (4%)
    ppermute x6, starting transfers between devices, faces(): lax.ppermute(last, axis, forward)  20.2 us
    pallas_call x1, Pallas kernels, stencil(): vmem_call(advance_kernel, jax.ShapeDtypeStruct(velocity.shape, jnp.float3...  18 us
    pallas_call x1, Pallas kernels, stencil(): vmem_call(viscosity_kernel, jax.ShapeDtypeStruct(velocity.shape[1:], jnp....  15.6 us
    all_to_all x1, starting transfers between devices, body(): lax.all_to_all(partial_sample.reshape(rows, per_row, -1), 'gx', split_axi...  9.98 us
    ppermute x6, starting transfers between devices, faces(): lax.ppermute(first, axis, backward)  9.76 us
    ppermute x4, starting transfers between devices, body(): owned = owned + lax.ppermute(owned, axis, pairs)  8.92 us
    dot_general x2, matrix products, faces(): jnp.einsum(letters + ',ky->k' + letters[:-3] + 'zx', block, ends, precisi...  7.75 us
    all_to_all x1, waiting for transfers between devices, body(): lax.all_to_all(partial_sample.reshape(rows, per_row, -1), 'gx', split_axi...  5.45 us
  transfers between devices with their start and end apart: 18, of which 2 were waited for; matrix products, arithmetic and copies ran while one was open for 14% of the time, Pallas kernels for 12%

profile of v7, /device:TPU:1, one launch (start us, length us, event | category | flops | bytes accessed | tf_op | source)
XLA Modules:
  0.0 127.9 jit_solution(4551748171595042634)
XLA Ops:
  0.6 1.3 %fusion.25 = (s32[1,1,1,1]{3,2,1,0:T(1,128)}, s32[1,1,1,1]{3,2,1,0:T(1,128)}) fusion(s32[1,1,1,2]{3,2,1,0:T(1,128)} %param.9), kind=kLoop, calls=%fused_computation.44 | loop fusion | bytes 16 | tf_op jit(solution)/shard_map/slice | solution.py:142
  6.7 4.7 %fusion.2 = f32[2,3,384]{2,1,0:T(4,128)S(1)} fusion(bf16[1,1,1,2,384,4096]{5,4,3,2,1,0:T(8,128)(2,1)} %param.10, bf16[1,3,4096]{2,1,0:T(4,128)(2,1)S(1)} %stack.10, bf16[1,3,4096]{2,1,0:T(4,128)(2,1)S(1)} %stack.9), kind=kOutput, calls=%fused_computation.2 | convolution fusion | flops 18972672 | bytes 6349824 | tf_op jit(solution)/shard_map/spq,scq->scp/dot_general | solution.py:144
  12.7 10.0 %all-to-all-start = ((f32[16,4,1152]{2,1,0:T(4,128)}), f32[16,4,1152]{2,1,0:T(4,128)S(1)}, u32[]{:S(2)}, u32[]{:S(2)}) async-start(f32[16,4,1152]{2,1,0:T(4,128)} %copy.41), calls=%async_computation | async-start | bytes 589824 | tf_op jit(solution)/shard_map/all_to_all | solution.py:158
  22.7 4.9 %fusion.4 = f32[2,3,64,32]{2,0,3,1:T(2,128)S(1)} fusion(f32[3,64,32,128]{3,2,1,0:T(8,128)S(1)} %copy-done, s32[2]{0:T(128)S(1)} %iota_multiply_fusion), kind=kOutput, calls=%fused_computation.4 | convolution fusion | flops 18874624 | bytes 3194888 | tf_op jit(solution)/shard_map/cxzy,ky->kczx/dot_general | solution.py:22
  29.5 5.4 %all-to-all-done = f32[16,4,1152]{2,1,0:T(4,128)S(1)} async-done(((f32[16,4,1152]{2,1,0:T(4,128)}), f32[16,4,1152]{2,1,0:T(4,128)S(1)}, u32[]{:S(2)}, u32[]{:S(2)}) %all-to-all-start) | async-done | bytes 294944 | tf_op jit(solution)/shard_map/all_to_all | solution.py:158
  37.1 3.2 %collective-permute-start.2 = (f32[3,64,128]{2,1,0:T(8,128)}, f32[3,64,128]{2,1,0:T(8,128)S(1)}, u32[]{:S(2)}, u32[]{:S(2)}) collective-permute-start(f32[3,64,128]{2,1,0:T(8,128)} %bitcast.3), channel_id=1, source_target_pairs={{0,1},{1,2},{2,3},{4,5},{5,6},{6,7},{8,9},{9,10},{10,11},{12,13},{... | collective-permute-start | bytes 294920 | tf_op jit(solution)/shard_map/ppermute | solution.py:36
  40.3 1.3 %collective-permute-start.3 = (f32[3,64,128]{2,1,0:T(8,128)}, f32[3,64,128]{2,1,0:T(8,128)S(1)}, u32[]{:S(2)}, u32[]{:S(2)}) collective-permute-start(f32[3,64,128]{2,1,0:T(8,128)} %bitcast.4), channel_id=1, source_target_pairs={{1,0},{2,1},{3,2},{5,4},{6,5},{7,6},{9,8},{10,9},{11,10},{13,12},{... | collective-permute-start | bytes 294920 | tf_op jit(solution)/shard_map/ppermute | solution.py:36
  41.7 2.5 %collective-permute-start.13 = (f32[4,1152]{1,0:T(4,128)S(1)}, f32[4,1152]{1,0:T(4,128)S(1)}, u32[]{:S(2)}, u32[]{:S(2)}) collective-permute-start(f32[4,1152]{1,0:T(4,128)S(1)} %add.35), channel_id=1, source_target_pairs={{0,8},{4,12},{8,0},{12,4},{1,9},{5,13},{9,1},{13,5},{2,10},{6,14},... | collective-permute-start | bytes 55304 | tf_op jit(solution)/shard_map/ppermute | solution.py:167
  44.8 2.3 %collective-permute-start.1 = (f32[3,32,128]{2,1,0:T(8,128)}, f32[3,32,128]{2,1,0:T(8,128)S(1)}, u32[]{:S(2)}, u32[]{:S(2)}) collective-permute-start(f32[3,32,128]{2,1,0:T(8,128)} %get-tuple-element.8), channel_id=1, source_target_pairs={{16,0},{32,16},{48,32},{64,48},{80,64},{96,80},{112,96},{128,112},... | collective-permute-start | bytes 147464 | tf_op jit(solution)/shard_map/ppermute | solution.py:36
  47.2 3.2 %collective-permute-start = (f32[3,32,128]{2,1,0:T(8,128)S(1)}, f32[3,32,128]{2,1,0:T(8,128)S(1)}, u32[]{:S(2)}, u32[]{:S(2)}) collective-permute-start(f32[3,32,128]{2,1,0:T(8,128)S(1)} %get-tuple-element.9), channel_id=1, source_target_pairs={{0,16},{16,32},{32,48},{48,64},{64,80},{80,96},{96,112},{112,128},... | collective-permute-start | bytes 147464 | tf_op jit(solution)/shard_map/ppermute | solution.py:36
  50.4 1.8 %collective-permute-start.4 = (f32[3,32,64]{2,1,0:T(8,128)}, f32[3,32,64]{2,1,0:T(8,128)S(1)}, u32[]{:S(2)}, u32[]{:S(2)}) collective-permute-start(f32[3,32,64]{2,1,0:T(8,128)} %get-tuple-element.15), channel_id=1, source_target_pairs={{0,4},{4,8},{8,12},{1,5},{5,9},{9,13},{2,6},{6,10},{10,14},{3,7},{... | collective-permute-start | bytes 73736 | tf_op jit(solution)/shard_map/ppermute | solution.py:36
  52.3 1.5 %collective-permute-done.4.ylo = f32[3,32,64]{2,1,0:T(8,128)S(1)} collective-permute-done((f32[3,32,64]{2,1,0:T(8,128)}, f32[3,32,64]{2,1,0:T(8,128)S(1)}, u32[]{:S(2)}, u32[]{:S(2)}) %collective-permute-start.4) | collective-permute-done | bytes 24608 | tf_op jit(solution)/shard_map/ppermute | solution.py:36
  53.8 2.4 %collective-permute-start.14 = (f32[4,1152]{1,0:T(4,128)S(1)}, f32[4,1152]{1,0:T(4,128)S(1)}, u32[]{:S(2)}, u32[]{:S(2)}) collective-permute-start(f32[4,1152]{1,0:T(4,128)S(1)} %add.36), channel_id=1, source_target_pairs={{0,1},{1,0},{2,3},{3,2},{4,5},{5,4},{6,7},{7,6},{8,9},{9,8},{10,11... | collective-permute-start | bytes 55304 | tf_op jit(solution)/shard_map/ppermute | solution.py:167
  57.5 15.6 %shard_map.86.nu = f32[64,32,128]{2,1,0:T(8,128)} custom-call(f32[3,64,32,128]{3,2,1,0:T(8,128)} %u.3, f32[3,32,128]{2,1,0:T(8,128)} %copy-done.6, f32[3,32,128]{2,1,0:T(8,128)} %copy-done.5, f32[3,64,128]{2,1,0:T(8,128)} %copy-done.2, f32[3,64,128]{2,1,0:T(8,128)} %copy-done.3, f32[3,32,64]{2,1,0:T(8,128)} %copy-done.7, f32[3,32,64]{2,1,0:T(8,128)} %copy-done.4), custom_call_target="tpu_custom_call" | custom-call | tf_op jit(solution)/shard_map/pallas_call | solution.py:120
  73.2 2.7 %collective-permute-start.15 = (f32[4,1152]{1,0:T(4,128)S(1)}, f32[4,1152]{1,0:T(4,128)S(1)}, u32[]{:S(2)}, u32[]{:S(2)}) collective-permute-start(f32[4,1152]{1,0:T(4,128)S(1)} %add.37), channel_id=1, source_target_pairs={{0,2},{1,3},{2,0},{3,1},{4,6},{5,7},{6,4},{7,5},{8,10},{9,11},{10,... | collective-permute-start | bytes 55304 | tf_op jit(solution)/shard_map/ppermute | solution.py:167
  75.9 2.9 %fusion.14 = f32[2,64,32]{1,0,2:T(2,128)S(1)} fusion(s32[2]{0:T(128)S(1)} %iota_multiply_fusion, f32[64,32,128]{2,1,0:T(8,128)} %shard_map.86.nu), kind=kOutput, calls=%fused_computation.31 | convolution fusion | flops 6291712 | bytes 1064968 | tf_op jit(solution)/shard_map/xzy,ky->kzx/dot_general | solution.py:22
  80.3 4.6 %all-to-all-start.1 = ((f32[16,4,1152]{2,1,0:T(4,128)}), f32[16,4,1152]{2,1,0:T(4,128)S(1)}, u32[]{:S(2)}, u32[]{:S(2)}) async-start(f32[16,4,1152]{2,1,0:T(4,128)} %broadcast_in_dim.2), calls=%async_computation.1 | async-start | bytes 589824 | tf_op jit(solution)/shard_map/all_to_all | solution.py:171
  85.0 1.8 %copy.37 = f32[64,32,128]{2,0,1:T(8,128)S(1)} copy(f32[64,32,128]{2,1,0:T(8,128)} %shard_map.86.nu) | data formatting | bytes 2097152 | tf_op jit(solution)/shard_map/pallas_call | solution.py:120
  88.1 4.5 %collective-permute-start.10 = (f32[32,64]{1,0:T(8,128)S(1)}, f32[32,64]{1,0:T(8,128)S(1)}, u32[]{:S(2)}, u32[]{:S(2)}) collective-permute-start(f32[32,64]{1,0:T(8,128)S(1)} %get-tuple-element.17), channel_id=1, source_target_pairs={{0,4},{4,8},{8,12},{1,5},{5,9},{9,13},{2,6},{6,10},{10,14},{3,7},{... | collective-permute-start | bytes 24584 | tf_op jit(solution)/shard_map/ppermute | solution.py:36
  93.3 2.3 %collective-permute-start.7 = (f32[32,128]{1,0:T(8,128)S(1)}, f32[32,128]{1,0:T(8,128)S(1)}, u32[]{:S(2)}, u32[]{:S(2)}) collective-permute-start(f32[32,128]{1,0:T(8,128)S(1)} %get-tuple-element.12), channel_id=1, source_target_pairs={{16,0},{32,16},{48,32},{64,48},{80,64},{96,80},{112,96},{128,112},... | collective-permute-start | bytes 49160 | tf_op jit(solution)/shard_map/ppermute | solution.py:36
  95.6 3.4 %collective-permute-start.6 = (f32[32,128]{1,0:T(8,128)S(1)}, f32[32,128]{1,0:T(8,128)S(1)}, u32[]{:S(2)}, u32[]{:S(2)}) collective-permute-start(f32[32,128]{1,0:T(8,128)S(1)} %get-tuple-element.13), channel_id=1, source_target_pairs={{0,16},{16,32},{32,48},{48,64},{64,80},{80,96},{96,112},{112,128},... | collective-permute-start | bytes 49160 | tf_op jit(solution)/shard_map/ppermute | solution.py:36
  100.8 4.0 %collective-permute-start.8 = (f32[64,128]{1,0:T(8,128)S(1)}, f32[64,128]{1,0:T(8,128)S(1)}, u32[]{:S(2)}, u32[]{:S(2)}) collective-permute-start(f32[64,128]{1,0:T(8,128)S(1)} %get-tuple-element.11), channel_id=1, source_target_pairs={{0,1},{1,2},{2,3},{4,5},{5,6},{6,7},{8,9},{9,10},{10,11},{12,13},{... | collective-permute-start | bytes 98312 | tf_op jit(solution)/shard_map/ppermute | solution.py:36
  104.8 3.7 %fusion = f32[2,3,4096]{2,1,0:T(4,128)S(1)} fusion(bf16[2,3,384]{2,1,0:T(4,128)(2,1)S(1)} %reshape.71, bf16[1,1,1,2,384,4096]{5,4,3,2,1,0:T(8,128)(2,1)} %param.10), kind=kOutput, calls=%fused_computation | convolution fusion | flops 18874368 | bytes 6394368 | tf_op jit(solution)/shard_map/axz,ahx->ahz/dot_general | solution.py:176
  109.9 18.0 %shard_map.87 = f32[3,64,32,128]{3,2,1,0:T(8,128)} custom-call(s32[2]{0:T(128)} %bitcast.66, f32[3,64,32,128]{3,2,1,0:T(8,128)} %u.3, f32[3,32,128]{2,1,0:T(8,128)} %copy-done.6, f32[3,32,128]{2,1,0:T(8,128)} %copy-done.5, f32[3,64,128]{2,1,0:T(8,128)} %copy-done.2, f32[3,64,128]{2,1,0:T(8,128)} %copy-done.3, f32[3,32,64]{2,1,0:T(8,128)} %copy-done.7, ...), custom_call_target="tpu_custom_call" | custom-call | tf_op jit(solution)/shard_map/pallas_call | solution.py:124
  (80 shorter events, 14.8 us)
Async XLA Ops:
  6.7 4.7 %copy-start.14 = (s32[1,1,1,2]{3,2,1,0:T(1,128)S(1)}, s32[1,1,1,2]{3,2,1,0:T(1,128)}, u32[]{:S(2)}) copy-start(s32[1,1,1,2]{3,2,1,0:T(1,128)} %param.8) | copy-start | bytes 28
  6.7 16.0 %copy-start = (f32[3,64,32,128]{3,2,1,0:T(8,128)S(1)}, f32[3,64,32,128]{3,2,1,0:T(8,128)}, u32[]{:S(2)}) copy-start(f32[3,64,32,128]{3,2,1,0:T(8,128)} %u.3) | copy-start | bytes 9437188
  12.7 22.3 %all-to-all-start = ((f32[16,4,1152]{2,1,0:T(4,128)}), f32[16,4,1152]{2,1,0:T(4,128)S(1)}, u32[]{:S(2)}, u32[]{:S(2)}) async-start(f32[16,4,1152]{2,1,0:T(4,128)} %copy.41), calls=%async_computation | async-start | bytes 589824 | tf_op jit(solution)/shard_map/all_to_all | solution.py:158
  28.2 18.9 %collective-permute-start.5 = (f32[3,32,64]{2,1,0:T(8,128)}, f32[3,32,64]{2,1,0:T(8,128)S(1)}, u32[]{:S(2)}, u32[]{:S(2)}) collective-permute-start(f32[3,32,64]{2,1,0:T(8,128)} %get-tuple-element.14), channel_id=1, source_target_pairs={{4,0},{8,4},{12,8},{5,1},{9,5},{13,9},{6,2},{10,6},{14,10},{7,3},{... | collective-permute-start | bytes 73736 | tf_op jit(solution)/shard_map/ppermute | solution.py:36
  35.0 6.6 %collective-permute-start.12 = (f32[4,1152]{1,0:T(4,128)S(1)}, f32[4,1152]{1,0:T(4,128)S(1)}, u32[]{:S(2)}, u32[]{:S(2)}) collective-permute-start(f32[4,1152]{1,0:T(4,128)S(1)} %reduce_sum.18), channel_id=1, source_target_pairs={{0,4},{4,0},{8,12},{12,8},{1,5},{5,1},{9,13},{13,9},{2,6},{6,2},{1... | collective-permute-start | bytes 55304 | tf_op jit(solution)/shard_map/ppermute | solution.py:167
  37.1 19.1 %collective-permute-start.2 = (f32[3,64,128]{2,1,0:T(8,128)}, f32[3,64,128]{2,1,0:T(8,128)S(1)}, u32[]{:S(2)}, u32[]{:S(2)}) collective-permute-start(f32[3,64,128]{2,1,0:T(8,128)} %bitcast.3), channel_id=1, source_target_pairs={{0,1},{1,2},{2,3},{4,5},{5,6},{6,7},{8,9},{9,10},{10,11},{12,13},{... | collective-permute-start | bytes 294920 | tf_op jit(solution)/shard_map/ppermute | solution.py:36
  40.3 15.9 %collective-permute-start.3 = (f32[3,64,128]{2,1,0:T(8,128)}, f32[3,64,128]{2,1,0:T(8,128)S(1)}, u32[]{:S(2)}, u32[]{:S(2)}) collective-permute-start(f32[3,64,128]{2,1,0:T(8,128)} %bitcast.4), channel_id=1, source_target_pairs={{1,0},{2,1},{3,2},{5,4},{6,5},{7,6},{9,8},{10,9},{11,10},{13,12},{... | collective-permute-start | bytes 294920 | tf_op jit(solution)/shard_map/ppermute | solution.py:36
  41.7 8.7 %collective-permute-start.13 = (f32[4,1152]{1,0:T(4,128)S(1)}, f32[4,1152]{1,0:T(4,128)S(1)}, u32[]{:S(2)}, u32[]{:S(2)}) collective-permute-start(f32[4,1152]{1,0:T(4,128)S(1)} %add.35), channel_id=1, source_target_pairs={{0,8},{4,12},{8,0},{12,4},{1,9},{5,13},{9,1},{13,5},{2,10},{6,14},... | collective-permute-start | bytes 55304 | tf_op jit(solution)/shard_map/ppermute | solution.py:167
  44.8 11.4 %collective-permute-start.1 = (f32[3,32,128]{2,1,0:T(8,128)}, f32[3,32,128]{2,1,0:T(8,128)S(1)}, u32[]{:S(2)}, u32[]{:S(2)}) collective-permute-start(f32[3,32,128]{2,1,0:T(8,128)} %get-tuple-element.8), channel_id=1, source_target_pairs={{16,0},{32,16},{48,32},{64,48},{80,64},{96,80},{112,96},{128,112},... | collective-permute-start | bytes 147464 | tf_op jit(solution)/shard_map/ppermute | solution.py:36
  47.2 9.1 %copy-start.4 = (f32[3,32,64]{2,1,0:T(8,128)}, f32[3,32,64]{2,1,0:T(8,128)S(1)}, u32[]{:S(2)}) copy-start(f32[3,32,64]{2,1,0:T(8,128)S(1)} %collective-permute-done.5.yhi) | copy-start | bytes 73732
  47.2 9.0 %collective-permute-start = (f32[3,32,128]{2,1,0:T(8,128)S(1)}, f32[3,32,128]{2,1,0:T(8,128)S(1)}, u32[]{:S(2)}, u32[]{:S(2)}) collective-permute-start(f32[3,32,128]{2,1,0:T(8,128)S(1)} %get-tuple-element.9), channel_id=1, source_target_pairs={{0,16},{16,32},{32,48},{48,64},{64,80},{80,96},{96,112},{112,128},... | collective-permute-start | bytes 147464 | tf_op jit(solution)/shard_map/ppermute | solution.py:36
  50.4 3.4 %collective-permute-start.4 = (f32[3,32,64]{2,1,0:T(8,128)}, f32[3,32,64]{2,1,0:T(8,128)S(1)}, u32[]{:S(2)}, u32[]{:S(2)}) collective-permute-start(f32[3,32,64]{2,1,0:T(8,128)} %get-tuple-element.15), channel_id=1, source_target_pairs={{0,4},{4,8},{8,12},{1,5},{5,9},{9,13},{2,6},{6,10},{10,14},{3,7},{... | collective-permute-start | bytes 73736 | tf_op jit(solution)/shard_map/ppermute | solution.py:36
  53.8 2.5 %copy-start.7 = (f32[3,32,64]{2,1,0:T(8,128)}, f32[3,32,64]{2,1,0:T(8,128)S(1)}, u32[]{:S(2)}) copy-start(f32[3,32,64]{2,1,0:T(8,128)S(1)} %collective-permute-done.4.ylo) | copy-start | bytes 73732
  53.8 19.4 %collective-permute-start.14 = (f32[4,1152]{1,0:T(4,128)S(1)}, f32[4,1152]{1,0:T(4,128)S(1)}, u32[]{:S(2)}, u32[]{:S(2)}) collective-permute-start(f32[4,1152]{1,0:T(4,128)S(1)} %add.36), channel_id=1, source_target_pairs={{0,1},{1,0},{2,3},{3,2},{4,5},{5,4},{6,7},{7,6},{8,9},{9,8},{10,11... | collective-permute-start | bytes 55304 | tf_op jit(solution)/shard_map/ppermute | solution.py:167
  73.2 5.6 %collective-permute-start.15 = (f32[4,1152]{1,0:T(4,128)S(1)}, f32[4,1152]{1,0:T(4,128)S(1)}, u32[]{:S(2)}, u32[]{:S(2)}) collective-permute-start(f32[4,1152]{1,0:T(4,128)S(1)} %add.37), channel_id=1, source_target_pairs={{0,2},{1,3},{2,0},{3,1},{4,6},{5,7},{6,4},{7,5},{8,10},{9,11},{10,... | collective-permute-start | bytes 55304 | tf_op jit(solution)/shard_map/ppermute | solution.py:167
  80.3 20.1 %all-to-all-start.1 = ((f32[16,4,1152]{2,1,0:T(4,128)}), f32[16,4,1152]{2,1,0:T(4,128)S(1)}, u32[]{:S(2)}, u32[]{:S(2)}) async-start(f32[16,4,1152]{2,1,0:T(4,128)} %broadcast_in_dim.2), calls=%async_computation.1 | async-start | bytes 589824 | tf_op jit(solution)/shard_map/all_to_all | solution.py:171
  86.8 14.0 %collective-permute-start.11 = (f32[32,64]{1,0:T(8,128)S(1)}, f32[32,64]{1,0:T(8,128)S(1)}, u32[]{:S(2)}, u32[]{:S(2)}) collective-permute-start(f32[32,64]{1,0:T(8,128)S(1)} %get-tuple-element.16), channel_id=1, source_target_pairs={{4,0},{8,4},{12,8},{5,1},{9,5},{13,9},{6,2},{10,6},{14,10},{7,3},{... | collective-permute-start | bytes 24584 | tf_op jit(solution)/shard_map/ppermute | solution.py:36
  88.1 21.1 %collective-permute-start.10 = (f32[32,64]{1,0:T(8,128)S(1)}, f32[32,64]{1,0:T(8,128)S(1)}, u32[]{:S(2)}, u32[]{:S(2)}) collective-permute-start(f32[32,64]{1,0:T(8,128)S(1)} %get-tuple-element.17), channel_id=1, source_target_pairs={{0,4},{4,8},{8,12},{1,5},{5,9},{9,13},{2,6},{6,10},{10,14},{3,7},{... | collective-permute-start | bytes 24584 | tf_op jit(solution)/shard_map/ppermute | solution.py:36
  93.3 15.9 %collective-permute-start.7 = (f32[32,128]{1,0:T(8,128)S(1)}, f32[32,128]{1,0:T(8,128)S(1)}, u32[]{:S(2)}, u32[]{:S(2)}) collective-permute-start(f32[32,128]{1,0:T(8,128)S(1)} %get-tuple-element.12), channel_id=1, source_target_pairs={{16,0},{32,16},{48,32},{64,48},{80,64},{96,80},{112,96},{128,112},... | collective-permute-start | bytes 49160 | tf_op jit(solution)/shard_map/ppermute | solution.py:36
  95.6 13.6 %collective-permute-start.6 = (f32[32,128]{1,0:T(8,128)S(1)}, f32[32,128]{1,0:T(8,128)S(1)}, u32[]{:S(2)}, u32[]{:S(2)}) collective-permute-start(f32[32,128]{1,0:T(8,128)S(1)} %get-tuple-element.13), channel_id=1, source_target_pairs={{0,16},{16,32},{32,48},{48,64},{64,80},{80,96},{96,112},{112,128},... | collective-permute-start | bytes 49160 | tf_op jit(solution)/shard_map/ppermute | solution.py:36
  99.1 10.2 %collective-permute-start.9 = (f32[64,128]{1,0:T(8,128)S(1)}, f32[64,128]{1,0:T(8,128)S(1)}, u32[]{:S(2)}, u32[]{:S(2)}) collective-permute-start(f32[64,128]{1,0:T(8,128)S(1)} %get-tuple-element.10), channel_id=1, source_target_pairs={{1,0},{2,1},{3,2},{5,4},{6,5},{7,6},{9,8},{10,9},{11,10},{13,12},{... | collective-permute-start | bytes 98312 | tf_op jit(solution)/shard_map/ppermute | solution.py:36
  100.5 8.0 %copy-start.1 = (f32[64,1152]{1,0:T(8,128)}, f32[64,1152]{1,0:T(8,128)S(1)}, u32[]{:S(2)}) copy-start(f32[64,1152]{1,0:T(8,128)S(1)} %reshape.70) | copy-start | bytes 884740
  100.8 7.7 %copy-start.10 = (f32[32,64]{1,0:T(8,128)}, f32[32,64]{1,0:T(8,128)S(1)}, u32[]{:S(2)}) copy-start(f32[32,64]{1,0:T(8,128)S(1)} %collective-permute-done.11.nyhi) | copy-start | bytes 24580
  100.8 8.5 %collective-permute-start.8 = (f32[64,128]{1,0:T(8,128)S(1)}, f32[64,128]{1,0:T(8,128)S(1)}, u32[]{:S(2)}, u32[]{:S(2)}) collective-permute-start(f32[64,128]{1,0:T(8,128)S(1)} %get-tuple-element.11), channel_id=1, source_target_pairs={{0,1},{1,2},{2,3},{4,5},{5,6},{6,7},{8,9},{9,10},{10,11},{12,13},{... | collective-permute-start | bytes 98312 | tf_op jit(solution)/shard_map/ppermute | solution.py:36
  (9 other events, 5.6 us)

commit v8 on v7

--- a/solution.py
+++ b/solution.py
@@ -72,7 +72,7 @@
         nu[x] = 0.05 + 1.0 * jnp.sqrt(2.0 * total + 1e-06)
         return carry
 
-    lax.fori_loop(0, u.shape[1], plane, 0)
+    lax.fori_loop(0, u.shape[1], plane, 0, unroll=2)
 
 
 def advance_kernel(planes, u, xlo, xhi, zlo, zhi, ylo, yhi, nu, nxlo, nxhi, nzlo, nzhi, nylo, nyhi, sent, out):
@@ -100,7 +100,7 @@
             out[c, x] = center + 0.25 * (spread - advect) + impulse
         return carry
 
-    lax.fori_loop(0, u.shape[1], plane, 0)
+    lax.fori_loop(0, u.shape[1], plane, 0, unroll=2)
 
 
 def vmem_call(kernel, out_shape, count, smem=0):

time: 129 us -> 125 us (0.969)
  Pallas kernels: 33.6 us -> 29.5 us
    pallas_call x1, Pallas kernels: 15.6 us -> 13.3 us  [stencil(): vmem_call(viscosity_kernel, jax.ShapeDtypeStruct(velocity.shape[1:], jnp....]
    pallas_call x1, Pallas kernels: 18 us -> 16.2 us  [stencil(): vmem_call(advance_kernel, jax.ShapeDtypeStruct(velocity.shape, jnp.float3...]
  transfers between devices with their start and end apart: 18 -> 18, of which waited for: 2 -> 2; matrix products, arithmetic and copies ran while one was open for 14% -> 14% of each run, Pallas kernels for 12% -> 11%
where the time goes in v8:
time: 125 us; the launch traced here: 124 us
  starting transfers between devices  53.5 us (43%)
  Pallas kernels  29.5 us (24%)
  matrix products  16.8 us (13%)
  local copies, waits for them, and re-layouts  11.2 us (9%)
  waiting for transfers between devices  6.98 us (6%)
  between operations  4.97 us (4%)
    ppermute x6, starting transfers between devices, faces(): lax.ppermute(last, axis, forward)  20.2 us
    pallas_call x1, Pallas kernels, stencil(): vmem_call(advance_kernel, jax.ShapeDtypeStruct(velocity.shape, jnp.float3...  16.2 us
    pallas_call x1, Pallas kernels, stencil(): vmem_call(viscosity_kernel, jax.ShapeDtypeStruct(velocity.shape[1:], jnp....  13.3 us
    all_to_all x1, starting transfers between devices, body(): lax.all_to_all(partial_sample.reshape(rows, per_row, -1), 'gx', split_axi...  10 us
    ppermute x6, starting transfers between devices, faces(): lax.ppermute(first, axis, backward)  9.76 us
    ppermute x4, starting transfers between devices, body(): owned = owned + lax.ppermute(owned, axis, pairs)  8.87 us
    dot_general x2, matrix products, faces(): jnp.einsum(letters + ',ky->k' + letters[:-3] + 'zx', block, ends, precisi...  7.75 us
    all_to_all x1, waiting for transfers between devices, body(): lax.all_to_all(partial_sample.reshape(rows, per_row, -1), 'gx', split_axi...  5.45 us
  transfers between devices with their start and end apart: 18, of which 2 were waited for; matrix products, arithmetic and copies ran while one was open for 14% of the time, Pallas kernels for 11%

profile of v8, /device:TPU:1, one launch (start us, length us, event | category | flops | bytes accessed | tf_op | source)
XLA Modules:
  0.0 123.8 jit_solution(16617137367329232585)
XLA Ops:
  0.6 1.3 %fusion.25 = (s32[1,1,1,1]{3,2,1,0:T(1,128)}, s32[1,1,1,1]{3,2,1,0:T(1,128)}) fusion(s32[1,1,1,2]{3,2,1,0:T(1,128)} %param.9), kind=kLoop, calls=%fused_computation.44 | loop fusion | bytes 16 | tf_op jit(solution)/shard_map/slice | solution.py:142
  6.7 4.7 %fusion.2 = f32[2,3,384]{2,1,0:T(4,128)S(1)} fusion(bf16[1,1,1,2,384,4096]{5,4,3,2,1,0:T(8,128)(2,1)} %param.10, bf16[1,3,4096]{2,1,0:T(4,128)(2,1)S(1)} %stack.10, bf16[1,3,4096]{2,1,0:T(4,128)(2,1)S(1)} %stack.9), kind=kOutput, calls=%fused_computation.2 | convolution fusion | flops 18972672 | bytes 6349824 | tf_op jit(solution)/shard_map/spq,scq->scp/dot_general | solution.py:144
  12.7 10.0 %all-to-all-start = ((f32[16,4,1152]{2,1,0:T(4,128)}), f32[16,4,1152]{2,1,0:T(4,128)S(1)}, u32[]{:S(2)}, u32[]{:S(2)}) async-start(f32[16,4,1152]{2,1,0:T(4,128)} %copy.41), calls=%async_computation | async-start | bytes 589824 | tf_op jit(solution)/shard_map/all_to_all | solution.py:158
  22.8 4.9 %fusion.4 = f32[2,3,64,32]{2,0,3,1:T(2,128)S(1)} fusion(f32[3,64,32,128]{3,2,1,0:T(8,128)S(1)} %copy-done, s32[2]{0:T(128)S(1)} %iota_multiply_fusion), kind=kOutput, calls=%fused_computation.4 | convolution fusion | flops 18874624 | bytes 3194888 | tf_op jit(solution)/shard_map/cxzy,ky->kczx/dot_general | solution.py:22
  29.6 5.4 %all-to-all-done = f32[16,4,1152]{2,1,0:T(4,128)S(1)} async-done(((f32[16,4,1152]{2,1,0:T(4,128)}), f32[16,4,1152]{2,1,0:T(4,128)S(1)}, u32[]{:S(2)}, u32[]{:S(2)}) %all-to-all-start) | async-done | bytes 294944 | tf_op jit(solution)/shard_map/all_to_all | solution.py:158
  37.1 3.2 %collective-permute-start.2 = (f32[3,64,128]{2,1,0:T(8,128)}, f32[3,64,128]{2,1,0:T(8,128)S(1)}, u32[]{:S(2)}, u32[]{:S(2)}) collective-permute-start(f32[3,64,128]{2,1,0:T(8,128)} %bitcast.3), channel_id=1, source_target_pairs={{0,1},{1,2},{2,3},{4,5},{5,6},{6,7},{8,9},{9,10},{10,11},{12,13},{... | collective-permute-start | bytes 294920 | tf_op jit(solution)/shard_map/ppermute | solution.py:36
  41.7 2.5 %collective-permute-start.13 = (f32[4,1152]{1,0:T(4,128)S(1)}, f32[4,1152]{1,0:T(4,128)S(1)}, u32[]{:S(2)}, u32[]{:S(2)}) collective-permute-start(f32[4,1152]{1,0:T(4,128)S(1)} %add.35), channel_id=1, source_target_pairs={{0,8},{4,12},{8,0},{12,4},{1,9},{5,13},{9,1},{13,5},{2,10},{6,14},... | collective-permute-start | bytes 55304 | tf_op jit(solution)/shard_map/ppermute | solution.py:167
  44.8 2.3 %collective-permute-start.1 = (f32[3,32,128]{2,1,0:T(8,128)}, f32[3,32,128]{2,1,0:T(8,128)S(1)}, u32[]{:S(2)}, u32[]{:S(2)}) collective-permute-start(f32[3,32,128]{2,1,0:T(8,128)} %get-tuple-element.8), channel_id=1, source_target_pairs={{16,0},{32,16},{48,32},{64,48},{80,64},{96,80},{112,96},{128,112},... | collective-permute-start | bytes 147464 | tf_op jit(solution)/shard_map/ppermute | solution.py:36
  47.2 3.2 %collective-permute-start = (f32[3,32,128]{2,1,0:T(8,128)S(1)}, f32[3,32,128]{2,1,0:T(8,128)S(1)}, u32[]{:S(2)}, u32[]{:S(2)}) collective-permute-start(f32[3,32,128]{2,1,0:T(8,128)S(1)} %get-tuple-element.9), channel_id=1, source_target_pairs={{0,16},{16,32},{32,48},{48,64},{64,80},{80,96},{96,112},{112,128},... | collective-permute-start | bytes 147464 | tf_op jit(solution)/shard_map/ppermute | solution.py:36
  50.4 1.8 %collective-permute-start.4 = (f32[3,32,64]{2,1,0:T(8,128)}, f32[3,32,64]{2,1,0:T(8,128)S(1)}, u32[]{:S(2)}, u32[]{:S(2)}) collective-permute-start(f32[3,32,64]{2,1,0:T(8,128)} %get-tuple-element.15), channel_id=1, source_target_pairs={{0,4},{4,8},{8,12},{1,5},{5,9},{9,13},{2,6},{6,10},{10,14},{3,7},{... | collective-permute-start | bytes 73736 | tf_op jit(solution)/shard_map/ppermute | solution.py:36
  52.3 1.5 %collective-permute-done.4.ylo = f32[3,32,64]{2,1,0:T(8,128)S(1)} collective-permute-done((f32[3,32,64]{2,1,0:T(8,128)}, f32[3,32,64]{2,1,0:T(8,128)S(1)}, u32[]{:S(2)}, u32[]{:S(2)}) %collective-permute-start.4) | collective-permute-done | bytes 24608 | tf_op jit(solution)/shard_map/ppermute | solution.py:36
  53.8 2.4 %collective-permute-start.14 = (f32[4,1152]{1,0:T(4,128)S(1)}, f32[4,1152]{1,0:T(4,128)S(1)}, u32[]{:S(2)}, u32[]{:S(2)}) collective-permute-start(f32[4,1152]{1,0:T(4,128)S(1)} %add.36), channel_id=1, source_target_pairs={{0,1},{1,0},{2,3},{3,2},{4,5},{5,4},{6,7},{7,6},{8,9},{9,8},{10,11... | collective-permute-start | bytes 55304 | tf_op jit(solution)/shard_map/ppermute | solution.py:167
  57.5 13.3 %shard_map.86.nu = f32[64,32,128]{2,1,0:T(8,128)} custom-call(f32[3,64,32,128]{3,2,1,0:T(8,128)} %u.3, f32[3,32,128]{2,1,0:T(8,128)} %copy-done.6, f32[3,32,128]{2,1,0:T(8,128)} %copy-done.5, f32[3,64,128]{2,1,0:T(8,128)} %copy-done.2, f32[3,64,128]{2,1,0:T(8,128)} %copy-done.3, f32[3,32,64]{2,1,0:T(8,128)} %copy-done.7, f32[3,32,64]{2,1,0:T(8,128)} %copy-done.4), custom_call_target="tpu_custom_call" | custom-call | tf_op jit(solution)/shard_map/pallas_call | solution.py:120
  70.8 2.7 %collective-permute-start.15 = (f32[4,1152]{1,0:T(4,128)S(1)}, f32[4,1152]{1,0:T(4,128)S(1)}, u32[]{:S(2)}, u32[]{:S(2)}) collective-permute-start(f32[4,1152]{1,0:T(4,128)S(1)} %add.37), channel_id=1, source_target_pairs={{0,2},{1,3},{2,0},{3,1},{4,6},{5,7},{6,4},{7,5},{8,10},{9,11},{10,... | collective-permute-start | bytes 55304 | tf_op jit(solution)/shard_map/ppermute | solution.py:167
  73.5 2.9 %fusion.14 = f32[2,64,32]{1,0,2:T(2,128)S(1)} fusion(s32[2]{0:T(128)S(1)} %iota_multiply_fusion, f32[64,32,128]{2,1,0:T(8,128)} %shard_map.86.nu), kind=kOutput, calls=%fused_computation.31 | convolution fusion | flops 6291712 | bytes 1064968 | tf_op jit(solution)/shard_map/xzy,ky->kzx/dot_general | solution.py:22
  77.9 4.6 %all-to-all-start.1 = ((f32[16,4,1152]{2,1,0:T(4,128)}), f32[16,4,1152]{2,1,0:T(4,128)S(1)}, u32[]{:S(2)}, u32[]{:S(2)}) async-start(f32[16,4,1152]{2,1,0:T(4,128)} %broadcast_in_dim.2), calls=%async_computation.1 | async-start | bytes 589824 | tf_op jit(solution)/shard_map/all_to_all | solution.py:171
  82.6 1.8 %copy.37 = f32[64,32,128]{2,0,1:T(8,128)S(1)} copy(f32[64,32,128]{2,1,0:T(8,128)} %shard_map.86.nu) | data formatting | bytes 2097152 | tf_op jit(solution)/shard_map/pallas_call | solution.py:120
  85.7 4.5 %collective-permute-start.10 = (f32[32,64]{1,0:T(8,128)S(1)}, f32[32,64]{1,0:T(8,128)S(1)}, u32[]{:S(2)}, u32[]{:S(2)}) collective-permute-start(f32[32,64]{1,0:T(8,128)S(1)} %get-tuple-element.17), channel_id=1, source_target_pairs={{0,4},{4,8},{8,12},{1,5},{5,9},{9,13},{2,6},{6,10},{10,14},{3,7},{... | collective-permute-start | bytes 24584 | tf_op jit(solution)/shard_map/ppermute | solution.py:36
  90.9 2.3 %collective-permute-start.7 = (f32[32,128]{1,0:T(8,128)S(1)}, f32[32,128]{1,0:T(8,128)S(1)}, u32[]{:S(2)}, u32[]{:S(2)}) collective-permute-start(f32[32,128]{1,0:T(8,128)S(1)} %get-tuple-element.12), channel_id=1, source_target_pairs={{16,0},{32,16},{48,32},{64,48},{80,64},{96,80},{112,96},{128,112},... | collective-permute-start | bytes 49160 | tf_op jit(solution)/shard_map/ppermute | solution.py:36
  93.2 3.4 %collective-permute-start.6 = (f32[32,128]{1,0:T(8,128)S(1)}, f32[32,128]{1,0:T(8,128)S(1)}, u32[]{:S(2)}, u32[]{:S(2)}) collective-permute-start(f32[32,128]{1,0:T(8,128)S(1)} %get-tuple-element.13), channel_id=1, source_target_pairs={{0,16},{16,32},{32,48},{48,64},{64,80},{80,96},{96,112},{112,128},... | collective-permute-start | bytes 49160 | tf_op jit(solution)/shard_map/ppermute | solution.py:36
  96.7 1.3 %collective-permute-start.9 = (f32[64,128]{1,0:T(8,128)S(1)}, f32[64,128]{1,0:T(8,128)S(1)}, u32[]{:S(2)}, u32[]{:S(2)}) collective-permute-start(f32[64,128]{1,0:T(8,128)S(1)} %get-tuple-element.10), channel_id=1, source_target_pairs={{1,0},{2,1},{3,2},{5,4},{6,5},{7,6},{9,8},{10,9},{11,10},{13,12},{... | collective-permute-start | bytes 98312 | tf_op jit(solution)/shard_map/ppermute | solution.py:36
  98.4 4.0 %collective-permute-start.8 = (f32[64,128]{1,0:T(8,128)S(1)}, f32[64,128]{1,0:T(8,128)S(1)}, u32[]{:S(2)}, u32[]{:S(2)}) collective-permute-start(f32[64,128]{1,0:T(8,128)S(1)} %get-tuple-element.11), channel_id=1, source_target_pairs={{0,1},{1,2},{2,3},{4,5},{5,6},{6,7},{8,9},{9,10},{10,11},{12,13},{... | collective-permute-start | bytes 98312 | tf_op jit(solution)/shard_map/ppermute | solution.py:36
  102.4 3.7 %fusion = f32[2,3,4096]{2,1,0:T(4,128)S(1)} fusion(bf16[2,3,384]{2,1,0:T(4,128)(2,1)S(1)} %reshape.71, bf16[1,1,1,2,384,4096]{5,4,3,2,1,0:T(8,128)(2,1)} %param.10), kind=kOutput, calls=%fused_computation | convolution fusion | flops 18874368 | bytes 6394368 | tf_op jit(solution)/shard_map/axz,ahx->ahz/dot_general | solution.py:176
  107.5 16.2 %shard_map.87 = f32[3,64,32,128]{3,2,1,0:T(8,128)} custom-call(s32[2]{0:T(128)} %bitcast.66, f32[3,64,32,128]{3,2,1,0:T(8,128)} %u.3, f32[3,32,128]{2,1,0:T(8,128)} %copy-done.6, f32[3,32,128]{2,1,0:T(8,128)} %copy-done.5, f32[3,64,128]{2,1,0:T(8,128)} %copy-done.2, f32[3,64,128]{2,1,0:T(8,128)} %copy-done.3, f32[3,32,64]{2,1,0:T(8,128)} %copy-done.7, ...), custom_call_target="tpu_custom_call" | custom-call | tf_op jit(solution)/shard_map/pallas_call | solution.py:124
  (80 shorter events, 14.7 us)
Async XLA Ops:
  6.7 4.7 %copy-start.14 = (s32[1,1,1,2]{3,2,1,0:T(1,128)S(1)}, s32[1,1,1,2]{3,2,1,0:T(1,128)}, u32[]{:S(2)}) copy-start(s32[1,1,1,2]{3,2,1,0:T(1,128)} %param.8) | copy-start | bytes 28
  6.7 16.0 %copy-start = (f32[3,64,32,128]{3,2,1,0:T(8,128)S(1)}, f32[3,64,32,128]{3,2,1,0:T(8,128)}, u32[]{:S(2)}) copy-start(f32[3,64,32,128]{3,2,1,0:T(8,128)} %u.3) | copy-start | bytes 9437188
  12.7 22.3 %all-to-all-start = ((f32[16,4,1152]{2,1,0:T(4,128)}), f32[16,4,1152]{2,1,0:T(4,128)S(1)}, u32[]{:S(2)}, u32[]{:S(2)}) async-start(f32[16,4,1152]{2,1,0:T(4,128)} %copy.41), calls=%async_computation | async-start | bytes 589824 | tf_op jit(solution)/shard_map/all_to_all | solution.py:158
  28.3 18.9 %collective-permute-start.5 = (f32[3,32,64]{2,1,0:T(8,128)}, f32[3,32,64]{2,1,0:T(8,128)S(1)}, u32[]{:S(2)}, u32[]{:S(2)}) collective-permute-start(f32[3,32,64]{2,1,0:T(8,128)} %get-tuple-element.14), channel_id=1, source_target_pairs={{4,0},{8,4},{12,8},{5,1},{9,5},{13,9},{6,2},{10,6},{14,10},{7,3},{... | collective-permute-start | bytes 73736 | tf_op jit(solution)/shard_map/ppermute | solution.py:36
  35.1 6.5 %collective-permute-start.12 = (f32[4,1152]{1,0:T(4,128)S(1)}, f32[4,1152]{1,0:T(4,128)S(1)}, u32[]{:S(2)}, u32[]{:S(2)}) collective-permute-start(f32[4,1152]{1,0:T(4,128)S(1)} %reduce_sum.18), channel_id=1, source_target_pairs={{0,4},{4,0},{8,12},{12,8},{1,5},{5,1},{9,13},{13,9},{2,6},{6,2},{1... | collective-permute-start | bytes 55304 | tf_op jit(solution)/shard_map/ppermute | solution.py:167
  37.1 19.1 %collective-permute-start.2 = (f32[3,64,128]{2,1,0:T(8,128)}, f32[3,64,128]{2,1,0:T(8,128)S(1)}, u32[]{:S(2)}, u32[]{:S(2)}) collective-permute-start(f32[3,64,128]{2,1,0:T(8,128)} %bitcast.3), channel_id=1, source_target_pairs={{0,1},{1,2},{2,3},{4,5},{5,6},{6,7},{8,9},{9,10},{10,11},{12,13},{... | collective-permute-start | bytes 294920 | tf_op jit(solution)/shard_map/ppermute | solution.py:36
  40.3 15.9 %collective-permute-start.3 = (f32[3,64,128]{2,1,0:T(8,128)}, f32[3,64,128]{2,1,0:T(8,128)S(1)}, u32[]{:S(2)}, u32[]{:S(2)}) collective-permute-start(f32[3,64,128]{2,1,0:T(8,128)} %bitcast.4), channel_id=1, source_target_pairs={{1,0},{2,1},{3,2},{5,4},{6,5},{7,6},{9,8},{10,9},{11,10},{13,12},{... | collective-permute-start | bytes 294920 | tf_op jit(solution)/shard_map/ppermute | solution.py:36
  41.7 8.7 %collective-permute-start.13 = (f32[4,1152]{1,0:T(4,128)S(1)}, f32[4,1152]{1,0:T(4,128)S(1)}, u32[]{:S(2)}, u32[]{:S(2)}) collective-permute-start(f32[4,1152]{1,0:T(4,128)S(1)} %add.35), channel_id=1, source_target_pairs={{0,8},{4,12},{8,0},{12,4},{1,9},{5,13},{9,1},{13,5},{2,10},{6,14},... | collective-permute-start | bytes 55304 | tf_op jit(solution)/shard_map/ppermute | solution.py:167
  44.8 11.4 %collective-permute-start.1 = (f32[3,32,128]{2,1,0:T(8,128)}, f32[3,32,128]{2,1,0:T(8,128)S(1)}, u32[]{:S(2)}, u32[]{:S(2)}) collective-permute-start(f32[3,32,128]{2,1,0:T(8,128)} %get-tuple-element.8), channel_id=1, source_target_pairs={{16,0},{32,16},{48,32},{64,48},{80,64},{96,80},{112,96},{128,112},... | collective-permute-start | bytes 147464 | tf_op jit(solution)/shard_map/ppermute | solution.py:36
  47.2 9.1 %copy-start.4 = (f32[3,32,64]{2,1,0:T(8,128)}, f32[3,32,64]{2,1,0:T(8,128)S(1)}, u32[]{:S(2)}) copy-start(f32[3,32,64]{2,1,0:T(8,128)S(1)} %collective-permute-done.5.yhi) | copy-start | bytes 73732
  47.2 9.0 %collective-permute-start = (f32[3,32,128]{2,1,0:T(8,128)S(1)}, f32[3,32,128]{2,1,0:T(8,128)S(1)}, u32[]{:S(2)}, u32[]{:S(2)}) collective-permute-start(f32[3,32,128]{2,1,0:T(8,128)S(1)} %get-tuple-element.9), channel_id=1, source_target_pairs={{0,16},{16,32},{32,48},{48,64},{64,80},{80,96},{96,112},{112,128},... | collective-permute-start | bytes 147464 | tf_op jit(solution)/shard_map/ppermute | solution.py:36
  50.4 3.4 %collective-permute-start.4 = (f32[3,32,64]{2,1,0:T(8,128)}, f32[3,32,64]{2,1,0:T(8,128)S(1)}, u32[]{:S(2)}, u32[]{:S(2)}) collective-permute-start(f32[3,32,64]{2,1,0:T(8,128)} %get-tuple-element.15), channel_id=1, source_target_pairs={{0,4},{4,8},{8,12},{1,5},{5,9},{9,13},{2,6},{6,10},{10,14},{3,7},{... | collective-permute-start | bytes 73736 | tf_op jit(solution)/shard_map/ppermute | solution.py:36
  53.8 2.5 %copy-start.7 = (f32[3,32,64]{2,1,0:T(8,128)}, f32[3,32,64]{2,1,0:T(8,128)S(1)}, u32[]{:S(2)}) copy-start(f32[3,32,64]{2,1,0:T(8,128)S(1)} %collective-permute-done.4.ylo) | copy-start | bytes 73732
  53.8 17.0 %collective-permute-start.14 = (f32[4,1152]{1,0:T(4,128)S(1)}, f32[4,1152]{1,0:T(4,128)S(1)}, u32[]{:S(2)}, u32[]{:S(2)}) collective-permute-start(f32[4,1152]{1,0:T(4,128)S(1)} %add.36), channel_id=1, source_target_pairs={{0,1},{1,0},{2,3},{3,2},{4,5},{5,4},{6,7},{7,6},{8,9},{9,8},{10,11... | collective-permute-start | bytes 55304 | tf_op jit(solution)/shard_map/ppermute | solution.py:167
  70.8 5.6 %collective-permute-start.15 = (f32[4,1152]{1,0:T(4,128)S(1)}, f32[4,1152]{1,0:T(4,128)S(1)}, u32[]{:S(2)}, u32[]{:S(2)}) collective-permute-start(f32[4,1152]{1,0:T(4,128)S(1)} %add.37), channel_id=1, source_target_pairs={{0,2},{1,3},{2,0},{3,1},{4,6},{5,7},{6,4},{7,5},{8,10},{9,11},{10,... | collective-permute-start | bytes 55304 | tf_op jit(solution)/shard_map/ppermute | solution.py:167
  77.9 20.1 %all-to-all-start.1 = ((f32[16,4,1152]{2,1,0:T(4,128)}), f32[16,4,1152]{2,1,0:T(4,128)S(1)}, u32[]{:S(2)}, u32[]{:S(2)}) async-start(f32[16,4,1152]{2,1,0:T(4,128)} %broadcast_in_dim.2), calls=%async_computation.1 | async-start | bytes 589824 | tf_op jit(solution)/shard_map/all_to_all | solution.py:171
  84.4 14.0 %collective-permute-start.11 = (f32[32,64]{1,0:T(8,128)S(1)}, f32[32,64]{1,0:T(8,128)S(1)}, u32[]{:S(2)}, u32[]{:S(2)}) collective-permute-start(f32[32,64]{1,0:T(8,128)S(1)} %get-tuple-element.16), channel_id=1, source_target_pairs={{4,0},{8,4},{12,8},{5,1},{9,5},{13,9},{6,2},{10,6},{14,10},{7,3},{... | collective-permute-start | bytes 24584 | tf_op jit(solution)/shard_map/ppermute | solution.py:36
  85.7 21.1 %collective-permute-start.10 = (f32[32,64]{1,0:T(8,128)S(1)}, f32[32,64]{1,0:T(8,128)S(1)}, u32[]{:S(2)}, u32[]{:S(2)}) collective-permute-start(f32[32,64]{1,0:T(8,128)S(1)} %get-tuple-element.17), channel_id=1, source_target_pairs={{0,4},{4,8},{8,12},{1,5},{5,9},{9,13},{2,6},{6,10},{10,14},{3,7},{... | collective-permute-start | bytes 24584 | tf_op jit(solution)/shard_map/ppermute | solution.py:36
  90.9 15.9 %collective-permute-start.7 = (f32[32,128]{1,0:T(8,128)S(1)}, f32[32,128]{1,0:T(8,128)S(1)}, u32[]{:S(2)}, u32[]{:S(2)}) collective-permute-start(f32[32,128]{1,0:T(8,128)S(1)} %get-tuple-element.12), channel_id=1, source_target_pairs={{16,0},{32,16},{48,32},{64,48},{80,64},{96,80},{112,96},{128,112},... | collective-permute-start | bytes 49160 | tf_op jit(solution)/shard_map/ppermute | solution.py:36
  93.2 13.6 %collective-permute-start.6 = (f32[32,128]{1,0:T(8,128)S(1)}, f32[32,128]{1,0:T(8,128)S(1)}, u32[]{:S(2)}, u32[]{:S(2)}) collective-permute-start(f32[32,128]{1,0:T(8,128)S(1)} %get-tuple-element.13), channel_id=1, source_target_pairs={{0,16},{16,32},{32,48},{48,64},{64,80},{80,96},{96,112},{112,128},... | collective-permute-start | bytes 49160 | tf_op jit(solution)/shard_map/ppermute | solution.py:36
  96.7 10.2 %collective-permute-start.9 = (f32[64,128]{1,0:T(8,128)S(1)}, f32[64,128]{1,0:T(8,128)S(1)}, u32[]{:S(2)}, u32[]{:S(2)}) collective-permute-start(f32[64,128]{1,0:T(8,128)S(1)} %get-tuple-element.10), channel_id=1, source_target_pairs={{1,0},{2,1},{3,2},{5,4},{6,5},{7,6},{9,8},{10,9},{11,10},{13,12},{... | collective-permute-start | bytes 98312 | tf_op jit(solution)/shard_map/ppermute | solution.py:36
  98.1 8.0 %copy-start.1 = (f32[64,1152]{1,0:T(8,128)}, f32[64,1152]{1,0:T(8,128)S(1)}, u32[]{:S(2)}) copy-start(f32[64,1152]{1,0:T(8,128)S(1)} %reshape.70) | copy-start | bytes 884740
  98.4 7.7 %copy-start.10 = (f32[32,64]{1,0:T(8,128)}, f32[32,64]{1,0:T(8,128)S(1)}, u32[]{:S(2)}) copy-start(f32[32,64]{1,0:T(8,128)S(1)} %collective-permute-done.11.nyhi) | copy-start | bytes 24580
  98.4 8.5 %collective-permute-start.8 = (f32[64,128]{1,0:T(8,128)S(1)}, f32[64,128]{1,0:T(8,128)S(1)}, u32[]{:S(2)}, u32[]{:S(2)}) collective-permute-start(f32[64,128]{1,0:T(8,128)S(1)} %get-tuple-element.11), channel_id=1, source_target_pairs={{0,1},{1,2},{2,3},{4,5},{5,6},{6,7},{8,9},{9,10},{10,11},{12,13},{... | collective-permute-start | bytes 98312 | tf_op jit(solution)/shard_map/ppermute | solution.py:36
  (9 other events, 5.6 us)

commit v9 on v8

--- a/solution.py
+++ b/solution.py
@@ -72,7 +72,7 @@
         nu[x] = 0.05 + 1.0 * jnp.sqrt(2.0 * total + 1e-06)
         return carry
 
-    lax.fori_loop(0, u.shape[1], plane, 0, unroll=2)
+    lax.fori_loop(0, u.shape[1], plane, 0, unroll=4)
 
 
 def advance_kernel(planes, u, xlo, xhi, zlo, zhi, ylo, yhi, nu, nxlo, nxhi, nzlo, nzhi, nylo, nyhi, sent, out):
@@ -100,7 +100,7 @@
             out[c, x] = center + 0.25 * (spread - advect) + impulse
         return carry
 
-    lax.fori_loop(0, u.shape[1], plane, 0, unroll=2)
+    lax.fori_loop(0, u.shape[1], plane, 0, unroll=4)
 
 
 def vmem_call(kernel, out_shape, count, smem=0):

time: 125 us -> 123 us (0.984)
  Pallas kernels: 29.5 us -> 27.4 us
  transfers between devices with their start and end apart: 18 -> 18, of which waited for: 2 -> 2; matrix products, arithmetic and copies ran while one was open for 14% -> 14% of each run, Pallas kernels for 11% -> 10%
where the time goes in v9:
time: 123 us; the launch traced here: 122 us
  starting transfers between devices  53.5 us (43%)
  Pallas kernels  27.4 us (22%)
  matrix products  16.8 us (14%)
  local copies, waits for them, and re-layouts  11.2 us (9%)
  waiting for transfers between devices  6.98 us (6%)
  between operations  4.97 us (4%)
    ppermute x6, starting transfers between devices, faces(): lax.ppermute(last, axis, forward)  20.2 us
    pallas_call x1, Pallas kernels, stencil(): vmem_call(advance_kernel, jax.ShapeDtypeStruct(velocity.shape, jnp.float3...  15.4 us
    pallas_call x1, Pallas kernels, stencil(): vmem_call(viscosity_kernel, jax.ShapeDtypeStruct(velocity.shape[1:], jnp....  12 us
    all_to_all x1, starting transfers between devices, body(): lax.all_to_all(partial_sample.reshape(rows, per_row, -1), 'gx', split_axi...  9.97 us
    ppermute x6, starting transfers between devices, faces(): lax.ppermute(first, axis, backward)  9.79 us
    ppermute x4, starting transfers between devices, body(): owned = owned + lax.ppermute(owned, axis, pairs)  8.93 us
    dot_general x2, matrix products, faces(): jnp.einsum(letters + ',ky->k' + letters[:-3] + 'zx', block, ends, precisi...  7.75 us
    all_to_all x1, waiting for transfers between devices, body(): lax.all_to_all(partial_sample.reshape(rows, per_row, -1), 'gx', split_axi...  5.45 us
  transfers between devices with their start and end apart: 18, of which 2 were waited for; matrix products, arithmetic and copies ran while one was open for 14% of the time, Pallas kernels for 10%

profile of v9, /device:TPU:1, one launch (start us, length us, event | category | flops | bytes accessed | tf_op | source)
XLA Modules:
  0.0 121.7 jit_solution(4611818990936494210)
XLA Ops:
  0.6 1.3 %fusion.25 = (s32[1,1,1,1]{3,2,1,0:T(1,128)}, s32[1,1,1,1]{3,2,1,0:T(1,128)}) fusion(s32[1,1,1,2]{3,2,1,0:T(1,128)} %param.9), kind=kLoop, calls=%fused_computation.44 | loop fusion | bytes 16 | tf_op jit(solution)/shard_map/slice | solution.py:142
  6.7 4.7 %fusion.2 = f32[2,3,384]{2,1,0:T(4,128)S(1)} fusion(bf16[1,1,1,2,384,4096]{5,4,3,2,1,0:T(8,128)(2,1)} %param.10, bf16[1,3,4096]{2,1,0:T(4,128)(2,1)S(1)} %stack.10, bf16[1,3,4096]{2,1,0:T(4,128)(2,1)S(1)} %stack.9), kind=kOutput, calls=%fused_computation.2 | convolution fusion | flops 18972672 | bytes 6349824 | tf_op jit(solution)/shard_map/spq,scq->scp/dot_general | solution.py:144
  12.7 10.0 %all-to-all-start = ((f32[16,4,1152]{2,1,0:T(4,128)}), f32[16,4,1152]{2,1,0:T(4,128)S(1)}, u32[]{:S(2)}, u32[]{:S(2)}) async-start(f32[16,4,1152]{2,1,0:T(4,128)} %copy.41), calls=%async_computation | async-start | bytes 589824 | tf_op jit(solution)/shard_map/all_to_all | solution.py:158
  22.7 4.9 %fusion.4 = f32[2,3,64,32]{2,0,3,1:T(2,128)S(1)} fusion(f32[3,64,32,128]{3,2,1,0:T(8,128)S(1)} %copy-done, s32[2]{0:T(128)S(1)} %iota_multiply_fusion), kind=kOutput, calls=%fused_computation.4 | convolution fusion | flops 18874624 | bytes 3194888 | tf_op jit(solution)/shard_map/cxzy,ky->kczx/dot_general | solution.py:22
  29.5 5.4 %all-to-all-done = f32[16,4,1152]{2,1,0:T(4,128)S(1)} async-done(((f32[16,4,1152]{2,1,0:T(4,128)}), f32[16,4,1152]{2,1,0:T(4,128)S(1)}, u32[]{:S(2)}, u32[]{:S(2)}) %all-to-all-start) | async-done | bytes 294944 | tf_op jit(solution)/shard_map/all_to_all | solution.py:158
  37.1 3.2 %collective-permute-start.2 = (f32[3,64,128]{2,1,0:T(8,128)}, f32[3,64,128]{2,1,0:T(8,128)S(1)}, u32[]{:S(2)}, u32[]{:S(2)}) collective-permute-start(f32[3,64,128]{2,1,0:T(8,128)} %bitcast.3), channel_id=1, source_target_pairs={{0,1},{1,2},{2,3},{4,5},{5,6},{6,7},{8,9},{9,10},{10,11},{12,13},{... | collective-permute-start | bytes 294920 | tf_op jit(solution)/shard_map/ppermute | solution.py:36
  40.3 1.3 %collective-permute-start.3 = (f32[3,64,128]{2,1,0:T(8,128)}, f32[3,64,128]{2,1,0:T(8,128)S(1)}, u32[]{:S(2)}, u32[]{:S(2)}) collective-permute-start(f32[3,64,128]{2,1,0:T(8,128)} %bitcast.4), channel_id=1, source_target_pairs={{1,0},{2,1},{3,2},{5,4},{6,5},{7,6},{9,8},{10,9},{11,10},{13,12},{... | collective-permute-start | bytes 294920 | tf_op jit(solution)/shard_map/ppermute | solution.py:36
  41.7 2.5 %collective-permute-start.13 = (f32[4,1152]{1,0:T(4,128)S(1)}, f32[4,1152]{1,0:T(4,128)S(1)}, u32[]{:S(2)}, u32[]{:S(2)}) collective-permute-start(f32[4,1152]{1,0:T(4,128)S(1)} %add.35), channel_id=1, source_target_pairs={{0,8},{4,12},{8,0},{12,4},{1,9},{5,13},{9,1},{13,5},{2,10},{6,14},... | collective-permute-start | bytes 55304 | tf_op jit(solution)/shard_map/ppermute | solution.py:167
  44.8 2.3 %collective-permute-start.1 = (f32[3,32,128]{2,1,0:T(8,128)}, f32[3,32,128]{2,1,0:T(8,128)S(1)}, u32[]{:S(2)}, u32[]{:S(2)}) collective-permute-start(f32[3,32,128]{2,1,0:T(8,128)} %get-tuple-element.8), channel_id=1, source_target_pairs={{16,0},{32,16},{48,32},{64,48},{80,64},{96,80},{112,96},{128,112},... | collective-permute-start | bytes 147464 | tf_op jit(solution)/shard_map/ppermute | solution.py:36
  47.2 3.2 %collective-permute-start = (f32[3,32,128]{2,1,0:T(8,128)S(1)}, f32[3,32,128]{2,1,0:T(8,128)S(1)}, u32[]{:S(2)}, u32[]{:S(2)}) collective-permute-start(f32[3,32,128]{2,1,0:T(8,128)S(1)} %get-tuple-element.9), channel_id=1, source_target_pairs={{0,16},{16,32},{32,48},{48,64},{64,80},{80,96},{96,112},{112,128},... | collective-permute-start | bytes 147464 | tf_op jit(solution)/shard_map/ppermute | solution.py:36
  50.4 1.8 %collective-permute-start.4 = (f32[3,32,64]{2,1,0:T(8,128)}, f32[3,32,64]{2,1,0:T(8,128)S(1)}, u32[]{:S(2)}, u32[]{:S(2)}) collective-permute-start(f32[3,32,64]{2,1,0:T(8,128)} %get-tuple-element.15), channel_id=1, source_target_pairs={{0,4},{4,8},{8,12},{1,5},{5,9},{9,13},{2,6},{6,10},{10,14},{3,7},{... | collective-permute-start | bytes 73736 | tf_op jit(solution)/shard_map/ppermute | solution.py:36
  52.3 1.5 %collective-permute-done.4.ylo = f32[3,32,64]{2,1,0:T(8,128)S(1)} collective-permute-done((f32[3,32,64]{2,1,0:T(8,128)}, f32[3,32,64]{2,1,0:T(8,128)S(1)}, u32[]{:S(2)}, u32[]{:S(2)}) %collective-permute-start.4) | collective-permute-done | bytes 24608 | tf_op jit(solution)/shard_map/ppermute | solution.py:36
  53.8 2.4 %collective-permute-start.14 = (f32[4,1152]{1,0:T(4,128)S(1)}, f32[4,1152]{1,0:T(4,128)S(1)}, u32[]{:S(2)}, u32[]{:S(2)}) collective-permute-start(f32[4,1152]{1,0:T(4,128)S(1)} %add.36), channel_id=1, source_target_pairs={{0,1},{1,0},{2,3},{3,2},{4,5},{5,4},{6,7},{7,6},{8,9},{9,8},{10,11... | collective-permute-start | bytes 55304 | tf_op jit(solution)/shard_map/ppermute | solution.py:167
  57.5 12.0 %shard_map.86.nu = f32[64,32,128]{2,1,0:T(8,128)} custom-call(f32[3,64,32,128]{3,2,1,0:T(8,128)} %u.3, f32[3,32,128]{2,1,0:T(8,128)} %copy-done.6, f32[3,32,128]{2,1,0:T(8,128)} %copy-done.5, f32[3,64,128]{2,1,0:T(8,128)} %copy-done.2, f32[3,64,128]{2,1,0:T(8,128)} %copy-done.3, f32[3,32,64]{2,1,0:T(8,128)} %copy-done.7, f32[3,32,64]{2,1,0:T(8,128)} %copy-done.4), custom_call_target="tpu_custom_call" | custom-call | tf_op jit(solution)/shard_map/pallas_call | solution.py:120
  69.6 2.7 %collective-permute-start.15 = (f32[4,1152]{1,0:T(4,128)S(1)}, f32[4,1152]{1,0:T(4,128)S(1)}, u32[]{:S(2)}, u32[]{:S(2)}) collective-permute-start(f32[4,1152]{1,0:T(4,128)S(1)} %add.37), channel_id=1, source_target_pairs={{0,2},{1,3},{2,0},{3,1},{4,6},{5,7},{6,4},{7,5},{8,10},{9,11},{10,... | collective-permute-start | bytes 55304 | tf_op jit(solution)/shard_map/ppermute | solution.py:167
  72.3 2.9 %fusion.14 = f32[2,64,32]{1,0,2:T(2,128)S(1)} fusion(s32[2]{0:T(128)S(1)} %iota_multiply_fusion, f32[64,32,128]{2,1,0:T(8,128)} %shard_map.86.nu), kind=kOutput, calls=%fused_computation.31 | convolution fusion | flops 6291712 | bytes 1064968 | tf_op jit(solution)/shard_map/xzy,ky->kzx/dot_general | solution.py:22
  76.7 4.6 %all-to-all-start.1 = ((f32[16,4,1152]{2,1,0:T(4,128)}), f32[16,4,1152]{2,1,0:T(4,128)S(1)}, u32[]{:S(2)}, u32[]{:S(2)}) async-start(f32[16,4,1152]{2,1,0:T(4,128)} %broadcast_in_dim.2), calls=%async_computation.1 | async-start | bytes 589824 | tf_op jit(solution)/shard_map/all_to_all | solution.py:171
  81.3 1.8 %copy.37 = f32[64,32,128]{2,0,1:T(8,128)S(1)} copy(f32[64,32,128]{2,1,0:T(8,128)} %shard_map.86.nu) | data formatting | bytes 2097152 | tf_op jit(solution)/shard_map/pallas_call | solution.py:120
  84.5 4.5 %collective-permute-start.10 = (f32[32,64]{1,0:T(8,128)S(1)}, f32[32,64]{1,0:T(8,128)S(1)}, u32[]{:S(2)}, u32[]{:S(2)}) collective-permute-start(f32[32,64]{1,0:T(8,128)S(1)} %get-tuple-element.17), channel_id=1, source_target_pairs={{0,4},{4,8},{8,12},{1,5},{5,9},{9,13},{2,6},{6,10},{10,14},{3,7},{... | collective-permute-start | bytes 24584 | tf_op jit(solution)/shard_map/ppermute | solution.py:36
  89.7 2.3 %collective-permute-start.7 = (f32[32,128]{1,0:T(8,128)S(1)}, f32[32,128]{1,0:T(8,128)S(1)}, u32[]{:S(2)}, u32[]{:S(2)}) collective-permute-start(f32[32,128]{1,0:T(8,128)S(1)} %get-tuple-element.12), channel_id=1, source_target_pairs={{16,0},{32,16},{48,32},{64,48},{80,64},{96,80},{112,96},{128,112},... | collective-permute-start | bytes 49160 | tf_op jit(solution)/shard_map/ppermute | solution.py:36
  92.0 3.4 %collective-permute-start.6 = (f32[32,128]{1,0:T(8,128)S(1)}, f32[32,128]{1,0:T(8,128)S(1)}, u32[]{:S(2)}, u32[]{:S(2)}) collective-permute-start(f32[32,128]{1,0:T(8,128)S(1)} %get-tuple-element.13), channel_id=1, source_target_pairs={{0,16},{16,32},{32,48},{48,64},{64,80},{80,96},{96,112},{112,128},... | collective-permute-start | bytes 49160 | tf_op jit(solution)/shard_map/ppermute | solution.py:36
  97.2 4.0 %collective-permute-start.8 = (f32[64,128]{1,0:T(8,128)S(1)}, f32[64,128]{1,0:T(8,128)S(1)}, u32[]{:S(2)}, u32[]{:S(2)}) collective-permute-start(f32[64,128]{1,0:T(8,128)S(1)} %get-tuple-element.11), channel_id=1, source_target_pairs={{0,1},{1,2},{2,3},{4,5},{5,6},{6,7},{8,9},{9,10},{10,11},{12,13},{... | collective-permute-start | bytes 98312 | tf_op jit(solution)/shard_map/ppermute | solution.py:36
  101.2 3.7 %fusion = f32[2,3,4096]{2,1,0:T(4,128)S(1)} fusion(bf16[2,3,384]{2,1,0:T(4,128)(2,1)S(1)} %reshape.71, bf16[1,1,1,2,384,4096]{5,4,3,2,1,0:T(8,128)(2,1)} %param.10), kind=kOutput, calls=%fused_computation | convolution fusion | flops 18874368 | bytes 6394368 | tf_op jit(solution)/shard_map/axz,ahx->ahz/dot_general | solution.py:176
  106.3 15.4 %shard_map.87 = f32[3,64,32,128]{3,2,1,0:T(8,128)} custom-call(s32[2]{0:T(128)} %bitcast.66, f32[3,64,32,128]{3,2,1,0:T(8,128)} %u.3, f32[3,32,128]{2,1,0:T(8,128)} %copy-done.6, f32[3,32,128]{2,1,0:T(8,128)} %copy-done.5, f32[3,64,128]{2,1,0:T(8,128)} %copy-done.2, f32[3,64,128]{2,1,0:T(8,128)} %copy-done.3, f32[3,32,64]{2,1,0:T(8,128)} %copy-done.7, ...), custom_call_target="tpu_custom_call" | custom-call | tf_op jit(solution)/shard_map/pallas_call | solution.py:124
  (80 shorter events, 14.8 us)
Async XLA Ops:
  6.7 4.7 %copy-start.14 = (s32[1,1,1,2]{3,2,1,0:T(1,128)S(1)}, s32[1,1,1,2]{3,2,1,0:T(1,128)}, u32[]{:S(2)}) copy-start(s32[1,1,1,2]{3,2,1,0:T(1,128)} %param.8) | copy-start | bytes 28
  6.7 16.0 %copy-start = (f32[3,64,32,128]{3,2,1,0:T(8,128)S(1)}, f32[3,64,32,128]{3,2,1,0:T(8,128)}, u32[]{:S(2)}) copy-start(f32[3,64,32,128]{3,2,1,0:T(8,128)} %u.3) | copy-start | bytes 9437188
  12.7 22.3 %all-to-all-start = ((f32[16,4,1152]{2,1,0:T(4,128)}), f32[16,4,1152]{2,1,0:T(4,128)S(1)}, u32[]{:S(2)}, u32[]{:S(2)}) async-start(f32[16,4,1152]{2,1,0:T(4,128)} %copy.41), calls=%async_computation | async-start | bytes 589824 | tf_op jit(solution)/shard_map/all_to_all | solution.py:158
  28.2 18.9 %collective-permute-start.5 = (f32[3,32,64]{2,1,0:T(8,128)}, f32[3,32,64]{2,1,0:T(8,128)S(1)}, u32[]{:S(2)}, u32[]{:S(2)}) collective-permute-start(f32[3,32,64]{2,1,0:T(8,128)} %get-tuple-element.14), channel_id=1, source_target_pairs={{4,0},{8,4},{12,8},{5,1},{9,5},{13,9},{6,2},{10,6},{14,10},{7,3},{... | collective-permute-start | bytes 73736 | tf_op jit(solution)/shard_map/ppermute | solution.py:36
  35.0 6.6 %collective-permute-start.12 = (f32[4,1152]{1,0:T(4,128)S(1)}, f32[4,1152]{1,0:T(4,128)S(1)}, u32[]{:S(2)}, u32[]{:S(2)}) collective-permute-start(f32[4,1152]{1,0:T(4,128)S(1)} %reduce_sum.18), channel_id=1, source_target_pairs={{0,4},{4,0},{8,12},{12,8},{1,5},{5,1},{9,13},{13,9},{2,6},{6,2},{1... | collective-permute-start | bytes 55304 | tf_op jit(solution)/shard_map/ppermute | solution.py:167
  37.1 19.1 %collective-permute-start.2 = (f32[3,64,128]{2,1,0:T(8,128)}, f32[3,64,128]{2,1,0:T(8,128)S(1)}, u32[]{:S(2)}, u32[]{:S(2)}) collective-permute-start(f32[3,64,128]{2,1,0:T(8,128)} %bitcast.3), channel_id=1, source_target_pairs={{0,1},{1,2},{2,3},{4,5},{5,6},{6,7},{8,9},{9,10},{10,11},{12,13},{... | collective-permute-start | bytes 294920 | tf_op jit(solution)/shard_map/ppermute | solution.py:36
  40.3 15.9 %collective-permute-start.3 = (f32[3,64,128]{2,1,0:T(8,128)}, f32[3,64,128]{2,1,0:T(8,128)S(1)}, u32[]{:S(2)}, u32[]{:S(2)}) collective-permute-start(f32[3,64,128]{2,1,0:T(8,128)} %bitcast.4), channel_id=1, source_target_pairs={{1,0},{2,1},{3,2},{5,4},{6,5},{7,6},{9,8},{10,9},{11,10},{13,12},{... | collective-permute-start | bytes 294920 | tf_op jit(solution)/shard_map/ppermute | solution.py:36
  41.7 8.8 %collective-permute-start.13 = (f32[4,1152]{1,0:T(4,128)S(1)}, f32[4,1152]{1,0:T(4,128)S(1)}, u32[]{:S(2)}, u32[]{:S(2)}) collective-permute-start(f32[4,1152]{1,0:T(4,128)S(1)} %add.35), channel_id=1, source_target_pairs={{0,8},{4,12},{8,0},{12,4},{1,9},{5,13},{9,1},{13,5},{2,10},{6,14},... | collective-permute-start | bytes 55304 | tf_op jit(solution)/shard_map/ppermute | solution.py:167
  44.8 11.3 %collective-permute-start.1 = (f32[3,32,128]{2,1,0:T(8,128)}, f32[3,32,128]{2,1,0:T(8,128)S(1)}, u32[]{:S(2)}, u32[]{:S(2)}) collective-permute-start(f32[3,32,128]{2,1,0:T(8,128)} %get-tuple-element.8), channel_id=1, source_target_pairs={{16,0},{32,16},{48,32},{64,48},{80,64},{96,80},{112,96},{128,112},... | collective-permute-start | bytes 147464 | tf_op jit(solution)/shard_map/ppermute | solution.py:36
  47.2 9.1 %copy-start.4 = (f32[3,32,64]{2,1,0:T(8,128)}, f32[3,32,64]{2,1,0:T(8,128)S(1)}, u32[]{:S(2)}) copy-start(f32[3,32,64]{2,1,0:T(8,128)S(1)} %collective-permute-done.5.yhi) | copy-start | bytes 73732
  47.2 9.0 %collective-permute-start = (f32[3,32,128]{2,1,0:T(8,128)S(1)}, f32[3,32,128]{2,1,0:T(8,128)S(1)}, u32[]{:S(2)}, u32[]{:S(2)}) collective-permute-start(f32[3,32,128]{2,1,0:T(8,128)S(1)} %get-tuple-element.9), channel_id=1, source_target_pairs={{0,16},{16,32},{32,48},{48,64},{64,80},{80,96},{96,112},{112,128},... | collective-permute-start | bytes 147464 | tf_op jit(solution)/shard_map/ppermute | solution.py:36
  50.4 3.4 %collective-permute-start.4 = (f32[3,32,64]{2,1,0:T(8,128)}, f32[3,32,64]{2,1,0:T(8,128)S(1)}, u32[]{:S(2)}, u32[]{:S(2)}) collective-permute-start(f32[3,32,64]{2,1,0:T(8,128)} %get-tuple-element.15), channel_id=1, source_target_pairs={{0,4},{4,8},{8,12},{1,5},{5,9},{9,13},{2,6},{6,10},{10,14},{3,7},{... | collective-permute-start | bytes 73736 | tf_op jit(solution)/shard_map/ppermute | solution.py:36
  53.8 2.5 %copy-start.7 = (f32[3,32,64]{2,1,0:T(8,128)}, f32[3,32,64]{2,1,0:T(8,128)S(1)}, u32[]{:S(2)}) copy-start(f32[3,32,64]{2,1,0:T(8,128)S(1)} %collective-permute-done.4.ylo) | copy-start | bytes 73732
  53.8 15.8 %collective-permute-start.14 = (f32[4,1152]{1,0:T(4,128)S(1)}, f32[4,1152]{1,0:T(4,128)S(1)}, u32[]{:S(2)}, u32[]{:S(2)}) collective-permute-start(f32[4,1152]{1,0:T(4,128)S(1)} %add.36), channel_id=1, source_target_pairs={{0,1},{1,0},{2,3},{3,2},{4,5},{5,4},{6,7},{7,6},{8,9},{9,8},{10,11... | collective-permute-start | bytes 55304 | tf_op jit(solution)/shard_map/ppermute | solution.py:167
  69.6 5.6 %collective-permute-start.15 = (f32[4,1152]{1,0:T(4,128)S(1)}, f32[4,1152]{1,0:T(4,128)S(1)}, u32[]{:S(2)}, u32[]{:S(2)}) collective-permute-start(f32[4,1152]{1,0:T(4,128)S(1)} %add.37), channel_id=1, source_target_pairs={{0,2},{1,3},{2,0},{3,1},{4,6},{5,7},{6,4},{7,5},{8,10},{9,11},{10,... | collective-permute-start | bytes 55304 | tf_op jit(solution)/shard_map/ppermute | solution.py:167
  76.7 20.1 %all-to-all-start.1 = ((f32[16,4,1152]{2,1,0:T(4,128)}), f32[16,4,1152]{2,1,0:T(4,128)S(1)}, u32[]{:S(2)}, u32[]{:S(2)}) async-start(f32[16,4,1152]{2,1,0:T(4,128)} %broadcast_in_dim.2), calls=%async_computation.1 | async-start | bytes 589824 | tf_op jit(solution)/shard_map/all_to_all | solution.py:171
  83.2 14.0 %collective-permute-start.11 = (f32[32,64]{1,0:T(8,128)S(1)}, f32[32,64]{1,0:T(8,128)S(1)}, u32[]{:S(2)}, u32[]{:S(2)}) collective-permute-start(f32[32,64]{1,0:T(8,128)S(1)} %get-tuple-element.16), channel_id=1, source_target_pairs={{4,0},{8,4},{12,8},{5,1},{9,5},{13,9},{6,2},{10,6},{14,10},{7,3},{... | collective-permute-start | bytes 24584 | tf_op jit(solution)/shard_map/ppermute | solution.py:36
  84.5 21.1 %collective-permute-start.10 = (f32[32,64]{1,0:T(8,128)S(1)}, f32[32,64]{1,0:T(8,128)S(1)}, u32[]{:S(2)}, u32[]{:S(2)}) collective-permute-start(f32[32,64]{1,0:T(8,128)S(1)} %get-tuple-element.17), channel_id=1, source_target_pairs={{0,4},{4,8},{8,12},{1,5},{5,9},{9,13},{2,6},{6,10},{10,14},{3,7},{... | collective-permute-start | bytes 24584 | tf_op jit(solution)/shard_map/ppermute | solution.py:36
  89.7 15.9 %collective-permute-start.7 = (f32[32,128]{1,0:T(8,128)S(1)}, f32[32,128]{1,0:T(8,128)S(1)}, u32[]{:S(2)}, u32[]{:S(2)}) collective-permute-start(f32[32,128]{1,0:T(8,128)S(1)} %get-tuple-element.12), channel_id=1, source_target_pairs={{16,0},{32,16},{48,32},{64,48},{80,64},{96,80},{112,96},{128,112},... | collective-permute-start | bytes 49160 | tf_op jit(solution)/shard_map/ppermute | solution.py:36
  92.0 13.6 %collective-permute-start.6 = (f32[32,128]{1,0:T(8,128)S(1)}, f32[32,128]{1,0:T(8,128)S(1)}, u32[]{:S(2)}, u32[]{:S(2)}) collective-permute-start(f32[32,128]{1,0:T(8,128)S(1)} %get-tuple-element.13), channel_id=1, source_target_pairs={{0,16},{16,32},{32,48},{48,64},{64,80},{80,96},{96,112},{112,128},... | collective-permute-start | bytes 49160 | tf_op jit(solution)/shard_map/ppermute | solution.py:36
  95.5 10.2 %collective-permute-start.9 = (f32[64,128]{1,0:T(8,128)S(1)}, f32[64,128]{1,0:T(8,128)S(1)}, u32[]{:S(2)}, u32[]{:S(2)}) collective-permute-start(f32[64,128]{1,0:T(8,128)S(1)} %get-tuple-element.10), channel_id=1, source_target_pairs={{1,0},{2,1},{3,2},{5,4},{6,5},{7,6},{9,8},{10,9},{11,10},{13,12},{... | collective-permute-start | bytes 98312 | tf_op jit(solution)/shard_map/ppermute | solution.py:36
  96.9 8.0 %copy-start.1 = (f32[64,1152]{1,0:T(8,128)}, f32[64,1152]{1,0:T(8,128)S(1)}, u32[]{:S(2)}) copy-start(f32[64,1152]{1,0:T(8,128)S(1)} %reshape.70) | copy-start | bytes 884740
  97.2 7.7 %copy-start.10 = (f32[32,64]{1,0:T(8,128)}, f32[32,64]{1,0:T(8,128)S(1)}, u32[]{:S(2)}) copy-start(f32[32,64]{1,0:T(8,128)S(1)} %collective-permute-done.11.nyhi) | copy-start | bytes 24580
  97.2 8.5 %collective-permute-start.8 = (f32[64,128]{1,0:T(8,128)S(1)}, f32[64,128]{1,0:T(8,128)S(1)}, u32[]{:S(2)}, u32[]{:S(2)}) collective-permute-start(f32[64,128]{1,0:T(8,128)S(1)} %get-tuple-element.11), channel_id=1, source_target_pairs={{0,1},{1,2},{2,3},{4,5},{5,6},{6,7},{8,9},{9,10},{10,11},{12,13},{... | collective-permute-start | bytes 98312 | tf_op jit(solution)/shard_map/ppermute | solution.py:36
  (9 other events, 5.6 us)

commit v10 on v9

--- a/solution.py
+++ b/solution.py
@@ -72,7 +72,7 @@
         nu[x] = 0.05 + 1.0 * jnp.sqrt(2.0 * total + 1e-06)
         return carry
 
-    lax.fori_loop(0, u.shape[1], plane, 0, unroll=4)
+    lax.fori_loop(0, u.shape[1], plane, 0, unroll=8)
 
 
 def advance_kernel(planes, u, xlo, xhi, zlo, zhi, ylo, yhi, nu, nxlo, nxhi, nzlo, nzhi, nylo, nyhi, sent, out):
@@ -100,7 +100,7 @@
             out[c, x] = center + 0.25 * (spread - advect) + impulse
         return carry
 
-    lax.fori_loop(0, u.shape[1], plane, 0, unroll=4)
+    lax.fori_loop(0, u.shape[1], plane, 0, unroll=8)
 
 
 def vmem_call(kernel, out_shape, count, smem=0):

time: 123 us -> 122 us (level)
  transfers between devices with their start and end apart: 18 -> 18, of which waited for: 2 -> 2; matrix products, arithmetic and copies ran while one was open for 14% -> 14% of each run, Pallas kernels for 10% -> 9%
where the time goes in v10:
time: 122 us; the launch traced here: 121 us
  starting transfers between devices  53.5 us (44%)
  Pallas kernels  26.4 us (22%)
  matrix products  16.8 us (14%)
  local copies, waits for them, and re-layouts  11.2 us (9%)
  waiting for transfers between devices  6.98 us (6%)
  between operations  4.97 us (4%)
    ppermute x6, starting transfers between devices, faces(): lax.ppermute(last, axis, forward)  20.2 us
    pallas_call x1, Pallas kernels, stencil(): vmem_call(advance_kernel, jax.ShapeDtypeStruct(velocity.shape, jnp.float3...  15 us
    pallas_call x1, Pallas kernels, stencil(): vmem_call(viscosity_kernel, jax.ShapeDtypeStruct(velocity.shape[1:], jnp....  11.4 us
    all_to_all x1, starting transfers between devices, body(): lax.all_to_all(partial_sample.reshape(rows, per_row, -1), 'gx', split_axi...  9.97 us
    ppermute x6, starting transfers between devices, faces(): lax.ppermute(first, axis, backward)  9.79 us
    ppermute x4, starting transfers between devices, body(): owned = owned + lax.ppermute(owned, axis, pairs)  8.93 us
    dot_general x2, matrix products, faces(): jnp.einsum(letters + ',ky->k' + letters[:-3] + 'zx', block, ends, precisi...  7.75 us
    all_to_all x1, waiting for transfers between devices, body(): lax.all_to_all(partial_sample.reshape(rows, per_row, -1), 'gx', split_axi...  5.45 us
  transfers between devices with their start and end apart: 18, of which 2 were waited for; matrix products, arithmetic and copies ran while one was open for 14% of the time, Pallas kernels for 9%

profile of v10, /device:TPU:1, one launch (start us, length us, event | category | flops | bytes accessed | tf_op | source)
XLA Modules:
  0.0 120.7 jit_solution(18416661449084116317)
XLA Ops:
  0.6 1.3 %fusion.25 = (s32[1,1,1,1]{3,2,1,0:T(1,128)}, s32[1,1,1,1]{3,2,1,0:T(1,128)}) fusion(s32[1,1,1,2]{3,2,1,0:T(1,128)} %param.9), kind=kLoop, calls=%fused_computation.44 | loop fusion | bytes 16 | tf_op jit(solution)/shard_map/slice | solution.py:142
  6.7 4.7 %fusion.2 = f32[2,3,384]{2,1,0:T(4,128)S(1)} fusion(bf16[1,1,1,2,384,4096]{5,4,3,2,1,0:T(8,128)(2,1)} %param.10, bf16[1,3,4096]{2,1,0:T(4,128)(2,1)S(1)} %stack.10, bf16[1,3,4096]{2,1,0:T(4,128)(2,1)S(1)} %stack.9), kind=kOutput, calls=%fused_computation.2 | convolution fusion | flops 18972672 | bytes 6349824 | tf_op jit(solution)/shard_map/spq,scq->scp/dot_general | solution.py:144
  12.7 10.0 %all-to-all-start = ((f32[16,4,1152]{2,1,0:T(4,128)}), f32[16,4,1152]{2,1,0:T(4,128)S(1)}, u32[]{:S(2)}, u32[]{:S(2)}) async-start(f32[16,4,1152]{2,1,0:T(4,128)} %copy.41), calls=%async_computation | async-start | bytes 589824 | tf_op jit(solution)/shard_map/all_to_all | solution.py:158
  22.7 4.9 %fusion.4 = f32[2,3,64,32]{2,0,3,1:T(2,128)S(1)} fusion(f32[3,64,32,128]{3,2,1,0:T(8,128)S(1)} %copy-done, s32[2]{0:T(128)S(1)} %iota_multiply_fusion), kind=kOutput, calls=%fused_computation.4 | convolution fusion | flops 18874624 | bytes 3194888 | tf_op jit(solution)/shard_map/cxzy,ky->kczx/dot_general | solution.py:22
  29.5 5.4 %all-to-all-done = f32[16,4,1152]{2,1,0:T(4,128)S(1)} async-done(((f32[16,4,1152]{2,1,0:T(4,128)}), f32[16,4,1152]{2,1,0:T(4,128)S(1)}, u32[]{:S(2)}, u32[]{:S(2)}) %all-to-all-start) | async-done | bytes 294944 | tf_op jit(solution)/shard_map/all_to_all | solution.py:158
  37.1 3.2 %collective-permute-start.2 = (f32[3,64,128]{2,1,0:T(8,128)}, f32[3,64,128]{2,1,0:T(8,128)S(1)}, u32[]{:S(2)}, u32[]{:S(2)}) collective-permute-start(f32[3,64,128]{2,1,0:T(8,128)} %bitcast.3), channel_id=1, source_target_pairs={{0,1},{1,2},{2,3},{4,5},{5,6},{6,7},{8,9},{9,10},{10,11},{12,13},{... | collective-permute-start | bytes 294920 | tf_op jit(solution)/shard_map/ppermute | solution.py:36
  41.7 2.5 %collective-permute-start.13 = (f32[4,1152]{1,0:T(4,128)S(1)}, f32[4,1152]{1,0:T(4,128)S(1)}, u32[]{:S(2)}, u32[]{:S(2)}) collective-permute-start(f32[4,1152]{1,0:T(4,128)S(1)} %add.35), channel_id=1, source_target_pairs={{0,8},{4,12},{8,0},{12,4},{1,9},{5,13},{9,1},{13,5},{2,10},{6,14},... | collective-permute-start | bytes 55304 | tf_op jit(solution)/shard_map/ppermute | solution.py:167
  44.8 2.3 %collective-permute-start.1 = (f32[3,32,128]{2,1,0:T(8,128)}, f32[3,32,128]{2,1,0:T(8,128)S(1)}, u32[]{:S(2)}, u32[]{:S(2)}) collective-permute-start(f32[3,32,128]{2,1,0:T(8,128)} %get-tuple-element.8), channel_id=1, source_target_pairs={{16,0},{32,16},{48,32},{64,48},{80,64},{96,80},{112,96},{128,112},... | collective-permute-start | bytes 147464 | tf_op jit(solution)/shard_map/ppermute | solution.py:36
  47.2 3.2 %collective-permute-start = (f32[3,32,128]{2,1,0:T(8,128)S(1)}, f32[3,32,128]{2,1,0:T(8,128)S(1)}, u32[]{:S(2)}, u32[]{:S(2)}) collective-permute-start(f32[3,32,128]{2,1,0:T(8,128)S(1)} %get-tuple-element.9), channel_id=1, source_target_pairs={{0,16},{16,32},{32,48},{48,64},{64,80},{80,96},{96,112},{112,128},... | collective-permute-start | bytes 147464 | tf_op jit(solution)/shard_map/ppermute | solution.py:36
  50.4 1.8 %collective-permute-start.4 = (f32[3,32,64]{2,1,0:T(8,128)}, f32[3,32,64]{2,1,0:T(8,128)S(1)}, u32[]{:S(2)}, u32[]{:S(2)}) collective-permute-start(f32[3,32,64]{2,1,0:T(8,128)} %get-tuple-element.15), channel_id=1, source_target_pairs={{0,4},{4,8},{8,12},{1,5},{5,9},{9,13},{2,6},{6,10},{10,14},{3,7},{... | collective-permute-start | bytes 73736 | tf_op jit(solution)/shard_map/ppermute | solution.py:36
  52.3 1.5 %collective-permute-done.4.ylo = f32[3,32,64]{2,1,0:T(8,128)S(1)} collective-permute-done((f32[3,32,64]{2,1,0:T(8,128)}, f32[3,32,64]{2,1,0:T(8,128)S(1)}, u32[]{:S(2)}, u32[]{:S(2)}) %collective-permute-start.4) | collective-permute-done | bytes 24608 | tf_op jit(solution)/shard_map/ppermute | solution.py:36
  53.8 2.4 %collective-permute-start.14 = (f32[4,1152]{1,0:T(4,128)S(1)}, f32[4,1152]{1,0:T(4,128)S(1)}, u32[]{:S(2)}, u32[]{:S(2)}) collective-permute-start(f32[4,1152]{1,0:T(4,128)S(1)} %add.36), channel_id=1, source_target_pairs={{0,1},{1,0},{2,3},{3,2},{4,5},{5,4},{6,7},{7,6},{8,9},{9,8},{10,11... | collective-permute-start | bytes 55304 | tf_op jit(solution)/shard_map/ppermute | solution.py:167
  57.5 11.4 %shard_map.86.nu = f32[64,32,128]{2,1,0:T(8,128)} custom-call(f32[3,64,32,128]{3,2,1,0:T(8,128)} %u.3, f32[3,32,128]{2,1,0:T(8,128)} %copy-done.6, f32[3,32,128]{2,1,0:T(8,128)} %copy-done.5, f32[3,64,128]{2,1,0:T(8,128)} %copy-done.2, f32[3,64,128]{2,1,0:T(8,128)} %copy-done.3, f32[3,32,64]{2,1,0:T(8,128)} %copy-done.7, f32[3,32,64]{2,1,0:T(8,128)} %copy-done.4), custom_call_target="tpu_custom_call" | custom-call | tf_op jit(solution)/shard_map/pallas_call | solution.py:120
  68.9 2.7 %collective-permute-start.15 = (f32[4,1152]{1,0:T(4,128)S(1)}, f32[4,1152]{1,0:T(4,128)S(1)}, u32[]{:S(2)}, u32[]{:S(2)}) collective-permute-start(f32[4,1152]{1,0:T(4,128)S(1)} %add.37), channel_id=1, source_target_pairs={{0,2},{1,3},{2,0},{3,1},{4,6},{5,7},{6,4},{7,5},{8,10},{9,11},{10,... | collective-permute-start | bytes 55304 | tf_op jit(solution)/shard_map/ppermute | solution.py:167
  71.6 2.9 %fusion.14 = f32[2,64,32]{1,0,2:T(2,128)S(1)} fusion(s32[2]{0:T(128)S(1)} %iota_multiply_fusion, f32[64,32,128]{2,1,0:T(8,128)} %shard_map.86.nu), kind=kOutput, calls=%fused_computation.31 | convolution fusion | flops 6291712 | bytes 1064968 | tf_op jit(solution)/shard_map/xzy,ky->kzx/dot_general | solution.py:22
  76.1 4.6 %all-to-all-start.1 = ((f32[16,4,1152]{2,1,0:T(4,128)}), f32[16,4,1152]{2,1,0:T(4,128)S(1)}, u32[]{:S(2)}, u32[]{:S(2)}) async-start(f32[16,4,1152]{2,1,0:T(4,128)} %broadcast_in_dim.2), calls=%async_computation.1 | async-start | bytes 589824 | tf_op jit(solution)/shard_map/all_to_all | solution.py:171
  80.7 1.8 %copy.37 = f32[64,32,128]{2,0,1:T(8,128)S(1)} copy(f32[64,32,128]{2,1,0:T(8,128)} %shard_map.86.nu) | data formatting | bytes 2097152 | tf_op jit(solution)/shard_map/pallas_call | solution.py:120
  82.6 1.3 %collective-permute-start.11 = (f32[32,64]{1,0:T(8,128)S(1)}, f32[32,64]{1,0:T(8,128)S(1)}, u32[]{:S(2)}, u32[]{:S(2)}) collective-permute-start(f32[32,64]{1,0:T(8,128)S(1)} %get-tuple-element.16), channel_id=1, source_target_pairs={{4,0},{8,4},{12,8},{5,1},{9,5},{13,9},{6,2},{10,6},{14,10},{7,3},{... | collective-permute-start | bytes 24584 | tf_op jit(solution)/shard_map/ppermute | solution.py:36
  83.9 4.5 %collective-permute-start.10 = (f32[32,64]{1,0:T(8,128)S(1)}, f32[32,64]{1,0:T(8,128)S(1)}, u32[]{:S(2)}, u32[]{:S(2)}) collective-permute-start(f32[32,64]{1,0:T(8,128)S(1)} %get-tuple-element.17), channel_id=1, source_target_pairs={{0,4},{4,8},{8,12},{1,5},{5,9},{9,13},{2,6},{6,10},{10,14},{3,7},{... | collective-permute-start | bytes 24584 | tf_op jit(solution)/shard_map/ppermute | solution.py:36
  89.1 2.3 %collective-permute-start.7 = (f32[32,128]{1,0:T(8,128)S(1)}, f32[32,128]{1,0:T(8,128)S(1)}, u32[]{:S(2)}, u32[]{:S(2)}) collective-permute-start(f32[32,128]{1,0:T(8,128)S(1)} %get-tuple-element.12), channel_id=1, source_target_pairs={{16,0},{32,16},{48,32},{64,48},{80,64},{96,80},{112,96},{128,112},... | collective-permute-start | bytes 49160 | tf_op jit(solution)/shard_map/ppermute | solution.py:36
  91.4 3.4 %collective-permute-start.6 = (f32[32,128]{1,0:T(8,128)S(1)}, f32[32,128]{1,0:T(8,128)S(1)}, u32[]{:S(2)}, u32[]{:S(2)}) collective-permute-start(f32[32,128]{1,0:T(8,128)S(1)} %get-tuple-element.13), channel_id=1, source_target_pairs={{0,16},{16,32},{32,48},{48,64},{64,80},{80,96},{96,112},{112,128},... | collective-permute-start | bytes 49160 | tf_op jit(solution)/shard_map/ppermute | solution.py:36
  96.6 4.0 %collective-permute-start.8 = (f32[64,128]{1,0:T(8,128)S(1)}, f32[64,128]{1,0:T(8,128)S(1)}, u32[]{:S(2)}, u32[]{:S(2)}) collective-permute-start(f32[64,128]{1,0:T(8,128)S(1)} %get-tuple-element.11), channel_id=1, source_target_pairs={{0,1},{1,2},{2,3},{4,5},{5,6},{6,7},{8,9},{9,10},{10,11},{12,13},{... | collective-permute-start | bytes 98312 | tf_op jit(solution)/shard_map/ppermute | solution.py:36
  100.6 3.7 %fusion = f32[2,3,4096]{2,1,0:T(4,128)S(1)} fusion(bf16[2,3,384]{2,1,0:T(4,128)(2,1)S(1)} %reshape.71, bf16[1,1,1,2,384,4096]{5,4,3,2,1,0:T(8,128)(2,1)} %param.10), kind=kOutput, calls=%fused_computation | convolution fusion | flops 18874368 | bytes 6394368 | tf_op jit(solution)/shard_map/axz,ahx->ahz/dot_general | solution.py:176
  105.7 15.0 %shard_map.87 = f32[3,64,32,128]{3,2,1,0:T(8,128)} custom-call(s32[2]{0:T(128)} %bitcast.66, f32[3,64,32,128]{3,2,1,0:T(8,128)} %u.3, f32[3,32,128]{2,1,0:T(8,128)} %copy-done.6, f32[3,32,128]{2,1,0:T(8,128)} %copy-done.5, f32[3,64,128]{2,1,0:T(8,128)} %copy-done.2, f32[3,64,128]{2,1,0:T(8,128)} %copy-done.3, f32[3,32,64]{2,1,0:T(8,128)} %copy-done.7, ...), custom_call_target="tpu_custom_call" | custom-call | tf_op jit(solution)/shard_map/pallas_call | solution.py:124
  (80 shorter events, 14.8 us)
Async XLA Ops:
  6.7 4.7 %copy-start.14 = (s32[1,1,1,2]{3,2,1,0:T(1,128)S(1)}, s32[1,1,1,2]{3,2,1,0:T(1,128)}, u32[]{:S(2)}) copy-start(s32[1,1,1,2]{3,2,1,0:T(1,128)} %param.8) | copy-start | bytes 28
  6.7 16.0 %copy-start = (f32[3,64,32,128]{3,2,1,0:T(8,128)S(1)}, f32[3,64,32,128]{3,2,1,0:T(8,128)}, u32[]{:S(2)}) copy-start(f32[3,64,32,128]{3,2,1,0:T(8,128)} %u.3) | copy-start | bytes 9437188
  12.7 22.3 %all-to-all-start = ((f32[16,4,1152]{2,1,0:T(4,128)}), f32[16,4,1152]{2,1,0:T(4,128)S(1)}, u32[]{:S(2)}, u32[]{:S(2)}) async-start(f32[16,4,1152]{2,1,0:T(4,128)} %copy.41), calls=%async_computation | async-start | bytes 589824 | tf_op jit(solution)/shard_map/all_to_all | solution.py:158
  28.2 18.9 %collective-permute-start.5 = (f32[3,32,64]{2,1,0:T(8,128)}, f32[3,32,64]{2,1,0:T(8,128)S(1)}, u32[]{:S(2)}, u32[]{:S(2)}) collective-permute-start(f32[3,32,64]{2,1,0:T(8,128)} %get-tuple-element.14), channel_id=1, source_target_pairs={{4,0},{8,4},{12,8},{5,1},{9,5},{13,9},{6,2},{10,6},{14,10},{7,3},{... | collective-permute-start | bytes 73736 | tf_op jit(solution)/shard_map/ppermute | solution.py:36
  35.0 6.6 %collective-permute-start.12 = (f32[4,1152]{1,0:T(4,128)S(1)}, f32[4,1152]{1,0:T(4,128)S(1)}, u32[]{:S(2)}, u32[]{:S(2)}) collective-permute-start(f32[4,1152]{1,0:T(4,128)S(1)} %reduce_sum.18), channel_id=1, source_target_pairs={{0,4},{4,0},{8,12},{12,8},{1,5},{5,1},{9,13},{13,9},{2,6},{6,2},{1... | collective-permute-start | bytes 55304 | tf_op jit(solution)/shard_map/ppermute | solution.py:167
  37.1 19.1 %collective-permute-start.2 = (f32[3,64,128]{2,1,0:T(8,128)}, f32[3,64,128]{2,1,0:T(8,128)S(1)}, u32[]{:S(2)}, u32[]{:S(2)}) collective-permute-start(f32[3,64,128]{2,1,0:T(8,128)} %bitcast.3), channel_id=1, source_target_pairs={{0,1},{1,2},{2,3},{4,5},{5,6},{6,7},{8,9},{9,10},{10,11},{12,13},{... | collective-permute-start | bytes 294920 | tf_op jit(solution)/shard_map/ppermute | solution.py:36
  40.3 15.9 %collective-permute-start.3 = (f32[3,64,128]{2,1,0:T(8,128)}, f32[3,64,128]{2,1,0:T(8,128)S(1)}, u32[]{:S(2)}, u32[]{:S(2)}) collective-permute-start(f32[3,64,128]{2,1,0:T(8,128)} %bitcast.4), channel_id=1, source_target_pairs={{1,0},{2,1},{3,2},{5,4},{6,5},{7,6},{9,8},{10,9},{11,10},{13,12},{... | collective-permute-start | bytes 294920 | tf_op jit(solution)/shard_map/ppermute | solution.py:36
  41.7 8.8 %collective-permute-start.13 = (f32[4,1152]{1,0:T(4,128)S(1)}, f32[4,1152]{1,0:T(4,128)S(1)}, u32[]{:S(2)}, u32[]{:S(2)}) collective-permute-start(f32[4,1152]{1,0:T(4,128)S(1)} %add.35), channel_id=1, source_target_pairs={{0,8},{4,12},{8,0},{12,4},{1,9},{5,13},{9,1},{13,5},{2,10},{6,14},... | collective-permute-start | bytes 55304 | tf_op jit(solution)/shard_map/ppermute | solution.py:167
  44.8 11.3 %collective-permute-start.1 = (f32[3,32,128]{2,1,0:T(8,128)}, f32[3,32,128]{2,1,0:T(8,128)S(1)}, u32[]{:S(2)}, u32[]{:S(2)}) collective-permute-start(f32[3,32,128]{2,1,0:T(8,128)} %get-tuple-element.8), channel_id=1, source_target_pairs={{16,0},{32,16},{48,32},{64,48},{80,64},{96,80},{112,96},{128,112},... | collective-permute-start | bytes 147464 | tf_op jit(solution)/shard_map/ppermute | solution.py:36
  47.2 9.1 %copy-start.4 = (f32[3,32,64]{2,1,0:T(8,128)}, f32[3,32,64]{2,1,0:T(8,128)S(1)}, u32[]{:S(2)}) copy-start(f32[3,32,64]{2,1,0:T(8,128)S(1)} %collective-permute-done.5.yhi) | copy-start | bytes 73732
  47.2 9.0 %collective-permute-start = (f32[3,32,128]{2,1,0:T(8,128)S(1)}, f32[3,32,128]{2,1,0:T(8,128)S(1)}, u32[]{:S(2)}, u32[]{:S(2)}) collective-permute-start(f32[3,32,128]{2,1,0:T(8,128)S(1)} %get-tuple-element.9), channel_id=1, source_target_pairs={{0,16},{16,32},{32,48},{48,64},{64,80},{80,96},{96,112},{112,128},... | collective-permute-start | bytes 147464 | tf_op jit(solution)/shard_map/ppermute | solution.py:36
  50.4 3.4 %collective-permute-start.4 = (f32[3,32,64]{2,1,0:T(8,128)}, f32[3,32,64]{2,1,0:T(8,128)S(1)}, u32[]{:S(2)}, u32[]{:S(2)}) collective-permute-start(f32[3,32,64]{2,1,0:T(8,128)} %get-tuple-element.15), channel_id=1, source_target_pairs={{0,4},{4,8},{8,12},{1,5},{5,9},{9,13},{2,6},{6,10},{10,14},{3,7},{... | collective-permute-start | bytes 73736 | tf_op jit(solution)/shard_map/ppermute | solution.py:36
  53.8 2.5 %copy-start.7 = (f32[3,32,64]{2,1,0:T(8,128)}, f32[3,32,64]{2,1,0:T(8,128)S(1)}, u32[]{:S(2)}) copy-start(f32[3,32,64]{2,1,0:T(8,128)S(1)} %collective-permute-done.4.ylo) | copy-start | bytes 73732
  53.8 15.1 %collective-permute-start.14 = (f32[4,1152]{1,0:T(4,128)S(1)}, f32[4,1152]{1,0:T(4,128)S(1)}, u32[]{:S(2)}, u32[]{:S(2)}) collective-permute-start(f32[4,1152]{1,0:T(4,128)S(1)} %add.36), channel_id=1, source_target_pairs={{0,1},{1,0},{2,3},{3,2},{4,5},{5,4},{6,7},{7,6},{8,9},{9,8},{10,11... | collective-permute-start | bytes 55304 | tf_op jit(solution)/shard_map/ppermute | solution.py:167
  68.9 5.6 %collective-permute-start.15 = (f32[4,1152]{1,0:T(4,128)S(1)}, f32[4,1152]{1,0:T(4,128)S(1)}, u32[]{:S(2)}, u32[]{:S(2)}) collective-permute-start(f32[4,1152]{1,0:T(4,128)S(1)} %add.37), channel_id=1, source_target_pairs={{0,2},{1,3},{2,0},{3,1},{4,6},{5,7},{6,4},{7,5},{8,10},{9,11},{10,... | collective-permute-start | bytes 55304 | tf_op jit(solution)/shard_map/ppermute | solution.py:167
  76.1 20.1 %all-to-all-start.1 = ((f32[16,4,1152]{2,1,0:T(4,128)}), f32[16,4,1152]{2,1,0:T(4,128)S(1)}, u32[]{:S(2)}, u32[]{:S(2)}) async-start(f32[16,4,1152]{2,1,0:T(4,128)} %broadcast_in_dim.2), calls=%async_computation.1 | async-start | bytes 589824 | tf_op jit(solution)/shard_map/all_to_all | solution.py:171
  82.6 14.0 %collective-permute-start.11 = (f32[32,64]{1,0:T(8,128)S(1)}, f32[32,64]{1,0:T(8,128)S(1)}, u32[]{:S(2)}, u32[]{:S(2)}) collective-permute-start(f32[32,64]{1,0:T(8,128)S(1)} %get-tuple-element.16), channel_id=1, source_target_pairs={{4,0},{8,4},{12,8},{5,1},{9,5},{13,9},{6,2},{10,6},{14,10},{7,3},{... | collective-permute-start | bytes 24584 | tf_op jit(solution)/shard_map/ppermute | solution.py:36
  83.9 21.1 %collective-permute-start.10 = (f32[32,64]{1,0:T(8,128)S(1)}, f32[32,64]{1,0:T(8,128)S(1)}, u32[]{:S(2)}, u32[]{:S(2)}) collective-permute-start(f32[32,64]{1,0:T(8,128)S(1)} %get-tuple-element.17), channel_id=1, source_target_pairs={{0,4},{4,8},{8,12},{1,5},{5,9},{9,13},{2,6},{6,10},{10,14},{3,7},{... | collective-permute-start | bytes 24584 | tf_op jit(solution)/shard_map/ppermute | solution.py:36
  89.1 15.9 %collective-permute-start.7 = (f32[32,128]{1,0:T(8,128)S(1)}, f32[32,128]{1,0:T(8,128)S(1)}, u32[]{:S(2)}, u32[]{:S(2)}) collective-permute-start(f32[32,128]{1,0:T(8,128)S(1)} %get-tuple-element.12), channel_id=1, source_target_pairs={{16,0},{32,16},{48,32},{64,48},{80,64},{96,80},{112,96},{128,112},... | collective-permute-start | bytes 49160 | tf_op jit(solution)/shard_map/ppermute | solution.py:36
  91.4 13.6 %collective-permute-start.6 = (f32[32,128]{1,0:T(8,128)S(1)}, f32[32,128]{1,0:T(8,128)S(1)}, u32[]{:S(2)}, u32[]{:S(2)}) collective-permute-start(f32[32,128]{1,0:T(8,128)S(1)} %get-tuple-element.13), channel_id=1, source_target_pairs={{0,16},{16,32},{32,48},{48,64},{64,80},{80,96},{96,112},{112,128},... | collective-permute-start | bytes 49160 | tf_op jit(solution)/shard_map/ppermute | solution.py:36
  94.8 10.2 %collective-permute-start.9 = (f32[64,128]{1,0:T(8,128)S(1)}, f32[64,128]{1,0:T(8,128)S(1)}, u32[]{:S(2)}, u32[]{:S(2)}) collective-permute-start(f32[64,128]{1,0:T(8,128)S(1)} %get-tuple-element.10), channel_id=1, source_target_pairs={{1,0},{2,1},{3,2},{5,4},{6,5},{7,6},{9,8},{10,9},{11,10},{13,12},{... | collective-permute-start | bytes 98312 | tf_op jit(solution)/shard_map/ppermute | solution.py:36
  96.3 8.0 %copy-start.1 = (f32[64,1152]{1,0:T(8,128)}, f32[64,1152]{1,0:T(8,128)S(1)}, u32[]{:S(2)}) copy-start(f32[64,1152]{1,0:T(8,128)S(1)} %reshape.70) | copy-start | bytes 884740
  96.6 7.7 %copy-start.10 = (f32[32,64]{1,0:T(8,128)}, f32[32,64]{1,0:T(8,128)S(1)}, u32[]{:S(2)}) copy-start(f32[32,64]{1,0:T(8,128)S(1)} %collective-permute-done.11.nyhi) | copy-start | bytes 24580
  96.6 8.5 %collective-permute-start.8 = (f32[64,128]{1,0:T(8,128)S(1)}, f32[64,128]{1,0:T(8,128)S(1)}, u32[]{:S(2)}, u32[]{:S(2)}) collective-permute-start(f32[64,128]{1,0:T(8,128)S(1)} %get-tuple-element.11), channel_id=1, source_target_pairs={{0,1},{1,2},{2,3},{4,5},{5,6},{6,7},{8,9},{9,10},{10,11},{12,13},{... | collective-permute-start | bytes 98312 | tf_op jit(solution)/shard_map/ppermute | solution.py:36
  (9 other events, 5.6 us)

commit v11 on v10

--- a/solution.py
+++ b/solution.py
@@ -17,11 +17,10 @@
 
 def faces(block, lead):
     ny = block.shape[-1]
-    ends = (lax.broadcasted_iota(jnp.int32, (2, ny), 1) == jnp.array([[0], [ny - 1]])).astype(jnp.float32)
-    letters = "cxzy"[1 - lead :]
-    columns = jnp.einsum(
-        letters + ",ky->k" + letters[:-3] + "zx", block, ends, precision=lax.Precision.HIGHEST
-    )
+    lane = lax.broadcasted_iota(jnp.int32, block.shape, block.ndim - 1)
+    columns = [
+        jnp.swapaxes(jnp.sum(jnp.where(lane == y, block, 0.0), axis=-1), -1, -2) for y in (0, ny - 1)
+    ]
     out = []
     for axis, dim in (("gx", lead), ("gz", lead + 1), ("gy", None)):
         count = lax.axis_size(axis)

time: 122 us -> 122 us (level)
  waiting for transfers between devices: 6.98 us -> 16.2 us
  matrix products: 16.8 us -> 9.04 us
  starting transfers between devices: 53.5 us -> 48.7 us
  other arithmetic: 0.85 us -> 4.39 us
    dot_general x2 -> x0, matrix products: 7.75 us -> none  [faces(): jnp.einsum(letters + ',ky->k' + letters[:-3] + 'zx', block, ends, precisi...]
    all_to_all x1, waiting for transfers between devices: 5.45 us -> 12.3 us  [body(): lax.all_to_all(partial_sample.reshape(rows, per_row, -1), 'gx', split_axi...]
    ppermute x6, starting transfers between devices: 20.2 us -> 14.4 us  [faces(): lax.ppermute(last, axis, forward)]
    ppermute x6, waiting for transfers between devices: 0.02 us -> 3.86 us  [faces(): lax.ppermute(first, axis, backward)]
    reduce_sum x0 -> x2, other arithmetic: none -> 3.53 us  [faces(): jnp.sum(jnp.where(lane == y, block, 0.0), axis=-1)]
    pallas_call x1 -> x0, local copies, waits for them, and re-layouts: 1.84 us -> none  [stencil(): vmem_call(viscosity_kernel, jax.ShapeDtypeStruct(velocity.shape[1:], jnp....]
    ppermute x6, waiting for transfers between devices: 1.5 us -> 0.02 us  [faces(): lax.ppermute(last, axis, forward)]
  transfers between devices with their start and end apart: 18 -> 18, of which waited for: 2 -> 2; matrix products, arithmetic and copies ran while one was open for 14% -> 10% of each run, Pallas kernels for 9% -> 10%
where the time goes in v11:
time: 122 us; the launch traced here: 120 us
  starting transfers between devices  48.7 us (40%)
  Pallas kernels  26.4 us (22%)
  waiting for transfers between devices  16.2 us (13%)
  local copies, waits for them, and re-layouts  10.7 us (9%)
  matrix products  9.04 us (7%)
  between operations  4.95 us (4%)
  other arithmetic  4.39 us (4%)
    pallas_call x1, Pallas kernels, stencil(): vmem_call(advance_kernel, jax.ShapeDtypeStruct(velocity.shape, jnp.float3...  15 us
    ppermute x6, starting transfers between devices, faces(): lax.ppermute(last, axis, forward)  14.4 us
    all_to_all x1, waiting for transfers between devices, body(): lax.all_to_all(partial_sample.reshape(rows, per_row, -1), 'gx', split_axi...  12.3 us
    pallas_call x1, Pallas kernels, stencil(): vmem_call(viscosity_kernel, jax.ShapeDtypeStruct(velocity.shape[1:], jnp....  11.4 us
    ppermute x6, starting transfers between devices, faces(): lax.ppermute(first, axis, backward)  10.3 us
    all_to_all x1, starting transfers between devices, body(): lax.all_to_all(partial_sample.reshape(rows, per_row, -1), 'gx', split_axi...  9.98 us
    ppermute x4, starting transfers between devices, body(): owned = owned + lax.ppermute(owned, axis, pairs)  8.9 us
    all_to_all x1, starting transfers between devices, body(): lax.all_to_all(jnp.broadcast_to(owned_force[None], (rows,) + owned_force....  5.16 us
  transfers between devices with their start and end apart: 18, of which 2 were waited for; matrix products, arithmetic and copies ran while one was open for 10% of the time, Pallas kernels for 10%

profile of v11, /device:TPU:1, one launch (start us, length us, event | category | flops | bytes accessed | tf_op | source)
XLA Modules:
  0.0 120.4 jit_solution(11749462078662282445)
XLA Ops:
  0.6 1.3 %fusion.18 = (s32[1,1,1,1]{3,2,1,0:T(1,128)}, s32[1,1,1,1]{3,2,1,0:T(1,128)}) fusion(s32[1,1,1,2]{3,2,1,0:T(1,128)} %param.7), kind=kLoop, calls=%fused_computation.33 | loop fusion | bytes 16 | tf_op jit(solution)/shard_map/slice | solution.py:141
  6.7 4.7 %fusion.2 = f32[2,3,384]{2,1,0:T(4,128)S(1)} fusion(bf16[1,1,1,2,384,4096]{5,4,3,2,1,0:T(8,128)(2,1)} %param.8, bf16[1,3,4096]{2,1,0:T(4,128)(2,1)S(1)} %stack.10, bf16[1,3,4096]{2,1,0:T(4,128)(2,1)S(1)} %stack.9), kind=kOutput, calls=%fused_computation.2 | convolution fusion | flops 18972672 | bytes 6349824 | tf_op jit(solution)/shard_map/spq,scq->scp/dot_general | solution.py:143
  12.7 10.0 %all-to-all-start = ((f32[16,4,1152]{2,1,0:T(4,128)}), f32[16,4,1152]{2,1,0:T(4,128)S(1)}, u32[]{:S(2)}, u32[]{:S(2)}) async-start(f32[16,4,1152]{2,1,0:T(4,128)} %copy.31), calls=%async_computation | async-start | bytes 589824 | tf_op jit(solution)/shard_map/all_to_all | solution.py:157
  22.7 12.3 %all-to-all-done = f32[16,4,1152]{2,1,0:T(4,128)S(1)} async-done(((f32[16,4,1152]{2,1,0:T(4,128)}), f32[16,4,1152]{2,1,0:T(4,128)S(1)}, u32[]{:S(2)}, u32[]{:S(2)}) %all-to-all-start) | async-done | bytes 294944 | tf_op jit(solution)/shard_map/all_to_all | solution.py:157
  36.3 1.7 %select_reduce_fusion = (f32[3,64,32]{2,1,0:T(8,128)S(1)}, f32[3,64,32]{2,1,0:T(8,128)S(1)}) fusion(f32[3,64,32,128]{3,2,1,0:T(8,128)S(1)} %copy-done, pred[128]{0:T(512)(128)(4,1)S(1)} %get-tuple-element.20, pred[128]{0:T(512)(128)(4,1)S(1)} %get-tuple-element.21), kind=kLoop, calls=%fused_computation.4 | loop fusion | flops 3133440 | bytes 3195136 | tf_op jit(solution)/shard_map/reduce_sum | solution.py:22
  38.7 2.2 %collective-permute-start.4 = (f32[3,32,64]{2,1,0:T(8,128)}, f32[3,32,64]{2,1,0:T(8,128)S(1)}, u32[]{:S(2)}, u32[]{:S(2)}) collective-permute-start(f32[3,32,64]{2,1,0:T(8,128)} %bitcast.5), channel_id=1, source_target_pairs={{0,4},{4,8},{8,12},{1,5},{5,9},{9,13},{2,6},{6,10},{10,14},{3,7},{... | collective-permute-start | bytes 73736 | tf_op jit(solution)/shard_map/ppermute | solution.py:35
  40.9 2.8 %collective-permute-start.13 = (f32[4,1152]{1,0:T(4,128)S(1)}, f32[4,1152]{1,0:T(4,128)S(1)}, u32[]{:S(2)}, u32[]{:S(2)}) collective-permute-start(f32[4,1152]{1,0:T(4,128)S(1)} %add.35), channel_id=1, source_target_pairs={{0,8},{4,12},{8,0},{12,4},{1,9},{5,13},{9,1},{13,5},{2,10},{6,14},... | collective-permute-start | bytes 55304 | tf_op jit(solution)/shard_map/ppermute | solution.py:166
  44.6 3.2 %collective-permute-start.2 = (f32[3,64,128]{2,1,0:T(8,128)}, f32[3,64,128]{2,1,0:T(8,128)S(1)}, u32[]{:S(2)}, u32[]{:S(2)}) collective-permute-start(f32[3,64,128]{2,1,0:T(8,128)} %bitcast.3), channel_id=1, source_target_pairs={{0,1},{1,2},{2,3},{4,5},{5,6},{6,7},{8,9},{9,10},{10,11},{12,13},{... | collective-permute-start | bytes 294920 | tf_op jit(solution)/shard_map/ppermute | solution.py:35
  47.8 1.3 %collective-permute-start.3 = (f32[3,64,128]{2,1,0:T(8,128)}, f32[3,64,128]{2,1,0:T(8,128)S(1)}, u32[]{:S(2)}, u32[]{:S(2)}) collective-permute-start(f32[3,64,128]{2,1,0:T(8,128)} %bitcast.4), channel_id=1, source_target_pairs={{1,0},{2,1},{3,2},{5,4},{6,5},{7,6},{9,8},{10,9},{11,10},{13,12},{... | collective-permute-start | bytes 294920 | tf_op jit(solution)/shard_map/ppermute | solution.py:35
  49.1 2.2 %collective-permute-start.14 = (f32[4,1152]{1,0:T(4,128)S(1)}, f32[4,1152]{1,0:T(4,128)S(1)}, u32[]{:S(2)}, u32[]{:S(2)}) collective-permute-start(f32[4,1152]{1,0:T(4,128)S(1)} %add.36), channel_id=1, source_target_pairs={{0,1},{1,0},{2,3},{3,2},{4,5},{5,4},{6,7},{7,6},{8,9},{9,8},{10,11... | collective-permute-start | bytes 55304 | tf_op jit(solution)/shard_map/ppermute | solution.py:166
  51.9 3.2 %collective-permute-start.1 = (f32[3,32,128]{2,1,0:T(8,128)}, f32[3,32,128]{2,1,0:T(8,128)S(1)}, u32[]{:S(2)}, u32[]{:S(2)}) collective-permute-start(f32[3,32,128]{2,1,0:T(8,128)} %get-tuple-element.12), channel_id=1, source_target_pairs={{16,0},{32,16},{48,32},{64,48},{80,64},{96,80},{112,96},{128,112},... | collective-permute-start | bytes 147464 | tf_op jit(solution)/shard_map/ppermute | solution.py:35
  55.1 2.4 %collective-permute-start = (f32[3,32,128]{2,1,0:T(8,128)}, f32[3,32,128]{2,1,0:T(8,128)S(1)}, u32[]{:S(2)}, u32[]{:S(2)}) collective-permute-start(f32[3,32,128]{2,1,0:T(8,128)} %get-tuple-element.13), channel_id=1, source_target_pairs={{0,16},{16,32},{32,48},{48,64},{64,80},{80,96},{96,112},{112,128},... | collective-permute-start | bytes 147464 | tf_op jit(solution)/shard_map/ppermute | solution.py:35
  58.9 3.9 %collective-permute-done.5.yhi = f32[3,32,64]{2,1,0:T(8,128)S(1)} collective-permute-done((f32[3,32,64]{2,1,0:T(8,128)S(1)}, f32[3,32,64]{2,1,0:T(8,128)S(1)}, u32[]{:S(2)}, u32[]{:S(2)}) %collective-permute-start.5) | collective-permute-done | bytes 24608 | tf_op jit(solution)/shard_map/ppermute | solution.py:35
  62.8 2.6 %collective-permute-start.15 = (f32[4,1152]{1,0:T(4,128)S(1)}, f32[4,1152]{1,0:T(4,128)S(1)}, u32[]{:S(2)}, u32[]{:S(2)}) collective-permute-start(f32[4,1152]{1,0:T(4,128)S(1)} %add.37), channel_id=1, source_target_pairs={{0,2},{1,3},{2,0},{3,1},{4,6},{5,7},{6,4},{7,5},{8,10},{9,11},{10,... | collective-permute-start | bytes 55304 | tf_op jit(solution)/shard_map/ppermute | solution.py:166
  66.7 11.4 %shard_map.68.nu = f32[64,32,128]{2,1,0:T(8,128)} custom-call(f32[3,64,32,128]{3,2,1,0:T(8,128)} %u.3, f32[3,32,128]{2,1,0:T(8,128)} %copy-done.6, f32[3,32,128]{2,1,0:T(8,128)} %copy-done.5, f32[3,64,128]{2,1,0:T(8,128)} %copy-done.2, f32[3,64,128]{2,1,0:T(8,128)} %copy-done.3, f32[3,32,64]{2,1,0:T(8,128)} %copy-done.4, f32[3,32,64]{2,1,0:T(8,128)} %copy-done.7), custom_call_target="tpu_custom_call" | custom-call | tf_op jit(solution)/shard_map/pallas_call | solution.py:119
  79.7 5.2 %all-to-all-start.1 = ((f32[16,4,1152]{2,1,0:T(4,128)}), f32[16,4,1152]{2,1,0:T(4,128)S(1)}, u32[]{:S(2)}, u32[]{:S(2)}) async-start(f32[16,4,1152]{2,1,0:T(4,128)} %broadcast_in_dim.20), calls=%async_computation.1 | async-start | bytes 589824 | tf_op jit(solution)/shard_map/all_to_all | solution.py:170
  85.6 2.0 %collective-permute-start.7 = (f32[32,128]{1,0:T(8,128)S(1)}, f32[32,128]{1,0:T(8,128)S(1)}, u32[]{:S(2)}, u32[]{:S(2)}) collective-permute-start(f32[32,128]{1,0:T(8,128)S(1)} %get-tuple-element.16), channel_id=1, source_target_pairs={{16,0},{32,16},{48,32},{64,48},{80,64},{96,80},{112,96},{128,112},... | collective-permute-start | bytes 49160 | tf_op jit(solution)/shard_map/ppermute | solution.py:35
  87.6 3.6 %collective-permute-start.6 = (f32[32,128]{1,0:T(8,128)S(1)}, f32[32,128]{1,0:T(8,128)S(1)}, u32[]{:S(2)}, u32[]{:S(2)}) collective-permute-start(f32[32,128]{1,0:T(8,128)S(1)} %get-tuple-element.17), channel_id=1, source_target_pairs={{0,16},{16,32},{32,48},{48,64},{64,80},{80,96},{96,112},{112,128},... | collective-permute-start | bytes 49160 | tf_op jit(solution)/shard_map/ppermute | solution.py:35
  91.1 1.8 %select_reduce_fusion.2 = (f32[64,32]{1,0:T(8,128)S(1)}, f32[64,32]{1,0:T(8,128)S(1)}) fusion(f32[64,32,128]{2,1,0:T(8,128)} %shard_map.68.nu, pred[128]{0:T(512)(128)(4,1)S(1)} %get-tuple-element.20, pred[128]{0:T(512)(128)(4,1)S(1)} %get-tuple-element.21), kind=kLoop, calls=%fused_computation.7 | loop fusion | flops 1044480 | bytes 1065216 | tf_op jit(solution)/shard_map/reduce_sum | solution.py:22
  93.1 1.3 %collective-permute-start.10 = (f32[32,64]{1,0:T(8,128)S(1)}, f32[32,64]{1,0:T(8,128)S(1)}, u32[]{:S(2)}, u32[]{:S(2)}) collective-permute-start(f32[32,64]{1,0:T(8,128)S(1)} %bitcast.52), channel_id=1, source_target_pairs={{0,4},{4,8},{8,12},{1,5},{5,9},{9,13},{2,6},{6,10},{10,14},{3,7},{... | collective-permute-start | bytes 24584 | tf_op jit(solution)/shard_map/ppermute | solution.py:35
  96.8 1.8 %collective-permute-start.8 = (f32[64,128]{1,0:T(8,128)S(1)}, f32[64,128]{1,0:T(8,128)S(1)}, u32[]{:S(2)}, u32[]{:S(2)}) collective-permute-start(f32[64,128]{1,0:T(8,128)S(1)} %bitcast.50), channel_id=1, source_target_pairs={{0,1},{1,2},{2,3},{4,5},{5,6},{6,7},{8,9},{9,10},{10,11},{12,13},{... | collective-permute-start | bytes 98312 | tf_op jit(solution)/shard_map/ppermute | solution.py:35
  99.0 1.3 %collective-permute-start.9 = (f32[64,128]{1,0:T(8,128)S(1)}, f32[64,128]{1,0:T(8,128)S(1)}, u32[]{:S(2)}, u32[]{:S(2)}) collective-permute-start(f32[64,128]{1,0:T(8,128)S(1)} %bitcast.49), channel_id=1, source_target_pairs={{1,0},{2,1},{3,2},{5,4},{6,5},{7,6},{9,8},{10,9},{11,10},{13,12},{... | collective-permute-start | bytes 98312 | tf_op jit(solution)/shard_map/ppermute | solution.py:35
  100.3 3.7 %fusion = f32[2,3,4096]{2,1,0:T(4,128)S(1)} fusion(bf16[2,3,384]{2,1,0:T(4,128)(2,1)S(1)} %reshape.71, bf16[1,1,1,2,384,4096]{5,4,3,2,1,0:T(8,128)(2,1)} %param.8), kind=kOutput, calls=%fused_computation | convolution fusion | flops 18874368 | bytes 6394368 | tf_op jit(solution)/shard_map/axz,ahx->ahz/dot_general | solution.py:175
  105.4 15.0 %shard_map.69 = f32[3,64,32,128]{3,2,1,0:T(8,128)} custom-call(s32[2]{0:T(128)} %bitcast.53, f32[3,64,32,128]{3,2,1,0:T(8,128)} %u.3, f32[3,32,128]{2,1,0:T(8,128)} %copy-done.6, f32[3,32,128]{2,1,0:T(8,128)} %copy-done.5, f32[3,64,128]{2,1,0:T(8,128)} %copy-done.2, f32[3,64,128]{2,1,0:T(8,128)} %copy-done.3, f32[3,32,64]{2,1,0:T(8,128)} %copy-done.4, ...), custom_call_target="tpu_custom_call" | custom-call | tf_op jit(solution)/shard_map/pallas_call | solution.py:123
  (79 shorter events, 14.8 us)
Async XLA Ops:
  6.7 4.7 %copy-start.14 = (s32[1,1,1,2]{3,2,1,0:T(1,128)S(1)}, s32[1,1,1,2]{3,2,1,0:T(1,128)}, u32[]{:S(2)}) copy-start(s32[1,1,1,2]{3,2,1,0:T(1,128)} %param.6) | copy-start | bytes 28
  6.7 29.6 %copy-start = (f32[3,64,32,128]{3,2,1,0:T(8,128)S(1)}, f32[3,64,32,128]{3,2,1,0:T(8,128)}, u32[]{:S(2)}) copy-start(f32[3,64,32,128]{3,2,1,0:T(8,128)} %u.3) | copy-start | bytes 9437188
  12.7 22.3 %all-to-all-start = ((f32[16,4,1152]{2,1,0:T(4,128)}), f32[16,4,1152]{2,1,0:T(4,128)S(1)}, u32[]{:S(2)}, u32[]{:S(2)}) async-start(f32[16,4,1152]{2,1,0:T(4,128)} %copy.31), calls=%async_computation | async-start | bytes 589824 | tf_op jit(solution)/shard_map/all_to_all | solution.py:157
  35.0 5.9 %collective-permute-start.12 = (f32[4,1152]{1,0:T(4,128)S(1)}, f32[4,1152]{1,0:T(4,128)S(1)}, u32[]{:S(2)}, u32[]{:S(2)}) collective-permute-start(f32[4,1152]{1,0:T(4,128)S(1)} %reduce_sum.58), channel_id=1, source_target_pairs={{0,4},{4,0},{8,12},{12,8},{1,5},{5,1},{9,13},{13,9},{2,6},{6,2},{1... | collective-permute-start | bytes 55304 | tf_op jit(solution)/shard_map/ppermute | solution.py:166
  38.7 16.3 %collective-permute-start.4 = (f32[3,32,64]{2,1,0:T(8,128)}, f32[3,32,64]{2,1,0:T(8,128)S(1)}, u32[]{:S(2)}, u32[]{:S(2)}) collective-permute-start(f32[3,32,64]{2,1,0:T(8,128)} %bitcast.5), channel_id=1, source_target_pairs={{0,4},{4,8},{8,12},{1,5},{5,9},{9,13},{2,6},{6,10},{10,14},{3,7},{... | collective-permute-start | bytes 73736 | tf_op jit(solution)/shard_map/ppermute | solution.py:35
  40.9 8.1 %collective-permute-start.13 = (f32[4,1152]{1,0:T(4,128)S(1)}, f32[4,1152]{1,0:T(4,128)S(1)}, u32[]{:S(2)}, u32[]{:S(2)}) collective-permute-start(f32[4,1152]{1,0:T(4,128)S(1)} %add.35), channel_id=1, source_target_pairs={{0,8},{4,12},{8,0},{12,4},{1,9},{5,13},{9,1},{13,5},{2,10},{6,14},... | collective-permute-start | bytes 55304 | tf_op jit(solution)/shard_map/ppermute | solution.py:166
  44.6 20.8 %collective-permute-start.2 = (f32[3,64,128]{2,1,0:T(8,128)}, f32[3,64,128]{2,1,0:T(8,128)S(1)}, u32[]{:S(2)}, u32[]{:S(2)}) collective-permute-start(f32[3,64,128]{2,1,0:T(8,128)} %bitcast.3), channel_id=1, source_target_pairs={{0,1},{1,2},{2,3},{4,5},{5,6},{6,7},{8,9},{9,10},{10,11},{12,13},{... | collective-permute-start | bytes 294920 | tf_op jit(solution)/shard_map/ppermute | solution.py:35
  47.8 17.6 %collective-permute-start.3 = (f32[3,64,128]{2,1,0:T(8,128)}, f32[3,64,128]{2,1,0:T(8,128)S(1)}, u32[]{:S(2)}, u32[]{:S(2)}) collective-permute-start(f32[3,64,128]{2,1,0:T(8,128)} %bitcast.4), channel_id=1, source_target_pairs={{1,0},{2,1},{3,2},{5,4},{6,5},{7,6},{9,8},{10,9},{11,10},{13,12},{... | collective-permute-start | bytes 294920 | tf_op jit(solution)/shard_map/ppermute | solution.py:35
  49.1 8.5 %collective-permute-start.14 = (f32[4,1152]{1,0:T(4,128)S(1)}, f32[4,1152]{1,0:T(4,128)S(1)}, u32[]{:S(2)}, u32[]{:S(2)}) collective-permute-start(f32[4,1152]{1,0:T(4,128)S(1)} %add.36), channel_id=1, source_target_pairs={{0,1},{1,0},{2,3},{3,2},{4,5},{5,4},{6,7},{7,6},{8,9},{9,8},{10,11... | collective-permute-start | bytes 55304 | tf_op jit(solution)/shard_map/ppermute | solution.py:166
  51.9 13.5 %collective-permute-start.1 = (f32[3,32,128]{2,1,0:T(8,128)}, f32[3,32,128]{2,1,0:T(8,128)S(1)}, u32[]{:S(2)}, u32[]{:S(2)}) collective-permute-start(f32[3,32,128]{2,1,0:T(8,128)} %get-tuple-element.12), channel_id=1, source_target_pairs={{16,0},{32,16},{48,32},{64,48},{80,64},{96,80},{112,96},{128,112},... | collective-permute-start | bytes 147464 | tf_op jit(solution)/shard_map/ppermute | solution.py:35
  55.1 10.3 %copy-start.4 = (f32[3,32,64]{2,1,0:T(8,128)}, f32[3,32,64]{2,1,0:T(8,128)S(1)}, u32[]{:S(2)}) copy-start(f32[3,32,64]{2,1,0:T(8,128)S(1)} %collective-permute-done.4.ylo) | copy-start | bytes 73732
  55.1 10.3 %collective-permute-start = (f32[3,32,128]{2,1,0:T(8,128)}, f32[3,32,128]{2,1,0:T(8,128)S(1)}, u32[]{:S(2)}, u32[]{:S(2)}) collective-permute-start(f32[3,32,128]{2,1,0:T(8,128)} %get-tuple-element.13), channel_id=1, source_target_pairs={{0,16},{16,32},{32,48},{48,64},{64,80},{80,96},{96,112},{112,128},... | collective-permute-start | bytes 147464 | tf_op jit(solution)/shard_map/ppermute | solution.py:35
  57.6 5.2 %collective-permute-start.5 = (f32[3,32,64]{2,1,0:T(8,128)S(1)}, f32[3,32,64]{2,1,0:T(8,128)S(1)}, u32[]{:S(2)}, u32[]{:S(2)}) collective-permute-start(f32[3,32,64]{2,1,0:T(8,128)S(1)} %bitcast.48), channel_id=1, source_target_pairs={{4,0},{8,4},{12,8},{5,1},{9,5},{13,9},{6,2},{10,6},{14,10},{7,3},{... | collective-permute-start | bytes 73736 | tf_op jit(solution)/shard_map/ppermute | solution.py:35
  62.7 2.7 %copy-start.7 = (f32[3,32,64]{2,1,0:T(8,128)}, f32[3,32,64]{2,1,0:T(8,128)S(1)}, u32[]{:S(2)}) copy-start(f32[3,32,64]{2,1,0:T(8,128)S(1)} %collective-permute-done.5.yhi) | copy-start | bytes 73732
  62.8 15.4 %collective-permute-start.15 = (f32[4,1152]{1,0:T(4,128)S(1)}, f32[4,1152]{1,0:T(4,128)S(1)}, u32[]{:S(2)}, u32[]{:S(2)}) collective-permute-start(f32[4,1152]{1,0:T(4,128)S(1)} %add.37), channel_id=1, source_target_pairs={{0,2},{1,3},{2,0},{3,1},{4,6},{5,7},{6,4},{7,5},{8,10},{9,11},{10,... | collective-permute-start | bytes 55304 | tf_op jit(solution)/shard_map/ppermute | solution.py:166
  79.7 18.9 %all-to-all-start.1 = ((f32[16,4,1152]{2,1,0:T(4,128)}), f32[16,4,1152]{2,1,0:T(4,128)S(1)}, u32[]{:S(2)}, u32[]{:S(2)}) async-start(f32[16,4,1152]{2,1,0:T(4,128)} %broadcast_in_dim.20), calls=%async_computation.1 | async-start | bytes 589824 | tf_op jit(solution)/shard_map/all_to_all | solution.py:170
  85.6 19.2 %collective-permute-start.7 = (f32[32,128]{1,0:T(8,128)S(1)}, f32[32,128]{1,0:T(8,128)S(1)}, u32[]{:S(2)}, u32[]{:S(2)}) collective-permute-start(f32[32,128]{1,0:T(8,128)S(1)} %get-tuple-element.16), channel_id=1, source_target_pairs={{16,0},{32,16},{48,32},{64,48},{80,64},{96,80},{112,96},{128,112},... | collective-permute-start | bytes 49160 | tf_op jit(solution)/shard_map/ppermute | solution.py:35
  87.6 17.2 %collective-permute-start.6 = (f32[32,128]{1,0:T(8,128)S(1)}, f32[32,128]{1,0:T(8,128)S(1)}, u32[]{:S(2)}, u32[]{:S(2)}) collective-permute-start(f32[32,128]{1,0:T(8,128)S(1)} %get-tuple-element.17), channel_id=1, source_target_pairs={{0,16},{16,32},{32,48},{48,64},{64,80},{80,96},{96,112},{112,128},... | collective-permute-start | bytes 49160 | tf_op jit(solution)/shard_map/ppermute | solution.py:35
  93.1 5.9 %collective-permute-start.10 = (f32[32,64]{1,0:T(8,128)S(1)}, f32[32,64]{1,0:T(8,128)S(1)}, u32[]{:S(2)}, u32[]{:S(2)}) collective-permute-start(f32[32,64]{1,0:T(8,128)S(1)} %bitcast.52), channel_id=1, source_target_pairs={{0,4},{4,8},{8,12},{1,5},{5,9},{9,13},{2,6},{6,10},{10,14},{3,7},{... | collective-permute-start | bytes 24584 | tf_op jit(solution)/shard_map/ppermute | solution.py:35
  94.4 10.3 %collective-permute-start.11 = (f32[32,64]{1,0:T(8,128)S(1)}, f32[32,64]{1,0:T(8,128)S(1)}, u32[]{:S(2)}, u32[]{:S(2)}) collective-permute-start(f32[32,64]{1,0:T(8,128)S(1)} %bitcast.51), channel_id=1, source_target_pairs={{4,0},{8,4},{12,8},{5,1},{9,5},{13,9},{6,2},{10,6},{14,10},{7,3},{... | collective-permute-start | bytes 24584 | tf_op jit(solution)/shard_map/ppermute | solution.py:35
  96.8 8.0 %collective-permute-start.8 = (f32[64,128]{1,0:T(8,128)S(1)}, f32[64,128]{1,0:T(8,128)S(1)}, u32[]{:S(2)}, u32[]{:S(2)}) collective-permute-start(f32[64,128]{1,0:T(8,128)S(1)} %bitcast.50), channel_id=1, source_target_pairs={{0,1},{1,2},{2,3},{4,5},{5,6},{6,7},{8,9},{9,10},{10,11},{12,13},{... | collective-permute-start | bytes 98312 | tf_op jit(solution)/shard_map/ppermute | solution.py:35
  98.7 5.3 %copy-start.1 = (f32[64,1152]{1,0:T(8,128)}, f32[64,1152]{1,0:T(8,128)S(1)}, u32[]{:S(2)}) copy-start(f32[64,1152]{1,0:T(8,128)S(1)} %reshape.70) | copy-start | bytes 884740
  99.0 5.0 %copy-start.12 = (f32[32,64]{1,0:T(8,128)}, f32[32,64]{1,0:T(8,128)S(1)}, u32[]{:S(2)}) copy-start(f32[32,64]{1,0:T(8,128)S(1)} %collective-permute-done.10.nylo) | copy-start | bytes 24580
  99.0 5.8 %collective-permute-start.9 = (f32[64,128]{1,0:T(8,128)S(1)}, f32[64,128]{1,0:T(8,128)S(1)}, u32[]{:S(2)}, u32[]{:S(2)}) collective-permute-start(f32[64,128]{1,0:T(8,128)S(1)} %bitcast.49), channel_id=1, source_target_pairs={{1,0},{2,1},{3,2},{5,4},{6,5},{7,6},{9,8},{10,9},{11,10},{13,12},{... | collective-permute-start | bytes 98312 | tf_op jit(solution)/shard_map/ppermute | solution.py:35
  (9 other events, 5.5 us)

commit v12 on v11

--- a/solution.py
+++ b/solution.py
@@ -114,8 +114,7 @@
     )
 
 
-def stencil(velocity, planes, sent):
-    u_faces = faces(velocity, 1)
+def stencil(velocity, planes, sent, u_faces):
     nu = vmem_call(
         viscosity_kernel, jax.ShapeDtypeStruct(velocity.shape[1:], jnp.float32), 7
     )(velocity, *u_faces)
@@ -152,6 +151,8 @@
         block_local.reshape(tile_count, -1),
         precision=lax.Precision.HIGHEST,
     )
+    u_faces = faces(velocity, 1)
+    partial_sample, u_faces = lax.optimization_barrier((partial_sample, u_faces))
     rows = lax.axis_size("gx")
     per_row = nturb // rows
     received = lax.all_to_all(
@@ -178,7 +179,7 @@
         tile_force.reshape(tile_count, 3, actuator_count),
         preferred_element_type=jnp.float32,
     ).reshape(tile_count, 3, vertical_coord, spanwise_coord)
-    predicted = stencil(velocity[:, :, :, :], rotor_planes, forces_sent)
+    predicted = stencil(velocity, rotor_planes, forces_sent, u_faces)
     return (predicted, forces)
 
 

time: 122 us -> 131 us (1.074)
  blocking collectives: 0 us -> 20.5 us
  waiting for transfers between devices: 16.2 us -> 8.61 us
  starting transfers between devices: 48.7 us -> 44.3 us
  local copies, waits for them, and re-layouts: 10.7 us -> 8.27 us
  other arithmetic: 4.39 us -> 6.28 us
    all_to_all x0 -> x1, blocking collectives: none -> 20.5 us  [body(): lax.all_to_all(partial_sample.reshape(rows, per_row, -1), 'gx', split_axi...]
    all_to_all x1 -> x0, waiting for transfers between devices: 12.3 us -> none  [body(): lax.all_to_all(partial_sample.reshape(rows, per_row, -1), 'gx', split_axi...]
    all_to_all x1 -> x0, starting transfers between devices: 9.98 us -> none  [body(): lax.all_to_all(partial_sample.reshape(rows, per_row, -1), 'gx', split_axi...]
    ppermute x4, waiting for transfers between devices: 0.01 us -> 3.67 us  [body(): owned = owned + lax.ppermute(owned, axis, pairs)]
    ppermute x6, starting transfers between devices: 14.4 us -> 16.4 us  [faces(): lax.ppermute(last, axis, forward)]
    ppermute x6, starting transfers between devices: 10.3 us -> 12.3 us  [faces(): lax.ppermute(first, axis, backward)]
    reduce_sum x2, other arithmetic: 3.53 us -> 5.44 us  [faces(): jnp.sum(jnp.where(lane == y, block, 0.0), axis=-1)]
  transfers between devices with their start and end apart: 18 -> 17, of which waited for: 2 -> 4; matrix products, arithmetic and copies ran while one was open for 10% -> 16% of each run, Pallas kernels for 10% -> 9%
where the time goes in v12:
time: 131 us; the launch traced here: 128 us
  starting transfers between devices  44.3 us (34%)
  Pallas kernels  26.4 us (20%)
  blocking collectives  20.5 us (16%)
  matrix products  8.85 us (7%)
  waiting for transfers between devices  8.61 us (7%)
  local copies, waits for them, and re-layouts  8.27 us (6%)
  other arithmetic  6.28 us (5%)
  between operations  4.95 us (4%)
    all_to_all x1, blocking collectives, body(): lax.all_to_all(partial_sample.reshape(rows, per_row, -1), 'gx', split_axi...  20.5 us
    ppermute x6, starting transfers between devices, faces(): lax.ppermute(last, axis, forward)  16.4 us
    pallas_call x1, Pallas kernels, stencil(): vmem_call(advance_kernel, jax.ShapeDtypeStruct(velocity.shape, jnp.float3...  15 us
    ppermute x6, starting transfers between devices, faces(): lax.ppermute(first, axis, backward)  12.3 us
    pallas_call x1, Pallas kernels, stencil(): vmem_call(viscosity_kernel, jax.ShapeDtypeStruct(velocity.shape[1:], jnp....  11.4 us
    ppermute x4, starting transfers between devices, body(): owned = owned + lax.ppermute(owned, axis, pairs)  9.46 us
    all_to_all x1, starting transfers between devices, body(): lax.all_to_all(jnp.broadcast_to(owned_force[None], (rows,) + owned_force....  6.11 us
    reduce_sum x2, other arithmetic, faces(): jnp.sum(jnp.where(lane == y, block, 0.0), axis=-1)  5.44 us
  transfers between devices with their start and end apart: 17, of which 4 were waited for; matrix products, arithmetic and copies ran while one was open for 16% of the time, Pallas kernels for 9%

profile of v12, /device:TPU:1, one launch (start us, length us, event | category | flops | bytes accessed | tf_op | source)
XLA Modules:
  0.0 128.2 jit_solution(11292494472189226482)
XLA Ops:
  1.5 5.1 %collective-permute-start.1 = (f32[3,32,128]{2,1,0:T(8,128)S(1)}, f32[3,32,128]{2,1,0:T(8,128)S(1)}, u32[]{:S(2)}, u32[]{:S(2)}) collective-permute-start(f32[3,32,128]{2,1,0:T(8,128)S(1)} %get-tuple-element.24), channel_id=1, source_target_pairs={{16,0},{32,16},{48,32},{64,48},{80,64},{96,80},{112,96},{128,112},... | collective-permute-start | bytes 147464 | tf_op jit(solution)/shard_map/ppermute | solution.py:35
  6.6 1.9 %collective-permute-start = (f32[3,32,128]{2,1,0:T(8,128)S(1)}, f32[3,32,128]{2,1,0:T(8,128)S(1)}, u32[]{:S(2)}, u32[]{:S(2)}) collective-permute-start(f32[3,32,128]{2,1,0:T(8,128)S(1)} %get-tuple-element.25), channel_id=1, source_target_pairs={{0,16},{16,32},{32,48},{48,64},{64,80},{80,96},{96,112},{112,128},... | collective-permute-start | bytes 147464 | tf_op jit(solution)/shard_map/ppermute | solution.py:35
  8.5 3.6 %select_reduce_fusion = (f32[3,64,32]{2,1,0:T(8,128)S(1)}, f32[3,64,32]{2,1,0:T(8,128)S(1)}) fusion(f32[3,64,32,128]{3,2,1,0:T(8,128)} %u.3, pred[128]{0:T(512)(128)(4,1)S(1)} %get-tuple-element.34, pred[128]{0:T(512)(128)(4,1)S(1)} %get-tuple-element.35), kind=kLoop, calls=%fused_computation.4 | loop fusion | flops 3133440 | bytes 3195136 | tf_op jit(solution)/shard_map/reduce_sum | solution.py:22
  12.2 2.9 %collective-permute-start.4 = (f32[3,32,64]{2,1,0:T(8,128)S(1)}, f32[3,32,64]{2,1,0:T(8,128)S(1)}, u32[]{:S(2)}, u32[]{:S(2)}) collective-permute-start(f32[3,32,64]{2,1,0:T(8,128)S(1)} %bitcast.56), channel_id=1, source_target_pairs={{0,4},{4,8},{8,12},{1,5},{5,9},{9,13},{2,6},{6,10},{10,14},{3,7},{... | collective-permute-start | bytes 73736 | tf_op jit(solution)/shard_map/ppermute | solution.py:35
  15.2 1.3 %collective-permute-start.5 = (f32[3,32,64]{2,1,0:T(8,128)S(1)}, f32[3,32,64]{2,1,0:T(8,128)S(1)}, u32[]{:S(2)}, u32[]{:S(2)}) collective-permute-start(f32[3,32,64]{2,1,0:T(8,128)S(1)} %bitcast.55), channel_id=1, source_target_pairs={{4,0},{8,4},{12,8},{5,1},{9,5},{13,9},{6,2},{10,6},{14,10},{7,3},{... | collective-permute-start | bytes 73736 | tf_op jit(solution)/shard_map/ppermute | solution.py:35
  16.5 1.5 %fusion.15 = (f32[3,64,1,128]{3,2,1,0:T(1,128)S(1)}, f32[3,64,1,128]{3,2,1,0:T(1,128)S(1)}) fusion(f32[3,64,32,128]{3,2,1,0:T(8,128)} %u.3), kind=kLoop, calls=%fused_computation.28 | loop fusion | bytes 393216 | tf_op jit(solution)/shard_map/slice | solution.py:33
  18.1 3.2 %collective-permute-start.2 = (f32[3,64,128]{2,1,0:T(8,128)S(1)}, f32[3,64,128]{2,1,0:T(8,128)S(1)}, u32[]{:S(2)}, u32[]{:S(2)}) collective-permute-start(f32[3,64,128]{2,1,0:T(8,128)S(1)} %bitcast.52), channel_id=1, source_target_pairs={{0,1},{1,2},{2,3},{4,5},{5,6},{6,7},{8,9},{9,10},{10,11},{12,13},{... | collective-permute-start | bytes 294920 | tf_op jit(solution)/shard_map/ppermute | solution.py:35
  26.7 4.5 %fusion.4 = f32[1,2,3,384]{3,2,1,0:T(4,128)S(1)} fusion(bf16[1,1,1,2,384,4096]{5,4,3,2,1,0:T(8,128)(2,1)} %param.8, bf16[1,3,4096]{2,1,0:T(4,128)(2,1)S(1)} %stack.10, bf16[1,3,4096]{2,1,0:T(4,128)(2,1)S(1)} %stack.9), kind=kOutput, calls=%fused_computation.7 | convolution fusion | flops 18972672 | bytes 6349824 | tf_op jit(solution)/shard_map/spq,scq->scp/dot_general | solution.py:142
  33.0 4.9 %collective-permute-done.3.zhi = f32[3,64,128]{2,1,0:T(8,128)S(1)} collective-permute-done((f32[3,64,128]{2,1,0:T(8,128)S(1)}, f32[3,64,128]{2,1,0:T(8,128)S(1)}, u32[]{:S(2)}, u32[]{:S(2)}) %collective-permute-start.3) | collective-permute-done | bytes 98336 | tf_op jit(solution)/shard_map/ppermute | solution.py:35
  38.0 20.5 %all_to_all.10 = f32[16,4,1152]{2,1,0:T(4,128)S(1)} all-to-all(f32[16,4,1152]{2,1,0:T(4,128)S(1)} %reshape.54), channel_id=1, replica_groups=mesh['gx'=16,'gy'=4,'gz'=4] {'gx'}, dimensions={0} | all-to-all | bytes 589824 | tf_op jit(solution)/shard_map/all_to_all | solution.py:158
  58.6 2.2 %collective-permute-start.12 = (f32[4,1152]{1,0:T(4,128)S(1)}, f32[4,1152]{1,0:T(4,128)S(1)}, u32[]{:S(2)}, u32[]{:S(2)}) collective-permute-start(f32[4,1152]{1,0:T(4,128)S(1)} %reduce_sum.58), channel_id=1, source_target_pairs={{0,4},{4,0},{8,12},{12,8},{1,5},{5,1},{9,13},{13,9},{2,6},{6,2},{1... | collective-permute-start | bytes 55304 | tf_op jit(solution)/shard_map/ppermute | solution.py:167
  61.9 3.4 %collective-permute-start.13 = (f32[4,1152]{1,0:T(4,128)S(1)}, f32[4,1152]{1,0:T(4,128)S(1)}, u32[]{:S(2)}, u32[]{:S(2)}) collective-permute-start(f32[4,1152]{1,0:T(4,128)S(1)} %add.31), channel_id=1, source_target_pairs={{0,8},{4,12},{8,0},{12,4},{1,9},{5,13},{9,1},{13,5},{2,10},{6,14},... | collective-permute-start | bytes 55304 | tf_op jit(solution)/shard_map/ppermute | solution.py:167
  66.5 1.3 %collective-permute-start.14 = (f32[4,1152]{1,0:T(4,128)S(1)}, f32[4,1152]{1,0:T(4,128)S(1)}, u32[]{:S(2)}, u32[]{:S(2)}) collective-permute-start(f32[4,1152]{1,0:T(4,128)S(1)} %add.32), channel_id=1, source_target_pairs={{0,1},{1,0},{2,3},{3,2},{4,5},{5,4},{6,7},{7,6},{8,9},{9,8},{10,11... | collective-permute-start | bytes 55304 | tf_op jit(solution)/shard_map/ppermute | solution.py:167
  67.8 1.3 %collective-permute-done.14 = f32[4,1152]{1,0:T(4,128)S(1)} collective-permute-done((f32[4,1152]{1,0:T(4,128)S(1)}, f32[4,1152]{1,0:T(4,128)S(1)}, u32[]{:S(2)}, u32[]{:S(2)}) %collective-permute-start.14) | collective-permute-done | bytes 18464 | tf_op jit(solution)/shard_map/ppermute | solution.py:167
  69.1 2.6 %collective-permute-start.15 = (f32[4,1152]{1,0:T(4,128)S(1)}, f32[4,1152]{1,0:T(4,128)S(1)}, u32[]{:S(2)}, u32[]{:S(2)}) collective-permute-start(f32[4,1152]{1,0:T(4,128)S(1)} %add.33), channel_id=1, source_target_pairs={{0,2},{1,3},{2,0},{3,1},{4,6},{5,7},{6,4},{7,5},{8,10},{9,11},{10,... | collective-permute-start | bytes 55304 | tf_op jit(solution)/shard_map/ppermute | solution.py:167
  71.7 11.4 %shard_map.68.nu = f32[64,32,128]{2,1,0:T(8,128)} custom-call(f32[3,64,32,128]{3,2,1,0:T(8,128)} %u.3, f32[3,32,128]{2,1,0:T(8,128)} %copy-done.4, f32[3,32,128]{2,1,0:T(8,128)} %copy-done.3, f32[3,64,128]{2,1,0:T(8,128)} %copy-done.1, f32[3,64,128]{2,1,0:T(8,128)} %copy-done.2, f32[3,32,64]{2,1,0:T(8,128)} %copy-done.5, f32[3,32,64]{2,1,0:T(8,128)} %copy-done.6), custom_call_target="tpu_custom_call" | custom-call | tf_op jit(solution)/shard_map/pallas_call | solution.py:118
  84.7 6.1 %all-to-all-start.1 = ((f32[16,4,1152]{2,1,0:T(4,128)}), f32[16,4,1152]{2,1,0:T(4,128)S(1)}, u32[]{:S(2)}, u32[]{:S(2)}) async-start(f32[16,4,1152]{2,1,0:T(4,128)} %broadcast_in_dim.20), calls=%async_computation.1 | async-start | bytes 589824 | tf_op jit(solution)/shard_map/all_to_all | solution.py:171
  91.6 2.1 %collective-permute-start.7 = (f32[32,128]{1,0:T(8,128)S(1)}, f32[32,128]{1,0:T(8,128)S(1)}, u32[]{:S(2)}, u32[]{:S(2)}) collective-permute-start(f32[32,128]{1,0:T(8,128)S(1)} %get-tuple-element.30), channel_id=1, source_target_pairs={{16,0},{32,16},{48,32},{64,48},{80,64},{96,80},{112,96},{128,112},... | collective-permute-start | bytes 49160 | tf_op jit(solution)/shard_map/ppermute | solution.py:35
  93.7 3.5 %collective-permute-start.6 = (f32[32,128]{1,0:T(8,128)S(1)}, f32[32,128]{1,0:T(8,128)S(1)}, u32[]{:S(2)}, u32[]{:S(2)}) collective-permute-start(f32[32,128]{1,0:T(8,128)S(1)} %get-tuple-element.31), channel_id=1, source_target_pairs={{0,16},{16,32},{32,48},{48,64},{64,80},{80,96},{96,112},{112,128},... | collective-permute-start | bytes 49160 | tf_op jit(solution)/shard_map/ppermute | solution.py:35
  97.2 1.8 %select_reduce_fusion.2 = (f32[64,32]{1,0:T(8,128)S(1)}, f32[64,32]{1,0:T(8,128)S(1)}) fusion(f32[64,32,128]{2,1,0:T(8,128)} %shard_map.68.nu, pred[128]{0:T(512)(128)(4,1)S(1)} %get-tuple-element.34, pred[128]{0:T(512)(128)(4,1)S(1)} %get-tuple-element.35), kind=kLoop, calls=%fused_computation.8 | loop fusion | flops 1044480 | bytes 1065216 | tf_op jit(solution)/shard_map/reduce_sum | solution.py:22
  99.1 3.6 %collective-permute-start.10 = (f32[32,64]{1,0:T(8,128)S(1)}, f32[32,64]{1,0:T(8,128)S(1)}, u32[]{:S(2)}, u32[]{:S(2)}) collective-permute-start(f32[32,64]{1,0:T(8,128)S(1)} %bitcast.61), channel_id=1, source_target_pairs={{0,4},{4,8},{8,12},{1,5},{5,9},{9,13},{2,6},{6,10},{10,14},{3,7},{... | collective-permute-start | bytes 24584 | tf_op jit(solution)/shard_map/ppermute | solution.py:35
  102.7 1.3 %collective-permute-start.11 = (f32[32,64]{1,0:T(8,128)S(1)}, f32[32,64]{1,0:T(8,128)S(1)}, u32[]{:S(2)}, u32[]{:S(2)}) collective-permute-start(f32[32,64]{1,0:T(8,128)S(1)} %bitcast.60), channel_id=1, source_target_pairs={{4,0},{8,4},{12,8},{5,1},{9,5},{13,9},{6,2},{10,6},{14,10},{7,3},{... | collective-permute-start | bytes 24584 | tf_op jit(solution)/shard_map/ppermute | solution.py:35
  108.1 3.7 %fusion = f32[2,3,4096]{2,1,0:T(4,128)S(1)} fusion(bf16[2,3,384]{2,1,0:T(4,128)(2,1)S(1)} %reshape.56, bf16[1,1,1,2,384,4096]{5,4,3,2,1,0:T(8,128)(2,1)} %param.8), kind=kOutput, calls=%fused_computation | convolution fusion | flops 18874368 | bytes 6394368 | tf_op jit(solution)/shard_map/axz,ahx->ahz/dot_general | solution.py:176
  113.2 15.0 %shard_map.69 = f32[3,64,32,128]{3,2,1,0:T(8,128)} custom-call(s32[2]{0:T(128)} %bitcast.62, f32[3,64,32,128]{3,2,1,0:T(8,128)} %u.3, f32[3,32,128]{2,1,0:T(8,128)} %copy-done.4, f32[3,32,128]{2,1,0:T(8,128)} %copy-done.3, f32[3,64,128]{2,1,0:T(8,128)} %copy-done.1, f32[3,64,128]{2,1,0:T(8,128)} %copy-done.2, f32[3,32,64]{2,1,0:T(8,128)} %copy-done.5, ...), custom_call_target="tpu_custom_call" | custom-call | tf_op jit(solution)/shard_map/pallas_call | solution.py:122
  (77 shorter events, 14.5 us)
Async XLA Ops:
  0.6 20.7 %copy-start.13 = (s32[1,1,1,2]{3,2,1,0:T(1,128)S(1)}, s32[1,1,1,2]{3,2,1,0:T(1,128)}, u32[]{:S(2)}) copy-start(s32[1,1,1,2]{3,2,1,0:T(1,128)} %param.7) | copy-start | bytes 28
  1.5 31.5 %collective-permute-start.1 = (f32[3,32,128]{2,1,0:T(8,128)S(1)}, f32[3,32,128]{2,1,0:T(8,128)S(1)}, u32[]{:S(2)}, u32[]{:S(2)}) collective-permute-start(f32[3,32,128]{2,1,0:T(8,128)S(1)} %get-tuple-element.24), channel_id=1, source_target_pairs={{16,0},{32,16},{48,32},{64,48},{80,64},{96,80},{112,96},{128,112},... | collective-permute-start | bytes 147464 | tf_op jit(solution)/shard_map/ppermute | solution.py:35
  6.6 26.4 %collective-permute-start = (f32[3,32,128]{2,1,0:T(8,128)S(1)}, f32[3,32,128]{2,1,0:T(8,128)S(1)}, u32[]{:S(2)}, u32[]{:S(2)}) collective-permute-start(f32[3,32,128]{2,1,0:T(8,128)S(1)} %get-tuple-element.25), channel_id=1, source_target_pairs={{0,16},{16,32},{32,48},{48,64},{64,80},{80,96},{96,112},{112,128},... | collective-permute-start | bytes 147464 | tf_op jit(solution)/shard_map/ppermute | solution.py:35
  12.2 19.0 %collective-permute-start.4 = (f32[3,32,64]{2,1,0:T(8,128)S(1)}, f32[3,32,64]{2,1,0:T(8,128)S(1)}, u32[]{:S(2)}, u32[]{:S(2)}) collective-permute-start(f32[3,32,64]{2,1,0:T(8,128)S(1)} %bitcast.56), channel_id=1, source_target_pairs={{0,4},{4,8},{8,12},{1,5},{5,9},{9,13},{2,6},{6,10},{10,14},{3,7},{... | collective-permute-start | bytes 73736 | tf_op jit(solution)/shard_map/ppermute | solution.py:35
  15.2 17.7 %collective-permute-start.5 = (f32[3,32,64]{2,1,0:T(8,128)S(1)}, f32[3,32,64]{2,1,0:T(8,128)S(1)}, u32[]{:S(2)}, u32[]{:S(2)}) collective-permute-start(f32[3,32,64]{2,1,0:T(8,128)S(1)} %bitcast.55), channel_id=1, source_target_pairs={{4,0},{8,4},{12,8},{5,1},{9,5},{13,9},{6,2},{10,6},{14,10},{7,3},{... | collective-permute-start | bytes 73736 | tf_op jit(solution)/shard_map/ppermute | solution.py:35
  18.1 14.9 %collective-permute-start.2 = (f32[3,64,128]{2,1,0:T(8,128)S(1)}, f32[3,64,128]{2,1,0:T(8,128)S(1)}, u32[]{:S(2)}, u32[]{:S(2)}) collective-permute-start(f32[3,64,128]{2,1,0:T(8,128)S(1)} %bitcast.52), channel_id=1, source_target_pairs={{0,1},{1,2},{2,3},{4,5},{5,6},{6,7},{8,9},{9,10},{10,11},{12,13},{... | collective-permute-start | bytes 294920 | tf_op jit(solution)/shard_map/ppermute | solution.py:35
  31.2 40.5 %copy-start.5 = (f32[3,32,64]{2,1,0:T(8,128)}, f32[3,32,64]{2,1,0:T(8,128)S(1)}, u32[]{:S(2)}) copy-start(f32[3,32,64]{2,1,0:T(8,128)S(1)} %collective-permute-done.4.ylo) | copy-start | bytes 73732
  31.2 6.7 %collective-permute-start.3 = (f32[3,64,128]{2,1,0:T(8,128)S(1)}, f32[3,64,128]{2,1,0:T(8,128)S(1)}, u32[]{:S(2)}, u32[]{:S(2)}) collective-permute-start(f32[3,64,128]{2,1,0:T(8,128)S(1)} %bitcast.51), channel_id=1, source_target_pairs={{1,0},{2,1},{3,2},{5,4},{6,5},{7,6},{9,8},{10,9},{11,10},{13,12},{... | collective-permute-start | bytes 294920 | tf_op jit(solution)/shard_map/ppermute | solution.py:35
  32.9 38.8 %copy-start.6 = (f32[3,32,64]{2,1,0:T(8,128)}, f32[3,32,64]{2,1,0:T(8,128)S(1)}, u32[]{:S(2)}) copy-start(f32[3,32,64]{2,1,0:T(8,128)S(1)} %collective-permute-done.5.yhi) | copy-start | bytes 73732
  33.0 38.8 %copy-start.3 = (f32[3,32,128]{2,1,0:T(8,128)}, f32[3,32,128]{2,1,0:T(8,128)S(1)}, u32[]{:S(2)}) copy-start(f32[3,32,128]{2,1,0:T(8,128)S(1)} %collective-permute-done.1.xhi) | copy-start | bytes 147460
  33.0 38.8 %copy-start.4 = (f32[3,32,128]{2,1,0:T(8,128)}, f32[3,32,128]{2,1,0:T(8,128)S(1)}, u32[]{:S(2)}) copy-start(f32[3,32,128]{2,1,0:T(8,128)S(1)} %collective-permute-done.xlo) | copy-start | bytes 147460
  33.0 38.7 %copy-start.1 = (f32[3,64,128]{2,1,0:T(8,128)}, f32[3,64,128]{2,1,0:T(8,128)S(1)}, u32[]{:S(2)}) copy-start(f32[3,64,128]{2,1,0:T(8,128)S(1)} %collective-permute-done.2.zlo) | copy-start | bytes 294916
  37.9 33.8 %copy-start.2 = (f32[3,64,128]{2,1,0:T(8,128)}, f32[3,64,128]{2,1,0:T(8,128)S(1)}, u32[]{:S(2)}) copy-start(f32[3,64,128]{2,1,0:T(8,128)S(1)} %collective-permute-done.3.zhi) | copy-start | bytes 294916
  58.6 3.4 %collective-permute-start.12 = (f32[4,1152]{1,0:T(4,128)S(1)}, f32[4,1152]{1,0:T(4,128)S(1)}, u32[]{:S(2)}, u32[]{:S(2)}) collective-permute-start(f32[4,1152]{1,0:T(4,128)S(1)} %reduce_sum.58), channel_id=1, source_target_pairs={{0,4},{4,0},{8,12},{12,8},{1,5},{5,1},{9,13},{13,9},{2,6},{6,2},{1... | collective-permute-start | bytes 55304 | tf_op jit(solution)/shard_map/ppermute | solution.py:167
  61.9 4.5 %collective-permute-start.13 = (f32[4,1152]{1,0:T(4,128)S(1)}, f32[4,1152]{1,0:T(4,128)S(1)}, u32[]{:S(2)}, u32[]{:S(2)}) collective-permute-start(f32[4,1152]{1,0:T(4,128)S(1)} %add.31), channel_id=1, source_target_pairs={{0,8},{4,12},{8,0},{12,4},{1,9},{5,13},{9,1},{13,5},{2,10},{6,14},... | collective-permute-start | bytes 55304 | tf_op jit(solution)/shard_map/ppermute | solution.py:167
  66.5 2.6 %collective-permute-start.14 = (f32[4,1152]{1,0:T(4,128)S(1)}, f32[4,1152]{1,0:T(4,128)S(1)}, u32[]{:S(2)}, u32[]{:S(2)}) collective-permute-start(f32[4,1152]{1,0:T(4,128)S(1)} %add.32), channel_id=1, source_target_pairs={{0,1},{1,0},{2,3},{3,2},{4,5},{5,4},{6,7},{7,6},{8,9},{9,8},{10,11... | collective-permute-start | bytes 55304 | tf_op jit(solution)/shard_map/ppermute | solution.py:167
  69.1 14.1 %collective-permute-start.15 = (f32[4,1152]{1,0:T(4,128)S(1)}, f32[4,1152]{1,0:T(4,128)S(1)}, u32[]{:S(2)}, u32[]{:S(2)}) collective-permute-start(f32[4,1152]{1,0:T(4,128)S(1)} %add.33), channel_id=1, source_target_pairs={{0,2},{1,3},{2,0},{3,1},{4,6},{5,7},{6,4},{7,5},{8,10},{9,11},{10,... | collective-permute-start | bytes 55304 | tf_op jit(solution)/shard_map/ppermute | solution.py:167
  84.7 21.7 %all-to-all-start.1 = ((f32[16,4,1152]{2,1,0:T(4,128)}), f32[16,4,1152]{2,1,0:T(4,128)S(1)}, u32[]{:S(2)}, u32[]{:S(2)}) async-start(f32[16,4,1152]{2,1,0:T(4,128)} %broadcast_in_dim.20), calls=%async_computation.1 | async-start | bytes 589824 | tf_op jit(solution)/shard_map/all_to_all | solution.py:171
  91.6 21.0 %collective-permute-start.7 = (f32[32,128]{1,0:T(8,128)S(1)}, f32[32,128]{1,0:T(8,128)S(1)}, u32[]{:S(2)}, u32[]{:S(2)}) collective-permute-start(f32[32,128]{1,0:T(8,128)S(1)} %get-tuple-element.30), channel_id=1, source_target_pairs={{16,0},{32,16},{48,32},{64,48},{80,64},{96,80},{112,96},{128,112},... | collective-permute-start | bytes 49160 | tf_op jit(solution)/shard_map/ppermute | solution.py:35
  93.7 18.9 %collective-permute-start.6 = (f32[32,128]{1,0:T(8,128)S(1)}, f32[32,128]{1,0:T(8,128)S(1)}, u32[]{:S(2)}, u32[]{:S(2)}) collective-permute-start(f32[32,128]{1,0:T(8,128)S(1)} %get-tuple-element.31), channel_id=1, source_target_pairs={{0,16},{16,32},{32,48},{48,64},{64,80},{80,96},{96,112},{112,128},... | collective-permute-start | bytes 49160 | tf_op jit(solution)/shard_map/ppermute | solution.py:35
  99.1 7.7 %collective-permute-start.10 = (f32[32,64]{1,0:T(8,128)S(1)}, f32[32,64]{1,0:T(8,128)S(1)}, u32[]{:S(2)}, u32[]{:S(2)}) collective-permute-start(f32[32,64]{1,0:T(8,128)S(1)} %bitcast.61), channel_id=1, source_target_pairs={{0,4},{4,8},{8,12},{1,5},{5,9},{9,13},{2,6},{6,10},{10,14},{3,7},{... | collective-permute-start | bytes 24584 | tf_op jit(solution)/shard_map/ppermute | solution.py:35
  102.7 9.8 %collective-permute-start.11 = (f32[32,64]{1,0:T(8,128)S(1)}, f32[32,64]{1,0:T(8,128)S(1)}, u32[]{:S(2)}, u32[]{:S(2)}) collective-permute-start(f32[32,64]{1,0:T(8,128)S(1)} %bitcast.60), channel_id=1, source_target_pairs={{4,0},{8,4},{12,8},{5,1},{9,5},{13,9},{6,2},{10,6},{14,10},{7,3},{... | collective-permute-start | bytes 24584 | tf_op jit(solution)/shard_map/ppermute | solution.py:35
  105.1 7.5 %collective-permute-start.8 = (f32[64,128]{1,0:T(8,128)S(1)}, f32[64,128]{1,0:T(8,128)S(1)}, u32[]{:S(2)}, u32[]{:S(2)}) collective-permute-start(f32[64,128]{1,0:T(8,128)S(1)} %bitcast.59), channel_id=1, source_target_pairs={{0,1},{1,2},{2,3},{4,5},{5,6},{6,7},{8,9},{9,10},{10,11},{12,13},{... | collective-permute-start | bytes 98312 | tf_op jit(solution)/shard_map/ppermute | solution.py:35
  106.8 5.8 %collective-permute-start.9 = (f32[64,128]{1,0:T(8,128)S(1)}, f32[64,128]{1,0:T(8,128)S(1)}, u32[]{:S(2)}, u32[]{:S(2)}) collective-permute-start(f32[64,128]{1,0:T(8,128)S(1)} %bitcast.58), channel_id=1, source_target_pairs={{1,0},{2,1},{3,2},{5,4},{6,5},{7,6},{9,8},{10,9},{11,10},{13,12},{... | collective-permute-start | bytes 98312 | tf_op jit(solution)/shard_map/ppermute | solution.py:35
  (8 other events, 19.2 us)

commit v13 on v10

--- a/solution.py
+++ b/solution.py
@@ -75,8 +75,7 @@
     lax.fori_loop(0, u.shape[1], plane, 0, unroll=8)
 
 
-def advance_kernel(planes, u, xlo, xhi, zlo, zhi, ylo, yhi, nu, nxlo, nxhi, nzlo, nzhi, nylo, nyhi, sent, out):
-    slots = sent.shape[0]
+def advance_kernel(u, xlo, xhi, zlo, zhi, ylo, yhi, nu, nxlo, nxhi, nzlo, nzhi, nylo, nyhi, out):
 
     def plane(x, carry):
         here = nu[x]
@@ -94,10 +93,7 @@
             for d in range(3):
                 advect = advect + centres[d] * 0.5 * (upper[d] - lower[d])
                 spread = spread + nu_up[d] * (upper[d] - center) - nu_low[d] * (center - lower[d])
-            impulse = jnp.zeros_like(center)
-            for s in range(slots):
-                impulse = impulse + jnp.where(planes[s] == x, sent[s, c], 0.0)
-            out[c, x] = center + 0.25 * (spread - advect) + impulse
+            out[c, x] = center + 0.25 * (spread - advect)
         return carry
 
     lax.fori_loop(0, u.shape[1], plane, 0, unroll=8)
@@ -121,9 +117,19 @@
         viscosity_kernel, jax.ShapeDtypeStruct(velocity.shape[1:], jnp.float32), 7
     )(velocity, *u_faces)
     nu_faces = faces(nu, 0)
-    return vmem_call(
-        advance_kernel, jax.ShapeDtypeStruct(velocity.shape, jnp.float32), 16, smem=1
-    )(planes, velocity, *u_faces, nu, *nu_faces, sent)
+    advanced = vmem_call(advance_kernel, jax.ShapeDtypeStruct(velocity.shape, jnp.float32), 14)(
+        velocity, *u_faces, nu, *nu_faces
+    )
+    slots = sent.shape[0]
+    updated = []
+    for s in range(slots):
+        impulse = jnp.zeros_like(sent[s])
+        for t in range(slots):
+            impulse = impulse + jnp.where(planes[t] == planes[s], sent[t], 0.0)
+        updated.append(lax.dynamic_index_in_dim(advanced, planes[s], 1) + impulse[:, None])
+    for s in range(slots):
+        advanced = lax.dynamic_update_index_in_dim(advanced, updated[s], planes[s], 1)
+    return advanced
 
 
 def body(velocity, tile_turbine, tile_plane, tile_weight, chord):

time: 122 us -> 127 us (1.041)
  local copies, waits for them, and re-layouts: 11.2 us -> 13.5 us
  between operations: 4.97 us -> 6.97 us
    unnamed x30 -> x37, local copies, waits for them, and re-layouts: 1.91 us -> 4.91 us
  transfers between devices with their start and end apart: 18 -> 18, of which waited for: 2 -> 2; matrix products, arithmetic and copies ran while one was open for 14% -> 10% of each run, Pallas kernels for 9% -> 21%
where the time goes in v13:
time: 127 us; the launch traced here: 126 us
  starting transfers between devices  53.9 us (42%)
  Pallas kernels  26.4 us (21%)
  matrix products  16.9 us (13%)
  local copies, waits for them, and re-layouts  13.5 us (11%)
  waiting for transfers between devices  6.97 us (5%)
  between operations  6.97 us (5%)
    ppermute x6, starting transfers between devices, faces(): lax.ppermute(last, axis, forward)  20.2 us
    pallas_call x1, Pallas kernels, stencil(): vmem_call(advance_kernel, jax.ShapeDtypeStruct(velocity.shape, jnp.float3...  15 us
    pallas_call x1, Pallas kernels, stencil(): vmem_call(viscosity_kernel, jax.ShapeDtypeStruct(velocity.shape[1:], jnp....  11.4 us
    ppermute x6, starting transfers between devices, faces(): lax.ppermute(first, axis, backward)  10 us
    all_to_all x1, starting transfers between devices, body(): lax.all_to_all(partial_sample.reshape(rows, per_row, -1), 'gx', split_axi...  9.98 us
    ppermute x4, starting transfers between devices, body(): owned = owned + lax.ppermute(owned, axis, pairs)  9.1 us
    dot_general x2, matrix products, faces(): jnp.einsum(letters + ',ky->k' + letters[:-3] + 'zx', block, ends, precisi...  7.75 us
    all_to_all x1, waiting for transfers between devices, body(): lax.all_to_all(partial_sample.reshape(rows, per_row, -1), 'gx', split_axi...  5.45 us
  transfers between devices with their start and end apart: 18, of which 2 were waited for; matrix products, arithmetic and copies ran while one was open for 10% of the time, Pallas kernels for 21%

profile of v13, /device:TPU:1, one launch (start us, length us, event | category | flops | bytes accessed | tf_op | source)
XLA Modules:
  0.0 125.6 jit_solution(12605951142968888932)
XLA Ops:
  0.6 1.3 %fusion.30 = (s32[1,1,1,1]{3,2,1,0:T(1,128)}, s32[1,1,1,1]{3,2,1,0:T(1,128)}) fusion(s32[1,1,1,2]{3,2,1,0:T(1,128)} %param.9), kind=kLoop, calls=%fused_computation.54 | loop fusion | bytes 16 | tf_op jit(solution)/shard_map/slice | solution.py:148
  6.4 4.7 %fusion.2 = f32[2,3,384]{2,1,0:T(4,128)S(1)} fusion(bf16[1,1,1,2,384,4096]{5,4,3,2,1,0:T(8,128)(2,1)} %param.10, bf16[1,3,4096]{2,1,0:T(4,128)(2,1)S(1)} %stack.10, bf16[1,3,4096]{2,1,0:T(4,128)(2,1)S(1)} %stack.9), kind=kOutput, calls=%fused_computation.2 | convolution fusion | flops 18972672 | bytes 6349824 | tf_op jit(solution)/shard_map/spq,scq->scp/dot_general | solution.py:150
  12.3 10.0 %all-to-all-start = ((f32[16,4,1152]{2,1,0:T(4,128)}), f32[16,4,1152]{2,1,0:T(4,128)S(1)}, u32[]{:S(2)}, u32[]{:S(2)}) async-start(f32[16,4,1152]{2,1,0:T(4,128)} %copy.39), calls=%async_computation | async-start | bytes 589824 | tf_op jit(solution)/shard_map/all_to_all | solution.py:164
  22.3 4.9 %fusion.4 = f32[2,3,64,32]{2,0,3,1:T(2,128)S(1)} fusion(f32[3,64,32,128]{3,2,1,0:T(8,128)S(1)} %copy-done, s32[2]{0:T(128)S(1)} %iota_multiply_fusion), kind=kOutput, calls=%fused_computation.4 | convolution fusion | flops 18874624 | bytes 3194888 | tf_op jit(solution)/shard_map/cxzy,ky->kczx/dot_general | solution.py:22
  29.1 5.4 %all-to-all-done = f32[16,4,1152]{2,1,0:T(4,128)S(1)} async-done(((f32[16,4,1152]{2,1,0:T(4,128)}), f32[16,4,1152]{2,1,0:T(4,128)S(1)}, u32[]{:S(2)}, u32[]{:S(2)}) %all-to-all-start) | async-done | bytes 294944 | tf_op jit(solution)/shard_map/all_to_all | solution.py:164
  36.7 3.2 %collective-permute-start.2 = (f32[3,64,128]{2,1,0:T(8,128)}, f32[3,64,128]{2,1,0:T(8,128)S(1)}, u32[]{:S(2)}, u32[]{:S(2)}) collective-permute-start(f32[3,64,128]{2,1,0:T(8,128)} %bitcast.2), channel_id=1, source_target_pairs={{0,1},{1,2},{2,3},{4,5},{5,6},{6,7},{8,9},{9,10},{10,11},{12,13},{... | collective-permute-start | bytes 294920 | tf_op jit(solution)/shard_map/ppermute | solution.py:36
  41.3 2.5 %collective-permute-start.13 = (f32[4,1152]{1,0:T(4,128)S(1)}, f32[4,1152]{1,0:T(4,128)S(1)}, u32[]{:S(2)}, u32[]{:S(2)}) collective-permute-start(f32[4,1152]{1,0:T(4,128)S(1)} %add.67), channel_id=1, source_target_pairs={{0,8},{4,12},{8,0},{12,4},{1,9},{5,13},{9,1},{13,5},{2,10},{6,14},... | collective-permute-start | bytes 55304 | tf_op jit(solution)/shard_map/ppermute | solution.py:173
  44.4 2.3 %collective-permute-start.1 = (f32[3,32,128]{2,1,0:T(8,128)}, f32[3,32,128]{2,1,0:T(8,128)S(1)}, u32[]{:S(2)}, u32[]{:S(2)}) collective-permute-start(f32[3,32,128]{2,1,0:T(8,128)} %get-tuple-element.8), channel_id=1, source_target_pairs={{16,0},{32,16},{48,32},{64,48},{80,64},{96,80},{112,96},{128,112},... | collective-permute-start | bytes 147464 | tf_op jit(solution)/shard_map/ppermute | solution.py:36
  46.8 3.2 %collective-permute-start = (f32[3,32,128]{2,1,0:T(8,128)S(1)}, f32[3,32,128]{2,1,0:T(8,128)S(1)}, u32[]{:S(2)}, u32[]{:S(2)}) collective-permute-start(f32[3,32,128]{2,1,0:T(8,128)S(1)} %get-tuple-element.9), channel_id=1, source_target_pairs={{0,16},{16,32},{32,48},{48,64},{64,80},{80,96},{96,112},{112,128},... | collective-permute-start | bytes 147464 | tf_op jit(solution)/shard_map/ppermute | solution.py:36
  50.0 1.8 %collective-permute-start.4 = (f32[3,32,64]{2,1,0:T(8,128)}, f32[3,32,64]{2,1,0:T(8,128)S(1)}, u32[]{:S(2)}, u32[]{:S(2)}) collective-permute-start(f32[3,32,64]{2,1,0:T(8,128)} %get-tuple-element.17), channel_id=1, source_target_pairs={{0,4},{4,8},{8,12},{1,5},{5,9},{9,13},{2,6},{6,10},{10,14},{3,7},{... | collective-permute-start | bytes 73736 | tf_op jit(solution)/shard_map/ppermute | solution.py:36
  51.9 1.5 %collective-permute-done.4.ylo = f32[3,32,64]{2,1,0:T(8,128)S(1)} collective-permute-done((f32[3,32,64]{2,1,0:T(8,128)}, f32[3,32,64]{2,1,0:T(8,128)S(1)}, u32[]{:S(2)}, u32[]{:S(2)}) %collective-permute-start.4) | collective-permute-done | bytes 24608 | tf_op jit(solution)/shard_map/ppermute | solution.py:36
  53.4 2.4 %collective-permute-start.14 = (f32[4,1152]{1,0:T(4,128)S(1)}, f32[4,1152]{1,0:T(4,128)S(1)}, u32[]{:S(2)}, u32[]{:S(2)}) collective-permute-start(f32[4,1152]{1,0:T(4,128)S(1)} %add.68), channel_id=1, source_target_pairs={{0,1},{1,0},{2,3},{3,2},{4,5},{5,4},{6,7},{7,6},{8,9},{9,8},{10,11... | collective-permute-start | bytes 55304 | tf_op jit(solution)/shard_map/ppermute | solution.py:173
  57.1 11.4 %shard_map.86.nu = f32[64,32,128]{2,1,0:T(8,128)} custom-call(f32[3,64,32,128]{3,2,1,0:T(8,128)} %u.3, f32[3,32,128]{2,1,0:T(8,128)} %copy-done.9, f32[3,32,128]{2,1,0:T(8,128)} %copy-done.8, f32[3,64,128]{2,1,0:T(8,128)} %copy-done.5, f32[3,64,128]{2,1,0:T(8,128)} %copy-done.6, f32[3,32,64]{2,1,0:T(8,128)} %copy-done.10, f32[3,32,64]{2,1,0:T(8,128)} %copy-done.7), custom_call_target="tpu_custom_call" | custom-call | tf_op jit(solution)/shard_map/pallas_call | solution.py:116
  68.6 2.9 %collective-permute-start.15 = (f32[4,1152]{1,0:T(4,128)S(1)}, f32[4,1152]{1,0:T(4,128)S(1)}, u32[]{:S(2)}, u32[]{:S(2)}) collective-permute-start(f32[4,1152]{1,0:T(4,128)S(1)} %add.69), channel_id=1, source_target_pairs={{0,2},{1,3},{2,0},{3,1},{4,6},{5,7},{6,4},{7,5},{8,10},{9,11},{10,... | collective-permute-start | bytes 55304 | tf_op jit(solution)/shard_map/ppermute | solution.py:173
  71.5 2.9 %fusion.19 = f32[2,64,32]{1,0,2:T(2,128)S(1)} fusion(s32[2]{0:T(128)S(1)} %iota_multiply_fusion, f32[64,32,128]{2,1,0:T(8,128)} %shard_map.86.nu), kind=kOutput, calls=%fused_computation.41 | convolution fusion | flops 6291712 | bytes 1064968 | tf_op jit(solution)/shard_map/xzy,ky->kzx/dot_general | solution.py:22
  74.3 1.9 %copy.35 = f32[64,32,128]{2,0,1:T(8,128)S(1)} copy(f32[64,32,128]{2,1,0:T(8,128)} %shard_map.86.nu) | data formatting | bytes 2097152 | tf_op jit(solution)/shard_map/pallas_call | solution.py:116
  77.7 4.6 %all-to-all-start.1 = ((f32[16,4,1152]{2,1,0:T(4,128)}), f32[16,4,1152]{2,1,0:T(4,128)S(1)}, u32[]{:S(2)}, u32[]{:S(2)}) async-start(f32[16,4,1152]{2,1,0:T(4,128)} %broadcast_in_dim.9), calls=%async_computation.1 | async-start | bytes 589824 | tf_op jit(solution)/shard_map/all_to_all | solution.py:177
  83.7 4.0 %collective-permute-start.8 = (f32[64,128]{1,0:T(8,128)S(1)}, f32[64,128]{1,0:T(8,128)S(1)}, u32[]{:S(2)}, u32[]{:S(2)}) collective-permute-start(f32[64,128]{1,0:T(8,128)S(1)} %get-tuple-element.11), channel_id=1, source_target_pairs={{0,1},{1,2},{2,3},{4,5},{5,6},{6,7},{8,9},{9,10},{10,11},{12,13},{... | collective-permute-start | bytes 98312 | tf_op jit(solution)/shard_map/ppermute | solution.py:36
  89.7 2.6 %collective-permute-start.7 = (f32[32,128]{1,0:T(8,128)S(1)}, f32[32,128]{1,0:T(8,128)S(1)}, u32[]{:S(2)}, u32[]{:S(2)}) collective-permute-start(f32[32,128]{1,0:T(8,128)S(1)} %get-tuple-element.12), channel_id=1, source_target_pairs={{16,0},{32,16},{48,32},{64,48},{80,64},{96,80},{112,96},{128,112},... | collective-permute-start | bytes 49160 | tf_op jit(solution)/shard_map/ppermute | solution.py:36
  92.3 3.4 %collective-permute-start.6 = (f32[32,128]{1,0:T(8,128)S(1)}, f32[32,128]{1,0:T(8,128)S(1)}, u32[]{:S(2)}, u32[]{:S(2)}) collective-permute-start(f32[32,128]{1,0:T(8,128)S(1)} %get-tuple-element.13), channel_id=1, source_target_pairs={{0,16},{16,32},{32,48},{48,64},{64,80},{80,96},{96,112},{112,128},... | collective-permute-start | bytes 49160 | tf_op jit(solution)/shard_map/ppermute | solution.py:36
  95.8 4.5 %collective-permute-start.10 = (f32[32,64]{1,0:T(8,128)S(1)}, f32[32,64]{1,0:T(8,128)S(1)}, u32[]{:S(2)}, u32[]{:S(2)}) collective-permute-start(f32[32,64]{1,0:T(8,128)S(1)} %get-tuple-element.19), channel_id=1, source_target_pairs={{0,4},{4,8},{8,12},{1,5},{5,9},{9,13},{2,6},{6,10},{10,14},{3,7},{... | collective-permute-start | bytes 24584 | tf_op jit(solution)/shard_map/ppermute | solution.py:36
  103.9 15.0 %shard_map.87 = f32[3,64,32,128]{3,2,1,0:T(8,128)} custom-call(f32[3,64,32,128]{3,2,1,0:T(8,128)} %u.3, f32[3,32,128]{2,1,0:T(8,128)} %copy-done.9, f32[3,32,128]{2,1,0:T(8,128)} %copy-done.8, f32[3,64,128]{2,1,0:T(8,128)} %copy-done.5, f32[3,64,128]{2,1,0:T(8,128)} %copy-done.6, f32[3,32,64]{2,1,0:T(8,128)} %copy-done.10, f32[3,32,64]{2,1,0:T(8,128)} %copy-done.7, ...), custom_call_target="tpu_custom_call" | custom-call | tf_op jit(solution)/shard_map/pallas_call | solution.py:120
  119.3 3.9 %fusion = f32[2,3,4096]{2,1,0:T(4,128)S(1)} fusion(bf16[2,3,384]{2,1,0:T(4,128)(2,1)S(1)} %reshape.110, bf16[1,1,1,2,384,4096]{5,4,3,2,1,0:T(8,128)(2,1)} %param.10), kind=kOutput, calls=%fused_computation | convolution fusion | flops 18874368 | bytes 6394368 | tf_op jit(solution)/shard_map/axz,ahx->ahz/dot_general | solution.py:182
  124.0 1.7 %copy-done.2 = f32[3,64,32,128]{3,2,1,0:T(8,128)} copy-done((f32[3,64,32,128]{3,2,1,0:T(8,128)}, f32[3,64,32,128]{3,2,1,0:T(8,128)S(1)}, u32[]{:S(2)}) %copy-start.2) | copy-done | bytes 3145752
  (88 shorter events, 16.7 us)
Async XLA Ops:
  6.3 4.7 %copy-start.17 = (s32[1,1,1,2]{3,2,1,0:T(1,128)S(1)}, s32[1,1,1,2]{3,2,1,0:T(1,128)}, u32[]{:S(2)}) copy-start(s32[1,1,1,2]{3,2,1,0:T(1,128)} %param.8) | copy-start | bytes 28
  6.3 16.0 %copy-start = (f32[3,64,32,128]{3,2,1,0:T(8,128)S(1)}, f32[3,64,32,128]{3,2,1,0:T(8,128)}, u32[]{:S(2)}) copy-start(f32[3,64,32,128]{3,2,1,0:T(8,128)} %u.3) | copy-start | bytes 9437188
  12.3 22.3 %all-to-all-start = ((f32[16,4,1152]{2,1,0:T(4,128)}), f32[16,4,1152]{2,1,0:T(4,128)S(1)}, u32[]{:S(2)}, u32[]{:S(2)}) async-start(f32[16,4,1152]{2,1,0:T(4,128)} %copy.39), calls=%async_computation | async-start | bytes 589824 | tf_op jit(solution)/shard_map/all_to_all | solution.py:164
  27.9 18.9 %collective-permute-start.5 = (f32[3,32,64]{2,1,0:T(8,128)}, f32[3,32,64]{2,1,0:T(8,128)S(1)}, u32[]{:S(2)}, u32[]{:S(2)}) collective-permute-start(f32[3,32,64]{2,1,0:T(8,128)} %get-tuple-element.16), channel_id=1, source_target_pairs={{4,0},{8,4},{12,8},{5,1},{9,5},{13,9},{6,2},{10,6},{14,10},{7,3},{... | collective-permute-start | bytes 73736 | tf_op jit(solution)/shard_map/ppermute | solution.py:36
  34.7 6.6 %collective-permute-start.12 = (f32[4,1152]{1,0:T(4,128)S(1)}, f32[4,1152]{1,0:T(4,128)S(1)}, u32[]{:S(2)}, u32[]{:S(2)}) collective-permute-start(f32[4,1152]{1,0:T(4,128)S(1)} %reduce_sum.18), channel_id=1, source_target_pairs={{0,4},{4,0},{8,12},{12,8},{1,5},{5,1},{9,13},{13,9},{2,6},{6,2},{1... | collective-permute-start | bytes 55304 | tf_op jit(solution)/shard_map/ppermute | solution.py:173
  36.7 19.1 %collective-permute-start.2 = (f32[3,64,128]{2,1,0:T(8,128)}, f32[3,64,128]{2,1,0:T(8,128)S(1)}, u32[]{:S(2)}, u32[]{:S(2)}) collective-permute-start(f32[3,64,128]{2,1,0:T(8,128)} %bitcast.2), channel_id=1, source_target_pairs={{0,1},{1,2},{2,3},{4,5},{5,6},{6,7},{8,9},{9,10},{10,11},{12,13},{... | collective-permute-start | bytes 294920 | tf_op jit(solution)/shard_map/ppermute | solution.py:36
  39.9 15.9 %collective-permute-start.3 = (f32[3,64,128]{2,1,0:T(8,128)}, f32[3,64,128]{2,1,0:T(8,128)S(1)}, u32[]{:S(2)}, u32[]{:S(2)}) collective-permute-start(f32[3,64,128]{2,1,0:T(8,128)} %bitcast.3), channel_id=1, source_target_pairs={{1,0},{2,1},{3,2},{5,4},{6,5},{7,6},{9,8},{10,9},{11,10},{13,12},{... | collective-permute-start | bytes 294920 | tf_op jit(solution)/shard_map/ppermute | solution.py:36
  41.3 8.8 %collective-permute-start.13 = (f32[4,1152]{1,0:T(4,128)S(1)}, f32[4,1152]{1,0:T(4,128)S(1)}, u32[]{:S(2)}, u32[]{:S(2)}) collective-permute-start(f32[4,1152]{1,0:T(4,128)S(1)} %add.67), channel_id=1, source_target_pairs={{0,8},{4,12},{8,0},{12,4},{1,9},{5,13},{9,1},{13,5},{2,10},{6,14},... | collective-permute-start | bytes 55304 | tf_op jit(solution)/shard_map/ppermute | solution.py:173
  44.4 11.4 %collective-permute-start.1 = (f32[3,32,128]{2,1,0:T(8,128)}, f32[3,32,128]{2,1,0:T(8,128)S(1)}, u32[]{:S(2)}, u32[]{:S(2)}) collective-permute-start(f32[3,32,128]{2,1,0:T(8,128)} %get-tuple-element.8), channel_id=1, source_target_pairs={{16,0},{32,16},{48,32},{64,48},{80,64},{96,80},{112,96},{128,112},... | collective-permute-start | bytes 147464 | tf_op jit(solution)/shard_map/ppermute | solution.py:36
  46.8 9.1 %copy-start.7 = (f32[3,32,64]{2,1,0:T(8,128)}, f32[3,32,64]{2,1,0:T(8,128)S(1)}, u32[]{:S(2)}) copy-start(f32[3,32,64]{2,1,0:T(8,128)S(1)} %collective-permute-done.5.yhi) | copy-start | bytes 73732
  46.8 9.0 %collective-permute-start = (f32[3,32,128]{2,1,0:T(8,128)S(1)}, f32[3,32,128]{2,1,0:T(8,128)S(1)}, u32[]{:S(2)}, u32[]{:S(2)}) collective-permute-start(f32[3,32,128]{2,1,0:T(8,128)S(1)} %get-tuple-element.9), channel_id=1, source_target_pairs={{0,16},{16,32},{32,48},{48,64},{64,80},{80,96},{96,112},{112,128},... | collective-permute-start | bytes 147464 | tf_op jit(solution)/shard_map/ppermute | solution.py:36
  50.0 3.4 %collective-permute-start.4 = (f32[3,32,64]{2,1,0:T(8,128)}, f32[3,32,64]{2,1,0:T(8,128)S(1)}, u32[]{:S(2)}, u32[]{:S(2)}) collective-permute-start(f32[3,32,64]{2,1,0:T(8,128)} %get-tuple-element.17), channel_id=1, source_target_pairs={{0,4},{4,8},{8,12},{1,5},{5,9},{9,13},{2,6},{6,10},{10,14},{3,7},{... | collective-permute-start | bytes 73736 | tf_op jit(solution)/shard_map/ppermute | solution.py:36
  53.4 15.2 %collective-permute-start.14 = (f32[4,1152]{1,0:T(4,128)S(1)}, f32[4,1152]{1,0:T(4,128)S(1)}, u32[]{:S(2)}, u32[]{:S(2)}) collective-permute-start(f32[4,1152]{1,0:T(4,128)S(1)} %add.68), channel_id=1, source_target_pairs={{0,1},{1,0},{2,3},{3,2},{4,5},{5,4},{6,7},{7,6},{8,9},{9,8},{10,11... | collective-permute-start | bytes 55304 | tf_op jit(solution)/shard_map/ppermute | solution.py:173
  68.6 7.6 %collective-permute-start.15 = (f32[4,1152]{1,0:T(4,128)S(1)}, f32[4,1152]{1,0:T(4,128)S(1)}, u32[]{:S(2)}, u32[]{:S(2)}) collective-permute-start(f32[4,1152]{1,0:T(4,128)S(1)} %add.69), channel_id=1, source_target_pairs={{0,2},{1,3},{2,0},{3,1},{4,6},{5,7},{6,4},{7,5},{8,10},{9,11},{10,... | collective-permute-start | bytes 55304 | tf_op jit(solution)/shard_map/ppermute | solution.py:173
  77.7 41.1 %all-to-all-start.1 = ((f32[16,4,1152]{2,1,0:T(4,128)}), f32[16,4,1152]{2,1,0:T(4,128)S(1)}, u32[]{:S(2)}, u32[]{:S(2)}) async-start(f32[16,4,1152]{2,1,0:T(4,128)} %broadcast_in_dim.9), calls=%async_computation.1 | async-start | bytes 589824 | tf_op jit(solution)/shard_map/all_to_all | solution.py:177
  82.4 20.3 %collective-permute-start.9 = (f32[64,128]{1,0:T(8,128)S(1)}, f32[64,128]{1,0:T(8,128)S(1)}, u32[]{:S(2)}, u32[]{:S(2)}) collective-permute-start(f32[64,128]{1,0:T(8,128)S(1)} %get-tuple-element.10), channel_id=1, source_target_pairs={{1,0},{2,1},{3,2},{5,4},{6,5},{7,6},{9,8},{10,9},{11,10},{13,12},{... | collective-permute-start | bytes 98312 | tf_op jit(solution)/shard_map/ppermute | solution.py:36
  83.7 19.0 %collective-permute-start.8 = (f32[64,128]{1,0:T(8,128)S(1)}, f32[64,128]{1,0:T(8,128)S(1)}, u32[]{:S(2)}, u32[]{:S(2)}) collective-permute-start(f32[64,128]{1,0:T(8,128)S(1)} %get-tuple-element.11), channel_id=1, source_target_pairs={{0,1},{1,2},{2,3},{4,5},{5,6},{6,7},{8,9},{9,10},{10,11},{12,13},{... | collective-permute-start | bytes 98312 | tf_op jit(solution)/shard_map/ppermute | solution.py:36
  88.4 7.3 %collective-permute-start.11 = (f32[32,64]{1,0:T(8,128)S(1)}, f32[32,64]{1,0:T(8,128)S(1)}, u32[]{:S(2)}, u32[]{:S(2)}) collective-permute-start(f32[32,64]{1,0:T(8,128)S(1)} %get-tuple-element.18), channel_id=1, source_target_pairs={{4,0},{8,4},{12,8},{5,1},{9,5},{13,9},{6,2},{10,6},{14,10},{7,3},{... | collective-permute-start | bytes 24584 | tf_op jit(solution)/shard_map/ppermute | solution.py:36
  89.7 12.9 %collective-permute-start.7 = (f32[32,128]{1,0:T(8,128)S(1)}, f32[32,128]{1,0:T(8,128)S(1)}, u32[]{:S(2)}, u32[]{:S(2)}) collective-permute-start(f32[32,128]{1,0:T(8,128)S(1)} %get-tuple-element.12), channel_id=1, source_target_pairs={{16,0},{32,16},{48,32},{64,48},{80,64},{96,80},{112,96},{128,112},... | collective-permute-start | bytes 49160 | tf_op jit(solution)/shard_map/ppermute | solution.py:36
  92.3 10.3 %collective-permute-start.6 = (f32[32,128]{1,0:T(8,128)S(1)}, f32[32,128]{1,0:T(8,128)S(1)}, u32[]{:S(2)}, u32[]{:S(2)}) collective-permute-start(f32[32,128]{1,0:T(8,128)S(1)} %get-tuple-element.13), channel_id=1, source_target_pairs={{0,16},{16,32},{32,48},{48,64},{64,80},{80,96},{96,112},{112,128},... | collective-permute-start | bytes 49160 | tf_op jit(solution)/shard_map/ppermute | solution.py:36
  95.8 6.9 %copy-start.13 = (f32[32,64]{1,0:T(8,128)}, f32[32,64]{1,0:T(8,128)S(1)}, u32[]{:S(2)}) copy-start(f32[32,64]{1,0:T(8,128)S(1)} %collective-permute-done.11.nyhi) | copy-start | bytes 24580
  95.8 6.8 %collective-permute-start.10 = (f32[32,64]{1,0:T(8,128)S(1)}, f32[32,64]{1,0:T(8,128)S(1)}, u32[]{:S(2)}, u32[]{:S(2)}) collective-permute-start(f32[32,64]{1,0:T(8,128)S(1)} %get-tuple-element.19), channel_id=1, source_target_pairs={{0,4},{4,8},{8,12},{1,5},{5,9},{9,13},{2,6},{6,10},{10,14},{3,7},{... | collective-permute-start | bytes 24584 | tf_op jit(solution)/shard_map/ppermute | solution.py:36
  119.0 4.2 %copy-start.4 = (f32[64,1152]{1,0:T(8,128)}, f32[64,1152]{1,0:T(8,128)S(1)}, u32[]{:S(2)}) copy-start(f32[64,1152]{1,0:T(8,128)S(1)} %reshape.109) | copy-start | bytes 884740
  119.3 4.7 %copy-start.1 = (f32[3,64,32,128]{3,2,1,0:T(8,128)S(1)}, f32[3,64,32,128]{3,2,1,0:T(8,128)}, u32[]{:S(2)}) copy-start(f32[3,64,32,128]{3,2,1,0:T(8,128)} %shard_map.87) | copy-start | bytes 9437188
  (12 other events, 13.6 us)

commit v14 on v10

--- a/solution.py
+++ b/solution.py
@@ -60,15 +60,20 @@
 
 def viscosity_kernel(u, xlo, xhi, zlo, zhi, ylo, yhi, nu):
     def plane(x, carry):
-        grads = []
+        diffs = []
         for c in range(3):
             xm, xp, ym, yp, zm, zp = neighbours(u, xlo, xhi, zlo, zhi, ylo, yhi, (c,), x, u[c, x])
-            grads.append([0.5 * (xp - xm), 0.5 * (yp - ym), 0.5 * (zp - zm)])
-        total = jnp.zeros_like(grads[0][0])
-        for c in range(3):
-            for d in range(3):
-                strain = 0.5 * (grads[c][d] + grads[d][c])
-                total = total + strain * strain
+            diffs.append([xp - xm, yp - ym, zp - zm])
+        diagonal = None
+        for c in range(3):
+            strain = 0.5 * diffs[c][c]
+            diagonal = strain * strain if diagonal is None else diagonal + strain * strain
+        cross = None
+        for c in range(3):
+            for d in range(c + 1, 3):
+                strain = 0.25 * (diffs[c][d] + diffs[d][c])
+                cross = strain * strain if cross is None else cross + strain * strain
+        total = diagonal + 2.0 * cross
         nu[x] = 0.05 + 1.0 * jnp.sqrt(2.0 * total + 1e-06)
         return carry
 
@@ -81,23 +86,25 @@
     def plane(x, carry):
         here = nu[x]
         nxm, nxp, nym, nyp, nzm, nzp = neighbours(nu, nxlo, nxhi, nzlo, nzhi, nylo, nyhi, (), x, here)
-        nu_up = [0.5 * (here + nxp), 0.5 * (here + nyp), 0.5 * (here + nzp)]
-        nu_low = [0.5 * (here + nxm), 0.5 * (here + nym), 0.5 * (here + nzm)]
+        nu_up = [here + nxp, here + nyp, here + nzp]
+        nu_low = [here + nxm, here + nym, here + nzm]
         centres = [u[c, x] for c in range(3)]
         for c in range(3):
             center = centres[c]
             xm, xp, ym, yp, zm, zp = neighbours(u, xlo, xhi, zlo, zhi, ylo, yhi, (c,), x, center)
             upper = (xp, yp, zp)
             lower = (xm, ym, zm)
-            advect = jnp.zeros_like(center)
-            spread = jnp.zeros_like(center)
+            advect = None
+            spread = None
             for d in range(3):
-                advect = advect + centres[d] * 0.5 * (upper[d] - lower[d])
-                spread = spread + nu_up[d] * (upper[d] - center) - nu_low[d] * (center - lower[d])
+                term = centres[d] * (upper[d] - lower[d])
+                flux = nu_up[d] * (upper[d] - center) - nu_low[d] * (center - lower[d])
+                advect = term if advect is None else advect + term
+                spread = flux if spread is None else spread + flux
             impulse = jnp.zeros_like(center)
             for s in range(slots):
                 impulse = impulse + jnp.where(planes[s] == x, sent[s, c], 0.0)
-            out[c, x] = center + 0.25 * (spread - advect) + impulse
+            out[c, x] = center + 0.125 * (spread - advect) + impulse
         return carry
 
     lax.fori_loop(0, u.shape[1], plane, 0, unroll=8)

time: 122 us -> 121 us (level)
  no operation moved by 1% of the time
where the time goes in v14:
time: 121 us; the launch traced here: 120 us
  starting transfers between devices  53.5 us (44%)
  Pallas kernels  26.1 us (22%)
  matrix products  16.8 us (14%)
  local copies, waits for them, and re-layouts  11.2 us (9%)
  waiting for transfers between devices  6.98 us (6%)
  between operations  4.97 us (4%)
    ppermute x6, starting transfers between devices, faces(): lax.ppermute(last, axis, forward)  20.2 us
    pallas_call x1, Pallas kernels, stencil(): vmem_call(advance_kernel, jax.ShapeDtypeStruct(velocity.shape, jnp.float3...  14.9 us
    pallas_call x1, Pallas kernels, stencil(): vmem_call(viscosity_kernel, jax.ShapeDtypeStruct(velocity.shape[1:], jnp....  11.2 us
    all_to_all x1, starting transfers between devices, body(): lax.all_to_all(partial_sample.reshape(rows, per_row, -1), 'gx', split_axi...  9.97 us
    ppermute x6, starting transfers between devices, faces(): lax.ppermute(first, axis, backward)  9.79 us
    ppermute x4, starting transfers between devices, body(): owned = owned + lax.ppermute(owned, axis, pairs)  8.93 us
    dot_general x2, matrix products, faces(): jnp.einsum(letters + ',ky->k' + letters[:-3] + 'zx', block, ends, precisi...  7.75 us
    all_to_all x1, waiting for transfers between devices, body(): lax.all_to_all(partial_sample.reshape(rows, per_row, -1), 'gx', split_axi...  5.45 us
  transfers between devices with their start and end apart: 18, of which 2 were waited for; matrix products, arithmetic and copies ran while one was open for 14% of the time, Pallas kernels for 9%

profile of v14, /device:TPU:1, one launch (start us, length us, event | category | flops | bytes accessed | tf_op | source)
XLA Modules:
  0.0 120.4 jit_solution(12342251012955877186)
XLA Ops:
  0.6 1.3 %fusion.25 = (s32[1,1,1,1]{3,2,1,0:T(1,128)}, s32[1,1,1,1]{3,2,1,0:T(1,128)}) fusion(s32[1,1,1,2]{3,2,1,0:T(1,128)} %param.9), kind=kLoop, calls=%fused_computation.44 | loop fusion | bytes 16 | tf_op jit(solution)/shard_map/slice | solution.py:149
  6.7 4.7 %fusion.2 = f32[2,3,384]{2,1,0:T(4,128)S(1)} fusion(bf16[1,1,1,2,384,4096]{5,4,3,2,1,0:T(8,128)(2,1)} %param.10, bf16[1,3,4096]{2,1,0:T(4,128)(2,1)S(1)} %stack.10, bf16[1,3,4096]{2,1,0:T(4,128)(2,1)S(1)} %stack.9), kind=kOutput, calls=%fused_computation.2 | convolution fusion | flops 18972672 | bytes 6349824 | tf_op jit(solution)/shard_map/spq,scq->scp/dot_general | solution.py:151
  12.7 10.0 %all-to-all-start = ((f32[16,4,1152]{2,1,0:T(4,128)}), f32[16,4,1152]{2,1,0:T(4,128)S(1)}, u32[]{:S(2)}, u32[]{:S(2)}) async-start(f32[16,4,1152]{2,1,0:T(4,128)} %copy.41), calls=%async_computation | async-start | bytes 589824 | tf_op jit(solution)/shard_map/all_to_all | solution.py:165
  22.7 4.9 %fusion.4 = f32[2,3,64,32]{2,0,3,1:T(2,128)S(1)} fusion(f32[3,64,32,128]{3,2,1,0:T(8,128)S(1)} %copy-done, s32[2]{0:T(128)S(1)} %iota_multiply_fusion), kind=kOutput, calls=%fused_computation.4 | convolution fusion | flops 18874624 | bytes 3194888 | tf_op jit(solution)/shard_map/cxzy,ky->kczx/dot_general | solution.py:22
  29.5 5.4 %all-to-all-done = f32[16,4,1152]{2,1,0:T(4,128)S(1)} async-done(((f32[16,4,1152]{2,1,0:T(4,128)}), f32[16,4,1152]{2,1,0:T(4,128)S(1)}, u32[]{:S(2)}, u32[]{:S(2)}) %all-to-all-start) | async-done | bytes 294944 | tf_op jit(solution)/shard_map/all_to_all | solution.py:165
  37.1 3.2 %collective-permute-start.2 = (f32[3,64,128]{2,1,0:T(8,128)}, f32[3,64,128]{2,1,0:T(8,128)S(1)}, u32[]{:S(2)}, u32[]{:S(2)}) collective-permute-start(f32[3,64,128]{2,1,0:T(8,128)} %bitcast.3), channel_id=1, source_target_pairs={{0,1},{1,2},{2,3},{4,5},{5,6},{6,7},{8,9},{9,10},{10,11},{12,13},{... | collective-permute-start | bytes 294920 | tf_op jit(solution)/shard_map/ppermute | solution.py:36
  41.7 2.5 %collective-permute-start.13 = (f32[4,1152]{1,0:T(4,128)S(1)}, f32[4,1152]{1,0:T(4,128)S(1)}, u32[]{:S(2)}, u32[]{:S(2)}) collective-permute-start(f32[4,1152]{1,0:T(4,128)S(1)} %add.35), channel_id=1, source_target_pairs={{0,8},{4,12},{8,0},{12,4},{1,9},{5,13},{9,1},{13,5},{2,10},{6,14},... | collective-permute-start | bytes 55304 | tf_op jit(solution)/shard_map/ppermute | solution.py:174
  44.8 2.3 %collective-permute-start.1 = (f32[3,32,128]{2,1,0:T(8,128)}, f32[3,32,128]{2,1,0:T(8,128)S(1)}, u32[]{:S(2)}, u32[]{:S(2)}) collective-permute-start(f32[3,32,128]{2,1,0:T(8,128)} %get-tuple-element.8), channel_id=1, source_target_pairs={{16,0},{32,16},{48,32},{64,48},{80,64},{96,80},{112,96},{128,112},... | collective-permute-start | bytes 147464 | tf_op jit(solution)/shard_map/ppermute | solution.py:36
  47.2 3.2 %collective-permute-start = (f32[3,32,128]{2,1,0:T(8,128)S(1)}, f32[3,32,128]{2,1,0:T(8,128)S(1)}, u32[]{:S(2)}, u32[]{:S(2)}) collective-permute-start(f32[3,32,128]{2,1,0:T(8,128)S(1)} %get-tuple-element.9), channel_id=1, source_target_pairs={{0,16},{16,32},{32,48},{48,64},{64,80},{80,96},{96,112},{112,128},... | collective-permute-start | bytes 147464 | tf_op jit(solution)/shard_map/ppermute | solution.py:36
  50.4 1.8 %collective-permute-start.4 = (f32[3,32,64]{2,1,0:T(8,128)}, f32[3,32,64]{2,1,0:T(8,128)S(1)}, u32[]{:S(2)}, u32[]{:S(2)}) collective-permute-start(f32[3,32,64]{2,1,0:T(8,128)} %get-tuple-element.15), channel_id=1, source_target_pairs={{0,4},{4,8},{8,12},{1,5},{5,9},{9,13},{2,6},{6,10},{10,14},{3,7},{... | collective-permute-start | bytes 73736 | tf_op jit(solution)/shard_map/ppermute | solution.py:36
  52.3 1.5 %collective-permute-done.4.ylo = f32[3,32,64]{2,1,0:T(8,128)S(1)} collective-permute-done((f32[3,32,64]{2,1,0:T(8,128)}, f32[3,32,64]{2,1,0:T(8,128)S(1)}, u32[]{:S(2)}, u32[]{:S(2)}) %collective-permute-start.4) | collective-permute-done | bytes 24608 | tf_op jit(solution)/shard_map/ppermute | solution.py:36
  53.8 2.4 %collective-permute-start.14 = (f32[4,1152]{1,0:T(4,128)S(1)}, f32[4,1152]{1,0:T(4,128)S(1)}, u32[]{:S(2)}, u32[]{:S(2)}) collective-permute-start(f32[4,1152]{1,0:T(4,128)S(1)} %add.36), channel_id=1, source_target_pairs={{0,1},{1,0},{2,3},{3,2},{4,5},{5,4},{6,7},{7,6},{8,9},{9,8},{10,11... | collective-permute-start | bytes 55304 | tf_op jit(solution)/shard_map/ppermute | solution.py:174
  57.5 11.2 %shard_map.86.nu = f32[64,32,128]{2,1,0:T(8,128)} custom-call(f32[3,64,32,128]{3,2,1,0:T(8,128)} %u.3, f32[3,32,128]{2,1,0:T(8,128)} %copy-done.6, f32[3,32,128]{2,1,0:T(8,128)} %copy-done.5, f32[3,64,128]{2,1,0:T(8,128)} %copy-done.2, f32[3,64,128]{2,1,0:T(8,128)} %copy-done.3, f32[3,32,64]{2,1,0:T(8,128)} %copy-done.7, f32[3,32,64]{2,1,0:T(8,128)} %copy-done.4), custom_call_target="tpu_custom_call" | custom-call | tf_op jit(solution)/shard_map/pallas_call | solution.py:127
  68.7 2.7 %collective-permute-start.15 = (f32[4,1152]{1,0:T(4,128)S(1)}, f32[4,1152]{1,0:T(4,128)S(1)}, u32[]{:S(2)}, u32[]{:S(2)}) collective-permute-start(f32[4,1152]{1,0:T(4,128)S(1)} %add.37), channel_id=1, source_target_pairs={{0,2},{1,3},{2,0},{3,1},{4,6},{5,7},{6,4},{7,5},{8,10},{9,11},{10,... | collective-permute-start | bytes 55304 | tf_op jit(solution)/shard_map/ppermute | solution.py:174
  71.5 2.9 %fusion.14 = f32[2,64,32]{1,0,2:T(2,128)S(1)} fusion(s32[2]{0:T(128)S(1)} %iota_multiply_fusion, f32[64,32,128]{2,1,0:T(8,128)} %shard_map.86.nu), kind=kOutput, calls=%fused_computation.31 | convolution fusion | flops 6291712 | bytes 1064968 | tf_op jit(solution)/shard_map/xzy,ky->kzx/dot_general | solution.py:22
  75.9 4.6 %all-to-all-start.1 = ((f32[16,4,1152]{2,1,0:T(4,128)}), f32[16,4,1152]{2,1,0:T(4,128)S(1)}, u32[]{:S(2)}, u32[]{:S(2)}) async-start(f32[16,4,1152]{2,1,0:T(4,128)} %broadcast_in_dim.2), calls=%async_computation.1 | async-start | bytes 589824 | tf_op jit(solution)/shard_map/all_to_all | solution.py:178
  80.5 1.8 %copy.37 = f32[64,32,128]{2,0,1:T(8,128)S(1)} copy(f32[64,32,128]{2,1,0:T(8,128)} %shard_map.86.nu) | data formatting | bytes 2097152 | tf_op jit(solution)/shard_map/pallas_call | solution.py:127
  82.4 1.3 %collective-permute-start.11 = (f32[32,64]{1,0:T(8,128)S(1)}, f32[32,64]{1,0:T(8,128)S(1)}, u32[]{:S(2)}, u32[]{:S(2)}) collective-permute-start(f32[32,64]{1,0:T(8,128)S(1)} %get-tuple-element.16), channel_id=1, source_target_pairs={{4,0},{8,4},{12,8},{5,1},{9,5},{13,9},{6,2},{10,6},{14,10},{7,3},{... | collective-permute-start | bytes 24584 | tf_op jit(solution)/shard_map/ppermute | solution.py:36
  83.7 4.5 %collective-permute-start.10 = (f32[32,64]{1,0:T(8,128)S(1)}, f32[32,64]{1,0:T(8,128)S(1)}, u32[]{:S(2)}, u32[]{:S(2)}) collective-permute-start(f32[32,64]{1,0:T(8,128)S(1)} %get-tuple-element.17), channel_id=1, source_target_pairs={{0,4},{4,8},{8,12},{1,5},{5,9},{9,13},{2,6},{6,10},{10,14},{3,7},{... | collective-permute-start | bytes 24584 | tf_op jit(solution)/shard_map/ppermute | solution.py:36
  88.9 2.3 %collective-permute-start.7 = (f32[32,128]{1,0:T(8,128)S(1)}, f32[32,128]{1,0:T(8,128)S(1)}, u32[]{:S(2)}, u32[]{:S(2)}) collective-permute-start(f32[32,128]{1,0:T(8,128)S(1)} %get-tuple-element.12), channel_id=1, source_target_pairs={{16,0},{32,16},{48,32},{64,48},{80,64},{96,80},{112,96},{128,112},... | collective-permute-start | bytes 49160 | tf_op jit(solution)/shard_map/ppermute | solution.py:36
  91.2 3.4 %collective-permute-start.6 = (f32[32,128]{1,0:T(8,128)S(1)}, f32[32,128]{1,0:T(8,128)S(1)}, u32[]{:S(2)}, u32[]{:S(2)}) collective-permute-start(f32[32,128]{1,0:T(8,128)S(1)} %get-tuple-element.13), channel_id=1, source_target_pairs={{0,16},{16,32},{32,48},{48,64},{64,80},{80,96},{96,112},{112,128},... | collective-permute-start | bytes 49160 | tf_op jit(solution)/shard_map/ppermute | solution.py:36
  96.4 4.0 %collective-permute-start.8 = (f32[64,128]{1,0:T(8,128)S(1)}, f32[64,128]{1,0:T(8,128)S(1)}, u32[]{:S(2)}, u32[]{:S(2)}) collective-permute-start(f32[64,128]{1,0:T(8,128)S(1)} %get-tuple-element.11), channel_id=1, source_target_pairs={{0,1},{1,2},{2,3},{4,5},{5,6},{6,7},{8,9},{9,10},{10,11},{12,13},{... | collective-permute-start | bytes 98312 | tf_op jit(solution)/shard_map/ppermute | solution.py:36
  100.4 3.7 %fusion = f32[2,3,4096]{2,1,0:T(4,128)S(1)} fusion(bf16[2,3,384]{2,1,0:T(4,128)(2,1)S(1)} %reshape.71, bf16[1,1,1,2,384,4096]{5,4,3,2,1,0:T(8,128)(2,1)} %param.10), kind=kOutput, calls=%fused_computation | convolution fusion | flops 18874368 | bytes 6394368 | tf_op jit(solution)/shard_map/axz,ahx->ahz/dot_general | solution.py:183
  105.5 14.9 %shard_map.87 = f32[3,64,32,128]{3,2,1,0:T(8,128)} custom-call(s32[2]{0:T(128)} %bitcast.66, f32[3,64,32,128]{3,2,1,0:T(8,128)} %u.3, f32[3,32,128]{2,1,0:T(8,128)} %copy-done.6, f32[3,32,128]{2,1,0:T(8,128)} %copy-done.5, f32[3,64,128]{2,1,0:T(8,128)} %copy-done.2, f32[3,64,128]{2,1,0:T(8,128)} %copy-done.3, f32[3,32,64]{2,1,0:T(8,128)} %copy-done.7, ...), custom_call_target="tpu_custom_call" | custom-call | tf_op jit(solution)/shard_map/pallas_call | solution.py:131
  (80 shorter events, 14.8 us)
Async XLA Ops:
  6.7 4.7 %copy-start.14 = (s32[1,1,1,2]{3,2,1,0:T(1,128)S(1)}, s32[1,1,1,2]{3,2,1,0:T(1,128)}, u32[]{:S(2)}) copy-start(s32[1,1,1,2]{3,2,1,0:T(1,128)} %param.8) | copy-start | bytes 28
  6.7 16.0 %copy-start = (f32[3,64,32,128]{3,2,1,0:T(8,128)S(1)}, f32[3,64,32,128]{3,2,1,0:T(8,128)}, u32[]{:S(2)}) copy-start(f32[3,64,32,128]{3,2,1,0:T(8,128)} %u.3) | copy-start | bytes 9437188
  12.7 22.3 %all-to-all-start = ((f32[16,4,1152]{2,1,0:T(4,128)}), f32[16,4,1152]{2,1,0:T(4,128)S(1)}, u32[]{:S(2)}, u32[]{:S(2)}) async-start(f32[16,4,1152]{2,1,0:T(4,128)} %copy.41), calls=%async_computation | async-start | bytes 589824 | tf_op jit(solution)/shard_map/all_to_all | solution.py:165
  28.2 18.9 %collective-permute-start.5 = (f32[3,32,64]{2,1,0:T(8,128)}, f32[3,32,64]{2,1,0:T(8,128)S(1)}, u32[]{:S(2)}, u32[]{:S(2)}) collective-permute-start(f32[3,32,64]{2,1,0:T(8,128)} %get-tuple-element.14), channel_id=1, source_target_pairs={{4,0},{8,4},{12,8},{5,1},{9,5},{13,9},{6,2},{10,6},{14,10},{7,3},{... | collective-permute-start | bytes 73736 | tf_op jit(solution)/shard_map/ppermute | solution.py:36
  35.0 6.6 %collective-permute-start.12 = (f32[4,1152]{1,0:T(4,128)S(1)}, f32[4,1152]{1,0:T(4,128)S(1)}, u32[]{:S(2)}, u32[]{:S(2)}) collective-permute-start(f32[4,1152]{1,0:T(4,128)S(1)} %reduce_sum.18), channel_id=1, source_target_pairs={{0,4},{4,0},{8,12},{12,8},{1,5},{5,1},{9,13},{13,9},{2,6},{6,2},{1... | collective-permute-start | bytes 55304 | tf_op jit(solution)/shard_map/ppermute | solution.py:174
  37.1 19.1 %collective-permute-start.2 = (f32[3,64,128]{2,1,0:T(8,128)}, f32[3,64,128]{2,1,0:T(8,128)S(1)}, u32[]{:S(2)}, u32[]{:S(2)}) collective-permute-start(f32[3,64,128]{2,1,0:T(8,128)} %bitcast.3), channel_id=1, source_target_pairs={{0,1},{1,2},{2,3},{4,5},{5,6},{6,7},{8,9},{9,10},{10,11},{12,13},{... | collective-permute-start | bytes 294920 | tf_op jit(solution)/shard_map/ppermute | solution.py:36
  40.3 15.9 %collective-permute-start.3 = (f32[3,64,128]{2,1,0:T(8,128)}, f32[3,64,128]{2,1,0:T(8,128)S(1)}, u32[]{:S(2)}, u32[]{:S(2)}) collective-permute-start(f32[3,64,128]{2,1,0:T(8,128)} %bitcast.4), channel_id=1, source_target_pairs={{1,0},{2,1},{3,2},{5,4},{6,5},{7,6},{9,8},{10,9},{11,10},{13,12},{... | collective-permute-start | bytes 294920 | tf_op jit(solution)/shard_map/ppermute | solution.py:36
  41.7 8.8 %collective-permute-start.13 = (f32[4,1152]{1,0:T(4,128)S(1)}, f32[4,1152]{1,0:T(4,128)S(1)}, u32[]{:S(2)}, u32[]{:S(2)}) collective-permute-start(f32[4,1152]{1,0:T(4,128)S(1)} %add.35), channel_id=1, source_target_pairs={{0,8},{4,12},{8,0},{12,4},{1,9},{5,13},{9,1},{13,5},{2,10},{6,14},... | collective-permute-start | bytes 55304 | tf_op jit(solution)/shard_map/ppermute | solution.py:174
  44.8 11.3 %collective-permute-start.1 = (f32[3,32,128]{2,1,0:T(8,128)}, f32[3,32,128]{2,1,0:T(8,128)S(1)}, u32[]{:S(2)}, u32[]{:S(2)}) collective-permute-start(f32[3,32,128]{2,1,0:T(8,128)} %get-tuple-element.8), channel_id=1, source_target_pairs={{16,0},{32,16},{48,32},{64,48},{80,64},{96,80},{112,96},{128,112},... | collective-permute-start | bytes 147464 | tf_op jit(solution)/shard_map/ppermute | solution.py:36
  47.2 9.1 %copy-start.4 = (f32[3,32,64]{2,1,0:T(8,128)}, f32[3,32,64]{2,1,0:T(8,128)S(1)}, u32[]{:S(2)}) copy-start(f32[3,32,64]{2,1,0:T(8,128)S(1)} %collective-permute-done.5.yhi) | copy-start | bytes 73732
  47.2 9.0 %collective-permute-start = (f32[3,32,128]{2,1,0:T(8,128)S(1)}, f32[3,32,128]{2,1,0:T(8,128)S(1)}, u32[]{:S(2)}, u32[]{:S(2)}) collective-permute-start(f32[3,32,128]{2,1,0:T(8,128)S(1)} %get-tuple-element.9), channel_id=1, source_target_pairs={{0,16},{16,32},{32,48},{48,64},{64,80},{80,96},{96,112},{112,128},... | collective-permute-start | bytes 147464 | tf_op jit(solution)/shard_map/ppermute | solution.py:36
  50.4 3.4 %collective-permute-start.4 = (f32[3,32,64]{2,1,0:T(8,128)}, f32[3,32,64]{2,1,0:T(8,128)S(1)}, u32[]{:S(2)}, u32[]{:S(2)}) collective-permute-start(f32[3,32,64]{2,1,0:T(8,128)} %get-tuple-element.15), channel_id=1, source_target_pairs={{0,4},{4,8},{8,12},{1,5},{5,9},{9,13},{2,6},{6,10},{10,14},{3,7},{... | collective-permute-start | bytes 73736 | tf_op jit(solution)/shard_map/ppermute | solution.py:36
  53.8 2.5 %copy-start.7 = (f32[3,32,64]{2,1,0:T(8,128)}, f32[3,32,64]{2,1,0:T(8,128)S(1)}, u32[]{:S(2)}) copy-start(f32[3,32,64]{2,1,0:T(8,128)S(1)} %collective-permute-done.4.ylo) | copy-start | bytes 73732
  53.8 15.0 %collective-permute-start.14 = (f32[4,1152]{1,0:T(4,128)S(1)}, f32[4,1152]{1,0:T(4,128)S(1)}, u32[]{:S(2)}, u32[]{:S(2)}) collective-permute-start(f32[4,1152]{1,0:T(4,128)S(1)} %add.36), channel_id=1, source_target_pairs={{0,1},{1,0},{2,3},{3,2},{4,5},{5,4},{6,7},{7,6},{8,9},{9,8},{10,11... | collective-permute-start | bytes 55304 | tf_op jit(solution)/shard_map/ppermute | solution.py:174
  68.7 5.6 %collective-permute-start.15 = (f32[4,1152]{1,0:T(4,128)S(1)}, f32[4,1152]{1,0:T(4,128)S(1)}, u32[]{:S(2)}, u32[]{:S(2)}) collective-permute-start(f32[4,1152]{1,0:T(4,128)S(1)} %add.37), channel_id=1, source_target_pairs={{0,2},{1,3},{2,0},{3,1},{4,6},{5,7},{6,4},{7,5},{8,10},{9,11},{10,... | collective-permute-start | bytes 55304 | tf_op jit(solution)/shard_map/ppermute | solution.py:174
  75.9 20.1 %all-to-all-start.1 = ((f32[16,4,1152]{2,1,0:T(4,128)}), f32[16,4,1152]{2,1,0:T(4,128)S(1)}, u32[]{:S(2)}, u32[]{:S(2)}) async-start(f32[16,4,1152]{2,1,0:T(4,128)} %broadcast_in_dim.2), calls=%async_computation.1 | async-start | bytes 589824 | tf_op jit(solution)/shard_map/all_to_all | solution.py:178
  82.4 14.0 %collective-permute-start.11 = (f32[32,64]{1,0:T(8,128)S(1)}, f32[32,64]{1,0:T(8,128)S(1)}, u32[]{:S(2)}, u32[]{:S(2)}) collective-permute-start(f32[32,64]{1,0:T(8,128)S(1)} %get-tuple-element.16), channel_id=1, source_target_pairs={{4,0},{8,4},{12,8},{5,1},{9,5},{13,9},{6,2},{10,6},{14,10},{7,3},{... | collective-permute-start | bytes 24584 | tf_op jit(solution)/shard_map/ppermute | solution.py:36
  83.7 21.1 %collective-permute-start.10 = (f32[32,64]{1,0:T(8,128)S(1)}, f32[32,64]{1,0:T(8,128)S(1)}, u32[]{:S(2)}, u32[]{:S(2)}) collective-permute-start(f32[32,64]{1,0:T(8,128)S(1)} %get-tuple-element.17), channel_id=1, source_target_pairs={{0,4},{4,8},{8,12},{1,5},{5,9},{9,13},{2,6},{6,10},{10,14},{3,7},{... | collective-permute-start | bytes 24584 | tf_op jit(solution)/shard_map/ppermute | solution.py:36
  88.9 15.9 %collective-permute-start.7 = (f32[32,128]{1,0:T(8,128)S(1)}, f32[32,128]{1,0:T(8,128)S(1)}, u32[]{:S(2)}, u32[]{:S(2)}) collective-permute-start(f32[32,128]{1,0:T(8,128)S(1)} %get-tuple-element.12), channel_id=1, source_target_pairs={{16,0},{32,16},{48,32},{64,48},{80,64},{96,80},{112,96},{128,112},... | collective-permute-start | bytes 49160 | tf_op jit(solution)/shard_map/ppermute | solution.py:36
  91.2 13.6 %collective-permute-start.6 = (f32[32,128]{1,0:T(8,128)S(1)}, f32[32,128]{1,0:T(8,128)S(1)}, u32[]{:S(2)}, u32[]{:S(2)}) collective-permute-start(f32[32,128]{1,0:T(8,128)S(1)} %get-tuple-element.13), channel_id=1, source_target_pairs={{0,16},{16,32},{32,48},{48,64},{64,80},{80,96},{96,112},{112,128},... | collective-permute-start | bytes 49160 | tf_op jit(solution)/shard_map/ppermute | solution.py:36
  94.7 10.2 %collective-permute-start.9 = (f32[64,128]{1,0:T(8,128)S(1)}, f32[64,128]{1,0:T(8,128)S(1)}, u32[]{:S(2)}, u32[]{:S(2)}) collective-permute-start(f32[64,128]{1,0:T(8,128)S(1)} %get-tuple-element.10), channel_id=1, source_target_pairs={{1,0},{2,1},{3,2},{5,4},{6,5},{7,6},{9,8},{10,9},{11,10},{13,12},{... | collective-permute-start | bytes 98312 | tf_op jit(solution)/shard_map/ppermute | solution.py:36
  96.1 8.0 %copy-start.1 = (f32[64,1152]{1,0:T(8,128)}, f32[64,1152]{1,0:T(8,128)S(1)}, u32[]{:S(2)}) copy-start(f32[64,1152]{1,0:T(8,128)S(1)} %reshape.70) | copy-start | bytes 884740
  96.4 7.7 %copy-start.10 = (f32[32,64]{1,0:T(8,128)}, f32[32,64]{1,0:T(8,128)S(1)}, u32[]{:S(2)}) copy-start(f32[32,64]{1,0:T(8,128)S(1)} %collective-permute-done.11.nyhi) | copy-start | bytes 24580
  96.4 8.5 %collective-permute-start.8 = (f32[64,128]{1,0:T(8,128)S(1)}, f32[64,128]{1,0:T(8,128)S(1)}, u32[]{:S(2)}, u32[]{:S(2)}) collective-permute-start(f32[64,128]{1,0:T(8,128)S(1)} %get-tuple-element.11), channel_id=1, source_target_pairs={{0,1},{1,2},{2,3},{4,5},{5,6},{6,7},{8,9},{9,10},{10,11},{12,13},{... | collective-permute-start | bytes 98312 | tf_op jit(solution)/shard_map/ppermute | solution.py:36
  (9 other events, 5.6 us)

commit v15 on v14

--- a/solution.py
+++ b/solution.py
@@ -28,7 +28,8 @@
         forward = [(i, i + 1) for i in range(count - 1)]
         backward = [(target, source) for source, target in forward]
         if dim is None:
-            first, last = columns[0], columns[1]
+            pad = [(0, 0)] * (columns.ndim - 2) + [(0, ny - columns.shape[-1])]
+            first, last = jnp.pad(columns[0], pad), jnp.pad(columns[1], pad)
         else:
             size = block.shape[dim]
             first = lax.index_in_dim(block, 0, dim, keepdims=False)
@@ -42,7 +43,6 @@
     nz, ny = centre.shape
     sub = lax.broadcasted_iota(jnp.int32, (nz, ny), 0)
     lane = lax.broadcasted_iota(jnp.int32, (nz, ny), 1)
-    column = lax.broadcasted_iota(jnp.int32, (nz, nx), 1)
     prev = ref[lead + (jnp.maximum(x - 1, 0),)]
     nxt = ref[lead + (jnp.minimum(x + 1, nx - 1),)]
     xm = jnp.where(x == 0, xlo[lead], prev)
@@ -51,8 +51,8 @@
     zh = zhi[lead + (pl.ds(x, 1), slice(None))]
     zm = jnp.where(sub == 0, zl, pltpu.roll(centre, 1, 0))
     zp = jnp.where(sub == nz - 1, zh, pltpu.roll(centre, nz - 1, 0))
-    yl = jnp.sum(jnp.where(column == x, ylo[lead], 0.0), axis=1, keepdims=True)
-    yh = jnp.sum(jnp.where(column == x, yhi[lead], 0.0), axis=1, keepdims=True)
+    yl = pltpu.roll(ylo[lead], jnp.where(x == 0, 0, ny - x), 1)
+    yh = pltpu.roll(yhi[lead], ny - 1 - x, 1)
     ym = jnp.where(lane == 0, yl, pltpu.roll(centre, 1, 1))
     yp = jnp.where(lane == ny - 1, yh, pltpu.roll(centre, ny - 1, 1))
     return xm, xp, ym, yp, zm, zp

time: 121 us -> 115 us (0.950)
  the two profiles are of different devices: /device:TPU:1 before, /device:TPU:5 now
where the time goes in v15:
time: 115 us; the launch traced here: 114 us
  starting transfers between devices  59.1 us (51%)
  Pallas kernels  17.6 us (15%)
  matrix products  16.8 us (15%)
  local copies, waits for them, and re-layouts  11.2 us (10%)
  between operations  4.99 us (4%)
  other arithmetic  2.17 us (2%)
  waiting for transfers between devices  1.86 us (2%)
    ppermute x6, starting transfers between devices, faces(): lax.ppermute(last, axis, forward)  20.9 us
    ppermute x6, starting transfers between devices, faces(): lax.ppermute(first, axis, backward)  13 us
    pallas_call x1, Pallas kernels, stencil(): vmem_call(advance_kernel, jax.ShapeDtypeStruct(velocity.shape, jnp.float3...  10.3 us
    all_to_all x1, starting transfers between devices, body(): lax.all_to_all(jnp.broadcast_to(owned_force[None], (rows,) + owned_force....  9.42 us
    all_to_all x1, starting transfers between devices, body(): lax.all_to_all(partial_sample.reshape(rows, per_row, -1), 'gx', split_axi...  9.16 us
    dot_general x2, matrix products, faces(): jnp.einsum(letters + ',ky->k' + letters[:-3] + 'zx', block, ends, precisi...  7.75 us
    pallas_call x1, Pallas kernels, stencil(): vmem_call(viscosity_kernel, jax.ShapeDtypeStruct(velocity.shape[1:], jnp....  7.3 us
    ppermute x4, starting transfers between devices, body(): owned = owned + lax.ppermute(owned, axis, pairs)  6.61 us
  transfers between devices with their start and end apart: 18, of which 2 were waited for; matrix products, arithmetic and copies ran while one was open for 16% of the time, Pallas kernels for 6%

profile of v15, /device:TPU:5, one launch (start us, length us, event | category | flops | bytes accessed | tf_op | source)
XLA Modules:
  0.0 113.7 jit_solution(9825960587582126260)
XLA Ops:
  0.6 1.3 %fusion.25 = (s32[1,1,1,1]{3,2,1,0:T(1,128)}, s32[1,1,1,1]{3,2,1,0:T(1,128)}) fusion(s32[1,1,1,2]{3,2,1,0:T(1,128)} %param.9), kind=kLoop, calls=%fused_computation.44 | loop fusion | bytes 16 | tf_op jit(solution)/shard_map/slice | solution.py:149
  6.7 4.7 %fusion.2 = f32[2,3,384]{2,1,0:T(4,128)S(1)} fusion(bf16[1,1,1,2,384,4096]{5,4,3,2,1,0:T(8,128)(2,1)} %param.10, bf16[1,3,4096]{2,1,0:T(4,128)(2,1)S(1)} %stack.10, bf16[1,3,4096]{2,1,0:T(4,128)(2,1)S(1)} %stack.9), kind=kOutput, calls=%fused_computation.2 | convolution fusion | flops 18972672 | bytes 6349824 | tf_op jit(solution)/shard_map/spq,scq->scp/dot_general | solution.py:151
  12.7 9.2 %all-to-all-start = ((f32[16,4,1152]{2,1,0:T(4,128)}), f32[16,4,1152]{2,1,0:T(4,128)S(1)}, u32[]{:S(2)}, u32[]{:S(2)}) async-start(f32[16,4,1152]{2,1,0:T(4,128)} %copy.41), calls=%async_computation | async-start | bytes 589824 | tf_op jit(solution)/shard_map/all_to_all | solution.py:165
  21.9 4.9 %fusion.4 = f32[2,3,64,32]{2,0,3,1:T(2,128)S(1)} fusion(f32[3,64,32,128]{3,2,1,0:T(8,128)S(1)} %copy-done, s32[2]{0:T(128)S(1)} %iota_multiply_fusion), kind=kOutput, calls=%fused_computation.4 | convolution fusion | flops 18874624 | bytes 3194888 | tf_op jit(solution)/shard_map/cxzy,ky->kczx/dot_general | solution.py:22
  27.4 2.8 %collective-permute-start.4 = (f32[3,32,128]{2,1,0:T(8,128)}, f32[3,32,128]{2,1,0:T(8,128)S(1)}, u32[]{:S(2)}, u32[]{:S(2)}) collective-permute-start(f32[3,32,128]{2,1,0:T(8,128)} %pad.14), channel_id=1, source_target_pairs={{0,4},{4,8},{8,12},{1,5},{5,9},{9,13},{2,6},{6,10},{10,14},{3,7},{... | collective-permute-start | bytes 147464 | tf_op jit(solution)/shard_map/ppermute | solution.py:37
  30.9 2.4 %collective-permute-start.5 = (f32[3,32,128]{2,1,0:T(8,128)}, f32[3,32,128]{2,1,0:T(8,128)S(1)}, u32[]{:S(2)}, u32[]{:S(2)}) collective-permute-start(f32[3,32,128]{2,1,0:T(8,128)} %pad.15), channel_id=1, source_target_pairs={{4,0},{8,4},{12,8},{5,1},{9,5},{13,9},{6,2},{10,6},{14,10},{7,3},{... | collective-permute-start | bytes 147464 | tf_op jit(solution)/shard_map/ppermute | solution.py:37
  36.5 3.2 %collective-permute-start.2 = (f32[3,64,128]{2,1,0:T(8,128)}, f32[3,64,128]{2,1,0:T(8,128)S(1)}, u32[]{:S(2)}, u32[]{:S(2)}) collective-permute-start(f32[3,64,128]{2,1,0:T(8,128)} %bitcast.3), channel_id=1, source_target_pairs={{0,1},{1,2},{2,3},{4,5},{5,6},{6,7},{8,9},{9,10},{10,11},{12,13},{... | collective-permute-start | bytes 294920 | tf_op jit(solution)/shard_map/ppermute | solution.py:37
  39.7 1.3 %collective-permute-start.3 = (f32[3,64,128]{2,1,0:T(8,128)}, f32[3,64,128]{2,1,0:T(8,128)S(1)}, u32[]{:S(2)}, u32[]{:S(2)}) collective-permute-start(f32[3,64,128]{2,1,0:T(8,128)} %bitcast.4), channel_id=1, source_target_pairs={{1,0},{2,1},{3,2},{5,4},{6,5},{7,6},{9,8},{10,9},{11,10},{13,12},{... | collective-permute-start | bytes 294920 | tf_op jit(solution)/shard_map/ppermute | solution.py:37
  42.3 2.6 %collective-permute-start.1 = (f32[3,32,128]{2,1,0:T(8,128)S(1)}, f32[3,32,128]{2,1,0:T(8,128)S(1)}, u32[]{:S(2)}, u32[]{:S(2)}) collective-permute-start(f32[3,32,128]{2,1,0:T(8,128)S(1)} %get-tuple-element.8), channel_id=1, source_target_pairs={{16,0},{32,16},{48,32},{64,48},{80,64},{96,80},{112,96},{128,112},... | collective-permute-start | bytes 147464 | tf_op jit(solution)/shard_map/ppermute | solution.py:37
  45.9 5.0 %collective-permute-start = (f32[3,32,128]{2,1,0:T(8,128)S(1)}, f32[3,32,128]{2,1,0:T(8,128)S(1)}, u32[]{:S(2)}, u32[]{:S(2)}) collective-permute-start(f32[3,32,128]{2,1,0:T(8,128)S(1)} %get-tuple-element.9), channel_id=1, source_target_pairs={{0,16},{16,32},{32,48},{48,64},{64,80},{80,96},{96,112},{112,128},... | collective-permute-start | bytes 147464 | tf_op jit(solution)/shard_map/ppermute | solution.py:37
  50.9 2.4 %collective-permute-start.14 = (f32[4,1152]{1,0:T(4,128)S(1)}, f32[4,1152]{1,0:T(4,128)S(1)}, u32[]{:S(2)}, u32[]{:S(2)}) collective-permute-start(f32[4,1152]{1,0:T(4,128)S(1)} %add.44), channel_id=1, source_target_pairs={{0,1},{1,0},{2,3},{3,2},{4,5},{5,4},{6,7},{7,6},{8,9},{9,8},{10,11... | collective-permute-start | bytes 55304 | tf_op jit(solution)/shard_map/ppermute | solution.py:174
  54.7 7.3 %shard_map.86.nu = f32[64,32,128]{2,1,0:T(8,128)} custom-call(f32[3,64,32,128]{3,2,1,0:T(8,128)} %u.3, f32[3,32,128]{2,1,0:T(8,128)} %copy-done.7, f32[3,32,128]{2,1,0:T(8,128)} %copy-done.6, f32[3,64,128]{2,1,0:T(8,128)} %copy-done.2, f32[3,64,128]{2,1,0:T(8,128)} %copy-done.3, f32[3,32,128]{2,1,0:T(8,128)} %copy-done.4, f32[3,32,128]{2,1,0:T(8,128)} %copy-done.5), custom_call_target="tpu_custom_call" | custom-call | tf_op jit(solution)/shard_map/pallas_call | solution.py:127
  62.0 2.7 %collective-permute-start.15 = (f32[4,1152]{1,0:T(4,128)S(1)}, f32[4,1152]{1,0:T(4,128)S(1)}, u32[]{:S(2)}, u32[]{:S(2)}) collective-permute-start(f32[4,1152]{1,0:T(4,128)S(1)} %add.45), channel_id=1, source_target_pairs={{0,2},{1,3},{2,0},{3,1},{4,6},{5,7},{6,4},{7,5},{8,10},{9,11},{10,... | collective-permute-start | bytes 55304 | tf_op jit(solution)/shard_map/ppermute | solution.py:174
  64.7 2.9 %fusion.14 = f32[2,64,32]{1,0,2:T(2,128)S(1)} fusion(s32[2]{0:T(128)S(1)} %iota_multiply_fusion, f32[64,32,128]{2,1,0:T(8,128)} %shard_map.86.nu), kind=kOutput, calls=%fused_computation.31 | convolution fusion | flops 6291712 | bytes 1064968 | tf_op jit(solution)/shard_map/xzy,ky->kzx/dot_general | solution.py:22
  69.2 9.4 %all-to-all-start.1 = ((f32[16,4,1152]{2,1,0:T(4,128)}), f32[16,4,1152]{2,1,0:T(4,128)S(1)}, u32[]{:S(2)}, u32[]{:S(2)}) async-start(f32[16,4,1152]{2,1,0:T(4,128)} %broadcast_in_dim.2), calls=%async_computation.1 | async-start | bytes 589824 | tf_op jit(solution)/shard_map/all_to_all | solution.py:178
  78.6 1.8 %copy.37 = f32[64,32,128]{2,0,1:T(8,128)S(1)} copy(f32[64,32,128]{2,1,0:T(8,128)} %shard_map.86.nu) | data formatting | bytes 2097152 | tf_op jit(solution)/shard_map/pallas_call | solution.py:127
  80.5 2.5 %collective-permute-start.10 = (f32[32,128]{1,0:T(8,128)S(1)}, f32[32,128]{1,0:T(8,128)S(1)}, u32[]{:S(2)}, u32[]{:S(2)}) collective-permute-start(f32[32,128]{1,0:T(8,128)S(1)} %pad.16), channel_id=1, source_target_pairs={{0,4},{4,8},{8,12},{1,5},{5,9},{9,13},{2,6},{6,10},{10,14},{3,7},{... | collective-permute-start | bytes 49160 | tf_op jit(solution)/shard_map/ppermute | solution.py:37
  82.9 2.8 %collective-permute-start.11 = (f32[32,128]{1,0:T(8,128)S(1)}, f32[32,128]{1,0:T(8,128)S(1)}, u32[]{:S(2)}, u32[]{:S(2)}) collective-permute-start(f32[32,128]{1,0:T(8,128)S(1)} %pad.17), channel_id=1, source_target_pairs={{4,0},{8,4},{12,8},{5,1},{9,5},{13,9},{6,2},{10,6},{14,10},{7,3},{... | collective-permute-start | bytes 49160 | tf_op jit(solution)/shard_map/ppermute | solution.py:37
  86.5 2.6 %collective-permute-start.7 = (f32[32,128]{1,0:T(8,128)S(1)}, f32[32,128]{1,0:T(8,128)S(1)}, u32[]{:S(2)}, u32[]{:S(2)}) collective-permute-start(f32[32,128]{1,0:T(8,128)S(1)} %get-tuple-element.12), channel_id=1, source_target_pairs={{16,0},{32,16},{48,32},{64,48},{80,64},{96,80},{112,96},{128,112},... | collective-permute-start | bytes 49160 | tf_op jit(solution)/shard_map/ppermute | solution.py:37
  89.1 3.4 %collective-permute-start.6 = (f32[32,128]{1,0:T(8,128)S(1)}, f32[32,128]{1,0:T(8,128)S(1)}, u32[]{:S(2)}, u32[]{:S(2)}) collective-permute-start(f32[32,128]{1,0:T(8,128)S(1)} %get-tuple-element.13), channel_id=1, source_target_pairs={{0,16},{16,32},{32,48},{48,64},{64,80},{80,96},{96,112},{112,128},... | collective-permute-start | bytes 49160 | tf_op jit(solution)/shard_map/ppermute | solution.py:37
  92.6 1.3 %collective-permute-start.9 = (f32[64,128]{1,0:T(8,128)S(1)}, f32[64,128]{1,0:T(8,128)S(1)}, u32[]{:S(2)}, u32[]{:S(2)}) collective-permute-start(f32[64,128]{1,0:T(8,128)S(1)} %get-tuple-element.10), channel_id=1, source_target_pairs={{1,0},{2,1},{3,2},{5,4},{6,5},{7,6},{9,8},{10,9},{11,10},{13,12},{... | collective-permute-start | bytes 98312 | tf_op jit(solution)/shard_map/ppermute | solution.py:37
  94.3 4.0 %collective-permute-start.8 = (f32[64,128]{1,0:T(8,128)S(1)}, f32[64,128]{1,0:T(8,128)S(1)}, u32[]{:S(2)}, u32[]{:S(2)}) collective-permute-start(f32[64,128]{1,0:T(8,128)S(1)} %get-tuple-element.11), channel_id=1, source_target_pairs={{0,1},{1,2},{2,3},{4,5},{5,6},{6,7},{8,9},{9,10},{10,11},{12,13},{... | collective-permute-start | bytes 98312 | tf_op jit(solution)/shard_map/ppermute | solution.py:37
  98.3 3.7 %fusion = f32[2,3,4096]{2,1,0:T(4,128)S(1)} fusion(bf16[2,3,384]{2,1,0:T(4,128)(2,1)S(1)} %reshape.71, bf16[1,1,1,2,384,4096]{5,4,3,2,1,0:T(8,128)(2,1)} %param.10), kind=kOutput, calls=%fused_computation | convolution fusion | flops 18874368 | bytes 6394368 | tf_op jit(solution)/shard_map/axz,ahx->ahz/dot_general | solution.py:183
  103.4 10.3 %shard_map.87 = f32[3,64,32,128]{3,2,1,0:T(8,128)} custom-call(s32[2]{0:T(128)} %bitcast.66, f32[3,64,32,128]{3,2,1,0:T(8,128)} %u.3, f32[3,32,128]{2,1,0:T(8,128)} %copy-done.7, f32[3,32,128]{2,1,0:T(8,128)} %copy-done.6, f32[3,64,128]{2,1,0:T(8,128)} %copy-done.2, f32[3,64,128]{2,1,0:T(8,128)} %copy-done.3, f32[3,32,128]{2,1,0:T(8,128)} %copy-done.4, ...), custom_call_target="tpu_custom_call" | custom-call | tf_op jit(solution)/shard_map/pallas_call | solution.py:131
  (84 shorter events, 14.2 us)
Async XLA Ops:
  6.7 4.7 %copy-start.14 = (s32[1,1,1,2]{3,2,1,0:T(1,128)S(1)}, s32[1,1,1,2]{3,2,1,0:T(1,128)}, u32[]{:S(2)}) copy-start(s32[1,1,1,2]{3,2,1,0:T(1,128)} %param.8) | copy-start | bytes 28
  6.7 15.2 %copy-start = (f32[3,64,32,128]{3,2,1,0:T(8,128)S(1)}, f32[3,64,32,128]{3,2,1,0:T(8,128)}, u32[]{:S(2)}) copy-start(f32[3,64,32,128]{3,2,1,0:T(8,128)} %u.3) | copy-start | bytes 9437188
  12.7 21.4 %all-to-all-start = ((f32[16,4,1152]{2,1,0:T(4,128)}), f32[16,4,1152]{2,1,0:T(4,128)S(1)}, u32[]{:S(2)}, u32[]{:S(2)}) async-start(f32[16,4,1152]{2,1,0:T(4,128)} %copy.41), calls=%async_computation | async-start | bytes 589824 | tf_op jit(solution)/shard_map/all_to_all | solution.py:165
  27.4 14.9 %collective-permute-start.4 = (f32[3,32,128]{2,1,0:T(8,128)}, f32[3,32,128]{2,1,0:T(8,128)S(1)}, u32[]{:S(2)}, u32[]{:S(2)}) collective-permute-start(f32[3,32,128]{2,1,0:T(8,128)} %pad.14), channel_id=1, source_target_pairs={{0,4},{4,8},{8,12},{1,5},{5,9},{9,13},{2,6},{6,10},{10,14},{3,7},{... | collective-permute-start | bytes 147464 | tf_op jit(solution)/shard_map/ppermute | solution.py:37
  30.9 20.0 %collective-permute-start.5 = (f32[3,32,128]{2,1,0:T(8,128)}, f32[3,32,128]{2,1,0:T(8,128)S(1)}, u32[]{:S(2)}, u32[]{:S(2)}) collective-permute-start(f32[3,32,128]{2,1,0:T(8,128)} %pad.15), channel_id=1, source_target_pairs={{4,0},{8,4},{12,8},{5,1},{9,5},{13,9},{6,2},{10,6},{14,10},{7,3},{... | collective-permute-start | bytes 147464 | tf_op jit(solution)/shard_map/ppermute | solution.py:37
  34.8 6.2 %collective-permute-start.12 = (f32[4,1152]{1,0:T(4,128)}, f32[4,1152]{1,0:T(4,128)S(1)}, u32[]{:S(2)}, u32[]{:S(2)}) collective-permute-start(f32[4,1152]{1,0:T(4,128)} %reduce_sum.18), channel_id=1, source_target_pairs={{0,4},{4,0},{8,12},{12,8},{1,5},{5,1},{9,13},{13,9},{2,6},{6,2},{1... | collective-permute-start | bytes 55304 | tf_op jit(solution)/shard_map/ppermute | solution.py:174
  36.5 16.9 %collective-permute-start.2 = (f32[3,64,128]{2,1,0:T(8,128)}, f32[3,64,128]{2,1,0:T(8,128)S(1)}, u32[]{:S(2)}, u32[]{:S(2)}) collective-permute-start(f32[3,64,128]{2,1,0:T(8,128)} %bitcast.3), channel_id=1, source_target_pairs={{0,1},{1,2},{2,3},{4,5},{5,6},{6,7},{8,9},{9,10},{10,11},{12,13},{... | collective-permute-start | bytes 294920 | tf_op jit(solution)/shard_map/ppermute | solution.py:37
  39.7 13.7 %collective-permute-start.3 = (f32[3,64,128]{2,1,0:T(8,128)}, f32[3,64,128]{2,1,0:T(8,128)S(1)}, u32[]{:S(2)}, u32[]{:S(2)}) collective-permute-start(f32[3,64,128]{2,1,0:T(8,128)} %bitcast.4), channel_id=1, source_target_pairs={{1,0},{2,1},{3,2},{5,4},{6,5},{7,6},{9,8},{10,9},{11,10},{13,12},{... | collective-permute-start | bytes 294920 | tf_op jit(solution)/shard_map/ppermute | solution.py:37
  41.8 4.1 %collective-permute-start.13 = (f32[4,1152]{1,0:T(4,128)S(1)}, f32[4,1152]{1,0:T(4,128)S(1)}, u32[]{:S(2)}, u32[]{:S(2)}) collective-permute-start(f32[4,1152]{1,0:T(4,128)S(1)} %add.43), channel_id=1, source_target_pairs={{0,8},{4,12},{8,0},{12,4},{1,9},{5,13},{9,1},{13,5},{2,10},{6,14},... | collective-permute-start | bytes 55304 | tf_op jit(solution)/shard_map/ppermute | solution.py:174
  42.3 11.1 %copy-start.4 = (f32[3,32,128]{2,1,0:T(8,128)}, f32[3,32,128]{2,1,0:T(8,128)S(1)}, u32[]{:S(2)}) copy-start(f32[3,32,128]{2,1,0:T(8,128)S(1)} %collective-permute-done.4.ylo) | copy-start | bytes 147460
  42.3 11.0 %collective-permute-start.1 = (f32[3,32,128]{2,1,0:T(8,128)S(1)}, f32[3,32,128]{2,1,0:T(8,128)S(1)}, u32[]{:S(2)}, u32[]{:S(2)}) collective-permute-start(f32[3,32,128]{2,1,0:T(8,128)S(1)} %get-tuple-element.8), channel_id=1, source_target_pairs={{16,0},{32,16},{48,32},{64,48},{80,64},{96,80},{112,96},{128,112},... | collective-permute-start | bytes 147464 | tf_op jit(solution)/shard_map/ppermute | solution.py:37
  45.9 7.5 %collective-permute-start = (f32[3,32,128]{2,1,0:T(8,128)S(1)}, f32[3,32,128]{2,1,0:T(8,128)S(1)}, u32[]{:S(2)}, u32[]{:S(2)}) collective-permute-start(f32[3,32,128]{2,1,0:T(8,128)S(1)} %get-tuple-element.9), channel_id=1, source_target_pairs={{0,16},{16,32},{32,48},{48,64},{64,80},{80,96},{96,112},{112,128},... | collective-permute-start | bytes 147464 | tf_op jit(solution)/shard_map/ppermute | solution.py:37
  50.9 2.5 %copy-start.5 = (f32[3,32,128]{2,1,0:T(8,128)}, f32[3,32,128]{2,1,0:T(8,128)S(1)}, u32[]{:S(2)}) copy-start(f32[3,32,128]{2,1,0:T(8,128)S(1)} %collective-permute-done.5.yhi) | copy-start | bytes 147460
  50.9 11.1 %collective-permute-start.14 = (f32[4,1152]{1,0:T(4,128)S(1)}, f32[4,1152]{1,0:T(4,128)S(1)}, u32[]{:S(2)}, u32[]{:S(2)}) collective-permute-start(f32[4,1152]{1,0:T(4,128)S(1)} %add.44), channel_id=1, source_target_pairs={{0,1},{1,0},{2,3},{3,2},{4,5},{5,4},{6,7},{7,6},{8,9},{9,8},{10,11... | collective-permute-start | bytes 55304 | tf_op jit(solution)/shard_map/ppermute | solution.py:174
  62.0 5.6 %collective-permute-start.15 = (f32[4,1152]{1,0:T(4,128)S(1)}, f32[4,1152]{1,0:T(4,128)S(1)}, u32[]{:S(2)}, u32[]{:S(2)}) collective-permute-start(f32[4,1152]{1,0:T(4,128)S(1)} %add.45), channel_id=1, source_target_pairs={{0,2},{1,3},{2,0},{3,1},{4,6},{5,7},{6,4},{7,5},{8,10},{9,11},{10,... | collective-permute-start | bytes 55304 | tf_op jit(solution)/shard_map/ppermute | solution.py:174
  69.2 24.7 %all-to-all-start.1 = ((f32[16,4,1152]{2,1,0:T(4,128)}), f32[16,4,1152]{2,1,0:T(4,128)S(1)}, u32[]{:S(2)}, u32[]{:S(2)}) async-start(f32[16,4,1152]{2,1,0:T(4,128)} %broadcast_in_dim.2), calls=%async_computation.1 | async-start | bytes 589824 | tf_op jit(solution)/shard_map/all_to_all | solution.py:178
  80.5 13.8 %collective-permute-start.10 = (f32[32,128]{1,0:T(8,128)S(1)}, f32[32,128]{1,0:T(8,128)S(1)}, u32[]{:S(2)}, u32[]{:S(2)}) collective-permute-start(f32[32,128]{1,0:T(8,128)S(1)} %pad.16), channel_id=1, source_target_pairs={{0,4},{4,8},{8,12},{1,5},{5,9},{9,13},{2,6},{6,10},{10,14},{3,7},{... | collective-permute-start | bytes 49160 | tf_op jit(solution)/shard_map/ppermute | solution.py:37
  82.9 19.8 %collective-permute-start.11 = (f32[32,128]{1,0:T(8,128)S(1)}, f32[32,128]{1,0:T(8,128)S(1)}, u32[]{:S(2)}, u32[]{:S(2)}) collective-permute-start(f32[32,128]{1,0:T(8,128)S(1)} %pad.17), channel_id=1, source_target_pairs={{4,0},{8,4},{12,8},{5,1},{9,5},{13,9},{6,2},{10,6},{14,10},{7,3},{... | collective-permute-start | bytes 49160 | tf_op jit(solution)/shard_map/ppermute | solution.py:37
  86.5 16.2 %collective-permute-start.7 = (f32[32,128]{1,0:T(8,128)S(1)}, f32[32,128]{1,0:T(8,128)S(1)}, u32[]{:S(2)}, u32[]{:S(2)}) collective-permute-start(f32[32,128]{1,0:T(8,128)S(1)} %get-tuple-element.12), channel_id=1, source_target_pairs={{16,0},{32,16},{48,32},{64,48},{80,64},{96,80},{112,96},{128,112},... | collective-permute-start | bytes 49160 | tf_op jit(solution)/shard_map/ppermute | solution.py:37
  89.1 13.6 %collective-permute-start.6 = (f32[32,128]{1,0:T(8,128)S(1)}, f32[32,128]{1,0:T(8,128)S(1)}, u32[]{:S(2)}, u32[]{:S(2)}) collective-permute-start(f32[32,128]{1,0:T(8,128)S(1)} %get-tuple-element.13), channel_id=1, source_target_pairs={{0,16},{16,32},{32,48},{48,64},{64,80},{80,96},{96,112},{112,128},... | collective-permute-start | bytes 49160 | tf_op jit(solution)/shard_map/ppermute | solution.py:37
  92.6 10.2 %collective-permute-start.9 = (f32[64,128]{1,0:T(8,128)S(1)}, f32[64,128]{1,0:T(8,128)S(1)}, u32[]{:S(2)}, u32[]{:S(2)}) collective-permute-start(f32[64,128]{1,0:T(8,128)S(1)} %get-tuple-element.10), channel_id=1, source_target_pairs={{1,0},{2,1},{3,2},{5,4},{6,5},{7,6},{9,8},{10,9},{11,10},{13,12},{... | collective-permute-start | bytes 98312 | tf_op jit(solution)/shard_map/ppermute | solution.py:37
  94.0 8.0 %copy-start.1 = (f32[64,1152]{1,0:T(8,128)}, f32[64,1152]{1,0:T(8,128)S(1)}, u32[]{:S(2)}) copy-start(f32[64,1152]{1,0:T(8,128)S(1)} %reshape.70) | copy-start | bytes 884740
  94.3 7.7 %copy-start.10 = (f32[32,128]{1,0:T(8,128)}, f32[32,128]{1,0:T(8,128)S(1)}, u32[]{:S(2)}) copy-start(f32[32,128]{1,0:T(8,128)S(1)} %collective-permute-done.10.nylo) | copy-start | bytes 49156
  94.3 8.5 %collective-permute-start.8 = (f32[64,128]{1,0:T(8,128)S(1)}, f32[64,128]{1,0:T(8,128)S(1)}, u32[]{:S(2)}, u32[]{:S(2)}) collective-permute-start(f32[64,128]{1,0:T(8,128)S(1)} %get-tuple-element.11), channel_id=1, source_target_pairs={{0,1},{1,2},{2,3},{4,5},{5,6},{6,7},{8,9},{9,10},{10,11},{12,13},{... | collective-permute-start | bytes 98312 | tf_op jit(solution)/shard_map/ppermute | solution.py:37
  (9 other events, 5.6 us)

commit v16 on v15

--- a/solution.py
+++ b/solution.py
@@ -17,11 +17,14 @@
 
 def faces(block, lead):
     ny = block.shape[-1]
-    ends = (lax.broadcasted_iota(jnp.int32, (2, ny), 1) == jnp.array([[0], [ny - 1]])).astype(jnp.float32)
-    letters = "cxzy"[1 - lead :]
-    columns = jnp.einsum(
-        letters + ",ky->k" + letters[:-3] + "zx", block, ends, precision=lax.Precision.HIGHEST
-    )
+    if lead:
+        ends = (lax.broadcasted_iota(jnp.int32, (2, ny), 1) == jnp.array([[0], [ny - 1]])).astype(jnp.float32)
+        columns = jnp.einsum("cxzy,ky->kczx", block, ends, precision=lax.Precision.HIGHEST)
+    else:
+        lane = lax.broadcasted_iota(jnp.int32, block.shape, block.ndim - 1)
+        columns = jnp.stack(
+            [jnp.swapaxes(jnp.sum(jnp.where(lane == y, block, 0.0), axis=-1), -1, -2) for y in (0, ny - 1)]
+        )
     out = []
     for axis, dim in (("gx", lead), ("gz", lead + 1), ("gy", None)):
         count = lax.axis_size(axis)

time: 115 us -> 112 us (0.974)
  the two profiles are of different devices: /device:TPU:5 before, /device:TPU:1 now
where the time goes in v16:
time: 112 us; the launch traced here: 110 us
  starting transfers between devices  52.6 us (47%)
  Pallas kernels  16.6 us (15%)
  matrix products  13.9 us (12%)
  local copies, waits for them, and re-layouts  9.19 us (8%)
  waiting for transfers between devices  9.12 us (8%)
  between operations  4.96 us (4%)
  other arithmetic  4.03 us (4%)
    ppermute x6, starting transfers between devices, faces(): lax.ppermute(last, axis, forward)  16.7 us
    ppermute x4, starting transfers between devices, body(): owned = owned + lax.ppermute(owned, axis, pairs)  10.7 us
    all_to_all x1, starting transfers between devices, body(): lax.all_to_all(partial_sample.reshape(rows, per_row, -1), 'gx', split_axi...  9.92 us
    ppermute x6, starting transfers between devices, faces(): lax.ppermute(first, axis, backward)  9.76 us
    pallas_call x1, Pallas kernels, stencil(): vmem_call(advance_kernel, jax.ShapeDtypeStruct(velocity.shape, jnp.float3...  9.65 us
    all_to_all x1, waiting for transfers between devices, body(): lax.all_to_all(partial_sample.reshape(rows, per_row, -1), 'gx', split_axi...  7.37 us
    pallas_call x1, Pallas kernels, stencil(): vmem_call(viscosity_kernel, jax.ShapeDtypeStruct(velocity.shape[1:], jnp....  6.98 us
    all_to_all x1, starting transfers between devices, body(): lax.all_to_all(jnp.broadcast_to(owned_force[None], (rows,) + owned_force....  5.58 us
  transfers between devices with their start and end apart: 18, of which 3 were waited for; matrix products, arithmetic and copies ran while one was open for 14% of the time, Pallas kernels for 6%

profile of v16, /device:TPU:1, one launch (start us, length us, event | category | flops | bytes accessed | tf_op | source)
XLA Modules:
  0.0 110.5 jit_solution(13715492893721884108)
XLA Ops:
  0.6 1.3 %fusion.24 = (s32[1,1,1,1]{3,2,1,0:T(1,128)}, s32[1,1,1,1]{3,2,1,0:T(1,128)}) fusion(s32[1,1,1,2]{3,2,1,0:T(1,128)} %param.8), kind=kLoop, calls=%fused_computation.41 | loop fusion | bytes 16 | tf_op jit(solution)/shard_map/slice | solution.py:152
  6.8 4.7 %fusion.2 = f32[2,3,384]{2,1,0:T(4,128)S(1)} fusion(bf16[1,1,1,2,384,4096]{5,4,3,2,1,0:T(8,128)(2,1)} %param.9, bf16[1,3,4096]{2,1,0:T(4,128)(2,1)S(1)} %stack.10, bf16[1,3,4096]{2,1,0:T(4,128)(2,1)S(1)} %stack.9), kind=kOutput, calls=%fused_computation.2 | convolution fusion | flops 18972672 | bytes 6349824 | tf_op jit(solution)/shard_map/spq,scq->scp/dot_general | solution.py:154
  12.8 9.9 %all-to-all-start = ((f32[16,4,1152]{2,1,0:T(4,128)}), f32[16,4,1152]{2,1,0:T(4,128)S(1)}, u32[]{:S(2)}, u32[]{:S(2)}) async-start(f32[16,4,1152]{2,1,0:T(4,128)} %copy.36), calls=%async_computation | async-start | bytes 589824 | tf_op jit(solution)/shard_map/all_to_all | solution.py:168
  22.7 4.9 %fusion.4 = f32[2,3,64,32]{2,0,3,1:T(2,128)S(1)} fusion(f32[3,64,32,128]{3,2,1,0:T(8,128)S(1)} %copy-done, s32[2]{0:T(128)S(1)} %iota_multiply_fusion), kind=kOutput, calls=%fused_computation.4 | convolution fusion | flops 18874624 | bytes 3194888 | tf_op jit(solution)/shard_map/cxzy,ky->kczx/dot_general | solution.py:22
  27.6 7.4 %all-to-all-done = f32[16,4,1152]{2,1,0:T(4,128)S(1)} async-done(((f32[16,4,1152]{2,1,0:T(4,128)}), f32[16,4,1152]{2,1,0:T(4,128)S(1)}, u32[]{:S(2)}, u32[]{:S(2)}) %all-to-all-start) | async-done | bytes 294944 | tf_op jit(solution)/shard_map/all_to_all | solution.py:168
  36.9 2.2 %collective-permute-start.4 = (f32[3,32,128]{2,1,0:T(8,128)S(1)}, f32[3,32,128]{2,1,0:T(8,128)S(1)}, u32[]{:S(2)}, u32[]{:S(2)}) collective-permute-start(f32[3,32,128]{2,1,0:T(8,128)S(1)} %pad.14), channel_id=1, source_target_pairs={{0,4},{4,8},{8,12},{1,5},{5,9},{9,13},{2,6},{6,10},{10,14},{3,7},{... | collective-permute-start | bytes 147464 | tf_op jit(solution)/shard_map/ppermute | solution.py:40
  39.1 1.3 %collective-permute-start.5 = (f32[3,32,128]{2,1,0:T(8,128)S(1)}, f32[3,32,128]{2,1,0:T(8,128)S(1)}, u32[]{:S(2)}, u32[]{:S(2)}) collective-permute-start(f32[3,32,128]{2,1,0:T(8,128)S(1)} %pad.15), channel_id=1, source_target_pairs={{4,0},{8,4},{12,8},{5,1},{9,5},{13,9},{6,2},{10,6},{14,10},{7,3},{... | collective-permute-start | bytes 147464 | tf_op jit(solution)/shard_map/ppermute | solution.py:40
  41.1 4.3 %collective-permute-start.13 = (f32[4,1152]{1,0:T(4,128)S(1)}, f32[4,1152]{1,0:T(4,128)S(1)}, u32[]{:S(2)}, u32[]{:S(2)}) collective-permute-start(f32[4,1152]{1,0:T(4,128)S(1)} %add.43), channel_id=1, source_target_pairs={{0,8},{4,12},{8,0},{12,4},{1,9},{5,13},{9,1},{13,5},{2,10},{6,14},... | collective-permute-start | bytes 55304 | tf_op jit(solution)/shard_map/ppermute | solution.py:177
  46.0 2.6 %collective-permute-start.1 = (f32[3,32,128]{2,1,0:T(8,128)}, f32[3,32,128]{2,1,0:T(8,128)S(1)}, u32[]{:S(2)}, u32[]{:S(2)}) collective-permute-start(f32[3,32,128]{2,1,0:T(8,128)} %get-tuple-element.10), channel_id=1, source_target_pairs={{16,0},{32,16},{48,32},{64,48},{80,64},{96,80},{112,96},{128,112},... | collective-permute-start | bytes 147464 | tf_op jit(solution)/shard_map/ppermute | solution.py:40
  48.6 3.0 %collective-permute-start = (f32[3,32,128]{2,1,0:T(8,128)}, f32[3,32,128]{2,1,0:T(8,128)S(1)}, u32[]{:S(2)}, u32[]{:S(2)}) collective-permute-start(f32[3,32,128]{2,1,0:T(8,128)} %get-tuple-element.11), channel_id=1, source_target_pairs={{0,16},{16,32},{32,48},{48,64},{64,80},{80,96},{96,112},{112,128},... | collective-permute-start | bytes 147464 | tf_op jit(solution)/shard_map/ppermute | solution.py:40
  51.6 1.4 %collective-permute-start.14 = (f32[4,1152]{1,0:T(4,128)S(1)}, f32[4,1152]{1,0:T(4,128)S(1)}, u32[]{:S(2)}, u32[]{:S(2)}) collective-permute-start(f32[4,1152]{1,0:T(4,128)S(1)} %add.44), channel_id=1, source_target_pairs={{0,1},{1,0},{2,3},{3,2},{4,5},{5,4},{6,7},{7,6},{8,9},{9,8},{10,11... | collective-permute-start | bytes 55304 | tf_op jit(solution)/shard_map/ppermute | solution.py:177
  53.1 1.5 %collective-permute-done.14 = f32[4,1152]{1,0:T(4,128)S(1)} collective-permute-done((f32[4,1152]{1,0:T(4,128)S(1)}, f32[4,1152]{1,0:T(4,128)S(1)}, u32[]{:S(2)}, u32[]{:S(2)}) %collective-permute-start.14) | collective-permute-done | bytes 18464 | tf_op jit(solution)/shard_map/ppermute | solution.py:177
  54.7 3.2 %collective-permute-start.2 = (f32[3,64,128]{2,1,0:T(8,128)S(1)}, f32[3,64,128]{2,1,0:T(8,128)S(1)}, u32[]{:S(2)}, u32[]{:S(2)}) collective-permute-start(f32[3,64,128]{2,1,0:T(8,128)S(1)} %bitcast.58), channel_id=1, source_target_pairs={{0,1},{1,2},{2,3},{4,5},{5,6},{6,7},{8,9},{9,10},{10,11},{12,13},{... | collective-permute-start | bytes 294920 | tf_op jit(solution)/shard_map/ppermute | solution.py:40
  59.2 3.8 %collective-permute-start.15 = (f32[4,1152]{1,0:T(4,128)S(1)}, f32[4,1152]{1,0:T(4,128)S(1)}, u32[]{:S(2)}, u32[]{:S(2)}) collective-permute-start(f32[4,1152]{1,0:T(4,128)S(1)} %add.45), channel_id=1, source_target_pairs={{0,2},{1,3},{2,0},{3,1},{4,6},{5,7},{6,4},{7,5},{8,10},{9,11},{10,... | collective-permute-start | bytes 55304 | tf_op jit(solution)/shard_map/ppermute | solution.py:177
  64.3 7.0 %shard_map.77.nu = f32[64,32,128]{2,1,0:T(8,128)} custom-call(f32[3,64,32,128]{3,2,1,0:T(8,128)} %u.3, f32[3,32,128]{2,1,0:T(8,128)} %copy-done.7, f32[3,32,128]{2,1,0:T(8,128)} %copy-done.6, f32[3,64,128]{2,1,0:T(8,128)} %copy-done.2, f32[3,64,128]{2,1,0:T(8,128)} %copy-done.3, f32[3,32,128]{2,1,0:T(8,128)} %copy-done.4, f32[3,32,128]{2,1,0:T(8,128)} %copy-done.5), custom_call_target="tpu_custom_call" | custom-call | tf_op jit(solution)/shard_map/pallas_call | solution.py:130
  72.9 5.6 %all-to-all-start.1 = ((f32[16,4,1152]{2,1,0:T(4,128)}), f32[16,4,1152]{2,1,0:T(4,128)S(1)}, u32[]{:S(2)}, u32[]{:S(2)}) async-start(f32[16,4,1152]{2,1,0:T(4,128)} %broadcast_in_dim.14), calls=%async_computation.1 | async-start | bytes 589824 | tf_op jit(solution)/shard_map/all_to_all | solution.py:181
  79.2 2.0 %collective-permute-start.7 = (f32[32,128]{1,0:T(8,128)S(1)}, f32[32,128]{1,0:T(8,128)S(1)}, u32[]{:S(2)}, u32[]{:S(2)}) collective-permute-start(f32[32,128]{1,0:T(8,128)S(1)} %get-tuple-element.14), channel_id=1, source_target_pairs={{16,0},{32,16},{48,32},{64,48},{80,64},{96,80},{112,96},{128,112},... | collective-permute-start | bytes 49160 | tf_op jit(solution)/shard_map/ppermute | solution.py:40
  81.2 3.6 %collective-permute-start.6 = (f32[32,128]{1,0:T(8,128)S(1)}, f32[32,128]{1,0:T(8,128)S(1)}, u32[]{:S(2)}, u32[]{:S(2)}) collective-permute-start(f32[32,128]{1,0:T(8,128)S(1)} %get-tuple-element.15), channel_id=1, source_target_pairs={{0,16},{16,32},{32,48},{48,64},{64,80},{80,96},{96,112},{112,128},... | collective-permute-start | bytes 49160 | tf_op jit(solution)/shard_map/ppermute | solution.py:40
  84.7 1.8 %select_reduce_fusion = (f32[64,32]{1,0:T(8,128)S(1)}, f32[64,32]{1,0:T(8,128)S(1)}) fusion(f32[64,32,128]{2,1,0:T(8,128)} %shard_map.77.nu, pred[128]{0:T(512)(128)(4,1)S(1)} %get-tuple-element.20, pred[128]{0:T(512)(128)(4,1)S(1)} %get-tuple-element.21), kind=kLoop, calls=%fused_computation.7 | loop fusion | flops 1044480 | bytes 1065216 | tf_op jit(solution)/shard_map/reduce_sum | solution.py:26
  86.7 1.8 %collective-permute-start.10 = (f32[32,128]{1,0:T(8,128)S(1)}, f32[32,128]{1,0:T(8,128)S(1)}, u32[]{:S(2)}, u32[]{:S(2)}) collective-permute-start(f32[32,128]{1,0:T(8,128)S(1)} %pad.16), channel_id=1, source_target_pairs={{0,4},{4,8},{8,12},{1,5},{5,9},{9,13},{2,6},{6,10},{10,14},{3,7},{... | collective-permute-start | bytes 49160 | tf_op jit(solution)/shard_map/ppermute | solution.py:40
  88.6 1.3 %collective-permute-start.11 = (f32[32,128]{1,0:T(8,128)S(1)}, f32[32,128]{1,0:T(8,128)S(1)}, u32[]{:S(2)}, u32[]{:S(2)}) collective-permute-start(f32[32,128]{1,0:T(8,128)S(1)} %pad.17), channel_id=1, source_target_pairs={{4,0},{8,4},{12,8},{5,1},{9,5},{13,9},{6,2},{10,6},{14,10},{7,3},{... | collective-permute-start | bytes 49160 | tf_op jit(solution)/shard_map/ppermute | solution.py:40
  91.0 3.0 %collective-permute-start.8 = (f32[64,128]{1,0:T(8,128)S(1)}, f32[64,128]{1,0:T(8,128)S(1)}, u32[]{:S(2)}, u32[]{:S(2)}) collective-permute-start(f32[64,128]{1,0:T(8,128)S(1)} %bitcast.64), channel_id=1, source_target_pairs={{0,1},{1,2},{2,3},{4,5},{5,6},{6,7},{8,9},{9,10},{10,11},{12,13},{... | collective-permute-start | bytes 98312 | tf_op jit(solution)/shard_map/ppermute | solution.py:40
  95.7 3.7 %fusion = f32[2,3,4096]{2,1,0:T(4,128)S(1)} fusion(bf16[2,3,384]{2,1,0:T(4,128)(2,1)S(1)} %reshape.71, bf16[1,1,1,2,384,4096]{5,4,3,2,1,0:T(8,128)(2,1)} %param.9), kind=kOutput, calls=%fused_computation | convolution fusion | flops 18874368 | bytes 6394368 | tf_op jit(solution)/shard_map/axz,ahx->ahz/dot_general | solution.py:186
  100.8 9.6 %shard_map.78 = f32[3,64,32,128]{3,2,1,0:T(8,128)} custom-call(s32[2]{0:T(128)} %bitcast.65, f32[3,64,32,128]{3,2,1,0:T(8,128)} %u.3, f32[3,32,128]{2,1,0:T(8,128)} %copy-done.7, f32[3,32,128]{2,1,0:T(8,128)} %copy-done.6, f32[3,64,128]{2,1,0:T(8,128)} %copy-done.2, f32[3,64,128]{2,1,0:T(8,128)} %copy-done.3, f32[3,32,128]{2,1,0:T(8,128)} %copy-done.4, ...), custom_call_target="tpu_custom_call" | custom-call | tf_op jit(solution)/shard_map/pallas_call | solution.py:134
  (84 shorter events, 14.8 us)
Async XLA Ops:
  6.8 4.7 %copy-start.14 = (s32[1,1,1,2]{3,2,1,0:T(1,128)S(1)}, s32[1,1,1,2]{3,2,1,0:T(1,128)}, u32[]{:S(2)}) copy-start(s32[1,1,1,2]{3,2,1,0:T(1,128)} %param.7) | copy-start | bytes 28
  6.8 15.9 %copy-start = (f32[3,64,32,128]{3,2,1,0:T(8,128)S(1)}, f32[3,64,32,128]{3,2,1,0:T(8,128)}, u32[]{:S(2)}) copy-start(f32[3,64,32,128]{3,2,1,0:T(8,128)} %u.3) | copy-start | bytes 9437188
  12.8 22.2 %all-to-all-start = ((f32[16,4,1152]{2,1,0:T(4,128)}), f32[16,4,1152]{2,1,0:T(4,128)S(1)}, u32[]{:S(2)}, u32[]{:S(2)}) async-start(f32[16,4,1152]{2,1,0:T(4,128)} %copy.36), calls=%async_computation | async-start | bytes 589824 | tf_op jit(solution)/shard_map/all_to_all | solution.py:168
  35.6 4.7 %collective-permute-start.12 = (f32[4,1152]{1,0:T(4,128)}, f32[4,1152]{1,0:T(4,128)S(1)}, u32[]{:S(2)}, u32[]{:S(2)}) collective-permute-start(f32[4,1152]{1,0:T(4,128)} %reduce_sum.38), channel_id=1, source_target_pairs={{0,4},{4,0},{8,12},{12,8},{1,5},{5,1},{9,13},{13,9},{2,6},{6,2},{1... | collective-permute-start | bytes 55304 | tf_op jit(solution)/shard_map/ppermute | solution.py:177
  36.9 21.0 %collective-permute-start.4 = (f32[3,32,128]{2,1,0:T(8,128)S(1)}, f32[3,32,128]{2,1,0:T(8,128)S(1)}, u32[]{:S(2)}, u32[]{:S(2)}) collective-permute-start(f32[3,32,128]{2,1,0:T(8,128)S(1)} %pad.14), channel_id=1, source_target_pairs={{0,4},{4,8},{8,12},{1,5},{5,9},{9,13},{2,6},{6,10},{10,14},{3,7},{... | collective-permute-start | bytes 147464 | tf_op jit(solution)/shard_map/ppermute | solution.py:40
  39.1 20.1 %collective-permute-start.5 = (f32[3,32,128]{2,1,0:T(8,128)S(1)}, f32[3,32,128]{2,1,0:T(8,128)S(1)}, u32[]{:S(2)}, u32[]{:S(2)}) collective-permute-start(f32[3,32,128]{2,1,0:T(8,128)S(1)} %pad.15), channel_id=1, source_target_pairs={{4,0},{8,4},{12,8},{5,1},{9,5},{13,9},{6,2},{10,6},{14,10},{7,3},{... | collective-permute-start | bytes 147464 | tf_op jit(solution)/shard_map/ppermute | solution.py:40
  41.1 10.5 %collective-permute-start.13 = (f32[4,1152]{1,0:T(4,128)S(1)}, f32[4,1152]{1,0:T(4,128)S(1)}, u32[]{:S(2)}, u32[]{:S(2)}) collective-permute-start(f32[4,1152]{1,0:T(4,128)S(1)} %add.43), channel_id=1, source_target_pairs={{0,8},{4,12},{8,0},{12,4},{1,9},{5,13},{9,1},{13,5},{2,10},{6,14},... | collective-permute-start | bytes 55304 | tf_op jit(solution)/shard_map/ppermute | solution.py:177
  46.0 17.0 %collective-permute-start.1 = (f32[3,32,128]{2,1,0:T(8,128)}, f32[3,32,128]{2,1,0:T(8,128)S(1)}, u32[]{:S(2)}, u32[]{:S(2)}) collective-permute-start(f32[3,32,128]{2,1,0:T(8,128)} %get-tuple-element.10), channel_id=1, source_target_pairs={{16,0},{32,16},{48,32},{64,48},{80,64},{96,80},{112,96},{128,112},... | collective-permute-start | bytes 147464 | tf_op jit(solution)/shard_map/ppermute | solution.py:40
  48.6 14.4 %collective-permute-start = (f32[3,32,128]{2,1,0:T(8,128)}, f32[3,32,128]{2,1,0:T(8,128)S(1)}, u32[]{:S(2)}, u32[]{:S(2)}) collective-permute-start(f32[3,32,128]{2,1,0:T(8,128)} %get-tuple-element.11), channel_id=1, source_target_pairs={{0,16},{16,32},{32,48},{48,64},{64,80},{80,96},{96,112},{112,128},... | collective-permute-start | bytes 147464 | tf_op jit(solution)/shard_map/ppermute | solution.py:40
  51.6 3.0 %collective-permute-start.14 = (f32[4,1152]{1,0:T(4,128)S(1)}, f32[4,1152]{1,0:T(4,128)S(1)}, u32[]{:S(2)}, u32[]{:S(2)}) collective-permute-start(f32[4,1152]{1,0:T(4,128)S(1)} %add.44), channel_id=1, source_target_pairs={{0,1},{1,0},{2,3},{3,2},{4,5},{5,4},{6,7},{7,6},{8,9},{9,8},{10,11... | collective-permute-start | bytes 55304 | tf_op jit(solution)/shard_map/ppermute | solution.py:177
  54.7 8.4 %collective-permute-start.2 = (f32[3,64,128]{2,1,0:T(8,128)S(1)}, f32[3,64,128]{2,1,0:T(8,128)S(1)}, u32[]{:S(2)}, u32[]{:S(2)}) collective-permute-start(f32[3,64,128]{2,1,0:T(8,128)S(1)} %bitcast.58), channel_id=1, source_target_pairs={{0,1},{1,2},{2,3},{4,5},{5,6},{6,7},{8,9},{9,10},{10,11},{12,13},{... | collective-permute-start | bytes 294920 | tf_op jit(solution)/shard_map/ppermute | solution.py:40
  57.9 5.4 %copy-start.4 = (f32[3,32,128]{2,1,0:T(8,128)}, f32[3,32,128]{2,1,0:T(8,128)S(1)}, u32[]{:S(2)}) copy-start(f32[3,32,128]{2,1,0:T(8,128)S(1)} %collective-permute-done.4.ylo) | copy-start | bytes 147460
  57.9 5.4 %collective-permute-start.3 = (f32[3,64,128]{2,1,0:T(8,128)S(1)}, f32[3,64,128]{2,1,0:T(8,128)S(1)}, u32[]{:S(2)}, u32[]{:S(2)}) collective-permute-start(f32[3,64,128]{2,1,0:T(8,128)S(1)} %bitcast.57), channel_id=1, source_target_pairs={{1,0},{2,1},{3,2},{5,4},{6,5},{7,6},{9,8},{10,9},{11,10},{13,12},{... | collective-permute-start | bytes 294920 | tf_op jit(solution)/shard_map/ppermute | solution.py:40
  59.2 4.1 %copy-start.5 = (f32[3,32,128]{2,1,0:T(8,128)}, f32[3,32,128]{2,1,0:T(8,128)S(1)}, u32[]{:S(2)}) copy-start(f32[3,32,128]{2,1,0:T(8,128)S(1)} %collective-permute-done.5.yhi) | copy-start | bytes 147460
  59.2 12.1 %collective-permute-start.15 = (f32[4,1152]{1,0:T(4,128)S(1)}, f32[4,1152]{1,0:T(4,128)S(1)}, u32[]{:S(2)}, u32[]{:S(2)}) collective-permute-start(f32[4,1152]{1,0:T(4,128)S(1)} %add.45), channel_id=1, source_target_pairs={{0,2},{1,3},{2,0},{3,1},{4,6},{5,7},{6,4},{7,5},{8,10},{9,11},{10,... | collective-permute-start | bytes 55304 | tf_op jit(solution)/shard_map/ppermute | solution.py:177
  72.9 21.2 %all-to-all-start.1 = ((f32[16,4,1152]{2,1,0:T(4,128)}), f32[16,4,1152]{2,1,0:T(4,128)S(1)}, u32[]{:S(2)}, u32[]{:S(2)}) async-start(f32[16,4,1152]{2,1,0:T(4,128)} %broadcast_in_dim.14), calls=%async_computation.1 | async-start | bytes 589824 | tf_op jit(solution)/shard_map/all_to_all | solution.py:181
  79.2 15.2 %collective-permute-start.7 = (f32[32,128]{1,0:T(8,128)S(1)}, f32[32,128]{1,0:T(8,128)S(1)}, u32[]{:S(2)}, u32[]{:S(2)}) collective-permute-start(f32[32,128]{1,0:T(8,128)S(1)} %get-tuple-element.14), channel_id=1, source_target_pairs={{16,0},{32,16},{48,32},{64,48},{80,64},{96,80},{112,96},{128,112},... | collective-permute-start | bytes 49160 | tf_op jit(solution)/shard_map/ppermute | solution.py:40
  81.2 19.0 %collective-permute-start.6 = (f32[32,128]{1,0:T(8,128)S(1)}, f32[32,128]{1,0:T(8,128)S(1)}, u32[]{:S(2)}, u32[]{:S(2)}) collective-permute-start(f32[32,128]{1,0:T(8,128)S(1)} %get-tuple-element.15), channel_id=1, source_target_pairs={{0,16},{16,32},{32,48},{48,64},{64,80},{80,96},{96,112},{112,128},... | collective-permute-start | bytes 49160 | tf_op jit(solution)/shard_map/ppermute | solution.py:40
  86.7 13.4 %collective-permute-start.10 = (f32[32,128]{1,0:T(8,128)S(1)}, f32[32,128]{1,0:T(8,128)S(1)}, u32[]{:S(2)}, u32[]{:S(2)}) collective-permute-start(f32[32,128]{1,0:T(8,128)S(1)} %pad.16), channel_id=1, source_target_pairs={{0,4},{4,8},{8,12},{1,5},{5,9},{9,13},{2,6},{6,10},{10,14},{3,7},{... | collective-permute-start | bytes 49160 | tf_op jit(solution)/shard_map/ppermute | solution.py:40
  88.6 11.6 %collective-permute-start.11 = (f32[32,128]{1,0:T(8,128)S(1)}, f32[32,128]{1,0:T(8,128)S(1)}, u32[]{:S(2)}, u32[]{:S(2)}) collective-permute-start(f32[32,128]{1,0:T(8,128)S(1)} %pad.17), channel_id=1, source_target_pairs={{4,0},{8,4},{12,8},{5,1},{9,5},{13,9},{6,2},{10,6},{14,10},{7,3},{... | collective-permute-start | bytes 49160 | tf_op jit(solution)/shard_map/ppermute | solution.py:40
  91.0 9.2 %collective-permute-start.8 = (f32[64,128]{1,0:T(8,128)S(1)}, f32[64,128]{1,0:T(8,128)S(1)}, u32[]{:S(2)}, u32[]{:S(2)}) collective-permute-start(f32[64,128]{1,0:T(8,128)S(1)} %bitcast.64), channel_id=1, source_target_pairs={{0,1},{1,2},{2,3},{4,5},{5,6},{6,7},{8,9},{9,10},{10,11},{12,13},{... | collective-permute-start | bytes 98312 | tf_op jit(solution)/shard_map/ppermute | solution.py:40
  94.1 5.3 %copy-start.1 = (f32[64,1152]{1,0:T(8,128)}, f32[64,1152]{1,0:T(8,128)S(1)}, u32[]{:S(2)}) copy-start(f32[64,1152]{1,0:T(8,128)S(1)} %reshape.70) | copy-start | bytes 884740
  94.4 5.0 %copy-start.10 = (f32[32,128]{1,0:T(8,128)}, f32[32,128]{1,0:T(8,128)S(1)}, u32[]{:S(2)}) copy-start(f32[32,128]{1,0:T(8,128)S(1)} %collective-permute-done.7.nxhi) | copy-start | bytes 49156
  94.4 5.8 %collective-permute-start.9 = (f32[64,128]{1,0:T(8,128)S(1)}, f32[64,128]{1,0:T(8,128)S(1)}, u32[]{:S(2)}, u32[]{:S(2)}) collective-permute-start(f32[64,128]{1,0:T(8,128)S(1)} %bitcast.63), channel_id=1, source_target_pairs={{1,0},{2,1},{3,2},{5,4},{6,5},{7,6},{9,8},{10,9},{11,10},{13,12},{... | collective-permute-start | bytes 98312 | tf_op jit(solution)/shard_map/ppermute | solution.py:40
  (9 other events, 5.5 us)

commit v17 on v16

--- a/solution.py
+++ b/solution.py
@@ -80,7 +80,7 @@
         nu[x] = 0.05 + 1.0 * jnp.sqrt(2.0 * total + 1e-06)
         return carry
 
-    lax.fori_loop(0, u.shape[1], plane, 0, unroll=8)
+    lax.fori_loop(0, u.shape[1], plane, 0, unroll=16)
 
 
 def advance_kernel(planes, u, xlo, xhi, zlo, zhi, ylo, yhi, nu, nxlo, nxhi, nzlo, nzhi, nylo, nyhi, sent, out):
@@ -110,7 +110,7 @@
             out[c, x] = center + 0.125 * (spread - advect) + impulse
         return carry
 
-    lax.fori_loop(0, u.shape[1], plane, 0, unroll=8)
+    lax.fori_loop(0, u.shape[1], plane, 0, unroll=16)
 
 
 def vmem_call(kernel, out_shape, count, smem=0):

time: 112 us -> 112 us (level)
  no operation moved by 1% of the time
where the time goes in v17:
time: 112 us; the launch traced here: 110 us
  starting transfers between devices  52.7 us (47%)
  Pallas kernels  15.9 us (14%)
  matrix products  13.9 us (12%)
  local copies, waits for them, and re-layouts  9.14 us (8%)
  waiting for transfers between devices  9.12 us (8%)
  between operations  4.96 us (4%)
  other arithmetic  4.03 us (4%)
    ppermute x6, starting transfers between devices, faces(): lax.ppermute(last, axis, forward)  16.7 us
    ppermute x4, starting transfers between devices, body(): owned = owned + lax.ppermute(owned, axis, pairs)  10.7 us
    all_to_all x1, starting transfers between devices, body(): lax.all_to_all(partial_sample.reshape(rows, per_row, -1), 'gx', split_axi...  9.97 us
    ppermute x6, starting transfers between devices, faces(): lax.ppermute(first, axis, backward)  9.76 us
    pallas_call x1, Pallas kernels, stencil(): vmem_call(advance_kernel, jax.ShapeDtypeStruct(velocity.shape, jnp.float3...  9.23 us
    all_to_all x1, waiting for transfers between devices, body(): lax.all_to_all(partial_sample.reshape(rows, per_row, -1), 'gx', split_axi...  7.37 us
    pallas_call x1, Pallas kernels, stencil(): vmem_call(viscosity_kernel, jax.ShapeDtypeStruct(velocity.shape[1:], jnp....  6.63 us
    all_to_all x1, starting transfers between devices, body(): lax.all_to_all(jnp.broadcast_to(owned_force[None], (rows,) + owned_force....  5.58 us
  transfers between devices with their start and end apart: 18, of which 3 were waited for; matrix products, arithmetic and copies ran while one was open for 14% of the time, Pallas kernels for 6%

profile of v17, /device:TPU:1, one launch (start us, length us, event | category | flops | bytes accessed | tf_op | source)
XLA Modules:
  0.0 109.7 jit_solution(8104578211513030067)
XLA Ops:
  0.6 1.3 %fusion.24 = (s32[1,1,1,1]{3,2,1,0:T(1,128)}, s32[1,1,1,1]{3,2,1,0:T(1,128)}) fusion(s32[1,1,1,2]{3,2,1,0:T(1,128)} %param.8), kind=kLoop, calls=%fused_computation.41 | loop fusion | bytes 16 | tf_op jit(solution)/shard_map/slice | solution.py:152
  6.7 4.7 %fusion.2 = f32[2,3,384]{2,1,0:T(4,128)S(1)} fusion(bf16[1,1,1,2,384,4096]{5,4,3,2,1,0:T(8,128)(2,1)} %param.9, bf16[1,3,4096]{2,1,0:T(4,128)(2,1)S(1)} %stack.10, bf16[1,3,4096]{2,1,0:T(4,128)(2,1)S(1)} %stack.9), kind=kOutput, calls=%fused_computation.2 | convolution fusion | flops 18972672 | bytes 6349824 | tf_op jit(solution)/shard_map/spq,scq->scp/dot_general | solution.py:154
  12.7 10.0 %all-to-all-start = ((f32[16,4,1152]{2,1,0:T(4,128)}), f32[16,4,1152]{2,1,0:T(4,128)S(1)}, u32[]{:S(2)}, u32[]{:S(2)}) async-start(f32[16,4,1152]{2,1,0:T(4,128)} %copy.36), calls=%async_computation | async-start | bytes 589824 | tf_op jit(solution)/shard_map/all_to_all | solution.py:168
  22.7 4.9 %fusion.4 = f32[2,3,64,32]{2,0,3,1:T(2,128)S(1)} fusion(f32[3,64,32,128]{3,2,1,0:T(8,128)S(1)} %copy-done, s32[2]{0:T(128)S(1)} %iota_multiply_fusion), kind=kOutput, calls=%fused_computation.4 | convolution fusion | flops 18874624 | bytes 3194888 | tf_op jit(solution)/shard_map/cxzy,ky->kczx/dot_general | solution.py:22
  27.6 7.4 %all-to-all-done = f32[16,4,1152]{2,1,0:T(4,128)S(1)} async-done(((f32[16,4,1152]{2,1,0:T(4,128)}), f32[16,4,1152]{2,1,0:T(4,128)S(1)}, u32[]{:S(2)}, u32[]{:S(2)}) %all-to-all-start) | async-done | bytes 294944 | tf_op jit(solution)/shard_map/all_to_all | solution.py:168
  36.9 2.2 %collective-permute-start.4 = (f32[3,32,128]{2,1,0:T(8,128)S(1)}, f32[3,32,128]{2,1,0:T(8,128)S(1)}, u32[]{:S(2)}, u32[]{:S(2)}) collective-permute-start(f32[3,32,128]{2,1,0:T(8,128)S(1)} %pad.14), channel_id=1, source_target_pairs={{0,4},{4,8},{8,12},{1,5},{5,9},{9,13},{2,6},{6,10},{10,14},{3,7},{... | collective-permute-start | bytes 147464 | tf_op jit(solution)/shard_map/ppermute | solution.py:40
  39.1 1.3 %collective-permute-start.5 = (f32[3,32,128]{2,1,0:T(8,128)S(1)}, f32[3,32,128]{2,1,0:T(8,128)S(1)}, u32[]{:S(2)}, u32[]{:S(2)}) collective-permute-start(f32[3,32,128]{2,1,0:T(8,128)S(1)} %pad.15), channel_id=1, source_target_pairs={{4,0},{8,4},{12,8},{5,1},{9,5},{13,9},{6,2},{10,6},{14,10},{7,3},{... | collective-permute-start | bytes 147464 | tf_op jit(solution)/shard_map/ppermute | solution.py:40
  41.1 4.3 %collective-permute-start.13 = (f32[4,1152]{1,0:T(4,128)S(1)}, f32[4,1152]{1,0:T(4,128)S(1)}, u32[]{:S(2)}, u32[]{:S(2)}) collective-permute-start(f32[4,1152]{1,0:T(4,128)S(1)} %add.43), channel_id=1, source_target_pairs={{0,8},{4,12},{8,0},{12,4},{1,9},{5,13},{9,1},{13,5},{2,10},{6,14},... | collective-permute-start | bytes 55304 | tf_op jit(solution)/shard_map/ppermute | solution.py:177
  46.0 2.6 %collective-permute-start.1 = (f32[3,32,128]{2,1,0:T(8,128)}, f32[3,32,128]{2,1,0:T(8,128)S(1)}, u32[]{:S(2)}, u32[]{:S(2)}) collective-permute-start(f32[3,32,128]{2,1,0:T(8,128)} %get-tuple-element.10), channel_id=1, source_target_pairs={{16,0},{32,16},{48,32},{64,48},{80,64},{96,80},{112,96},{128,112},... | collective-permute-start | bytes 147464 | tf_op jit(solution)/shard_map/ppermute | solution.py:40
  48.6 3.0 %collective-permute-start = (f32[3,32,128]{2,1,0:T(8,128)}, f32[3,32,128]{2,1,0:T(8,128)S(1)}, u32[]{:S(2)}, u32[]{:S(2)}) collective-permute-start(f32[3,32,128]{2,1,0:T(8,128)} %get-tuple-element.11), channel_id=1, source_target_pairs={{0,16},{16,32},{32,48},{48,64},{64,80},{80,96},{96,112},{112,128},... | collective-permute-start | bytes 147464 | tf_op jit(solution)/shard_map/ppermute | solution.py:40
  51.6 1.4 %collective-permute-start.14 = (f32[4,1152]{1,0:T(4,128)S(1)}, f32[4,1152]{1,0:T(4,128)S(1)}, u32[]{:S(2)}, u32[]{:S(2)}) collective-permute-start(f32[4,1152]{1,0:T(4,128)S(1)} %add.44), channel_id=1, source_target_pairs={{0,1},{1,0},{2,3},{3,2},{4,5},{5,4},{6,7},{7,6},{8,9},{9,8},{10,11... | collective-permute-start | bytes 55304 | tf_op jit(solution)/shard_map/ppermute | solution.py:177
  53.1 1.5 %collective-permute-done.14 = f32[4,1152]{1,0:T(4,128)S(1)} collective-permute-done((f32[4,1152]{1,0:T(4,128)S(1)}, f32[4,1152]{1,0:T(4,128)S(1)}, u32[]{:S(2)}, u32[]{:S(2)}) %collective-permute-start.14) | collective-permute-done | bytes 18464 | tf_op jit(solution)/shard_map/ppermute | solution.py:177
  54.7 3.2 %collective-permute-start.2 = (f32[3,64,128]{2,1,0:T(8,128)S(1)}, f32[3,64,128]{2,1,0:T(8,128)S(1)}, u32[]{:S(2)}, u32[]{:S(2)}) collective-permute-start(f32[3,64,128]{2,1,0:T(8,128)S(1)} %bitcast.58), channel_id=1, source_target_pairs={{0,1},{1,2},{2,3},{4,5},{5,6},{6,7},{8,9},{9,10},{10,11},{12,13},{... | collective-permute-start | bytes 294920 | tf_op jit(solution)/shard_map/ppermute | solution.py:40
  57.9 1.3 %collective-permute-start.3 = (f32[3,64,128]{2,1,0:T(8,128)S(1)}, f32[3,64,128]{2,1,0:T(8,128)S(1)}, u32[]{:S(2)}, u32[]{:S(2)}) collective-permute-start(f32[3,64,128]{2,1,0:T(8,128)S(1)} %bitcast.57), channel_id=1, source_target_pairs={{1,0},{2,1},{3,2},{5,4},{6,5},{7,6},{9,8},{10,9},{11,10},{13,12},{... | collective-permute-start | bytes 294920 | tf_op jit(solution)/shard_map/ppermute | solution.py:40
  59.2 3.8 %collective-permute-start.15 = (f32[4,1152]{1,0:T(4,128)S(1)}, f32[4,1152]{1,0:T(4,128)S(1)}, u32[]{:S(2)}, u32[]{:S(2)}) collective-permute-start(f32[4,1152]{1,0:T(4,128)S(1)} %add.45), channel_id=1, source_target_pairs={{0,2},{1,3},{2,0},{3,1},{4,6},{5,7},{6,4},{7,5},{8,10},{9,11},{10,... | collective-permute-start | bytes 55304 | tf_op jit(solution)/shard_map/ppermute | solution.py:177
  64.3 6.6 %shard_map.77.nu = f32[64,32,128]{2,1,0:T(8,128)} custom-call(f32[3,64,32,128]{3,2,1,0:T(8,128)} %u.3, f32[3,32,128]{2,1,0:T(8,128)} %copy-done.7, f32[3,32,128]{2,1,0:T(8,128)} %copy-done.6, f32[3,64,128]{2,1,0:T(8,128)} %copy-done.2, f32[3,64,128]{2,1,0:T(8,128)} %copy-done.3, f32[3,32,128]{2,1,0:T(8,128)} %copy-done.4, f32[3,32,128]{2,1,0:T(8,128)} %copy-done.5), custom_call_target="tpu_custom_call" | custom-call | tf_op jit(solution)/shard_map/pallas_call | solution.py:130
  72.5 5.6 %all-to-all-start.1 = ((f32[16,4,1152]{2,1,0:T(4,128)}), f32[16,4,1152]{2,1,0:T(4,128)S(1)}, u32[]{:S(2)}, u32[]{:S(2)}) async-start(f32[16,4,1152]{2,1,0:T(4,128)} %broadcast_in_dim.14), calls=%async_computation.1 | async-start | bytes 589824 | tf_op jit(solution)/shard_map/all_to_all | solution.py:181
  78.8 2.0 %collective-permute-start.7 = (f32[32,128]{1,0:T(8,128)S(1)}, f32[32,128]{1,0:T(8,128)S(1)}, u32[]{:S(2)}, u32[]{:S(2)}) collective-permute-start(f32[32,128]{1,0:T(8,128)S(1)} %get-tuple-element.14), channel_id=1, source_target_pairs={{16,0},{32,16},{48,32},{64,48},{80,64},{96,80},{112,96},{128,112},... | collective-permute-start | bytes 49160 | tf_op jit(solution)/shard_map/ppermute | solution.py:40
  80.8 3.6 %collective-permute-start.6 = (f32[32,128]{1,0:T(8,128)S(1)}, f32[32,128]{1,0:T(8,128)S(1)}, u32[]{:S(2)}, u32[]{:S(2)}) collective-permute-start(f32[32,128]{1,0:T(8,128)S(1)} %get-tuple-element.15), channel_id=1, source_target_pairs={{0,16},{16,32},{32,48},{48,64},{64,80},{80,96},{96,112},{112,128},... | collective-permute-start | bytes 49160 | tf_op jit(solution)/shard_map/ppermute | solution.py:40
  84.4 1.8 %select_reduce_fusion = (f32[64,32]{1,0:T(8,128)S(1)}, f32[64,32]{1,0:T(8,128)S(1)}) fusion(f32[64,32,128]{2,1,0:T(8,128)} %shard_map.77.nu, pred[128]{0:T(512)(128)(4,1)S(1)} %get-tuple-element.20, pred[128]{0:T(512)(128)(4,1)S(1)} %get-tuple-element.21), kind=kLoop, calls=%fused_computation.7 | loop fusion | flops 1044480 | bytes 1065216 | tf_op jit(solution)/shard_map/reduce_sum | solution.py:26
  86.4 1.8 %collective-permute-start.10 = (f32[32,128]{1,0:T(8,128)S(1)}, f32[32,128]{1,0:T(8,128)S(1)}, u32[]{:S(2)}, u32[]{:S(2)}) collective-permute-start(f32[32,128]{1,0:T(8,128)S(1)} %pad.16), channel_id=1, source_target_pairs={{0,4},{4,8},{8,12},{1,5},{5,9},{9,13},{2,6},{6,10},{10,14},{3,7},{... | collective-permute-start | bytes 49160 | tf_op jit(solution)/shard_map/ppermute | solution.py:40
  90.6 3.0 %collective-permute-start.8 = (f32[64,128]{1,0:T(8,128)S(1)}, f32[64,128]{1,0:T(8,128)S(1)}, u32[]{:S(2)}, u32[]{:S(2)}) collective-permute-start(f32[64,128]{1,0:T(8,128)S(1)} %bitcast.64), channel_id=1, source_target_pairs={{0,1},{1,2},{2,3},{4,5},{5,6},{6,7},{8,9},{9,10},{10,11},{12,13},{... | collective-permute-start | bytes 98312 | tf_op jit(solution)/shard_map/ppermute | solution.py:40
  95.4 3.7 %fusion = f32[2,3,4096]{2,1,0:T(4,128)S(1)} fusion(bf16[2,3,384]{2,1,0:T(4,128)(2,1)S(1)} %reshape.71, bf16[1,1,1,2,384,4096]{5,4,3,2,1,0:T(8,128)(2,1)} %param.9), kind=kOutput, calls=%fused_computation | convolution fusion | flops 18874368 | bytes 6394368 | tf_op jit(solution)/shard_map/axz,ahx->ahz/dot_general | solution.py:186
  100.5 9.2 %shard_map.78 = f32[3,64,32,128]{3,2,1,0:T(8,128)} custom-call(s32[2]{0:T(128)} %bitcast.65, f32[3,64,32,128]{3,2,1,0:T(8,128)} %u.3, f32[3,32,128]{2,1,0:T(8,128)} %copy-done.7, f32[3,32,128]{2,1,0:T(8,128)} %copy-done.6, f32[3,64,128]{2,1,0:T(8,128)} %copy-done.2, f32[3,64,128]{2,1,0:T(8,128)} %copy-done.3, f32[3,32,128]{2,1,0:T(8,128)} %copy-done.4, ...), custom_call_target="tpu_custom_call" | custom-call | tf_op jit(solution)/shard_map/pallas_call | solution.py:134
  (84 shorter events, 14.7 us)
Async XLA Ops:
  6.7 4.7 %copy-start.14 = (s32[1,1,1,2]{3,2,1,0:T(1,128)S(1)}, s32[1,1,1,2]{3,2,1,0:T(1,128)}, u32[]{:S(2)}) copy-start(s32[1,1,1,2]{3,2,1,0:T(1,128)} %param.7) | copy-start | bytes 28
  6.7 16.0 %copy-start = (f32[3,64,32,128]{3,2,1,0:T(8,128)S(1)}, f32[3,64,32,128]{3,2,1,0:T(8,128)}, u32[]{:S(2)}) copy-start(f32[3,64,32,128]{3,2,1,0:T(8,128)} %u.3) | copy-start | bytes 9437188
  12.7 22.3 %all-to-all-start = ((f32[16,4,1152]{2,1,0:T(4,128)}), f32[16,4,1152]{2,1,0:T(4,128)S(1)}, u32[]{:S(2)}, u32[]{:S(2)}) async-start(f32[16,4,1152]{2,1,0:T(4,128)} %copy.36), calls=%async_computation | async-start | bytes 589824 | tf_op jit(solution)/shard_map/all_to_all | solution.py:168
  35.6 4.7 %collective-permute-start.12 = (f32[4,1152]{1,0:T(4,128)}, f32[4,1152]{1,0:T(4,128)S(1)}, u32[]{:S(2)}, u32[]{:S(2)}) collective-permute-start(f32[4,1152]{1,0:T(4,128)} %reduce_sum.38), channel_id=1, source_target_pairs={{0,4},{4,0},{8,12},{12,8},{1,5},{5,1},{9,13},{13,9},{2,6},{6,2},{1... | collective-permute-start | bytes 55304 | tf_op jit(solution)/shard_map/ppermute | solution.py:177
  36.9 21.0 %collective-permute-start.4 = (f32[3,32,128]{2,1,0:T(8,128)S(1)}, f32[3,32,128]{2,1,0:T(8,128)S(1)}, u32[]{:S(2)}, u32[]{:S(2)}) collective-permute-start(f32[3,32,128]{2,1,0:T(8,128)S(1)} %pad.14), channel_id=1, source_target_pairs={{0,4},{4,8},{8,12},{1,5},{5,9},{9,13},{2,6},{6,10},{10,14},{3,7},{... | collective-permute-start | bytes 147464 | tf_op jit(solution)/shard_map/ppermute | solution.py:40
  39.1 20.1 %collective-permute-start.5 = (f32[3,32,128]{2,1,0:T(8,128)S(1)}, f32[3,32,128]{2,1,0:T(8,128)S(1)}, u32[]{:S(2)}, u32[]{:S(2)}) collective-permute-start(f32[3,32,128]{2,1,0:T(8,128)S(1)} %pad.15), channel_id=1, source_target_pairs={{4,0},{8,4},{12,8},{5,1},{9,5},{13,9},{6,2},{10,6},{14,10},{7,3},{... | collective-permute-start | bytes 147464 | tf_op jit(solution)/shard_map/ppermute | solution.py:40
  41.1 10.5 %collective-permute-start.13 = (f32[4,1152]{1,0:T(4,128)S(1)}, f32[4,1152]{1,0:T(4,128)S(1)}, u32[]{:S(2)}, u32[]{:S(2)}) collective-permute-start(f32[4,1152]{1,0:T(4,128)S(1)} %add.43), channel_id=1, source_target_pairs={{0,8},{4,12},{8,0},{12,4},{1,9},{5,13},{9,1},{13,5},{2,10},{6,14},... | collective-permute-start | bytes 55304 | tf_op jit(solution)/shard_map/ppermute | solution.py:177
  46.0 17.0 %collective-permute-start.1 = (f32[3,32,128]{2,1,0:T(8,128)}, f32[3,32,128]{2,1,0:T(8,128)S(1)}, u32[]{:S(2)}, u32[]{:S(2)}) collective-permute-start(f32[3,32,128]{2,1,0:T(8,128)} %get-tuple-element.10), channel_id=1, source_target_pairs={{16,0},{32,16},{48,32},{64,48},{80,64},{96,80},{112,96},{128,112},... | collective-permute-start | bytes 147464 | tf_op jit(solution)/shard_map/ppermute | solution.py:40
  48.6 14.4 %collective-permute-start = (f32[3,32,128]{2,1,0:T(8,128)}, f32[3,32,128]{2,1,0:T(8,128)S(1)}, u32[]{:S(2)}, u32[]{:S(2)}) collective-permute-start(f32[3,32,128]{2,1,0:T(8,128)} %get-tuple-element.11), channel_id=1, source_target_pairs={{0,16},{16,32},{32,48},{48,64},{64,80},{80,96},{96,112},{112,128},... | collective-permute-start | bytes 147464 | tf_op jit(solution)/shard_map/ppermute | solution.py:40
  51.6 3.0 %collective-permute-start.14 = (f32[4,1152]{1,0:T(4,128)S(1)}, f32[4,1152]{1,0:T(4,128)S(1)}, u32[]{:S(2)}, u32[]{:S(2)}) collective-permute-start(f32[4,1152]{1,0:T(4,128)S(1)} %add.44), channel_id=1, source_target_pairs={{0,1},{1,0},{2,3},{3,2},{4,5},{5,4},{6,7},{7,6},{8,9},{9,8},{10,11... | collective-permute-start | bytes 55304 | tf_op jit(solution)/shard_map/ppermute | solution.py:177
  54.7 8.4 %collective-permute-start.2 = (f32[3,64,128]{2,1,0:T(8,128)S(1)}, f32[3,64,128]{2,1,0:T(8,128)S(1)}, u32[]{:S(2)}, u32[]{:S(2)}) collective-permute-start(f32[3,64,128]{2,1,0:T(8,128)S(1)} %bitcast.58), channel_id=1, source_target_pairs={{0,1},{1,2},{2,3},{4,5},{5,6},{6,7},{8,9},{9,10},{10,11},{12,13},{... | collective-permute-start | bytes 294920 | tf_op jit(solution)/shard_map/ppermute | solution.py:40
  57.9 5.4 %copy-start.4 = (f32[3,32,128]{2,1,0:T(8,128)}, f32[3,32,128]{2,1,0:T(8,128)S(1)}, u32[]{:S(2)}) copy-start(f32[3,32,128]{2,1,0:T(8,128)S(1)} %collective-permute-done.4.ylo) | copy-start | bytes 147460
  57.9 5.4 %collective-permute-start.3 = (f32[3,64,128]{2,1,0:T(8,128)S(1)}, f32[3,64,128]{2,1,0:T(8,128)S(1)}, u32[]{:S(2)}, u32[]{:S(2)}) collective-permute-start(f32[3,64,128]{2,1,0:T(8,128)S(1)} %bitcast.57), channel_id=1, source_target_pairs={{1,0},{2,1},{3,2},{5,4},{6,5},{7,6},{9,8},{10,9},{11,10},{13,12},{... | collective-permute-start | bytes 294920 | tf_op jit(solution)/shard_map/ppermute | solution.py:40
  59.2 4.1 %copy-start.5 = (f32[3,32,128]{2,1,0:T(8,128)}, f32[3,32,128]{2,1,0:T(8,128)S(1)}, u32[]{:S(2)}) copy-start(f32[3,32,128]{2,1,0:T(8,128)S(1)} %collective-permute-done.5.yhi) | copy-start | bytes 147460
  59.2 11.7 %collective-permute-start.15 = (f32[4,1152]{1,0:T(4,128)S(1)}, f32[4,1152]{1,0:T(4,128)S(1)}, u32[]{:S(2)}, u32[]{:S(2)}) collective-permute-start(f32[4,1152]{1,0:T(4,128)S(1)} %add.45), channel_id=1, source_target_pairs={{0,2},{1,3},{2,0},{3,1},{4,6},{5,7},{6,4},{7,5},{8,10},{9,11},{10,... | collective-permute-start | bytes 55304 | tf_op jit(solution)/shard_map/ppermute | solution.py:177
  72.5 21.2 %all-to-all-start.1 = ((f32[16,4,1152]{2,1,0:T(4,128)}), f32[16,4,1152]{2,1,0:T(4,128)S(1)}, u32[]{:S(2)}, u32[]{:S(2)}) async-start(f32[16,4,1152]{2,1,0:T(4,128)} %broadcast_in_dim.14), calls=%async_computation.1 | async-start | bytes 589824 | tf_op jit(solution)/shard_map/all_to_all | solution.py:181
  78.8 15.2 %collective-permute-start.7 = (f32[32,128]{1,0:T(8,128)S(1)}, f32[32,128]{1,0:T(8,128)S(1)}, u32[]{:S(2)}, u32[]{:S(2)}) collective-permute-start(f32[32,128]{1,0:T(8,128)S(1)} %get-tuple-element.14), channel_id=1, source_target_pairs={{16,0},{32,16},{48,32},{64,48},{80,64},{96,80},{112,96},{128,112},... | collective-permute-start | bytes 49160 | tf_op jit(solution)/shard_map/ppermute | solution.py:40
  80.8 19.0 %collective-permute-start.6 = (f32[32,128]{1,0:T(8,128)S(1)}, f32[32,128]{1,0:T(8,128)S(1)}, u32[]{:S(2)}, u32[]{:S(2)}) collective-permute-start(f32[32,128]{1,0:T(8,128)S(1)} %get-tuple-element.15), channel_id=1, source_target_pairs={{0,16},{16,32},{32,48},{48,64},{64,80},{80,96},{96,112},{112,128},... | collective-permute-start | bytes 49160 | tf_op jit(solution)/shard_map/ppermute | solution.py:40
  86.4 13.4 %collective-permute-start.10 = (f32[32,128]{1,0:T(8,128)S(1)}, f32[32,128]{1,0:T(8,128)S(1)}, u32[]{:S(2)}, u32[]{:S(2)}) collective-permute-start(f32[32,128]{1,0:T(8,128)S(1)} %pad.16), channel_id=1, source_target_pairs={{0,4},{4,8},{8,12},{1,5},{5,9},{9,13},{2,6},{6,10},{10,14},{3,7},{... | collective-permute-start | bytes 49160 | tf_op jit(solution)/shard_map/ppermute | solution.py:40
  88.2 11.6 %collective-permute-start.11 = (f32[32,128]{1,0:T(8,128)S(1)}, f32[32,128]{1,0:T(8,128)S(1)}, u32[]{:S(2)}, u32[]{:S(2)}) collective-permute-start(f32[32,128]{1,0:T(8,128)S(1)} %pad.17), channel_id=1, source_target_pairs={{4,0},{8,4},{12,8},{5,1},{9,5},{13,9},{6,2},{10,6},{14,10},{7,3},{... | collective-permute-start | bytes 49160 | tf_op jit(solution)/shard_map/ppermute | solution.py:40
  90.6 9.2 %collective-permute-start.8 = (f32[64,128]{1,0:T(8,128)S(1)}, f32[64,128]{1,0:T(8,128)S(1)}, u32[]{:S(2)}, u32[]{:S(2)}) collective-permute-start(f32[64,128]{1,0:T(8,128)S(1)} %bitcast.64), channel_id=1, source_target_pairs={{0,1},{1,2},{2,3},{4,5},{5,6},{6,7},{8,9},{9,10},{10,11},{12,13},{... | collective-permute-start | bytes 98312 | tf_op jit(solution)/shard_map/ppermute | solution.py:40
  93.8 5.3 %copy-start.1 = (f32[64,1152]{1,0:T(8,128)}, f32[64,1152]{1,0:T(8,128)S(1)}, u32[]{:S(2)}) copy-start(f32[64,1152]{1,0:T(8,128)S(1)} %reshape.70) | copy-start | bytes 884740
  94.1 5.0 %copy-start.10 = (f32[32,128]{1,0:T(8,128)}, f32[32,128]{1,0:T(8,128)S(1)}, u32[]{:S(2)}) copy-start(f32[32,128]{1,0:T(8,128)S(1)} %collective-permute-done.7.nxhi) | copy-start | bytes 49156
  94.1 5.8 %collective-permute-start.9 = (f32[64,128]{1,0:T(8,128)S(1)}, f32[64,128]{1,0:T(8,128)S(1)}, u32[]{:S(2)}, u32[]{:S(2)}) collective-permute-start(f32[64,128]{1,0:T(8,128)S(1)} %bitcast.63), channel_id=1, source_target_pairs={{1,0},{2,1},{3,2},{5,4},{6,5},{7,6},{9,8},{10,9},{11,10},{13,12},{... | collective-permute-start | bytes 98312 | tf_op jit(solution)/shard_map/ppermute | solution.py:40
  (9 other events, 5.5 us)

commit v18 on v17

--- a/solution.py
+++ b/solution.py
@@ -80,7 +80,7 @@
         nu[x] = 0.05 + 1.0 * jnp.sqrt(2.0 * total + 1e-06)
         return carry
 
-    lax.fori_loop(0, u.shape[1], plane, 0, unroll=16)
+    lax.fori_loop(0, u.shape[1], plane, 0, unroll=32)
 
 
 def advance_kernel(planes, u, xlo, xhi, zlo, zhi, ylo, yhi, nu, nxlo, nxhi, nzlo, nzhi, nylo, nyhi, sent, out):
@@ -110,7 +110,7 @@
             out[c, x] = center + 0.125 * (spread - advect) + impulse
         return carry
 
-    lax.fori_loop(0, u.shape[1], plane, 0, unroll=16)
+    lax.fori_loop(0, u.shape[1], plane, 0, unroll=32)
 
 
 def vmem_call(kernel, out_shape, count, smem=0):

time: 112 us -> 111 us (level)
  no operation moved by 1% of the time
where the time goes in v18:
time: 111 us; the launch traced here: 109 us
  starting transfers between devices  52.9 us (48%)
  Pallas kernels  15.4 us (14%)
  matrix products  13.9 us (13%)
  local copies, waits for them, and re-layouts  9.15 us (8%)
  waiting for transfers between devices  9.12 us (8%)
  between operations  4.96 us (4%)
  other arithmetic  4.03 us (4%)
    ppermute x6, starting transfers between devices, faces(): lax.ppermute(last, axis, forward)  16.9 us
    ppermute x4, starting transfers between devices, body(): owned = owned + lax.ppermute(owned, axis, pairs)  10.7 us
    all_to_all x1, starting transfers between devices, body(): lax.all_to_all(partial_sample.reshape(rows, per_row, -1), 'gx', split_axi...  9.97 us
    ppermute x6, starting transfers between devices, faces(): lax.ppermute(first, axis, backward)  9.76 us
    pallas_call x1, Pallas kernels, stencil(): vmem_call(advance_kernel, jax.ShapeDtypeStruct(velocity.shape, jnp.float3...  9.02 us
    all_to_all x1, waiting for transfers between devices, body(): lax.all_to_all(partial_sample.reshape(rows, per_row, -1), 'gx', split_axi...  7.37 us
    pallas_call x1, Pallas kernels, stencil(): vmem_call(viscosity_kernel, jax.ShapeDtypeStruct(velocity.shape[1:], jnp....  6.42 us
    all_to_all x1, starting transfers between devices, body(): lax.all_to_all(jnp.broadcast_to(owned_force[None], (rows,) + owned_force....  5.58 us
  transfers between devices with their start and end apart: 18, of which 3 were waited for; matrix products, arithmetic and copies ran while one was open for 14% of the time, Pallas kernels for 6%

profile of v18, /device:TPU:1, one launch (start us, length us, event | category | flops | bytes accessed | tf_op | source)
XLA Modules:
  0.0 109.5 jit_solution(15490164304458983390)
XLA Ops:
  0.6 1.3 %fusion.24 = (s32[1,1,1,1]{3,2,1,0:T(1,128)}, s32[1,1,1,1]{3,2,1,0:T(1,128)}) fusion(s32[1,1,1,2]{3,2,1,0:T(1,128)} %param.8), kind=kLoop, calls=%fused_computation.41 | loop fusion | bytes 16 | tf_op jit(solution)/shard_map/slice | solution.py:152
  6.7 4.7 %fusion.2 = f32[2,3,384]{2,1,0:T(4,128)S(1)} fusion(bf16[1,1,1,2,384,4096]{5,4,3,2,1,0:T(8,128)(2,1)} %param.9, bf16[1,3,4096]{2,1,0:T(4,128)(2,1)S(1)} %stack.10, bf16[1,3,4096]{2,1,0:T(4,128)(2,1)S(1)} %stack.9), kind=kOutput, calls=%fused_computation.2 | convolution fusion | flops 18972672 | bytes 6349824 | tf_op jit(solution)/shard_map/spq,scq->scp/dot_general | solution.py:154
  12.7 10.0 %all-to-all-start = ((f32[16,4,1152]{2,1,0:T(4,128)}), f32[16,4,1152]{2,1,0:T(4,128)S(1)}, u32[]{:S(2)}, u32[]{:S(2)}) async-start(f32[16,4,1152]{2,1,0:T(4,128)} %copy.36), calls=%async_computation | async-start | bytes 589824 | tf_op jit(solution)/shard_map/all_to_all | solution.py:168
  22.7 4.9 %fusion.4 = f32[2,3,64,32]{2,0,3,1:T(2,128)S(1)} fusion(f32[3,64,32,128]{3,2,1,0:T(8,128)S(1)} %copy-done, s32[2]{0:T(128)S(1)} %iota_multiply_fusion), kind=kOutput, calls=%fused_computation.4 | convolution fusion | flops 18874624 | bytes 3194888 | tf_op jit(solution)/shard_map/cxzy,ky->kczx/dot_general | solution.py:22
  27.6 7.4 %all-to-all-done = f32[16,4,1152]{2,1,0:T(4,128)S(1)} async-done(((f32[16,4,1152]{2,1,0:T(4,128)}), f32[16,4,1152]{2,1,0:T(4,128)S(1)}, u32[]{:S(2)}, u32[]{:S(2)}) %all-to-all-start) | async-done | bytes 294944 | tf_op jit(solution)/shard_map/all_to_all | solution.py:168
  36.9 2.2 %collective-permute-start.4 = (f32[3,32,128]{2,1,0:T(8,128)S(1)}, f32[3,32,128]{2,1,0:T(8,128)S(1)}, u32[]{:S(2)}, u32[]{:S(2)}) collective-permute-start(f32[3,32,128]{2,1,0:T(8,128)S(1)} %pad.14), channel_id=1, source_target_pairs={{0,4},{4,8},{8,12},{1,5},{5,9},{9,13},{2,6},{6,10},{10,14},{3,7},{... | collective-permute-start | bytes 147464 | tf_op jit(solution)/shard_map/ppermute | solution.py:40
  39.1 1.3 %collective-permute-start.5 = (f32[3,32,128]{2,1,0:T(8,128)S(1)}, f32[3,32,128]{2,1,0:T(8,128)S(1)}, u32[]{:S(2)}, u32[]{:S(2)}) collective-permute-start(f32[3,32,128]{2,1,0:T(8,128)S(1)} %pad.15), channel_id=1, source_target_pairs={{4,0},{8,4},{12,8},{5,1},{9,5},{13,9},{6,2},{10,6},{14,10},{7,3},{... | collective-permute-start | bytes 147464 | tf_op jit(solution)/shard_map/ppermute | solution.py:40
  41.1 4.3 %collective-permute-start.13 = (f32[4,1152]{1,0:T(4,128)S(1)}, f32[4,1152]{1,0:T(4,128)S(1)}, u32[]{:S(2)}, u32[]{:S(2)}) collective-permute-start(f32[4,1152]{1,0:T(4,128)S(1)} %add.43), channel_id=1, source_target_pairs={{0,8},{4,12},{8,0},{12,4},{1,9},{5,13},{9,1},{13,5},{2,10},{6,14},... | collective-permute-start | bytes 55304 | tf_op jit(solution)/shard_map/ppermute | solution.py:177
  46.0 2.6 %collective-permute-start.1 = (f32[3,32,128]{2,1,0:T(8,128)}, f32[3,32,128]{2,1,0:T(8,128)S(1)}, u32[]{:S(2)}, u32[]{:S(2)}) collective-permute-start(f32[3,32,128]{2,1,0:T(8,128)} %get-tuple-element.10), channel_id=1, source_target_pairs={{16,0},{32,16},{48,32},{64,48},{80,64},{96,80},{112,96},{128,112},... | collective-permute-start | bytes 147464 | tf_op jit(solution)/shard_map/ppermute | solution.py:40
  48.6 3.0 %collective-permute-start = (f32[3,32,128]{2,1,0:T(8,128)}, f32[3,32,128]{2,1,0:T(8,128)S(1)}, u32[]{:S(2)}, u32[]{:S(2)}) collective-permute-start(f32[3,32,128]{2,1,0:T(8,128)} %get-tuple-element.11), channel_id=1, source_target_pairs={{0,16},{16,32},{32,48},{48,64},{64,80},{80,96},{96,112},{112,128},... | collective-permute-start | bytes 147464 | tf_op jit(solution)/shard_map/ppermute | solution.py:40
  51.6 1.4 %collective-permute-start.14 = (f32[4,1152]{1,0:T(4,128)S(1)}, f32[4,1152]{1,0:T(4,128)S(1)}, u32[]{:S(2)}, u32[]{:S(2)}) collective-permute-start(f32[4,1152]{1,0:T(4,128)S(1)} %add.44), channel_id=1, source_target_pairs={{0,1},{1,0},{2,3},{3,2},{4,5},{5,4},{6,7},{7,6},{8,9},{9,8},{10,11... | collective-permute-start | bytes 55304 | tf_op jit(solution)/shard_map/ppermute | solution.py:177
  53.1 1.5 %collective-permute-done.14 = f32[4,1152]{1,0:T(4,128)S(1)} collective-permute-done((f32[4,1152]{1,0:T(4,128)S(1)}, f32[4,1152]{1,0:T(4,128)S(1)}, u32[]{:S(2)}, u32[]{:S(2)}) %collective-permute-start.14) | collective-permute-done | bytes 18464 | tf_op jit(solution)/shard_map/ppermute | solution.py:177
  54.7 3.2 %collective-permute-start.2 = (f32[3,64,128]{2,1,0:T(8,128)S(1)}, f32[3,64,128]{2,1,0:T(8,128)S(1)}, u32[]{:S(2)}, u32[]{:S(2)}) collective-permute-start(f32[3,64,128]{2,1,0:T(8,128)S(1)} %bitcast.58), channel_id=1, source_target_pairs={{0,1},{1,2},{2,3},{4,5},{5,6},{6,7},{8,9},{9,10},{10,11},{12,13},{... | collective-permute-start | bytes 294920 | tf_op jit(solution)/shard_map/ppermute | solution.py:40
  57.9 1.3 %collective-permute-start.3 = (f32[3,64,128]{2,1,0:T(8,128)S(1)}, f32[3,64,128]{2,1,0:T(8,128)S(1)}, u32[]{:S(2)}, u32[]{:S(2)}) collective-permute-start(f32[3,64,128]{2,1,0:T(8,128)S(1)} %bitcast.57), channel_id=1, source_target_pairs={{1,0},{2,1},{3,2},{5,4},{6,5},{7,6},{9,8},{10,9},{11,10},{13,12},{... | collective-permute-start | bytes 294920 | tf_op jit(solution)/shard_map/ppermute | solution.py:40
  59.2 3.8 %collective-permute-start.15 = (f32[4,1152]{1,0:T(4,128)S(1)}, f32[4,1152]{1,0:T(4,128)S(1)}, u32[]{:S(2)}, u32[]{:S(2)}) collective-permute-start(f32[4,1152]{1,0:T(4,128)S(1)} %add.45), channel_id=1, source_target_pairs={{0,2},{1,3},{2,0},{3,1},{4,6},{5,7},{6,4},{7,5},{8,10},{9,11},{10,... | collective-permute-start | bytes 55304 | tf_op jit(solution)/shard_map/ppermute | solution.py:177
  64.3 6.4 %shard_map.77.nu = f32[64,32,128]{2,1,0:T(8,128)} custom-call(f32[3,64,32,128]{3,2,1,0:T(8,128)} %u.3, f32[3,32,128]{2,1,0:T(8,128)} %copy-done.7, f32[3,32,128]{2,1,0:T(8,128)} %copy-done.6, f32[3,64,128]{2,1,0:T(8,128)} %copy-done.2, f32[3,64,128]{2,1,0:T(8,128)} %copy-done.3, f32[3,32,128]{2,1,0:T(8,128)} %copy-done.4, f32[3,32,128]{2,1,0:T(8,128)} %copy-done.5), custom_call_target="tpu_custom_call" | custom-call | tf_op jit(solution)/shard_map/pallas_call | solution.py:130
  72.3 5.6 %all-to-all-start.1 = ((f32[16,4,1152]{2,1,0:T(4,128)}), f32[16,4,1152]{2,1,0:T(4,128)S(1)}, u32[]{:S(2)}, u32[]{:S(2)}) async-start(f32[16,4,1152]{2,1,0:T(4,128)} %broadcast_in_dim.14), calls=%async_computation.1 | async-start | bytes 589824 | tf_op jit(solution)/shard_map/all_to_all | solution.py:181
  78.6 2.0 %collective-permute-start.7 = (f32[32,128]{1,0:T(8,128)S(1)}, f32[32,128]{1,0:T(8,128)S(1)}, u32[]{:S(2)}, u32[]{:S(2)}) collective-permute-start(f32[32,128]{1,0:T(8,128)S(1)} %get-tuple-element.14), channel_id=1, source_target_pairs={{16,0},{32,16},{48,32},{64,48},{80,64},{96,80},{112,96},{128,112},... | collective-permute-start | bytes 49160 | tf_op jit(solution)/shard_map/ppermute | solution.py:40
  80.6 3.7 %collective-permute-start.6 = (f32[32,128]{1,0:T(8,128)S(1)}, f32[32,128]{1,0:T(8,128)S(1)}, u32[]{:S(2)}, u32[]{:S(2)}) collective-permute-start(f32[32,128]{1,0:T(8,128)S(1)} %get-tuple-element.15), channel_id=1, source_target_pairs={{0,16},{16,32},{32,48},{48,64},{64,80},{80,96},{96,112},{112,128},... | collective-permute-start | bytes 49160 | tf_op jit(solution)/shard_map/ppermute | solution.py:40
  84.4 1.8 %select_reduce_fusion = (f32[64,32]{1,0:T(8,128)S(1)}, f32[64,32]{1,0:T(8,128)S(1)}) fusion(f32[64,32,128]{2,1,0:T(8,128)} %shard_map.77.nu, pred[128]{0:T(512)(128)(4,1)S(1)} %get-tuple-element.20, pred[128]{0:T(512)(128)(4,1)S(1)} %get-tuple-element.21), kind=kLoop, calls=%fused_computation.7 | loop fusion | flops 1044480 | bytes 1065216 | tf_op jit(solution)/shard_map/reduce_sum | solution.py:26
  86.3 1.9 %collective-permute-start.10 = (f32[32,128]{1,0:T(8,128)S(1)}, f32[32,128]{1,0:T(8,128)S(1)}, u32[]{:S(2)}, u32[]{:S(2)}) collective-permute-start(f32[32,128]{1,0:T(8,128)S(1)} %pad.16), channel_id=1, source_target_pairs={{0,4},{4,8},{8,12},{1,5},{5,9},{9,13},{2,6},{6,10},{10,14},{3,7},{... | collective-permute-start | bytes 49160 | tf_op jit(solution)/shard_map/ppermute | solution.py:40
  90.6 3.0 %collective-permute-start.8 = (f32[64,128]{1,0:T(8,128)S(1)}, f32[64,128]{1,0:T(8,128)S(1)}, u32[]{:S(2)}, u32[]{:S(2)}) collective-permute-start(f32[64,128]{1,0:T(8,128)S(1)} %bitcast.64), channel_id=1, source_target_pairs={{0,1},{1,2},{2,3},{4,5},{5,6},{6,7},{8,9},{9,10},{10,11},{12,13},{... | collective-permute-start | bytes 98312 | tf_op jit(solution)/shard_map/ppermute | solution.py:40
  95.3 3.7 %fusion = f32[2,3,4096]{2,1,0:T(4,128)S(1)} fusion(bf16[2,3,384]{2,1,0:T(4,128)(2,1)S(1)} %reshape.71, bf16[1,1,1,2,384,4096]{5,4,3,2,1,0:T(8,128)(2,1)} %param.9), kind=kOutput, calls=%fused_computation | convolution fusion | flops 18874368 | bytes 6394368 | tf_op jit(solution)/shard_map/axz,ahx->ahz/dot_general | solution.py:186
  100.5 9.0 %shard_map.78 = f32[3,64,32,128]{3,2,1,0:T(8,128)} custom-call(s32[2]{0:T(128)} %bitcast.65, f32[3,64,32,128]{3,2,1,0:T(8,128)} %u.3, f32[3,32,128]{2,1,0:T(8,128)} %copy-done.7, f32[3,32,128]{2,1,0:T(8,128)} %copy-done.6, f32[3,64,128]{2,1,0:T(8,128)} %copy-done.2, f32[3,64,128]{2,1,0:T(8,128)} %copy-done.3, f32[3,32,128]{2,1,0:T(8,128)} %copy-done.4, ...), custom_call_target="tpu_custom_call" | custom-call | tf_op jit(solution)/shard_map/pallas_call | solution.py:134
  (84 shorter events, 14.7 us)
Async XLA Ops:
  6.7 4.7 %copy-start.14 = (s32[1,1,1,2]{3,2,1,0:T(1,128)S(1)}, s32[1,1,1,2]{3,2,1,0:T(1,128)}, u32[]{:S(2)}) copy-start(s32[1,1,1,2]{3,2,1,0:T(1,128)} %param.7) | copy-start | bytes 28
  6.7 16.0 %copy-start = (f32[3,64,32,128]{3,2,1,0:T(8,128)S(1)}, f32[3,64,32,128]{3,2,1,0:T(8,128)}, u32[]{:S(2)}) copy-start(f32[3,64,32,128]{3,2,1,0:T(8,128)} %u.3) | copy-start | bytes 9437188
  12.7 22.3 %all-to-all-start = ((f32[16,4,1152]{2,1,0:T(4,128)}), f32[16,4,1152]{2,1,0:T(4,128)S(1)}, u32[]{:S(2)}, u32[]{:S(2)}) async-start(f32[16,4,1152]{2,1,0:T(4,128)} %copy.36), calls=%async_computation | async-start | bytes 589824 | tf_op jit(solution)/shard_map/all_to_all | solution.py:168
  35.6 4.7 %collective-permute-start.12 = (f32[4,1152]{1,0:T(4,128)}, f32[4,1152]{1,0:T(4,128)S(1)}, u32[]{:S(2)}, u32[]{:S(2)}) collective-permute-start(f32[4,1152]{1,0:T(4,128)} %reduce_sum.38), channel_id=1, source_target_pairs={{0,4},{4,0},{8,12},{12,8},{1,5},{5,1},{9,13},{13,9},{2,6},{6,2},{1... | collective-permute-start | bytes 55304 | tf_op jit(solution)/shard_map/ppermute | solution.py:177
  36.9 21.0 %collective-permute-start.4 = (f32[3,32,128]{2,1,0:T(8,128)S(1)}, f32[3,32,128]{2,1,0:T(8,128)S(1)}, u32[]{:S(2)}, u32[]{:S(2)}) collective-permute-start(f32[3,32,128]{2,1,0:T(8,128)S(1)} %pad.14), channel_id=1, source_target_pairs={{0,4},{4,8},{8,12},{1,5},{5,9},{9,13},{2,6},{6,10},{10,14},{3,7},{... | collective-permute-start | bytes 147464 | tf_op jit(solution)/shard_map/ppermute | solution.py:40
  39.1 20.1 %collective-permute-start.5 = (f32[3,32,128]{2,1,0:T(8,128)S(1)}, f32[3,32,128]{2,1,0:T(8,128)S(1)}, u32[]{:S(2)}, u32[]{:S(2)}) collective-permute-start(f32[3,32,128]{2,1,0:T(8,128)S(1)} %pad.15), channel_id=1, source_target_pairs={{4,0},{8,4},{12,8},{5,1},{9,5},{13,9},{6,2},{10,6},{14,10},{7,3},{... | collective-permute-start | bytes 147464 | tf_op jit(solution)/shard_map/ppermute | solution.py:40
  41.1 10.5 %collective-permute-start.13 = (f32[4,1152]{1,0:T(4,128)S(1)}, f32[4,1152]{1,0:T(4,128)S(1)}, u32[]{:S(2)}, u32[]{:S(2)}) collective-permute-start(f32[4,1152]{1,0:T(4,128)S(1)} %add.43), channel_id=1, source_target_pairs={{0,8},{4,12},{8,0},{12,4},{1,9},{5,13},{9,1},{13,5},{2,10},{6,14},... | collective-permute-start | bytes 55304 | tf_op jit(solution)/shard_map/ppermute | solution.py:177
  46.0 17.0 %collective-permute-start.1 = (f32[3,32,128]{2,1,0:T(8,128)}, f32[3,32,128]{2,1,0:T(8,128)S(1)}, u32[]{:S(2)}, u32[]{:S(2)}) collective-permute-start(f32[3,32,128]{2,1,0:T(8,128)} %get-tuple-element.10), channel_id=1, source_target_pairs={{16,0},{32,16},{48,32},{64,48},{80,64},{96,80},{112,96},{128,112},... | collective-permute-start | bytes 147464 | tf_op jit(solution)/shard_map/ppermute | solution.py:40
  48.6 14.4 %collective-permute-start = (f32[3,32,128]{2,1,0:T(8,128)}, f32[3,32,128]{2,1,0:T(8,128)S(1)}, u32[]{:S(2)}, u32[]{:S(2)}) collective-permute-start(f32[3,32,128]{2,1,0:T(8,128)} %get-tuple-element.11), channel_id=1, source_target_pairs={{0,16},{16,32},{32,48},{48,64},{64,80},{80,96},{96,112},{112,128},... | collective-permute-start | bytes 147464 | tf_op jit(solution)/shard_map/ppermute | solution.py:40
  51.6 3.0 %collective-permute-start.14 = (f32[4,1152]{1,0:T(4,128)S(1)}, f32[4,1152]{1,0:T(4,128)S(1)}, u32[]{:S(2)}, u32[]{:S(2)}) collective-permute-start(f32[4,1152]{1,0:T(4,128)S(1)} %add.44), channel_id=1, source_target_pairs={{0,1},{1,0},{2,3},{3,2},{4,5},{5,4},{6,7},{7,6},{8,9},{9,8},{10,11... | collective-permute-start | bytes 55304 | tf_op jit(solution)/shard_map/ppermute | solution.py:177
  54.7 8.4 %collective-permute-start.2 = (f32[3,64,128]{2,1,0:T(8,128)S(1)}, f32[3,64,128]{2,1,0:T(8,128)S(1)}, u32[]{:S(2)}, u32[]{:S(2)}) collective-permute-start(f32[3,64,128]{2,1,0:T(8,128)S(1)} %bitcast.58), channel_id=1, source_target_pairs={{0,1},{1,2},{2,3},{4,5},{5,6},{6,7},{8,9},{9,10},{10,11},{12,13},{... | collective-permute-start | bytes 294920 | tf_op jit(solution)/shard_map/ppermute | solution.py:40
  57.9 5.4 %copy-start.4 = (f32[3,32,128]{2,1,0:T(8,128)}, f32[3,32,128]{2,1,0:T(8,128)S(1)}, u32[]{:S(2)}) copy-start(f32[3,32,128]{2,1,0:T(8,128)S(1)} %collective-permute-done.4.ylo) | copy-start | bytes 147460
  57.9 5.4 %collective-permute-start.3 = (f32[3,64,128]{2,1,0:T(8,128)S(1)}, f32[3,64,128]{2,1,0:T(8,128)S(1)}, u32[]{:S(2)}, u32[]{:S(2)}) collective-permute-start(f32[3,64,128]{2,1,0:T(8,128)S(1)} %bitcast.57), channel_id=1, source_target_pairs={{1,0},{2,1},{3,2},{5,4},{6,5},{7,6},{9,8},{10,9},{11,10},{13,12},{... | collective-permute-start | bytes 294920 | tf_op jit(solution)/shard_map/ppermute | solution.py:40
  59.2 4.1 %copy-start.5 = (f32[3,32,128]{2,1,0:T(8,128)}, f32[3,32,128]{2,1,0:T(8,128)S(1)}, u32[]{:S(2)}) copy-start(f32[3,32,128]{2,1,0:T(8,128)S(1)} %collective-permute-done.5.yhi) | copy-start | bytes 147460
  59.2 11.5 %collective-permute-start.15 = (f32[4,1152]{1,0:T(4,128)S(1)}, f32[4,1152]{1,0:T(4,128)S(1)}, u32[]{:S(2)}, u32[]{:S(2)}) collective-permute-start(f32[4,1152]{1,0:T(4,128)S(1)} %add.45), channel_id=1, source_target_pairs={{0,2},{1,3},{2,0},{3,1},{4,6},{5,7},{6,4},{7,5},{8,10},{9,11},{10,... | collective-permute-start | bytes 55304 | tf_op jit(solution)/shard_map/ppermute | solution.py:177
  72.3 21.3 %all-to-all-start.1 = ((f32[16,4,1152]{2,1,0:T(4,128)}), f32[16,4,1152]{2,1,0:T(4,128)S(1)}, u32[]{:S(2)}, u32[]{:S(2)}) async-start(f32[16,4,1152]{2,1,0:T(4,128)} %broadcast_in_dim.14), calls=%async_computation.1 | async-start | bytes 589824 | tf_op jit(solution)/shard_map/all_to_all | solution.py:181
  78.6 15.4 %collective-permute-start.7 = (f32[32,128]{1,0:T(8,128)S(1)}, f32[32,128]{1,0:T(8,128)S(1)}, u32[]{:S(2)}, u32[]{:S(2)}) collective-permute-start(f32[32,128]{1,0:T(8,128)S(1)} %get-tuple-element.14), channel_id=1, source_target_pairs={{16,0},{32,16},{48,32},{64,48},{80,64},{96,80},{112,96},{128,112},... | collective-permute-start | bytes 49160 | tf_op jit(solution)/shard_map/ppermute | solution.py:40
  80.6 19.2 %collective-permute-start.6 = (f32[32,128]{1,0:T(8,128)S(1)}, f32[32,128]{1,0:T(8,128)S(1)}, u32[]{:S(2)}, u32[]{:S(2)}) collective-permute-start(f32[32,128]{1,0:T(8,128)S(1)} %get-tuple-element.15), channel_id=1, source_target_pairs={{0,16},{16,32},{32,48},{48,64},{64,80},{80,96},{96,112},{112,128},... | collective-permute-start | bytes 49160 | tf_op jit(solution)/shard_map/ppermute | solution.py:40
  86.3 13.4 %collective-permute-start.10 = (f32[32,128]{1,0:T(8,128)S(1)}, f32[32,128]{1,0:T(8,128)S(1)}, u32[]{:S(2)}, u32[]{:S(2)}) collective-permute-start(f32[32,128]{1,0:T(8,128)S(1)} %pad.16), channel_id=1, source_target_pairs={{0,4},{4,8},{8,12},{1,5},{5,9},{9,13},{2,6},{6,10},{10,14},{3,7},{... | collective-permute-start | bytes 49160 | tf_op jit(solution)/shard_map/ppermute | solution.py:40
  88.2 11.6 %collective-permute-start.11 = (f32[32,128]{1,0:T(8,128)S(1)}, f32[32,128]{1,0:T(8,128)S(1)}, u32[]{:S(2)}, u32[]{:S(2)}) collective-permute-start(f32[32,128]{1,0:T(8,128)S(1)} %pad.17), channel_id=1, source_target_pairs={{4,0},{8,4},{12,8},{5,1},{9,5},{13,9},{6,2},{10,6},{14,10},{7,3},{... | collective-permute-start | bytes 49160 | tf_op jit(solution)/shard_map/ppermute | solution.py:40
  90.6 9.2 %collective-permute-start.8 = (f32[64,128]{1,0:T(8,128)S(1)}, f32[64,128]{1,0:T(8,128)S(1)}, u32[]{:S(2)}, u32[]{:S(2)}) collective-permute-start(f32[64,128]{1,0:T(8,128)S(1)} %bitcast.64), channel_id=1, source_target_pairs={{0,1},{1,2},{2,3},{4,5},{5,6},{6,7},{8,9},{9,10},{10,11},{12,13},{... | collective-permute-start | bytes 98312 | tf_op jit(solution)/shard_map/ppermute | solution.py:40
  93.7 5.3 %copy-start.1 = (f32[64,1152]{1,0:T(8,128)}, f32[64,1152]{1,0:T(8,128)S(1)}, u32[]{:S(2)}) copy-start(f32[64,1152]{1,0:T(8,128)S(1)} %reshape.70) | copy-start | bytes 884740
  94.0 5.0 %copy-start.10 = (f32[32,128]{1,0:T(8,128)}, f32[32,128]{1,0:T(8,128)S(1)}, u32[]{:S(2)}) copy-start(f32[32,128]{1,0:T(8,128)S(1)} %collective-permute-done.7.nxhi) | copy-start | bytes 49156
  94.0 5.8 %collective-permute-start.9 = (f32[64,128]{1,0:T(8,128)S(1)}, f32[64,128]{1,0:T(8,128)S(1)}, u32[]{:S(2)}, u32[]{:S(2)}) collective-permute-start(f32[64,128]{1,0:T(8,128)S(1)} %bitcast.63), channel_id=1, source_target_pairs={{1,0},{2,1},{3,2},{5,4},{6,5},{7,6},{9,8},{10,9},{11,10},{13,12},{... | collective-permute-start | bytes 98312 | tf_op jit(solution)/shard_map/ppermute | solution.py:40
  (9 other events, 5.5 us)

commit v19 on v18

--- a/solution.py
+++ b/solution.py
@@ -80,7 +80,7 @@
         nu[x] = 0.05 + 1.0 * jnp.sqrt(2.0 * total + 1e-06)
         return carry
 
-    lax.fori_loop(0, u.shape[1], plane, 0, unroll=32)
+    lax.fori_loop(0, u.shape[1], plane, 0, unroll=64)
 
 
 def advance_kernel(planes, u, xlo, xhi, zlo, zhi, ylo, yhi, nu, nxlo, nxhi, nzlo, nzhi, nylo, nyhi, sent, out):
@@ -110,7 +110,7 @@
             out[c, x] = center + 0.125 * (spread - advect) + impulse
         return carry
 
-    lax.fori_loop(0, u.shape[1], plane, 0, unroll=32)
+    lax.fori_loop(0, u.shape[1], plane, 0, unroll=64)
 
 
 def vmem_call(kernel, out_shape, count, smem=0):

time: 111 us -> 111 us (level)
  transfers between devices with their start and end apart: 18 -> 18, of which waited for: 3 -> 2; matrix products, arithmetic and copies ran while one was open for 14% -> 14% of each run, Pallas kernels for 6% -> 6%
where the time goes in v19:
time: 111 us; the launch traced here: 109 us
  starting transfers between devices  52.9 us (48%)
  Pallas kernels  15 us (14%)
  matrix products  13.9 us (13%)
  local copies, waits for them, and re-layouts  9.32 us (8%)
  waiting for transfers between devices  8.94 us (8%)
  between operations  4.96 us (4%)
  other arithmetic  4.03 us (4%)
    ppermute x6, starting transfers between devices, faces(): lax.ppermute(last, axis, forward)  16.9 us
    ppermute x4, starting transfers between devices, body(): owned = owned + lax.ppermute(owned, axis, pairs)  10.8 us
    all_to_all x1, starting transfers between devices, body(): lax.all_to_all(partial_sample.reshape(rows, per_row, -1), 'gx', split_axi...  9.97 us
    ppermute x6, starting transfers between devices, faces(): lax.ppermute(first, axis, backward)  9.76 us
    pallas_call x1, Pallas kernels, stencil(): vmem_call(advance_kernel, jax.ShapeDtypeStruct(velocity.shape, jnp.float3...  8.72 us
    all_to_all x1, waiting for transfers between devices, body(): lax.all_to_all(partial_sample.reshape(rows, per_row, -1), 'gx', split_axi...  7.37 us
    pallas_call x1, Pallas kernels, stencil(): vmem_call(viscosity_kernel, jax.ShapeDtypeStruct(velocity.shape[1:], jnp....  6.3 us
    all_to_all x1, starting transfers between devices, body(): lax.all_to_all(jnp.broadcast_to(owned_force[None], (rows,) + owned_force....  5.4 us
  transfers between devices with their start and end apart: 18, of which 2 were waited for; matrix products, arithmetic and copies ran while one was open for 14% of the time, Pallas kernels for 6%

profile of v19, /device:TPU:1, one launch (start us, length us, event | category | flops | bytes accessed | tf_op | source)
XLA Modules:
  0.0 109.1 jit_solution(3890866699798222990)
XLA Ops:
  0.6 1.3 %fusion.24 = (s32[1,1,1,1]{3,2,1,0:T(1,128)}, s32[1,1,1,1]{3,2,1,0:T(1,128)}) fusion(s32[1,1,1,2]{3,2,1,0:T(1,128)} %param.8), kind=kLoop, calls=%fused_computation.41 | loop fusion | bytes 16 | tf_op jit(solution)/shard_map/slice | solution.py:152
  6.7 4.7 %fusion.2 = f32[2,3,384]{2,1,0:T(4,128)S(1)} fusion(bf16[1,1,1,2,384,4096]{5,4,3,2,1,0:T(8,128)(2,1)} %param.9, bf16[1,3,4096]{2,1,0:T(4,128)(2,1)S(1)} %stack.10, bf16[1,3,4096]{2,1,0:T(4,128)(2,1)S(1)} %stack.9), kind=kOutput, calls=%fused_computation.2 | convolution fusion | flops 18972672 | bytes 6349824 | tf_op jit(solution)/shard_map/spq,scq->scp/dot_general | solution.py:154
  12.7 10.0 %all-to-all-start = ((f32[16,4,1152]{2,1,0:T(4,128)}), f32[16,4,1152]{2,1,0:T(4,128)S(1)}, u32[]{:S(2)}, u32[]{:S(2)}) async-start(f32[16,4,1152]{2,1,0:T(4,128)} %copy.36), calls=%async_computation | async-start | bytes 589824 | tf_op jit(solution)/shard_map/all_to_all | solution.py:168
  22.7 4.9 %fusion.4 = f32[2,3,64,32]{2,0,3,1:T(2,128)S(1)} fusion(f32[3,64,32,128]{3,2,1,0:T(8,128)S(1)} %copy-done, s32[2]{0:T(128)S(1)} %iota_multiply_fusion), kind=kOutput, calls=%fused_computation.4 | convolution fusion | flops 18874624 | bytes 3194888 | tf_op jit(solution)/shard_map/cxzy,ky->kczx/dot_general | solution.py:22
  27.6 7.4 %all-to-all-done = f32[16,4,1152]{2,1,0:T(4,128)S(1)} async-done(((f32[16,4,1152]{2,1,0:T(4,128)}), f32[16,4,1152]{2,1,0:T(4,128)S(1)}, u32[]{:S(2)}, u32[]{:S(2)}) %all-to-all-start) | async-done | bytes 294944 | tf_op jit(solution)/shard_map/all_to_all | solution.py:168
  36.9 2.2 %collective-permute-start.4 = (f32[3,32,128]{2,1,0:T(8,128)S(1)}, f32[3,32,128]{2,1,0:T(8,128)S(1)}, u32[]{:S(2)}, u32[]{:S(2)}) collective-permute-start(f32[3,32,128]{2,1,0:T(8,128)S(1)} %pad.14), channel_id=1, source_target_pairs={{0,4},{4,8},{8,12},{1,5},{5,9},{9,13},{2,6},{6,10},{10,14},{3,7},{... | collective-permute-start | bytes 147464 | tf_op jit(solution)/shard_map/ppermute | solution.py:40
  41.1 4.3 %collective-permute-start.13 = (f32[4,1152]{1,0:T(4,128)S(1)}, f32[4,1152]{1,0:T(4,128)S(1)}, u32[]{:S(2)}, u32[]{:S(2)}) collective-permute-start(f32[4,1152]{1,0:T(4,128)S(1)} %add.43), channel_id=1, source_target_pairs={{0,8},{4,12},{8,0},{12,4},{1,9},{5,13},{9,1},{13,5},{2,10},{6,14},... | collective-permute-start | bytes 55304 | tf_op jit(solution)/shard_map/ppermute | solution.py:177
  46.0 2.6 %collective-permute-start.1 = (f32[3,32,128]{2,1,0:T(8,128)}, f32[3,32,128]{2,1,0:T(8,128)S(1)}, u32[]{:S(2)}, u32[]{:S(2)}) collective-permute-start(f32[3,32,128]{2,1,0:T(8,128)} %get-tuple-element.10), channel_id=1, source_target_pairs={{16,0},{32,16},{48,32},{64,48},{80,64},{96,80},{112,96},{128,112},... | collective-permute-start | bytes 147464 | tf_op jit(solution)/shard_map/ppermute | solution.py:40
  48.6 3.0 %collective-permute-start = (f32[3,32,128]{2,1,0:T(8,128)}, f32[3,32,128]{2,1,0:T(8,128)S(1)}, u32[]{:S(2)}, u32[]{:S(2)}) collective-permute-start(f32[3,32,128]{2,1,0:T(8,128)} %get-tuple-element.11), channel_id=1, source_target_pairs={{0,16},{16,32},{32,48},{48,64},{64,80},{80,96},{96,112},{112,128},... | collective-permute-start | bytes 147464 | tf_op jit(solution)/shard_map/ppermute | solution.py:40
  51.6 1.4 %collective-permute-start.14 = (f32[4,1152]{1,0:T(4,128)S(1)}, f32[4,1152]{1,0:T(4,128)S(1)}, u32[]{:S(2)}, u32[]{:S(2)}) collective-permute-start(f32[4,1152]{1,0:T(4,128)S(1)} %add.44), channel_id=1, source_target_pairs={{0,1},{1,0},{2,3},{3,2},{4,5},{5,4},{6,7},{7,6},{8,9},{9,8},{10,11... | collective-permute-start | bytes 55304 | tf_op jit(solution)/shard_map/ppermute | solution.py:177
  53.1 1.5 %collective-permute-done.14 = f32[4,1152]{1,0:T(4,128)S(1)} collective-permute-done((f32[4,1152]{1,0:T(4,128)S(1)}, f32[4,1152]{1,0:T(4,128)S(1)}, u32[]{:S(2)}, u32[]{:S(2)}) %collective-permute-start.14) | collective-permute-done | bytes 18464 | tf_op jit(solution)/shard_map/ppermute | solution.py:177
  54.7 3.2 %collective-permute-start.2 = (f32[3,64,128]{2,1,0:T(8,128)S(1)}, f32[3,64,128]{2,1,0:T(8,128)S(1)}, u32[]{:S(2)}, u32[]{:S(2)}) collective-permute-start(f32[3,64,128]{2,1,0:T(8,128)S(1)} %bitcast.58), channel_id=1, source_target_pairs={{0,1},{1,2},{2,3},{4,5},{5,6},{6,7},{8,9},{9,10},{10,11},{12,13},{... | collective-permute-start | bytes 294920 | tf_op jit(solution)/shard_map/ppermute | solution.py:40
  57.9 1.3 %collective-permute-start.3 = (f32[3,64,128]{2,1,0:T(8,128)S(1)}, f32[3,64,128]{2,1,0:T(8,128)S(1)}, u32[]{:S(2)}, u32[]{:S(2)}) collective-permute-start(f32[3,64,128]{2,1,0:T(8,128)S(1)} %bitcast.57), channel_id=1, source_target_pairs={{1,0},{2,1},{3,2},{5,4},{6,5},{7,6},{9,8},{10,9},{11,10},{13,12},{... | collective-permute-start | bytes 294920 | tf_op jit(solution)/shard_map/ppermute | solution.py:40
  59.2 4.0 %collective-permute-start.15 = (f32[4,1152]{1,0:T(4,128)S(1)}, f32[4,1152]{1,0:T(4,128)S(1)}, u32[]{:S(2)}, u32[]{:S(2)}) collective-permute-start(f32[4,1152]{1,0:T(4,128)S(1)} %add.45), channel_id=1, source_target_pairs={{0,2},{1,3},{2,0},{3,1},{4,6},{5,7},{6,4},{7,5},{8,10},{9,11},{10,... | collective-permute-start | bytes 55304 | tf_op jit(solution)/shard_map/ppermute | solution.py:177
  64.5 6.3 %shard_map.77.nu = f32[64,32,128]{2,1,0:T(8,128)} custom-call(f32[3,64,32,128]{3,2,1,0:T(8,128)} %u.3, f32[3,32,128]{2,1,0:T(8,128)} %copy-done.7, f32[3,32,128]{2,1,0:T(8,128)} %copy-done.6, f32[3,64,128]{2,1,0:T(8,128)} %copy-done.2, f32[3,64,128]{2,1,0:T(8,128)} %copy-done.3, f32[3,32,128]{2,1,0:T(8,128)} %copy-done.4, f32[3,32,128]{2,1,0:T(8,128)} %copy-done.5), custom_call_target="tpu_custom_call" | custom-call | tf_op jit(solution)/shard_map/pallas_call | solution.py:130
  72.3 5.4 %all-to-all-start.1 = ((f32[16,4,1152]{2,1,0:T(4,128)}), f32[16,4,1152]{2,1,0:T(4,128)S(1)}, u32[]{:S(2)}, u32[]{:S(2)}) async-start(f32[16,4,1152]{2,1,0:T(4,128)} %broadcast_in_dim.14), calls=%async_computation.1 | async-start | bytes 589824 | tf_op jit(solution)/shard_map/all_to_all | solution.py:181
  78.5 2.0 %collective-permute-start.7 = (f32[32,128]{1,0:T(8,128)S(1)}, f32[32,128]{1,0:T(8,128)S(1)}, u32[]{:S(2)}, u32[]{:S(2)}) collective-permute-start(f32[32,128]{1,0:T(8,128)S(1)} %get-tuple-element.14), channel_id=1, source_target_pairs={{16,0},{32,16},{48,32},{64,48},{80,64},{96,80},{112,96},{128,112},... | collective-permute-start | bytes 49160 | tf_op jit(solution)/shard_map/ppermute | solution.py:40
  80.5 3.6 %collective-permute-start.6 = (f32[32,128]{1,0:T(8,128)S(1)}, f32[32,128]{1,0:T(8,128)S(1)}, u32[]{:S(2)}, u32[]{:S(2)}) collective-permute-start(f32[32,128]{1,0:T(8,128)S(1)} %get-tuple-element.15), channel_id=1, source_target_pairs={{0,16},{16,32},{32,48},{48,64},{64,80},{80,96},{96,112},{112,128},... | collective-permute-start | bytes 49160 | tf_op jit(solution)/shard_map/ppermute | solution.py:40
  84.0 1.8 %select_reduce_fusion = (f32[64,32]{1,0:T(8,128)S(1)}, f32[64,32]{1,0:T(8,128)S(1)}) fusion(f32[64,32,128]{2,1,0:T(8,128)} %shard_map.77.nu, pred[128]{0:T(512)(128)(4,1)S(1)} %get-tuple-element.20, pred[128]{0:T(512)(128)(4,1)S(1)} %get-tuple-element.21), kind=kLoop, calls=%fused_computation.7 | loop fusion | flops 1044480 | bytes 1065216 | tf_op jit(solution)/shard_map/reduce_sum | solution.py:26
  86.0 1.9 %collective-permute-start.10 = (f32[32,128]{1,0:T(8,128)S(1)}, f32[32,128]{1,0:T(8,128)S(1)}, u32[]{:S(2)}, u32[]{:S(2)}) collective-permute-start(f32[32,128]{1,0:T(8,128)S(1)} %pad.16), channel_id=1, source_target_pairs={{0,4},{4,8},{8,12},{1,5},{5,9},{9,13},{2,6},{6,10},{10,14},{3,7},{... | collective-permute-start | bytes 49160 | tf_op jit(solution)/shard_map/ppermute | solution.py:40
  87.9 1.3 %collective-permute-start.11 = (f32[32,128]{1,0:T(8,128)S(1)}, f32[32,128]{1,0:T(8,128)S(1)}, u32[]{:S(2)}, u32[]{:S(2)}) collective-permute-start(f32[32,128]{1,0:T(8,128)S(1)} %pad.17), channel_id=1, source_target_pairs={{4,0},{8,4},{12,8},{5,1},{9,5},{13,9},{6,2},{10,6},{14,10},{7,3},{... | collective-permute-start | bytes 49160 | tf_op jit(solution)/shard_map/ppermute | solution.py:40
  90.3 3.2 %collective-permute-start.8 = (f32[64,128]{1,0:T(8,128)S(1)}, f32[64,128]{1,0:T(8,128)S(1)}, u32[]{:S(2)}, u32[]{:S(2)}) collective-permute-start(f32[64,128]{1,0:T(8,128)S(1)} %bitcast.64), channel_id=1, source_target_pairs={{0,1},{1,2},{2,3},{4,5},{5,6},{6,7},{8,9},{9,10},{10,11},{12,13},{... | collective-permute-start | bytes 98312 | tf_op jit(solution)/shard_map/ppermute | solution.py:40
  95.2 3.7 %fusion = f32[2,3,4096]{2,1,0:T(4,128)S(1)} fusion(bf16[2,3,384]{2,1,0:T(4,128)(2,1)S(1)} %reshape.71, bf16[1,1,1,2,384,4096]{5,4,3,2,1,0:T(8,128)(2,1)} %param.9), kind=kOutput, calls=%fused_computation | convolution fusion | flops 18874368 | bytes 6394368 | tf_op jit(solution)/shard_map/axz,ahx->ahz/dot_general | solution.py:186
  100.3 8.7 %shard_map.78 = f32[3,64,32,128]{3,2,1,0:T(8,128)} custom-call(s32[2]{0:T(128)} %bitcast.65, f32[3,64,32,128]{3,2,1,0:T(8,128)} %u.3, f32[3,32,128]{2,1,0:T(8,128)} %copy-done.7, f32[3,32,128]{2,1,0:T(8,128)} %copy-done.6, f32[3,64,128]{2,1,0:T(8,128)} %copy-done.2, f32[3,64,128]{2,1,0:T(8,128)} %copy-done.3, f32[3,32,128]{2,1,0:T(8,128)} %copy-done.4, ...), custom_call_target="tpu_custom_call" | custom-call | tf_op jit(solution)/shard_map/pallas_call | solution.py:134
  (84 shorter events, 14.7 us)
Async XLA Ops:
  6.7 4.7 %copy-start.14 = (s32[1,1,1,2]{3,2,1,0:T(1,128)S(1)}, s32[1,1,1,2]{3,2,1,0:T(1,128)}, u32[]{:S(2)}) copy-start(s32[1,1,1,2]{3,2,1,0:T(1,128)} %param.7) | copy-start | bytes 28
  6.7 16.0 %copy-start = (f32[3,64,32,128]{3,2,1,0:T(8,128)S(1)}, f32[3,64,32,128]{3,2,1,0:T(8,128)}, u32[]{:S(2)}) copy-start(f32[3,64,32,128]{3,2,1,0:T(8,128)} %u.3) | copy-start | bytes 9437188
  12.7 22.3 %all-to-all-start = ((f32[16,4,1152]{2,1,0:T(4,128)}), f32[16,4,1152]{2,1,0:T(4,128)S(1)}, u32[]{:S(2)}, u32[]{:S(2)}) async-start(f32[16,4,1152]{2,1,0:T(4,128)} %copy.36), calls=%async_computation | async-start | bytes 589824 | tf_op jit(solution)/shard_map/all_to_all | solution.py:168
  35.6 4.7 %collective-permute-start.12 = (f32[4,1152]{1,0:T(4,128)}, f32[4,1152]{1,0:T(4,128)S(1)}, u32[]{:S(2)}, u32[]{:S(2)}) collective-permute-start(f32[4,1152]{1,0:T(4,128)} %reduce_sum.38), channel_id=1, source_target_pairs={{0,4},{4,0},{8,12},{12,8},{1,5},{5,1},{9,13},{13,9},{2,6},{6,2},{1... | collective-permute-start | bytes 55304 | tf_op jit(solution)/shard_map/ppermute | solution.py:177
  36.9 21.0 %collective-permute-start.4 = (f32[3,32,128]{2,1,0:T(8,128)S(1)}, f32[3,32,128]{2,1,0:T(8,128)S(1)}, u32[]{:S(2)}, u32[]{:S(2)}) collective-permute-start(f32[3,32,128]{2,1,0:T(8,128)S(1)} %pad.14), channel_id=1, source_target_pairs={{0,4},{4,8},{8,12},{1,5},{5,9},{9,13},{2,6},{6,10},{10,14},{3,7},{... | collective-permute-start | bytes 147464 | tf_op jit(solution)/shard_map/ppermute | solution.py:40
  39.1 20.1 %collective-permute-start.5 = (f32[3,32,128]{2,1,0:T(8,128)S(1)}, f32[3,32,128]{2,1,0:T(8,128)S(1)}, u32[]{:S(2)}, u32[]{:S(2)}) collective-permute-start(f32[3,32,128]{2,1,0:T(8,128)S(1)} %pad.15), channel_id=1, source_target_pairs={{4,0},{8,4},{12,8},{5,1},{9,5},{13,9},{6,2},{10,6},{14,10},{7,3},{... | collective-permute-start | bytes 147464 | tf_op jit(solution)/shard_map/ppermute | solution.py:40
  41.1 10.5 %collective-permute-start.13 = (f32[4,1152]{1,0:T(4,128)S(1)}, f32[4,1152]{1,0:T(4,128)S(1)}, u32[]{:S(2)}, u32[]{:S(2)}) collective-permute-start(f32[4,1152]{1,0:T(4,128)S(1)} %add.43), channel_id=1, source_target_pairs={{0,8},{4,12},{8,0},{12,4},{1,9},{5,13},{9,1},{13,5},{2,10},{6,14},... | collective-permute-start | bytes 55304 | tf_op jit(solution)/shard_map/ppermute | solution.py:177
  46.0 17.2 %collective-permute-start.1 = (f32[3,32,128]{2,1,0:T(8,128)}, f32[3,32,128]{2,1,0:T(8,128)S(1)}, u32[]{:S(2)}, u32[]{:S(2)}) collective-permute-start(f32[3,32,128]{2,1,0:T(8,128)} %get-tuple-element.10), channel_id=1, source_target_pairs={{16,0},{32,16},{48,32},{64,48},{80,64},{96,80},{112,96},{128,112},... | collective-permute-start | bytes 147464 | tf_op jit(solution)/shard_map/ppermute | solution.py:40
  48.6 14.6 %collective-permute-start = (f32[3,32,128]{2,1,0:T(8,128)}, f32[3,32,128]{2,1,0:T(8,128)S(1)}, u32[]{:S(2)}, u32[]{:S(2)}) collective-permute-start(f32[3,32,128]{2,1,0:T(8,128)} %get-tuple-element.11), channel_id=1, source_target_pairs={{0,16},{16,32},{32,48},{48,64},{64,80},{80,96},{96,112},{112,128},... | collective-permute-start | bytes 147464 | tf_op jit(solution)/shard_map/ppermute | solution.py:40
  51.6 3.0 %collective-permute-start.14 = (f32[4,1152]{1,0:T(4,128)S(1)}, f32[4,1152]{1,0:T(4,128)S(1)}, u32[]{:S(2)}, u32[]{:S(2)}) collective-permute-start(f32[4,1152]{1,0:T(4,128)S(1)} %add.44), channel_id=1, source_target_pairs={{0,1},{1,0},{2,3},{3,2},{4,5},{5,4},{6,7},{7,6},{8,9},{9,8},{10,11... | collective-permute-start | bytes 55304 | tf_op jit(solution)/shard_map/ppermute | solution.py:177
  54.7 8.6 %collective-permute-start.2 = (f32[3,64,128]{2,1,0:T(8,128)S(1)}, f32[3,64,128]{2,1,0:T(8,128)S(1)}, u32[]{:S(2)}, u32[]{:S(2)}) collective-permute-start(f32[3,64,128]{2,1,0:T(8,128)S(1)} %bitcast.58), channel_id=1, source_target_pairs={{0,1},{1,2},{2,3},{4,5},{5,6},{6,7},{8,9},{9,10},{10,11},{12,13},{... | collective-permute-start | bytes 294920 | tf_op jit(solution)/shard_map/ppermute | solution.py:40
  57.9 5.4 %copy-start.4 = (f32[3,32,128]{2,1,0:T(8,128)}, f32[3,32,128]{2,1,0:T(8,128)S(1)}, u32[]{:S(2)}) copy-start(f32[3,32,128]{2,1,0:T(8,128)S(1)} %collective-permute-done.4.ylo) | copy-start | bytes 147460
  57.9 5.4 %collective-permute-start.3 = (f32[3,64,128]{2,1,0:T(8,128)S(1)}, f32[3,64,128]{2,1,0:T(8,128)S(1)}, u32[]{:S(2)}, u32[]{:S(2)}) collective-permute-start(f32[3,64,128]{2,1,0:T(8,128)S(1)} %bitcast.57), channel_id=1, source_target_pairs={{1,0},{2,1},{3,2},{5,4},{6,5},{7,6},{9,8},{10,9},{11,10},{13,12},{... | collective-permute-start | bytes 294920 | tf_op jit(solution)/shard_map/ppermute | solution.py:40
  59.2 4.1 %copy-start.5 = (f32[3,32,128]{2,1,0:T(8,128)}, f32[3,32,128]{2,1,0:T(8,128)S(1)}, u32[]{:S(2)}) copy-start(f32[3,32,128]{2,1,0:T(8,128)S(1)} %collective-permute-done.5.yhi) | copy-start | bytes 147460
  59.2 11.6 %collective-permute-start.15 = (f32[4,1152]{1,0:T(4,128)S(1)}, f32[4,1152]{1,0:T(4,128)S(1)}, u32[]{:S(2)}, u32[]{:S(2)}) collective-permute-start(f32[4,1152]{1,0:T(4,128)S(1)} %add.45), channel_id=1, source_target_pairs={{0,2},{1,3},{2,0},{3,1},{4,6},{5,7},{6,4},{7,5},{8,10},{9,11},{10,... | collective-permute-start | bytes 55304 | tf_op jit(solution)/shard_map/ppermute | solution.py:177
  72.3 21.2 %all-to-all-start.1 = ((f32[16,4,1152]{2,1,0:T(4,128)}), f32[16,4,1152]{2,1,0:T(4,128)S(1)}, u32[]{:S(2)}, u32[]{:S(2)}) async-start(f32[16,4,1152]{2,1,0:T(4,128)} %broadcast_in_dim.14), calls=%async_computation.1 | async-start | bytes 589824 | tf_op jit(solution)/shard_map/all_to_all | solution.py:181
  78.5 15.4 %collective-permute-start.7 = (f32[32,128]{1,0:T(8,128)S(1)}, f32[32,128]{1,0:T(8,128)S(1)}, u32[]{:S(2)}, u32[]{:S(2)}) collective-permute-start(f32[32,128]{1,0:T(8,128)S(1)} %get-tuple-element.14), channel_id=1, source_target_pairs={{16,0},{32,16},{48,32},{64,48},{80,64},{96,80},{112,96},{128,112},... | collective-permute-start | bytes 49160 | tf_op jit(solution)/shard_map/ppermute | solution.py:40
  80.5 19.2 %collective-permute-start.6 = (f32[32,128]{1,0:T(8,128)S(1)}, f32[32,128]{1,0:T(8,128)S(1)}, u32[]{:S(2)}, u32[]{:S(2)}) collective-permute-start(f32[32,128]{1,0:T(8,128)S(1)} %get-tuple-element.15), channel_id=1, source_target_pairs={{0,16},{16,32},{32,48},{48,64},{64,80},{80,96},{96,112},{112,128},... | collective-permute-start | bytes 49160 | tf_op jit(solution)/shard_map/ppermute | solution.py:40
  86.0 13.6 %collective-permute-start.10 = (f32[32,128]{1,0:T(8,128)S(1)}, f32[32,128]{1,0:T(8,128)S(1)}, u32[]{:S(2)}, u32[]{:S(2)}) collective-permute-start(f32[32,128]{1,0:T(8,128)S(1)} %pad.16), channel_id=1, source_target_pairs={{0,4},{4,8},{8,12},{1,5},{5,9},{9,13},{2,6},{6,10},{10,14},{3,7},{... | collective-permute-start | bytes 49160 | tf_op jit(solution)/shard_map/ppermute | solution.py:40
  87.9 11.8 %collective-permute-start.11 = (f32[32,128]{1,0:T(8,128)S(1)}, f32[32,128]{1,0:T(8,128)S(1)}, u32[]{:S(2)}, u32[]{:S(2)}) collective-permute-start(f32[32,128]{1,0:T(8,128)S(1)} %pad.17), channel_id=1, source_target_pairs={{4,0},{8,4},{12,8},{5,1},{9,5},{13,9},{6,2},{10,6},{14,10},{7,3},{... | collective-permute-start | bytes 49160 | tf_op jit(solution)/shard_map/ppermute | solution.py:40
  90.3 9.4 %collective-permute-start.8 = (f32[64,128]{1,0:T(8,128)S(1)}, f32[64,128]{1,0:T(8,128)S(1)}, u32[]{:S(2)}, u32[]{:S(2)}) collective-permute-start(f32[64,128]{1,0:T(8,128)S(1)} %bitcast.64), channel_id=1, source_target_pairs={{0,1},{1,2},{2,3},{4,5},{5,6},{6,7},{8,9},{9,10},{10,11},{12,13},{... | collective-permute-start | bytes 98312 | tf_op jit(solution)/shard_map/ppermute | solution.py:40
  93.6 5.3 %copy-start.1 = (f32[64,1152]{1,0:T(8,128)}, f32[64,1152]{1,0:T(8,128)S(1)}, u32[]{:S(2)}) copy-start(f32[64,1152]{1,0:T(8,128)S(1)} %reshape.70) | copy-start | bytes 884740
  93.9 5.0 %copy-start.10 = (f32[32,128]{1,0:T(8,128)}, f32[32,128]{1,0:T(8,128)S(1)}, u32[]{:S(2)}) copy-start(f32[32,128]{1,0:T(8,128)S(1)} %collective-permute-done.7.nxhi) | copy-start | bytes 49156
  93.9 5.8 %collective-permute-start.9 = (f32[64,128]{1,0:T(8,128)S(1)}, f32[64,128]{1,0:T(8,128)S(1)}, u32[]{:S(2)}, u32[]{:S(2)}) collective-permute-start(f32[64,128]{1,0:T(8,128)S(1)} %bitcast.63), channel_id=1, source_target_pairs={{1,0},{2,1},{3,2},{5,4},{6,5},{7,6},{9,8},{10,9},{11,10},{13,12},{... | collective-permute-start | bytes 98312 | tf_op jit(solution)/shard_map/ppermute | solution.py:40
  (9 other events, 5.5 us)
